TPU v7x, 16 devices: a whole 2x2x2 slice. The times are simulated.
16 devices in a mesh: dp: 4 (over z, y), cp: 4 (over x, core).
Axes of the slice: x: 2, y: 2, z: 2, core: 2. Of those that a mesh axis runs over, the one named last changes fastest.
Arguments:
- x_in: bfloat16 [4, 4096, 1152], P('dp', 'cp'), parts along dimension 0
- positions: int32 [4, 4096], P('dp', 'cp'), parts along dimension 0
- dy_out: bfloat16 [4, 4096, 1152], P('dp', 'cp'), parts along dimension 0
- w_query: bfloat16 [1152, 4, 256], replicated
- w_key: bfloat16 [1152, 1, 256], replicated
- w_value: bfloat16 [1152, 1, 256], replicated
- w_out: bfloat16 [4, 256, 1152], replicated
- w_pre: float32 [1152], replicated
- w_post: float32 [1152], replicated
Outputs:
- output 1: bfloat16 [4, 4096, 1152], P('dp', 'cp'), parts along dimension 0
- output 2: bfloat16 [4, 4096, 1152], P('dp', 'cp'), parts along dimension 0
- output 3: float32 [4608, 4, 256], P('dp'), parts along dimension 0
- output 4: float32 [4608, 1, 256], P('dp'), parts along dimension 0
- output 5: float32 [4608, 1, 256], P('dp'), parts along dimension 0
- output 6: float32 [16, 256, 1152], P('dp'), parts along dimension 0
- output 7: float32 [4608], P('dp'), parts along dimension 0
- output 8: float32 [4608], P('dp'), parts along dimension 0
There are 4 independent parts. A program takes and returns all parts, laid end to end along the dimension named above; an argument that names none is the same for every part.
All inputs are finite; a program needn't handle non-finite values.
Results may differ from a plain program's by a relative error of at most 0.02.
Values are sent between devices in bfloat16 or wider.
A program may use at most 1 GiB of HBM per device.

v0:
```python
import jax
import jax.numpy as jnp
from jax import lax
from jax.sharding import PartitionSpec as P

NORM_EPS = 1e-6
SOFT_CAP = 50.0
QUERY_SCALE = 144.0
ROPE_BASE = 10000.0


def rms_scale(values, gain):
    return values * lax.rsqrt(jnp.mean(values * values, axis=-1, keepdims=True) + NORM_EPS) * (1.0 + gain)


def rope_tables(positions, head_dim):
    half = head_dim // 2
    inv_freq = ROPE_BASE ** (jnp.arange(half, dtype=jnp.float32) * (-2.0 / head_dim))
    angles = positions.astype(jnp.float32)[:, :, None, None] * inv_freq
    return jnp.cos(angles), jnp.sin(angles)


def rotate(values, cosine, sine):
    half = values.shape[-1] // 2
    first = values[..., :half]
    second = values[..., half:]
    return jnp.concatenate([first * cosine - second * sine, second * cosine + first * sine], axis=-1)


def rotate_back(values, cosine, sine):
    half = values.shape[-1] // 2
    first = values[..., :half]
    second = values[..., half:]
    return jnp.concatenate([first * cosine + second * sine, second * cosine - first * sine], axis=-1)


def solution(mesh):
    groups = mesh.shape["cp"]
    send_pairs = [(source, (source + 1) % groups) for source in range(groups)]
    rows_contract = (((0,), (0,)), ((), ()))
    cols_contract = (((1,), (1,)), ((), ()))

    def local_step(x_in, positions, dy_out, w_query, w_key, w_value, w_out, w_pre, w_post):
        batch, piece_len, model_dim = x_in.shape
        heads, head_dim = w_query.shape[1], w_query.shape[2]
        kv_heads = w_key.shape[1]
        group = heads // kv_heads
        tokens = batch * piece_len
        wq_flat = w_query.reshape(model_dim, heads * head_dim)
        wk_flat = w_key.reshape(model_dim, kv_heads * head_dim)
        wv_flat = w_value.reshape(model_dim, kv_heads * head_dim)
        wo_flat = w_out.reshape(heads * head_dim, model_dim)
        x_float = x_in.astype(jnp.float32).reshape(tokens, model_dim)
        normed, pre_vjp = jax.vjp(rms_scale, x_float, w_pre)
        act_flat = normed.astype(jnp.bfloat16)
        query_proj = jnp.dot(act_flat, wq_flat, preferred_element_type=jnp.float32).astype(jnp.bfloat16)
        key_proj = jnp.dot(act_flat, wk_flat, preferred_element_type=jnp.float32).astype(jnp.bfloat16)
        value_proj = jnp.dot(act_flat, wv_flat, preferred_element_type=jnp.float32).astype(jnp.bfloat16).reshape(batch, piece_len, kv_heads, head_dim)
        cosine, sine = rope_tables(positions, head_dim)
        query_rot = (rotate(query_proj.astype(jnp.float32).reshape(batch, piece_len, heads, head_dim), cosine, sine) * QUERY_SCALE ** -0.5).astype(jnp.bfloat16).reshape(batch, piece_len, kv_heads, group, head_dim)
        key_rot = rotate(key_proj.astype(jnp.float32).reshape(batch, piece_len, kv_heads, head_dim), cosine, sine).astype(jnp.bfloat16)

        def block_scores(key_blk, pos_blk):
            scores = jnp.einsum("bqngd,bknd->bnqgk", query_rot, key_blk, preferred_element_type=jnp.float32)
            capped = SOFT_CAP * jnp.tanh(scores / SOFT_CAP)
            allowed = pos_blk[:, None, None, None, :] <= positions[:, None, :, None, None]
            return jnp.where(allowed, capped, -1e30), capped

        def absorb(state, key_blk, value_blk, pos_blk):
            run_max, run_sum, out_sum = state
            masked, capped = block_scores(key_blk, pos_blk)
            new_max = jnp.maximum(run_max, jnp.max(masked, axis=-1))
            rescale = jnp.exp(run_max - new_max)
            weights = jnp.exp(masked - new_max[..., None])
            run_sum = run_sum * rescale + jnp.sum(weights, axis=-1)
            out_sum = out_sum * rescale[..., None] + jnp.einsum("bnqgk,bknd->bnqgd", weights.astype(jnp.bfloat16), value_blk, preferred_element_type=jnp.float32)
            return new_max, run_sum, out_sum

        stat_shape = (batch, kv_heads, piece_len, group)
        state = absorb((jnp.full(stat_shape, -1e30, jnp.float32), jnp.zeros(stat_shape, jnp.float32), jnp.zeros(stat_shape + (head_dim,), jnp.float32)), key_rot, value_proj, positions)

        def forward_body(step, carry):
            state, key_blk, value_blk, pos_blk = carry
            key_blk, value_blk, pos_blk = lax.ppermute((key_blk, value_blk, pos_blk), "cp", send_pairs)
            return absorb(state, key_blk, value_blk, pos_blk), key_blk, value_blk, pos_blk

        state = lax.fori_loop(1, groups, forward_body, (state, key_rot, value_proj, positions))[0]
        run_max, run_sum, out_sum = state
        log_sum = run_max + jnp.log(run_sum)
        attn_float = jnp.transpose(out_sum / run_sum[..., None], (0, 2, 1, 3, 4))
        attn_flat = attn_float.astype(jnp.bfloat16).reshape(tokens, heads * head_dim)
        z_out = jnp.dot(attn_flat, wo_flat, preferred_element_type=jnp.float32).astype(jnp.bfloat16)
        post_normed, post_vjp = jax.vjp(rms_scale, z_out.astype(jnp.float32), w_post)
        y_out = (x_float + post_normed.astype(jnp.bfloat16).astype(jnp.float32)).astype(jnp.bfloat16)

        dy_float = dy_out.astype(jnp.float32).reshape(tokens, model_dim)
        dz_float, dw_post_part = post_vjp(dy_float)
        dz_out = dz_float.astype(jnp.bfloat16)
        dw_out_part = lax.dot_general(attn_flat, dz_out, rows_contract, preferred_element_type=jnp.float32)
        d_attn = lax.dot_general(dz_out, wo_flat, cols_contract, preferred_element_type=jnp.float32).astype(jnp.bfloat16).reshape(batch, piece_len, kv_heads, group, head_dim)
        row_dot = jnp.transpose(jnp.sum(d_attn.astype(jnp.float32) * attn_float, axis=-1), (0, 2, 1, 3))

        def gradient_block(dquery_sum, key_blk, value_blk, pos_blk, dkey_sum, dvalue_sum):
            masked, capped = block_scores(key_blk, pos_blk)
            soft_probs = jnp.exp(masked - log_sum[..., None])
            d_probs = jnp.einsum("bqngd,bknd->bnqgk", d_attn, value_blk, preferred_element_type=jnp.float32)
            dvalue_sum = dvalue_sum + jnp.einsum("bnqgk,bqngd->bknd", soft_probs.astype(jnp.bfloat16), d_attn, preferred_element_type=jnp.float32)
            d_scores = (soft_probs * (d_probs - row_dot[..., None]) * (1.0 - (capped / SOFT_CAP) ** 2)).astype(jnp.bfloat16)
            dquery_sum = dquery_sum + jnp.einsum("bnqgk,bknd->bqngd", d_scores, key_blk, preferred_element_type=jnp.float32)
            dkey_sum = dkey_sum + jnp.einsum("bnqgk,bqngd->bknd", d_scores, query_rot, preferred_element_type=jnp.float32)
            return dquery_sum, dkey_sum, dvalue_sum

        kv_zeros = jnp.zeros((batch, piece_len, kv_heads, head_dim), jnp.float32)
        dquery_sum, dkey_sum, dvalue_sum = gradient_block(jnp.zeros((batch, piece_len, kv_heads, group, head_dim), jnp.float32), key_rot, value_proj, positions, kv_zeros, kv_zeros)

        def backward_body(step, carry):
            dquery_sum, key_blk, value_blk, pos_blk, dkey_sum, dvalue_sum = carry
            key_blk, value_blk, pos_blk, dkey_sum, dvalue_sum = lax.ppermute((key_blk, value_blk, pos_blk, dkey_sum, dvalue_sum), "cp", send_pairs)
            dquery_sum, dkey_sum, dvalue_sum = gradient_block(dquery_sum, key_blk, value_blk, pos_blk, dkey_sum, dvalue_sum)
            return dquery_sum, key_blk, value_blk, pos_blk, dkey_sum, dvalue_sum

        carry = lax.fori_loop(1, groups, backward_body, (dquery_sum, key_rot, value_proj, positions, dkey_sum, dvalue_sum))
        dkey_rot, dvalue_rot = lax.ppermute((carry[4], carry[5]), "cp", send_pairs)
        dquery = (rotate_back(carry[0].reshape(batch, piece_len, heads, head_dim), cosine, sine) * QUERY_SCALE ** -0.5).astype(jnp.bfloat16).reshape(tokens, heads * head_dim)
        dkey = rotate_back(dkey_rot, cosine, sine).astype(jnp.bfloat16).reshape(tokens, kv_heads * head_dim)
        dvalue = dvalue_rot.astype(jnp.bfloat16).reshape(tokens, kv_heads * head_dim)
        dw_query_part = lax.dot_general(act_flat, dquery, rows_contract, preferred_element_type=jnp.float32)
        dw_key_part = lax.dot_general(act_flat, dkey, rows_contract, preferred_element_type=jnp.float32)
        dw_value_part = lax.dot_general(act_flat, dvalue, rows_contract, preferred_element_type=jnp.float32)
        d_act = (lax.dot_general(dquery, wq_flat, cols_contract, preferred_element_type=jnp.float32) + lax.dot_general(dkey, wk_flat, cols_contract, preferred_element_type=jnp.float32) + lax.dot_general(dvalue, wv_flat, cols_contract, preferred_element_type=jnp.float32))
        dx_float, dw_pre_part = pre_vjp(d_act)
        dx_in = (dy_float + dx_float).astype(jnp.bfloat16).reshape(batch, piece_len, model_dim)
        sums = lax.psum((dw_query_part, dw_key_part, dw_value_part, dw_out_part, dw_pre_part, dw_post_part), "cp")
        return (y_out.reshape(batch, piece_len, model_dim), dx_in, sums[0].reshape(model_dim, heads, head_dim), sums[1].reshape(model_dim, kv_heads, head_dim), sums[2].reshape(model_dim, kv_heads, head_dim), sums[3].reshape(heads, head_dim, model_dim), sums[4], sums[5])

    seq_spec = P("dp", "cp", None)
    in_specs = (seq_spec, P("dp", "cp"), seq_spec, P(), P(), P(), P(), P(), P())
    out_specs = (seq_spec, seq_spec, P("dp", None, None), P("dp", None, None), P("dp", None, None), P("dp", None, None), P("dp"), P("dp"))
    return jax.shard_map(local_step, mesh=mesh, in_specs=in_specs, out_specs=out_specs, check_vma=False)
```

profile of v0, /device:TPU:0, one launch (start us, length us, event | category | flops | bytes accessed | tf_op | source)
XLA Modules:
  0.0 663.2 jit_solution(18198380590718435770)
XLA Ops:
  54.3 11.5 %add_bitcast_fusion = f32[1,1,1024,4,256]{4,2,3,1,0:T(8,128)} fusion(f32[1024,4]{0,1:T(4,128)S(1)} %get-tuple-element.342, f32[1024,4,1024]{0,2,1:T(8,128)} %copy-done.9, f32[1024,4]{0,1:T(4,128)S(1)} %get-tuple-element.344, pred[1024,1024]{0,1:T(8,128)(4,1)S(1)} %broadcast_compare_fusion.2, bf16[1024,256]{1,0:T(8,128)(2,1)} %convolution_convert_fusion.3), kind=kOutput, calls=%fused_computation.100 | convolution fusion | flops 2169503744 | bytes 22577152 | tf_op jit(solution)/shard_map/bnqgk,bknd->bnqgd/dot_general | solution.py:76
  70.6 95.0 %while.42 = (s32[]{:T(128)}, f32[1,1,1024,4]{2,3,1,0:T(4,128)S(1)}, f32[1,1,1024,4]{2,3,1,0:T(4,128)S(1)}, f32[1,1,1024,4,256]{4,2,3,1,0:T(8,128)}, bf16[1,1024,...) while((s32[]{:T(128)}, f32[1,1,1024,4]{2,3,1,0:T(4,128)S(1)}, ...), condition=%wide.region_6.7_spmd, body=%wide.region_3.6_spmd.sunk | while | flops 4356845568 | bytes 72646872 | solution.py:87
  74.0 6.2 collective-permute-done
  94.2 8.7 %bitcast_add_fusion.8 = f32[1,1,1024,4,256]{4,2,3,1,0:T(8,128)} fusion(f32[1,1,1024,4,256]{4,2,3,1,0:T(8,128)} %get-tuple-element.501, f32[1024,4,1024]{0,2,1:T(8,128)S(1)} %get-tuple-element.474, f32[1024,4]{0,1:T(4,128)S(1)} %bitcast.319, pred[1024,1024]{0,1:T(8,128)(4,1)S(1)} %broadcast_compare_fusion.5, f32[1024,4]{0,1:T(4,128)S(1)} %get-tuple-element.475, ...), kind=kOutput, calls=%fused_computation.7.clone.1 | convolution fusion | flops 2170552320 | bytes 26771456 | tf_op jit(solution)/shard_map/while/body/eval_jaxpr/bnqgk,bknd->bnqgd/dot_general | solution.py:76
  105.3 6.2 collective-permute-done
  125.5 8.7 %bitcast_add_fusion.8 = f32[1,1,1024,4,256]{4,2,3,1,0:T(8,128)} fusion(f32[1,1,1024,4,256]{4,2,3,1,0:T(8,128)} %get-tuple-element.501, f32[1024,4,1024]{0,2,1:T(8,128)S(1)} %get-tuple-element.474, f32[1024,4]{0,1:T(4,128)S(1)} %bitcast.319, pred[1024,1024]{0,1:T(8,128)(4,1)S(1)} %broadcast_compare_fusion.5, f32[1024,4]{0,1:T(4,128)S(1)} %get-tuple-element.475, ...), kind=kOutput, calls=%fused_computation.7.clone.1 | convolution fusion | flops 2170552320 | bytes 26771456 | tf_op jit(solution)/shard_map/while/body/eval_jaxpr/bnqgk,bknd->bnqgd/dot_general | solution.py:76
  136.7 6.2 collective-permute-done
  156.9 8.7 %bitcast_add_fusion.8 = f32[1,1,1024,4,256]{4,2,3,1,0:T(8,128)} fusion(f32[1,1,1024,4,256]{4,2,3,1,0:T(8,128)} %get-tuple-element.501, f32[1024,4,1024]{0,2,1:T(8,128)S(1)} %get-tuple-element.474, f32[1024,4]{0,1:T(4,128)S(1)} %bitcast.319, pred[1024,1024]{0,1:T(8,128)(4,1)S(1)} %broadcast_compare_fusion.5, f32[1024,4]{0,1:T(4,128)S(1)} %get-tuple-element.475, ...), kind=kOutput, calls=%fused_computation.7.clone.1 | convolution fusion | flops 2170552320 | bytes 26771456 | tf_op jit(solution)/shard_map/while/body/eval_jaxpr/bnqgk,bknd->bnqgd/dot_general | solution.py:76
  189.6 6.5 fusion.93
  196.1 14.0 %multiply_convert_fusion.1 = bf16[1024,4,1024]{0,2,1:T(8,128)(2,1)} fusion(f32[1024,4,1024]{0,2,1:T(8,128)} %copy-done.9, bf16[1024,4,256]{0,2,1:T(8,128)(2,1)S(1)} %bitcast.315, f32[1024,4]{0,1:T(4,128)S(1)} %fusion.83, f32[1024,4]{0,1:T(4,128)S(1)} %bitcast.350, pred[1024,1024]{0,1:T(8,128)(4,1)S(1)} %copy-done.18, bf16[1024,256]{1,0:T(8,128)(2,1)S(1)} %copy-done.41), kind=kOutput, calls=%fused_computation.44 | convolution fusion | flops 2189426688 | bytes 28868608 | tf_op jit(solution)/shard_map/bqngd,bknd->bnqgk/dot_general | solution.py:106
  210.1 7.0 %convolution_bitcast_fusion.3 = f32[1,1024,1,256]{1,3,2,0:T(8,128)} fusion(bf16[1024,4,1024]{0,2,1:T(8,128)(2,1)} %multiply_convert_fusion.1, f32[1024,4,128]{2,0,1:T(8,128)S(1)} %copy-done.24, f32[1024,4,128]{2,0,1:T(8,128)S(1)} %copy-done.26), kind=kOutput, calls=%fused_computation.120 | convolution fusion | flops 2150629376 | bytes 13631488 | tf_op jit(solution)/shard_map/bnqgk,bqngd->bknd/dot_general | solution.py:110
  233.5 159.8 %while.43 = (s32[]{:T(128)}, f32[1,1024,1,4,256]{4,1,3,2,0:T(8,128)}, bf16[1,1024,1,256]{3,1,2,0:T(8,128)(2,1)}, bf16[1,1024,1,256]{3,1,2,0:T(8,128)(2,1)}, s32[...) while((s32[]{:T(128)}, ...), condition=%wide.region_11.12_spmd, body=%wide.region_10.11_spmd.sunk | while | flops 10802954240 | bytes 124338520 | solution.py:122
  236.5 6.1 collective-permute-done.4
  243.3 8.2 %fusion.208 = f32[1024,4,1024]{2,0,1:T(8,128)} fusion(bf16[1,1024,1,4,256]{4,1,3,2,0:T(8,128)(2,1)S(1)} %get-tuple-element.552, bf16[1,1024,1,256]{3,1,2,0:T(8,128)(2,1)S(1)} %collective-permute-done.3), kind=kOutput, calls=%fused_computation.31.clone.1 | convolution fusion | flops 2147483648 | bytes 19398656 | tf_op jit(solution)/shard_map/while/body/eval_jaxpr/bqngd,bknd->bnqgk/dot_general | solution.py:64
  251.4 11.9 %multiply_convert_fusion.3 = bf16[1024,4,1024]{2,0,1:T(8,128)(2,1)S(1)} fusion(f32[1024,4,1024]{2,0,1:T(8,128)} %fusion.208, f32[1024,4]{0,1:T(4,128)S(1)} %bitcast.348, f32[1024,4]{0,1:T(4,128)S(1)} %bitcast.351, pred[1024,1024]{1,0:T(8,128)(4,1)S(1)} %broadcast_compare_fusion.6, bf16[1,1024,1,4,256]{4,1,3,2,0:T(8,128)(2,1)} %get-tuple-element.554, ...), kind=kOutput, calls=%fused_computation.20.clone.1 | convolution fusion | flops 2189426688 | bytes 28868608 | tf_op jit(solution)/shard_map/while/body/eval_jaxpr/bqngd,bknd->bnqgk/dot_general | solution.py:106
  263.3 6.6 bitcast_add_fusion.9
  276.2 10.8 %fusion.210 = f32[1,1024,1,256]{3,1,2,0:T(8,128)} fusion(f32[1,1024,1,256]{3,1,2,0:T(8,128)} %collective-permute-done.7, bf16[1,1024,1,4,256]{4,1,3,2,0:T(8,128)(2,1)S(1)} %copy-done.22, f32[1024,4,1024]{2,0,1:T(8,128)} %fusion.208, f32[1024,4]{0,1:T(4,128)S(1)} %bitcast.352, pred[1024,1024]{1,0:T(8,128)(4,1)S(1)} %broadcast_compare_fusion.6), kind=kOutput, calls=%fused_computation.36.clone.1 | convolution fusion | flops 2168717312 | bytes 22036480 | tf_op jit(solution)/shard_map/while/body/eval_jaxpr/bnqgk,bqngd->bknd/dot_general | solution.py:107
  289.5 6.1 collective-permute-done.4
  296.3 8.2 %fusion.208 = f32[1024,4,1024]{2,0,1:T(8,128)} fusion(bf16[1,1024,1,4,256]{4,1,3,2,0:T(8,128)(2,1)S(1)} %get-tuple-element.552, bf16[1,1024,1,256]{3,1,2,0:T(8,128)(2,1)S(1)} %collective-permute-done.3), kind=kOutput, calls=%fused_computation.31.clone.1 | convolution fusion | flops 2147483648 | bytes 19398656 | tf_op jit(solution)/shard_map/while/body/eval_jaxpr/bqngd,bknd->bnqgk/dot_general | solution.py:64
  304.5 11.9 %multiply_convert_fusion.3 = bf16[1024,4,1024]{2,0,1:T(8,128)(2,1)S(1)} fusion(f32[1024,4,1024]{2,0,1:T(8,128)} %fusion.208, f32[1024,4]{0,1:T(4,128)S(1)} %bitcast.348, f32[1024,4]{0,1:T(4,128)S(1)} %bitcast.351, pred[1024,1024]{1,0:T(8,128)(4,1)S(1)} %broadcast_compare_fusion.6, bf16[1,1024,1,4,256]{4,1,3,2,0:T(8,128)(2,1)} %get-tuple-element.554, ...), kind=kOutput, calls=%fused_computation.20.clone.1 | convolution fusion | flops 2189426688 | bytes 28868608 | tf_op jit(solution)/shard_map/while/body/eval_jaxpr/bqngd,bknd->bnqgk/dot_general | solution.py:106
  316.4 6.6 bitcast_add_fusion.9
  329.3 10.8 %fusion.210 = f32[1,1024,1,256]{3,1,2,0:T(8,128)} fusion(f32[1,1024,1,256]{3,1,2,0:T(8,128)} %collective-permute-done.7, bf16[1,1024,1,4,256]{4,1,3,2,0:T(8,128)(2,1)S(1)} %copy-done.22, f32[1024,4,1024]{2,0,1:T(8,128)} %fusion.208, f32[1024,4]{0,1:T(4,128)S(1)} %bitcast.352, pred[1024,1024]{1,0:T(8,128)(4,1)S(1)} %broadcast_compare_fusion.6), kind=kOutput, calls=%fused_computation.36.clone.1 | convolution fusion | flops 2168717312 | bytes 22036480 | tf_op jit(solution)/shard_map/while/body/eval_jaxpr/bnqgk,bqngd->bknd/dot_general | solution.py:107
  342.6 6.1 collective-permute-done.4
  349.4 8.2 %fusion.208 = f32[1024,4,1024]{2,0,1:T(8,128)} fusion(bf16[1,1024,1,4,256]{4,1,3,2,0:T(8,128)(2,1)S(1)} %get-tuple-element.552, bf16[1,1024,1,256]{3,1,2,0:T(8,128)(2,1)S(1)} %collective-permute-done.3), kind=kOutput, calls=%fused_computation.31.clone.1 | convolution fusion | flops 2147483648 | bytes 19398656 | tf_op jit(solution)/shard_map/while/body/eval_jaxpr/bqngd,bknd->bnqgk/dot_general | solution.py:64
  357.6 11.9 %multiply_convert_fusion.3 = bf16[1024,4,1024]{2,0,1:T(8,128)(2,1)S(1)} fusion(f32[1024,4,1024]{2,0,1:T(8,128)} %fusion.208, f32[1024,4]{0,1:T(4,128)S(1)} %bitcast.348, f32[1024,4]{0,1:T(4,128)S(1)} %bitcast.351, pred[1024,1024]{1,0:T(8,128)(4,1)S(1)} %broadcast_compare_fusion.6, bf16[1,1024,1,4,256]{4,1,3,2,0:T(8,128)(2,1)} %get-tuple-element.554, ...), kind=kOutput, calls=%fused_computation.20.clone.1 | convolution fusion | flops 2189426688 | bytes 28868608 | tf_op jit(solution)/shard_map/while/body/eval_jaxpr/bqngd,bknd->bnqgk/dot_general | solution.py:106
  369.5 6.6 bitcast_add_fusion.9
  382.4 10.8 %fusion.210 = f32[1,1024,1,256]{3,1,2,0:T(8,128)} fusion(f32[1,1024,1,256]{3,1,2,0:T(8,128)} %collective-permute-done.7, bf16[1,1024,1,4,256]{4,1,3,2,0:T(8,128)(2,1)S(1)} %copy-done.22, f32[1024,4,1024]{2,0,1:T(8,128)} %fusion.208, f32[1024,4]{0,1:T(4,128)S(1)} %bitcast.352, pred[1024,1024]{1,0:T(8,128)(4,1)S(1)} %broadcast_compare_fusion.6), kind=kOutput, calls=%fused_computation.36.clone.1 | convolution fusion | flops 2168717312 | bytes 22036480 | tf_op jit(solution)/shard_map/while/body/eval_jaxpr/bnqgk,bqngd->bknd/dot_general | solution.py:107
  409.1 6.8 %fusion.151 = f32[1152,1024]{0,1:T(8,128)} fusion(bf16[1024,1024]{0,1:T(8,128)(2,1)} %bitcast.329, bf16[1,1024,1152]{2,1,0:T(8,128)(2,1)S(1)} %copy-done.7, f32[1152]{0:T(1024)S(1)} %copy-done.43, f32[1024]{0:T(1024)S(1)} %copy-done.47), kind=kOutput, calls=%fused_computation.193 | convolution fusion | flops 2420637696 | bytes 9183744 | tf_op jit(solution)/shard_map/dot_general | solution.py:127
  415.9 6.5 copy.63
  422.4 7.3 %fusion.158 = f32[1024,1152]{1,0:T(8,128)} fusion(bf16[1024,1024]{0,1:T(8,128)(2,1)} %bitcast.328, bf16[1024,1152]{1,0:T(8,128)(2,1)} %copy-done.20), kind=kOutput, calls=%fused_computation.196 | convolution fusion | flops 2415919104 | bytes 9175040 | tf_op jit(solution)/shard_map/dot_general | solution.py:99
  448.8 11.9 %all-reduce = (f32[1152]{0:T(1024)}, f32[1152]{0:T(1024)}) all-reduce(f32[1152]{0:T(1024)S(1)} %get-tuple-element.272, f32[1152]{0:T(1024)S(1)} %copy-done.50), channel_id=1, replica_groups=mesh['dp'=4,'cp'=4] {'cp'}, use_global_device_ids=true, to_apply=%region_18.19 | all-reduce | flops 2304 | bytes 18432 | tf_op jit(solution)/shard_map/psum | solution.py:133
  465.5 176.6 %all-reduce.4.cloned.1.call-done = (f32[1152,4,256]{2,1,0:T(4,128)}, f32[1152,1,256]{2,0,1:T(8,128)}, f32[1152,1,256]{2,0,1:T(8,128)}, f32[4,256,1152]{2,1,0:T(8,128)}) async-done(((f32[1152,4,256]{2,1,0:T(4,128)}, f32[1152,1,256]{2,0,1:T(8,128)}, f32[1152,1,256]{2,0,1:T(8,128)}, f32[4,256,1152]{2,1,0:T(8,128)}), (f32[1152,4,256]{2,1,0:T(4,128)}, f32[1152,1,256]{2,0,1:T(8,128)}, f32[1152,1,256]{2,0,1:T(8,128)}, ...) | async-done | bytes 11796496 | tf_op jit(solution)/shard_map/psum | solution.py:133
  (278 shorter events, 224.2 us)
Async XLA Ops:
  7.2 166.6 %copy-start = (bf16[4,256,1152]{2,1,0:T(8,128)(2,1)S(1)}, bf16[4,256,1152]{2,1,0:T(8,128)(2,1)}, u32[]{:S(2)}) copy-start(bf16[4,256,1152]{2,1,0:T(8,128)(2,1)} %param.19) | copy-start | bytes 7077892
  7.2 634.9 %all-reduce.4.cloned.1.call-start = ((), (), s32[]{:S(2)}) async-start(), calls=%async_computation | async-start | bytes 23592960 | tf_op jit(solution)/shard_map/psum | solution.py:133
  7.3 23.5 %copy-start.52 = (f32[128]{0:T(128)}, f32[128]{0:T(128)S(1)}, u32[]{:S(2)}) copy-start(f32[128]{0:T(128)S(1)} %multiply_power_fusion) | copy-start | bytes 1540
  8.1 22.7 %copy-start.44 = (f32[1,1024]{1,0:T(1,128)}, f32[1,1024]{1,0:T(1,128)S(1)}, u32[]{:S(2)}) copy-start(f32[1,1024]{1,0:T(1,128)S(1)} %convert_element_type.168) | copy-start | bytes 12292
  11.2 31.3 %copy-start.46 = (f32[1024]{0:T(1024)}, f32[1024]{0:T(1024)S(1)}, u32[]{:S(2)}) copy-start(f32[1024]{0:T(1024)S(1)} %fusion.133) | copy-start | bytes 12292
  11.9 30.6 %copy-start.42 = (f32[1152]{0:T(1024)}, f32[1152]{0:T(1024)S(1)}, u32[]{:S(2)}) copy-start(f32[1152]{0:T(1024)S(1)} %broadcast_add_fusion.1) | copy-start | bytes 13828
  70.6 10.2 %collective-permute-start.1 = (bf16[1,1024,1,256]{3,1,2,0:T(8,128)(2,1)}, bf16[1,1024,1,256]{3,1,2,0:T(8,128)(2,1)S(1)}, u32[]{:S(2)}, u32[]{:S(2)}) collective-permute-start(bf16[1,1024,1,256]{3,1,2,0:T(8,128)(2,1)} %get-tuple-element.502), channel_id=1, source_target_pairs={{0,1},{1,2},{2,3},{3,0},{4,5},{5,6},{6,7},{7,4},{8,9},{9,10},{10,1... | collective-permute-start | bytes 1572872 | tf_op jit(solution)/shard_map/while/body/eval_jaxpr/ppermute | solution.py:84
  71.3 8.8 %collective-permute-start = (s32[1,1024]{1,0:T(1,128)S(1)}, s32[1,1024]{1,0:T(1,128)S(1)}, u32[]{:S(2)}, u32[]{:S(2)}) collective-permute-start(s32[1,1024]{1,0:T(1,128)S(1)} %get-tuple-element.504), channel_id=1, source_target_pairs={{0,1},{1,2},{2,3},{3,0},{4,5},{5,6},{6,7},{7,4},{8,9},{9,10},{10,1... | collective-permute-start | bytes 12296 | tf_op jit(solution)/shard_map/while/body/eval_jaxpr/ppermute | solution.py:84
  73.9 19.4 %collective-permute-start.2 = (bf16[1,1024,1,256]{3,1,2,0:T(8,128)(2,1)}, bf16[1,1024,1,256]{3,1,2,0:T(8,128)(2,1)S(1)}, u32[]{:S(2)}, u32[]{:S(2)}) collective-permute-start(bf16[1,1024,1,256]{3,1,2,0:T(8,128)(2,1)} %get-tuple-element.503), channel_id=1, source_target_pairs={{0,1},{1,2},{2,3},{3,0},{4,5},{5,6},{6,7},{7,4},{8,9},{9,10},{10,1... | collective-permute-start | bytes 1572872 | tf_op jit(solution)/shard_map/while/body/eval_jaxpr/ppermute | solution.py:84
  102.9 9.3 %collective-permute-start.1 = (bf16[1,1024,1,256]{3,1,2,0:T(8,128)(2,1)}, bf16[1,1024,1,256]{3,1,2,0:T(8,128)(2,1)S(1)}, u32[]{:S(2)}, u32[]{:S(2)}) collective-permute-start(bf16[1,1024,1,256]{3,1,2,0:T(8,128)(2,1)} %get-tuple-element.502), channel_id=1, source_target_pairs={{0,1},{1,2},{2,3},{3,0},{4,5},{5,6},{6,7},{7,4},{8,9},{9,10},{10,1... | collective-permute-start | bytes 1572872 | tf_op jit(solution)/shard_map/while/body/eval_jaxpr/ppermute | solution.py:84
  102.9 8.6 %collective-permute-start = (s32[1,1024]{1,0:T(1,128)S(1)}, s32[1,1024]{1,0:T(1,128)S(1)}, u32[]{:S(2)}, u32[]{:S(2)}) collective-permute-start(s32[1,1024]{1,0:T(1,128)S(1)} %get-tuple-element.504), channel_id=1, source_target_pairs={{0,1},{1,2},{2,3},{3,0},{4,5},{5,6},{6,7},{7,4},{8,9},{9,10},{10,1... | collective-permute-start | bytes 12296 | tf_op jit(solution)/shard_map/while/body/eval_jaxpr/ppermute | solution.py:84
  105.3 19.4 %collective-permute-start.2 = (bf16[1,1024,1,256]{3,1,2,0:T(8,128)(2,1)}, bf16[1,1024,1,256]{3,1,2,0:T(8,128)(2,1)S(1)}, u32[]{:S(2)}, u32[]{:S(2)}) collective-permute-start(bf16[1,1024,1,256]{3,1,2,0:T(8,128)(2,1)} %get-tuple-element.503), channel_id=1, source_target_pairs={{0,1},{1,2},{2,3},{3,0},{4,5},{5,6},{6,7},{7,4},{8,9},{9,10},{10,1... | collective-permute-start | bytes 1572872 | tf_op jit(solution)/shard_map/while/body/eval_jaxpr/ppermute | solution.py:84
  134.2 9.3 %collective-permute-start.1 = (bf16[1,1024,1,256]{3,1,2,0:T(8,128)(2,1)}, bf16[1,1024,1,256]{3,1,2,0:T(8,128)(2,1)S(1)}, u32[]{:S(2)}, u32[]{:S(2)}) collective-permute-start(bf16[1,1024,1,256]{3,1,2,0:T(8,128)(2,1)} %get-tuple-element.502), channel_id=1, source_target_pairs={{0,1},{1,2},{2,3},{3,0},{4,5},{5,6},{6,7},{7,4},{8,9},{9,10},{10,1... | collective-permute-start | bytes 1572872 | tf_op jit(solution)/shard_map/while/body/eval_jaxpr/ppermute | solution.py:84
  134.2 8.6 %collective-permute-start = (s32[1,1024]{1,0:T(1,128)S(1)}, s32[1,1024]{1,0:T(1,128)S(1)}, u32[]{:S(2)}, u32[]{:S(2)}) collective-permute-start(s32[1,1024]{1,0:T(1,128)S(1)} %get-tuple-element.504), channel_id=1, source_target_pairs={{0,1},{1,2},{2,3},{3,0},{4,5},{5,6},{6,7},{7,4},{8,9},{9,10},{10,1... | collective-permute-start | bytes 12296 | tf_op jit(solution)/shard_map/while/body/eval_jaxpr/ppermute | solution.py:84
  136.6 19.4 %collective-permute-start.2 = (bf16[1,1024,1,256]{3,1,2,0:T(8,128)(2,1)}, bf16[1,1024,1,256]{3,1,2,0:T(8,128)(2,1)S(1)}, u32[]{:S(2)}, u32[]{:S(2)}) collective-permute-start(bf16[1,1024,1,256]{3,1,2,0:T(8,128)(2,1)} %get-tuple-element.503), channel_id=1, source_target_pairs={{0,1},{1,2},{2,3},{3,0},{4,5},{5,6},{6,7},{7,4},{8,9},{9,10},{10,1... | collective-permute-start | bytes 1572872 | tf_op jit(solution)/shard_map/while/body/eval_jaxpr/ppermute | solution.py:84
  233.9 9.4 %collective-permute-start.3 = (bf16[1,1024,1,256]{3,1,2,0:T(8,128)(2,1)}, bf16[1,1024,1,256]{3,1,2,0:T(8,128)(2,1)S(1)}, u32[]{:S(2)}, u32[]{:S(2)}) collective-permute-start(bf16[1,1024,1,256]{3,1,2,0:T(8,128)(2,1)} %get-tuple-element.533), channel_id=1, source_target_pairs={{0,1},{1,2},{2,3},{3,0},{4,5},{5,6},{6,7},{7,4},{8,9},{9,10},{10,1... | collective-permute-start | bytes 1572872 | tf_op jit(solution)/shard_map/while/body/eval_jaxpr/ppermute | solution.py:118
  234.0 8.6 %collective-permute-start.4 = (s32[1,1024]{1,0:T(1,128)S(1)}, s32[1,1024]{1,0:T(1,128)S(1)}, u32[]{:S(2)}, u32[]{:S(2)}) collective-permute-start(s32[1,1024]{1,0:T(1,128)S(1)} %get-tuple-element.535), channel_id=1, source_target_pairs={{0,1},{1,2},{2,3},{3,0},{4,5},{5,6},{6,7},{7,4},{8,9},{9,10},{10,1... | collective-permute-start | bytes 12296 | tf_op jit(solution)/shard_map/while/body/eval_jaxpr/ppermute | solution.py:118
  236.4 15.1 %collective-permute-start.5 = (bf16[1,1024,1,256]{3,1,2,0:T(8,128)(2,1)}, bf16[1,1024,1,256]{3,1,2,0:T(8,128)(2,1)S(1)}, u32[]{:S(2)}, u32[]{:S(2)}) collective-permute-start(bf16[1,1024,1,256]{3,1,2,0:T(8,128)(2,1)} %get-tuple-element.534), channel_id=1, source_target_pairs={{0,1},{1,2},{2,3},{3,0},{4,5},{5,6},{6,7},{7,4},{8,9},{9,10},{10,1... | collective-permute-start | bytes 1572872 | tf_op jit(solution)/shard_map/while/body/eval_jaxpr/ppermute | solution.py:118
  236.4 35.1 %collective-permute-start.6 = (f32[1,1024,1,256]{3,1,2,0:T(8,128)}, f32[1,1024,1,256]{3,1,2,0:T(8,128)}, u32[]{:S(2)}, u32[]{:S(2)}) collective-permute-start(f32[1,1024,1,256]{3,1,2,0:T(8,128)} %get-tuple-element.536), channel_id=1, source_target_pairs={{0,1},{1,2},{2,3},{3,0},{4,5},{5,6},{6,7},{7,4},{8,9},{9,10},{10,1... | collective-permute-start | bytes 3145736 | tf_op jit(solution)/shard_map/while/body/eval_jaxpr/ppermute | solution.py:118
  236.5 39.8 %collective-permute-start.7 = (f32[1,1024,1,256]{3,1,2,0:T(8,128)}, f32[1,1024,1,256]{3,1,2,0:T(8,128)}, u32[]{:S(2)}, u32[]{:S(2)}) collective-permute-start(f32[1,1024,1,256]{3,1,2,0:T(8,128)} %get-tuple-element.537), channel_id=1, source_target_pairs={{0,1},{1,2},{2,3},{3,0},{4,5},{5,6},{6,7},{7,4},{8,9},{9,10},{10,1... | collective-permute-start | bytes 3145736 | tf_op jit(solution)/shard_map/while/body/eval_jaxpr/ppermute | solution.py:118
  287.0 9.3 %collective-permute-start.3 = (bf16[1,1024,1,256]{3,1,2,0:T(8,128)(2,1)}, bf16[1,1024,1,256]{3,1,2,0:T(8,128)(2,1)S(1)}, u32[]{:S(2)}, u32[]{:S(2)}) collective-permute-start(bf16[1,1024,1,256]{3,1,2,0:T(8,128)(2,1)} %get-tuple-element.533), channel_id=1, source_target_pairs={{0,1},{1,2},{2,3},{3,0},{4,5},{5,6},{6,7},{7,4},{8,9},{9,10},{10,1... | collective-permute-start | bytes 1572872 | tf_op jit(solution)/shard_map/while/body/eval_jaxpr/ppermute | solution.py:118
  287.0 8.6 %collective-permute-start.4 = (s32[1,1024]{1,0:T(1,128)S(1)}, s32[1,1024]{1,0:T(1,128)S(1)}, u32[]{:S(2)}, u32[]{:S(2)}) collective-permute-start(s32[1,1024]{1,0:T(1,128)S(1)} %get-tuple-element.535), channel_id=1, source_target_pairs={{0,1},{1,2},{2,3},{3,0},{4,5},{5,6},{6,7},{7,4},{8,9},{9,10},{10,1... | collective-permute-start | bytes 12296 | tf_op jit(solution)/shard_map/while/body/eval_jaxpr/ppermute | solution.py:118
  289.4 15.1 %collective-permute-start.5 = (bf16[1,1024,1,256]{3,1,2,0:T(8,128)(2,1)}, bf16[1,1024,1,256]{3,1,2,0:T(8,128)(2,1)S(1)}, u32[]{:S(2)}, u32[]{:S(2)}) collective-permute-start(bf16[1,1024,1,256]{3,1,2,0:T(8,128)(2,1)} %get-tuple-element.534), channel_id=1, source_target_pairs={{0,1},{1,2},{2,3},{3,0},{4,5},{5,6},{6,7},{7,4},{8,9},{9,10},{10,1... | collective-permute-start | bytes 1572872 | tf_op jit(solution)/shard_map/while/body/eval_jaxpr/ppermute | solution.py:118
  289.4 35.1 %collective-permute-start.6 = (f32[1,1024,1,256]{3,1,2,0:T(8,128)}, f32[1,1024,1,256]{3,1,2,0:T(8,128)}, u32[]{:S(2)}, u32[]{:S(2)}) collective-permute-start(f32[1,1024,1,256]{3,1,2,0:T(8,128)} %get-tuple-element.536), channel_id=1, source_target_pairs={{0,1},{1,2},{2,3},{3,0},{4,5},{5,6},{6,7},{7,4},{8,9},{9,10},{10,1... | collective-permute-start | bytes 3145736 | tf_op jit(solution)/shard_map/while/body/eval_jaxpr/ppermute | solution.py:118
  289.5 39.8 %collective-permute-start.7 = (f32[1,1024,1,256]{3,1,2,0:T(8,128)}, f32[1,1024,1,256]{3,1,2,0:T(8,128)}, u32[]{:S(2)}, u32[]{:S(2)}) collective-permute-start(f32[1,1024,1,256]{3,1,2,0:T(8,128)} %get-tuple-element.537), channel_id=1, source_target_pairs={{0,1},{1,2},{2,3},{3,0},{4,5},{5,6},{6,7},{7,4},{8,9},{9,10},{10,1... | collective-permute-start | bytes 3145736 | tf_op jit(solution)/shard_map/while/body/eval_jaxpr/ppermute | solution.py:118
  340.1 9.3 %collective-permute-start.3 = (bf16[1,1024,1,256]{3,1,2,0:T(8,128)(2,1)}, bf16[1,1024,1,256]{3,1,2,0:T(8,128)(2,1)S(1)}, u32[]{:S(2)}, u32[]{:S(2)}) collective-permute-start(bf16[1,1024,1,256]{3,1,2,0:T(8,128)(2,1)} %get-tuple-element.533), channel_id=1, source_target_pairs={{0,1},{1,2},{2,3},{3,0},{4,5},{5,6},{6,7},{7,4},{8,9},{9,10},{10,1... | collective-permute-start | bytes 1572872 | tf_op jit(solution)/shard_map/while/body/eval_jaxpr/ppermute | solution.py:118
  340.1 8.6 %collective-permute-start.4 = (s32[1,1024]{1,0:T(1,128)S(1)}, s32[1,1024]{1,0:T(1,128)S(1)}, u32[]{:S(2)}, u32[]{:S(2)}) collective-permute-start(s32[1,1024]{1,0:T(1,128)S(1)} %get-tuple-element.535), channel_id=1, source_target_pairs={{0,1},{1,2},{2,3},{3,0},{4,5},{5,6},{6,7},{7,4},{8,9},{9,10},{10,1... | collective-permute-start | bytes 12296 | tf_op jit(solution)/shard_map/while/body/eval_jaxpr/ppermute | solution.py:118
  342.5 15.1 %collective-permute-start.5 = (bf16[1,1024,1,256]{3,1,2,0:T(8,128)(2,1)}, bf16[1,1024,1,256]{3,1,2,0:T(8,128)(2,1)S(1)}, u32[]{:S(2)}, u32[]{:S(2)}) collective-permute-start(bf16[1,1024,1,256]{3,1,2,0:T(8,128)(2,1)} %get-tuple-element.534), channel_id=1, source_target_pairs={{0,1},{1,2},{2,3},{3,0},{4,5},{5,6},{6,7},{7,4},{8,9},{9,10},{10,1... | collective-permute-start | bytes 1572872 | tf_op jit(solution)/shard_map/while/body/eval_jaxpr/ppermute | solution.py:118
  342.5 35.1 %collective-permute-start.6 = (f32[1,1024,1,256]{3,1,2,0:T(8,128)}, f32[1,1024,1,256]{3,1,2,0:T(8,128)}, u32[]{:S(2)}, u32[]{:S(2)}) collective-permute-start(f32[1,1024,1,256]{3,1,2,0:T(8,128)} %get-tuple-element.536), channel_id=1, source_target_pairs={{0,1},{1,2},{2,3},{3,0},{4,5},{5,6},{6,7},{7,4},{8,9},{9,10},{10,1... | collective-permute-start | bytes 3145736 | tf_op jit(solution)/shard_map/while/body/eval_jaxpr/ppermute | solution.py:118
  342.5 39.8 %collective-permute-start.7 = (f32[1,1024,1,256]{3,1,2,0:T(8,128)}, f32[1,1024,1,256]{3,1,2,0:T(8,128)}, u32[]{:S(2)}, u32[]{:S(2)}) collective-permute-start(f32[1,1024,1,256]{3,1,2,0:T(8,128)} %get-tuple-element.537), channel_id=1, source_target_pairs={{0,1},{1,2},{2,3},{3,0},{4,5},{5,6},{6,7},{7,4},{8,9},{9,10},{10,1... | collective-permute-start | bytes 3145736 | tf_op jit(solution)/shard_map/while/body/eval_jaxpr/ppermute | solution.py:118
  395.8 37.0 %collective-permute-start.8 = (f32[1,1024,1,256]{1,3,2,0:T(8,128)}, f32[1,1024,1,256]{1,3,2,0:T(8,128)S(1)}, u32[]{:S(2)}, u32[]{:S(2)}) collective-permute-start(f32[1,1024,1,256]{1,3,2,0:T(8,128)} %copy.62), channel_id=1, source_target_pairs={{0,1},{1,2},{2,3},{3,0},{4,5},{5,6},{6,7},{7,4},{8,9},{9,10},{10,1... | collective-permute-start | bytes 3145736 | tf_op jit(solution)/shard_map/ppermute | solution.py:123
  397.9 31.8 %collective-permute-start.9 = (bf16[1,1024,1,256]{3,1,2,0:T(8,128)(2,1)}, bf16[1,1024,1,256]{3,1,2,0:T(8,128)(2,1)}, u32[]{:S(2)}, u32[]{:S(2)}) collective-permute-start(bf16[1,1024,1,256]{3,1,2,0:T(8,128)(2,1)} %convert.64), channel_id=1, source_target_pairs={{0,1},{1,2},{2,3},{3,0},{4,5},{5,6},{6,7},{7,4},{8,9},{9,10},{10,1... | collective-permute-start | bytes 1572872 | tf_op jit(solution)/shard_map/ppermute | solution.py:123
  (58 other events, 352.6 us)
Sparse Core Ops, SparseCore 0:
  437.6 204.4 all-reduce.3
where the time goes:
time: 670 us; the launch traced here: 663 us
  matrix products  264 us (39%)
  waiting for transfers between devices  214 us (32%)
  local copies, waits for them, and re-layouts  73.1 us (11%)
  other arithmetic  66.1 us (10%)
  starting transfers between devices  18.3 us (3%)
  between operations  15 us (2%)
  blocking collectives  11.9 us (2%)
    psum x1, waiting for transfers between devices, local_step(): lax.psum((dw_query_part, dw_key_part, dw_value_part, dw_out_part, dw_pre_...  177 us
    dot_general x4, matrix products, gradient_block(): jnp.einsum('bqngd,bknd->bnqgk', d_attn, value_blk, preferred_element_type...  49.7 us
    dot_general x7, matrix products, block_scores(): jnp.einsum('bqngd,bknd->bnqgk', query_rot, key_blk, preferred_element_typ...  47.4 us
    dot_general x4, matrix products, gradient_block(): jnp.einsum('bnqgk,bqngd->bknd', soft_probs.astype(jnp.bfloat16), d_attn,...  38.8 us
    dot_general x4, matrix products, absorb(): jnp.einsum('bnqgk,bknd->bnqgd', weights.astype(jnp.bfloat16), value_blk,...  37.6 us
    unnamed x131, local copies, waits for them, and re-layouts  28.5 us
    dot_general x4, matrix products, gradient_block(): jnp.einsum('bnqgk,bknd->bqngd', d_scores, key_blk, preferred_element_type...  24.1 us
    reduce_sum x4, other arithmetic, absorb(): run_sum = run_sum * rescale + jnp.sum(weights, axis=-1)  22.3 us
  transfers between devices with their start and end apart: 27, of which 7 were waited for; matrix products, arithmetic and copies ran while one was open for 29% of the time, Pallas kernels for 0%

commit v1 on v0

v1 whole, which is shorter than its diff:
```python
import functools
import math

import jax
import jax.numpy as jnp
from jax import lax
from jax.experimental import pallas as pl
from jax.experimental.pallas import tpu as pltpu
from jax.sharding import PartitionSpec as P

NORM_EPS = 1e-6
SOFT_CAP = 50.0
QUERY_SCALE = 144.0
ROPE_BASE = 10000.0
LOG2E = math.log2(math.e)
CAP2 = SOFT_CAP * LOG2E
INV_CAP = 1.0 / SOFT_CAP

F32 = jnp.float32
BF16 = jnp.bfloat16
VMEM_LIMIT = 60 * 1024 * 1024

NT = (((1,), (1,)), ((), ()))
NN = (((1,), (0,)), ((), ()))


def dot(a, b, dims=NN):
    return lax.dot_general(a, b, dims, preferred_element_type=F32)


def params():
    return pltpu.CompilerParams(vmem_limit_bytes=VMEM_LIMIT)


def whole(shape):
    zeros = (0,) * len(shape)
    return pl.BlockSpec(shape, lambda *_: zeros)


def cost(flops, nbytes, trans=0):
    return pl.CostEstimate(flops=int(flops), bytes_accessed=int(nbytes), transcendentals=int(trans))


def kv_kernel(x_ref, gain_ref, wk_ref, wv_ref, cos_ref, sin_ref, a_ref, at_ref, kv_ref):
    half = cos_ref.shape[1]
    x = x_ref[...].astype(F32)
    rstd = lax.rsqrt(jnp.mean(x * x, axis=-1, keepdims=True) + NORM_EPS)
    a = (x * rstd * (1.0 + gain_ref[...])).astype(BF16)
    a_ref[...] = a
    at_ref[...] = a.T
    k = dot(a, wk_ref[...]).astype(BF16).astype(F32)
    first, second = k[:, :half], k[:, half:]
    cosine, sine = cos_ref[...], sin_ref[...]
    kv_ref[0, :, :half] = (first * cosine - second * sine).astype(BF16)
    kv_ref[0, :, half:] = (second * cosine + first * sine).astype(BF16)
    kv_ref[1] = dot(a, wv_ref[...]).astype(BF16)


def project_kv(x, gain, wk, wv, cosine, sine):
    tokens, dim = x.shape
    hd = wk.shape[1]
    half = hd // 2
    bt = 256
    return pl.pallas_call(
        kv_kernel,
        grid=(tokens // bt,),
        in_specs=[
            pl.BlockSpec((bt, dim), lambda i: (i, 0)),
            whole((1, dim)),
            whole((dim, hd)),
            whole((dim, hd)),
            pl.BlockSpec((bt, half), lambda i: (i, 0)),
            pl.BlockSpec((bt, half), lambda i: (i, 0)),
        ],
        out_specs=[
            pl.BlockSpec((bt, dim), lambda i: (i, 0)),
            pl.BlockSpec((dim, bt), lambda i: (0, i)),
            pl.BlockSpec((2, bt, hd), lambda i: (0, i, 0)),
        ],
        out_shape=[
            jax.ShapeDtypeStruct((tokens, dim), BF16),
            jax.ShapeDtypeStruct((dim, tokens), BF16),
            jax.ShapeDtypeStruct((2, tokens, hd), BF16),
        ],
        compiler_params=params(),
        cost_estimate=cost(4 * tokens * dim * hd, 6 * tokens * dim),
        name="project_kv",
    )(x, gain, wk, wv, cosine, sine)


def q_kernel(a_ref, wq_ref, cos_ref, sin_ref, q_ref):
    heads, _, hd = q_ref.shape
    half = hd // 2
    cosine, sine = cos_ref[...], sin_ref[...]
    a = a_ref[...]
    scale = QUERY_SCALE ** -0.5
    for h in range(heads):
        q = dot(a, wq_ref[:, h * hd:(h + 1) * hd]).astype(BF16).astype(F32)
        first, second = q[:, :half], q[:, half:]
        q_ref[h, :, :half] = ((first * cosine - second * sine) * scale).astype(BF16)
        q_ref[h, :, half:] = ((second * cosine + first * sine) * scale).astype(BF16)


def project_q(a, wq, cosine, sine, heads):
    tokens, dim = a.shape
    hd = wq.shape[1] // heads
    half = hd // 2
    bt = 256
    return pl.pallas_call(
        q_kernel,
        grid=(tokens // bt,),
        in_specs=[
            pl.BlockSpec((bt, dim), lambda i: (i, 0)),
            whole(wq.shape),
            pl.BlockSpec((bt, half), lambda i: (i, 0)),
            pl.BlockSpec((bt, half), lambda i: (i, 0)),
        ],
        out_specs=pl.BlockSpec((heads, bt, hd), lambda i: (0, i, 0)),
        out_shape=jax.ShapeDtypeStruct((heads, tokens, hd), BF16),
        compiler_params=params(),
        cost_estimate=cost(2 * tokens * dim * heads * hd, 6 * tokens * dim),
        name="project_q",
    )(a, wq, cosine, sine)


def forward_tile(q_ref, acc_ref, sum_ref, k, v, masked):
    heads, bq, _ = q_ref.shape
    bk = k.shape[0]
    if masked:
        keep = lax.broadcasted_iota(jnp.int32, (bq, bk), 1) <= lax.broadcasted_iota(jnp.int32, (bq, bk), 0)
    for h in range(heads):
        s = dot(q_ref[h], k, NT)
        p = jnp.exp2(jnp.tanh(s * INV_CAP) * CAP2)
        if masked:
            p = jnp.where(keep, p, 0.0)
        part = p[:, 0:128]
        for c in range(128, bk, 128):
            part = part + p[:, c:c + 128]
        sum_ref[h] += part
        acc_ref[h] += dot(p.astype(BF16), v)


def forward_local_kernel(idx_ref, q_ref, own_ref, near_ref, acc_ref, sum_ref):
    bq = q_ref.shape[1]
    tokens = own_ref.shape[1]
    i = pl.program_id(0)
    acc_ref[...] = jnp.zeros_like(acc_ref)
    sum_ref[...] = jnp.zeros_like(sum_ref)

    def keys(ref, start, size):
        rows = pl.ds(pl.multiple_of(start, 128), size)
        return ref[0, rows, :], ref[1, rows, :]

    forward_tile(q_ref, acc_ref, sum_ref, *keys(own_ref, i * bq, bq), True)

    def own_step(j, _):
        forward_tile(q_ref, acc_ref, sum_ref, *keys(own_ref, j * bq, bq), False)
        return 0

    lax.fori_loop(0, i, own_step, 0)

    @pl.when(idx_ref[0] % 2 == 1)
    def _():
        def near_step(j, _):
            forward_tile(q_ref, acc_ref, sum_ref, *keys(near_ref, j * 512, 512), False)
            return 0

        lax.fori_loop(0, tokens // 512, near_step, 0)


def forward_local(idx, q, own, near):
    heads, tokens, hd = q.shape
    bq = 256
    return pl.pallas_call(
        forward_local_kernel,
        grid=(tokens // bq,),
        in_specs=[
            pl.BlockSpec(memory_space=pltpu.SMEM),
            pl.BlockSpec((heads, bq, hd), lambda i: (0, i, 0)),
            whole(own.shape),
            whole(near.shape),
        ],
        out_specs=[
            pl.BlockSpec((heads, bq, hd), lambda i: (0, i, 0)),
            pl.BlockSpec((heads, bq, 128), lambda i: (0, i, 0)),
        ],
        out_shape=[
            jax.ShapeDtypeStruct((heads, tokens, hd), F32),
            jax.ShapeDtypeStruct((heads, tokens, 128), F32),
        ],
        compiler_params=params(),
        cost_estimate=cost(6 * heads * tokens * tokens * hd, 8 * heads * tokens * hd),
        name="forward_local",
    )(idx, q, own, near)


def forward_post_kernel(idx_ref, q_ref, far_ref, mid_ref, acc_in_ref, sum_in_ref, x_ref, dy_ref, wo_ref, gain_ref,
                        y_ref, do_ref, stat_ref, dwo_ref, dgain_ref, acc_ref, sum_ref, o_ref, dz_ref):
    heads, bq, hd = q_ref.shape
    tokens = far_ref.shape[1]
    i = pl.program_id(0)
    steps = pl.num_programs(0)
    acc_ref[...] = acc_in_ref[...]
    sum_ref[...] = sum_in_ref[...]

    @pl.when(idx_ref[0] >= 2)
    def _():
        def step(j, _):
            rows = pl.ds(pl.multiple_of(j * 512, 512), 512)
            forward_tile(q_ref, acc_ref, sum_ref, far_ref[0, rows, :], far_ref[1, rows, :], False)
            forward_tile(q_ref, acc_ref, sum_ref, mid_ref[0, rows, :], mid_ref[1, rows, :], False)
            return 0

        lax.fori_loop(0, tokens // 512, step, 0)

    lane = lax.broadcasted_iota(jnp.int32, (bq, 128), 1)
    stat = jnp.zeros((bq, 128), F32)
    for h in range(heads):
        total = jnp.sum(sum_ref[h], axis=-1, keepdims=True)
        stat = jnp.where(lane == h, jnp.log2(total), stat)
        out = acc_ref[h] / total
        acc_ref[h] = out
        o_ref[pl.ds(pl.multiple_of(i * bq, bq), bq), h * hd:(h + 1) * hd] = out.astype(BF16)
    rows = pl.ds(pl.multiple_of(i * bq, bq), bq)
    z = dot(o_ref[rows, :], wo_ref[...]).astype(BF16).astype(F32)
    gain = 1.0 + gain_ref[...]
    rstd = lax.rsqrt(jnp.mean(z * z, axis=-1, keepdims=True) + NORM_EPS)
    z_unit = z * rstd
    y_ref[...] = (x_ref[...].astype(F32) + (z_unit * gain).astype(BF16).astype(F32)).astype(BF16)
    dy = dy_ref[...].astype(F32)

    @pl.when(i == 0)
    def _():
        dgain_ref[...] = jnp.zeros_like(dgain_ref)

    dgain_ref[...] += jnp.sum(dy * z_unit, axis=0, keepdims=True)
    g = dy * gain
    dz = (rstd * (g - z_unit * jnp.mean(g * z_unit, axis=-1, keepdims=True))).astype(BF16)
    dz_ref[rows, :] = dz
    for h in range(heads):
        d_out = dot(dz, wo_ref[h * hd:(h + 1) * hd, :], NT).astype(BF16)
        do_ref[h] = d_out
        delta = jnp.sum(d_out.astype(F32) * acc_ref[h], axis=-1, keepdims=True)
        stat = jnp.where(lane == heads + h, delta, stat)
    stat_ref[...] = stat.T[0:8, :]

    @pl.when(i == steps - 1)
    def _():
        core = idx_ref[0] % 2
        per = heads // 2
        for which in range(2):
            for hh in range(per):
                cols = pl.ds(pl.multiple_of((((core + which) % 2) * per + hh) * hd, hd), hd)
                dwo_ref[which, hh * hd:(hh + 1) * hd, :] = dot(o_ref[:, cols].T, dz_ref[...])


def forward_post(idx, q, far, mid, acc, row_sum, x, dy, wo, gain):
    heads, tokens, hd = q.shape
    dim = x.shape[1]
    bq = 256
    rows3 = lambda last: pl.BlockSpec((heads, bq, last), lambda i: (0, i, 0))
    rows2 = pl.BlockSpec((bq, dim), lambda i: (i, 0))
    return pl.pallas_call(
        forward_post_kernel,
        grid=(tokens // bq,),
        in_specs=[
            pl.BlockSpec(memory_space=pltpu.SMEM),
            rows3(hd),
            whole(far.shape),
            whole(mid.shape),
            rows3(hd),
            rows3(128),
            rows2,
            rows2,
            whole(wo.shape),
            whole((1, dim)),
        ],
        out_specs=[
            rows2,
            rows3(hd),
            pl.BlockSpec((8, bq), lambda i: (0, i)),
            whole((2, heads * hd // 2, dim)),
            whole((1, dim)),
        ],
        out_shape=[
            jax.ShapeDtypeStruct((tokens, dim), BF16),
            jax.ShapeDtypeStruct((heads, tokens, hd), BF16),
            jax.ShapeDtypeStruct((8, tokens), F32),
            jax.ShapeDtypeStruct((2, heads * hd // 2, dim), F32),
            jax.ShapeDtypeStruct((1, dim), F32),
        ],
        scratch_shapes=[
            pltpu.VMEM((heads, bq, hd), F32),
            pltpu.VMEM((heads, bq, 128), F32),
            pltpu.VMEM((tokens, heads * hd), BF16),
            pltpu.VMEM((tokens, dim), BF16),
        ],
        compiler_params=params(),
        cost_estimate=cost(8 * heads * tokens * tokens * hd + 6 * tokens * heads * hd * dim, 12 * heads * tokens * hd),
        name="forward_post",
    )(idx, q, far, mid, acc, row_sum, x, dy, wo, gain)


def backward_tile(q_ref, do_ref, stat_ref, dqt_ref, dkv_ref, k, v, kt, start, bq, masked):
    heads = q_ref.shape[0]
    bk = k.shape[0]
    rows = pl.ds(pl.multiple_of(start, 128), bq)
    if masked:
        keep = lax.broadcasted_iota(jnp.int32, (bk, bq), 0) <= lax.broadcasted_iota(jnp.int32, (bk, bq), 1)
    for h in range(heads):
        q = q_ref[h, rows, :]
        d_out = do_ref[h, rows, :]
        t = jnp.tanh(dot(k, q, NT) * INV_CAP)
        p = jnp.exp2(t * CAP2 - stat_ref[h:h + 1, rows])
        if masked:
            p = jnp.where(keep, p, 0.0)
        dp = dot(v, d_out, NT)
        ds = (p * (dp - stat_ref[heads + h:heads + h + 1, rows]) * (1.0 - t * t)).astype(BF16)
        dkv_ref[1] += dot(p.astype(BF16), d_out)
        dkv_ref[0] += dot(ds, q)
        dqt_ref[h, :, rows] += dot(kt, ds)


def backward_far_kernel(idx_ref, q_ref, do_ref, stat_ref, kv_ref, dqt_in_ref, dkv_ref, dqt_ref, *, first):
    tokens = q_ref.shape[1]
    bq = 512

    @pl.when(pl.program_id(0) == 0)
    def _():
        dqt_ref[...] = jnp.zeros_like(dqt_ref) if first else dqt_in_ref[...]

    dkv_ref[...] = jnp.zeros_like(dkv_ref)

    @pl.when(idx_ref[0] >= 2)
    def _():
        k, v = kv_ref[0], kv_ref[1]
        kt = k.T

        def step(j, _):
            backward_tile(q_ref, do_ref, stat_ref, dqt_ref, dkv_ref, k, v, kt, j * bq, bq, False)
            return 0

        lax.fori_loop(0, tokens // bq, step, 0)


def backward_far(idx, q, d_out, stat, kv, dqt):
    heads, tokens, hd = q.shape
    bk = 256
    first = dqt is None
    if first:
        dqt = jnp.zeros((8, 128), F32)
    return pl.pallas_call(
        functools.partial(backward_far_kernel, first=first),
        grid=(tokens // bk,),
        in_specs=[
            pl.BlockSpec(memory_space=pltpu.SMEM),
            whole(q.shape),
            whole(d_out.shape),
            whole(stat.shape),
            pl.BlockSpec((2, bk, hd), lambda i: (0, i, 0)),
            whole(dqt.shape),
        ],
        out_specs=[
            pl.BlockSpec((2, bk, hd), lambda i: (0, i, 0)),
            whole((heads, hd, tokens)),
        ],
        out_shape=[
            jax.ShapeDtypeStruct((2, tokens, hd), F32),
            jax.ShapeDtypeStruct((heads, hd, tokens), F32),
        ],
        compiler_params=params(),
        cost_estimate=cost(10 * heads * tokens * tokens * hd, 12 * heads * tokens * hd),
        name="backward_far",
    )(idx, q, d_out, stat, kv, dqt)


def backward_local_kernel(idx_ref, q_ref, do_ref, stat_ref, own_ref, near_ref, dqt_in_ref, cos_ref, sin_ref,
                          dnear_ref, down_ref, dq_ref, dqt_ref):
    heads, tokens, hd = q_ref.shape
    half = hd // 2
    bk = own_ref.shape[1]
    i = pl.program_id(0)
    steps = pl.num_programs(0)

    @pl.when(i == 0)
    def _():
        dqt_ref[...] = dqt_in_ref[...]

    dnear_ref[...] = jnp.zeros_like(dnear_ref)
    down_ref[...] = jnp.zeros_like(down_ref)

    @pl.when(idx_ref[0] % 2 == 1)
    def _():
        k, v = near_ref[0], near_ref[1]
        kt = k.T

        def step(j, _):
            backward_tile(q_ref, do_ref, stat_ref, dqt_ref, dnear_ref, k, v, kt, j * 512, 512, False)
            return 0

        lax.fori_loop(0, tokens // 512, step, 0)

    k, v = own_ref[0], own_ref[1]
    kt = k.T
    backward_tile(q_ref, do_ref, stat_ref, dqt_ref, down_ref, k, v, kt, i * bk, bk, True)

    def own_step(j, _):
        backward_tile(q_ref, do_ref, stat_ref, dqt_ref, down_ref, k, v, kt, j * bk, bk, False)
        return 0

    lax.fori_loop(i + 1, steps, own_step, 0)

    @pl.when(i == steps - 1)
    def _():
        scale = QUERY_SCALE ** -0.5
        for h in range(heads):
            dq = dqt_ref[h].T
            first, second = dq[:, :half], dq[:, half:]
            cosine, sine = cos_ref[...], sin_ref[...]
            dq_ref[:, h * hd:h * hd + half] = ((first * cosine + second * sine) * scale).astype(BF16)
            dq_ref[:, h * hd + half:(h + 1) * hd] = ((second * cosine - first * sine) * scale).astype(BF16)


def backward_local(idx, q, d_out, stat, own, near, dqt, cosine, sine):
    heads, tokens, hd = q.shape
    bk = 256
    kv_spec = pl.BlockSpec((2, bk, hd), lambda i: (0, i, 0))
    return pl.pallas_call(
        backward_local_kernel,
        grid=(tokens // bk,),
        in_specs=[
            pl.BlockSpec(memory_space=pltpu.SMEM),
            whole(q.shape),
            whole(d_out.shape),
            whole(stat.shape),
            kv_spec,
            kv_spec,
            whole(dqt.shape),
            whole(cosine.shape),
            whole(sine.shape),
        ],
        out_specs=[kv_spec, kv_spec, whole((tokens, heads * hd))],
        out_shape=[
            jax.ShapeDtypeStruct((2, tokens, hd), F32),
            jax.ShapeDtypeStruct((2, tokens, hd), F32),
            jax.ShapeDtypeStruct((tokens, heads * hd), BF16),
        ],
        scratch_shapes=[pltpu.VMEM((heads, hd, tokens), F32)],
        compiler_params=params(),
        cost_estimate=cost(15 * heads * tokens * tokens * hd, 12 * heads * tokens * hd),
        name="backward_local",
    )(idx, q, d_out, stat, own, near, dqt, cosine, sine)


def dwq_kernel(idx_ref, at_ref, dq_ref, out_ref):
    out_ref[0] = dot(at_ref[...], dq_ref[...])


def grad_wq(idx, at, dq):
    dim, tokens = at.shape
    width = dq.shape[1]
    cols = 256
    per = width // 2 // cols
    grid_spec = pltpu.PrefetchScalarGridSpec(
        num_scalar_prefetch=1,
        grid=(2, per),
        in_specs=[
            pl.BlockSpec((dim, tokens), lambda w, j, idx: (0, 0)),
            pl.BlockSpec((tokens, cols), lambda w, j, idx: (0, ((w + 1 + idx[0]) % 2) * per + j)),
        ],
        out_specs=pl.BlockSpec((1, dim, cols), lambda w, j, idx: (1 - w, 0, j)),
    )
    return pl.pallas_call(
        dwq_kernel,
        grid_spec=grid_spec,
        out_shape=jax.ShapeDtypeStruct((2, dim, width // 2), F32),
        compiler_params=params(),
        cost_estimate=cost(2 * dim * tokens * width, 4 * dim * width),
        name="grad_wq",
    )(idx, at, dq)


def tail_kernel(idx_ref, down_ref, dnear_ref, dfar_ref, cos_ref, sin_ref, at_ref, dq_ref, wq_ref, wk_ref, wv_ref,
                x_ref, dy_ref, gain_ref, dx_ref, dwkv_ref, dgain_ref):
    bt, half = cos_ref.shape
    i = pl.program_id(0)
    dk = down_ref[0] + dnear_ref[0] + dfar_ref[0]
    cosine, sine = cos_ref[...], sin_ref[...]
    first, second = dk[:, :half], dk[:, half:]
    dk = jnp.concatenate([first * cosine + second * sine, second * cosine - first * sine], axis=1).astype(BF16)
    dv = (down_ref[1] + dnear_ref[1] + dfar_ref[1]).astype(BF16)

    @pl.when(i == 0)
    def _():
        dwkv_ref[...] = jnp.zeros_like(dwkv_ref)
        dgain_ref[...] = jnp.zeros_like(dgain_ref)

    core = idx_ref[0] % 2
    at = at_ref[...]
    is_core0 = core == 0
    mine = jnp.where(is_core0, dk, dv)
    theirs = jnp.where(is_core0, dv, dk)
    dwkv_ref[0] += dot(at, mine)
    dwkv_ref[1] += dot(at, theirs)
    da = dot(dq_ref[...], wq_ref[...], NT) + dot(dk, wk_ref[...], NT) + dot(dv, wv_ref[...], NT)
    x = x_ref[...].astype(F32)
    rstd = lax.rsqrt(jnp.mean(x * x, axis=-1, keepdims=True) + NORM_EPS)
    unit = x * rstd
    dgain_ref[...] += jnp.sum(da * unit, axis=0, keepdims=True)
    g = da * (1.0 + gain_ref[...])
    dx = rstd * (g - unit * jnp.mean(g * unit, axis=-1, keepdims=True))
    dx_ref[...] = (dy_ref[...].astype(F32) + dx).astype(BF16)


def tail(idx, down, dnear, dfar, cosine, sine, at, dq, wq, wk, wv, x, dy, gain):
    tokens, dim = x.shape
    hd = wk.shape[1]
    width = wq.shape[1]
    bt = 256
    kv_spec = pl.BlockSpec((2, bt, hd), lambda i: (0, i, 0))
    rope_spec = pl.BlockSpec((bt, hd // 2), lambda i: (i, 0))
    rows2 = pl.BlockSpec((bt, dim), lambda i: (i, 0))
    return pl.pallas_call(
        tail_kernel,
        grid=(tokens // bt,),
        in_specs=[
            pl.BlockSpec(memory_space=pltpu.SMEM),
            kv_spec,
            kv_spec,
            kv_spec,
            rope_spec,
            rope_spec,
            pl.BlockSpec((dim, bt), lambda i: (0, i)),
            pl.BlockSpec((bt, width), lambda i: (i, 0)),
            whole(wq.shape),
            whole(wk.shape),
            whole(wv.shape),
            rows2,
            rows2,
            whole((1, dim)),
        ],
        out_specs=[rows2, whole((2, dim, hd)), whole((1, dim))],
        out_shape=[
            jax.ShapeDtypeStruct((tokens, dim), BF16),
            jax.ShapeDtypeStruct((2, dim, hd), F32),
            jax.ShapeDtypeStruct((1, dim), F32),
        ],
        compiler_params=params(),
        cost_estimate=cost(2 * tokens * dim * (width + 4 * hd), 8 * tokens * dim),
        name="tail",
    )(idx, down, dnear, dfar, cosine, sine, at, dq, wq, wk, wv, x, dy, gain)


def solution(mesh):
    across = [(0, 2), (2, 0), (1, 3), (3, 1)]
    beside = [(0, 1), (1, 0), (2, 3), (3, 2)]

    def permute(value, pairs):
        return lax.ppermute(value, "cp", pairs)

    def sum_halves(parts):
        mine = parts[0] + permute(parts[1], beside)
        return mine + permute(mine, across)

    def local_step(x_in, positions, dy_out, w_query, w_key, w_value, w_out, w_pre, w_post):
        batch, tokens, dim = x_in.shape
        heads, hd = w_query.shape[1], w_query.shape[2]
        half = hd // 2
        rank = lax.axis_index("cp").astype(jnp.int32)
        idx = rank.reshape(1)
        core = rank % 2
        wq = w_query.reshape(dim, heads * hd)
        wk = w_key.reshape(dim, hd)
        wv = w_value.reshape(dim, hd)
        wo = w_out.reshape(heads * hd, dim)
        x = x_in.reshape(tokens, dim)
        dy = dy_out.reshape(tokens, dim)
        gain_pre = w_pre.reshape(1, dim)
        gain_post = w_post.reshape(1, dim)
        inv_freq = ROPE_BASE ** (jnp.arange(half, dtype=F32) * (-2.0 / hd))
        angles = positions.reshape(tokens, 1).astype(F32) * inv_freq
        cosine, sine = jnp.cos(angles), jnp.sin(angles)

        act, act_t, own = project_kv(x, gain_pre, wk, wv, cosine, sine)
        far = permute(own, [(0, 2), (1, 3)])
        near = permute(own, [(0, 1), (2, 3)])
        q = project_q(act, wq, cosine, sine, heads)
        acc, row_sum = forward_local(idx, q, own, near)
        mid = permute(far, [(2, 3), (3, 2)])
        y, d_out, stat, dwo, dgain_post = forward_post(idx, q, far, mid, acc, row_sum, x, dy, wo, gain_post)
        dwo_mine = sum_halves(dwo)

        dmid, dqt = backward_far(idx, q, d_out, stat, mid, None)
        dmid_in = permute(dmid, [(2, 3), (3, 2)])
        dfar, dqt = backward_far(idx, q, d_out, stat, far, dqt)
        dfar_in = permute(dfar + dmid_in, [(2, 0), (3, 1)])
        dnear, down, dq = backward_local(idx, q, d_out, stat, own, near, dqt, cosine, sine)
        dnear_in = permute(dnear, [(1, 0), (3, 2)])
        dwq = grad_wq(idx, act_t, dq)
        dwq_mine = sum_halves(dwq)
        dx, dwkv, dgain_pre = tail(idx, down, dnear_in, dfar_in, cosine, sine, act_t, dq, wq, wk, wv, x, dy, gain_pre)
        dwkv_mine = sum_halves(dwkv)
        gains = jnp.concatenate([dgain_pre, dgain_post], axis=0)
        gains = gains + permute(gains, beside)
        gains = gains + permute(gains, across)

        def join(mine, axis):
            other = permute(mine, beside)
            low = jnp.where(core == 0, mine, other)
            high = jnp.where(core == 0, other, mine)
            return low, high

        dwo_full = jnp.concatenate(join(dwo_mine, 0), axis=0)
        dwq_full = jnp.concatenate(join(dwq_mine, 1), axis=1)
        dwk_full, dwv_full = join(dwkv_mine, 0)
        return (
            y.reshape(batch, tokens, dim),
            dx.reshape(batch, tokens, dim),
            dwq_full.reshape(dim, heads, hd),
            dwk_full.reshape(dim, 1, hd),
            dwv_full.reshape(dim, 1, hd),
            dwo_full.reshape(heads, hd, dim),
            gains[0],
            gains[1],
        )

    seq_spec = P("dp", "cp", None)
    in_specs = (seq_spec, P("dp", "cp"), seq_spec, P(), P(), P(), P(), P(), P())
    out_specs = (seq_spec, seq_spec, P("dp", None, None), P("dp", None, None), P("dp", None, None), P("dp", None, None), P("dp"), P("dp"))
    return jax.shard_map(local_step, mesh=mesh, in_specs=in_specs, out_specs=out_specs, check_vma=False)
```

time: 670 us -> 411 us (0.61)
  matrix products: 264 us -> 0 us
  Pallas kernels: 0 us -> 98 us
  starting transfers between devices: 18.3 us -> 82.9 us
  waiting for transfers between devices: 214 us -> 168 us
  local copies, waits for them, and re-layouts: 73.1 us -> 32 us
  other arithmetic: 66.1 us -> 27.8 us
  between operations: 15 us -> 0.87 us
  blocking collectives: 11.9 us -> 0 us
    dot_general x39 -> x0, matrix products: 264 us -> none  [the longest x4 49.7 us: gradient_block(): jnp.einsum('bqngd,bknd->bnqgk', d_attn, value_blk, preferred_element_type...]
    psum x1 -> x0, waiting for transfers between devices: 177 us -> none  [local_step(): lax.psum((dw_query_part, dw_key_part, dw_value_part, dw_out_part, dw_pre_...]
    ppermute x26 -> x17, waiting for transfers between devices: 37 us -> 168 us  [permute(): return lax.ppermute(value, 'cp', pairs)]
    pallas_call x0 -> x9, Pallas kernels: none -> 98 us  [the longest x1 20.5 us: backward_local(): pl.pallas_call(backward_local_kernel, grid=(tokens // bk,), in_specs=[pl....]
    ppermute x26 -> x17, starting transfers between devices: 18.3 us -> 82.9 us  [permute(): return lax.ppermute(value, 'cp', pairs)]
    while x34 -> x0, local copies, waits for them, and re-layouts: 31.6 us -> none  [the longest x5 14.5 us: local_step(): lax.fori_loop(1, groups, backward_body, (dquery_sum, key_rot, value_proj,...]
    reduce_sum x7 -> x0, other arithmetic: 27.7 us -> none  [the longest x4 22.3 us: absorb(): run_sum = run_sum * rescale + jnp.sum(weights, axis=-1)]
    convert_element_type x5 -> x1, other arithmetic: 12.6 us -> 0.69 us  [local_step(): angles = positions.reshape(tokens, 1).astype(F32) * inv_freq]
  transfers between devices with their start and end apart: 27 -> 17, of which waited for: 7 -> 6; matrix products, arithmetic and copies ran while one was open for 29% -> 9% of each run, Pallas kernels for 0% -> 16%
where the time goes in v1:
time: 411 us; the launch traced here: 410 us
  waiting for transfers between devices  168 us (41%)
  Pallas kernels  98 us (24%)
  starting transfers between devices  82.9 us (20%)
  local copies, waits for them, and re-layouts  32 us (8%)
  other arithmetic  27.8 us (7%)
    ppermute x17, waiting for transfers between devices, permute(): return lax.ppermute(value, 'cp', pairs)  168 us
    ppermute x17, starting transfers between devices, permute(): return lax.ppermute(value, 'cp', pairs)  82.9 us
    pallas_call x1, Pallas kernels, backward_local(): pl.pallas_call(backward_local_kernel, grid=(tokens // bk,), in_specs=[pl....  20.5 us
    pallas_call x1, Pallas kernels, forward_post(): pl.pallas_call(forward_post_kernel, grid=(tokens // bq,), in_specs=[pl.Bl...  20.1 us
    unnamed x33, local copies, waits for them, and re-layouts  16.9 us
    pallas_call x2, Pallas kernels, backward_far(): pl.pallas_call(functools.partial(backward_far_kernel, first=first), grid=...  14.4 us
    pallas_call x1, Pallas kernels, tail(): pl.pallas_call(tail_kernel, grid=(tokens // bt,), in_specs=[pl.BlockSpec(...  12.7 us
    pallas_call x1, Pallas kernels, forward_local(): pl.pallas_call(forward_local_kernel, grid=(tokens // bq,), in_specs=[pl.B...  10.3 us
  transfers between devices with their start and end apart: 17, of which 6 were waited for; matrix products, arithmetic and copies ran while one was open for 9% of the time, Pallas kernels for 16%

profile of v1, /device:TPU:0, one launch (start us, length us, event | category | flops | bytes accessed | tf_op | source)
XLA Modules:
  0.0 409.5 jit_solution(9116788179800546085)
XLA Ops:
  2.6 3.0 multiply_sine_fusion
  5.7 6.0 %project_kv.1 = (bf16[1024,1152]{1,0:T(8,128)(2,1)}, bf16[1152,1024]{1,0:T(8,128)(2,1)}, bf16[2,1024,256]{2,1,0:T(8,128)(2,1)}) custom-call(bf16[1024,1152]{1,0:T(8,128)(2,1)} %bitcast.34, f32[1,1152]{1,0:T(1,128)} %reshape.77.gain_ref, bf16[1152,256]{1,0:T(8,128)(2,1)} %bitcast.40, bf16[1152,256]{1,0:T(8,128)(2,1)} %bitcast.42, ...), custom_call_target="tpu_custom_call" | custom-call | flops 1207959552 | bytes 7077888 | tf_op jit(solution)/shard_map/project_kv/pallas_call | solution.py:64
  11.7 6.1 %collective-permute-start = (bf16[2,1024,256]{2,1,0:T(8,128)(2,1)}, bf16[2,1024,256]{2,1,0:T(8,128)(2,1)}, u32[]{:S(2)}, u32[]{:S(2)}) collective-permute-start(bf16[2,1024,256]{2,1,0:T(8,128)(2,1)} %get-tuple-element.29.own_ref), channel_id=1, source_target_pairs={{0,2},{1,3},{4,6},{5,7},{8,10},{9,11},{12,14},{13,15}} | collective-permute-start | bytes 3145736 | tf_op jit(solution)/shard_map/ppermute | solution.py:559
  19.3 19.9 %collective-permute-done.far_ref.kv_ref = bf16[2,1024,256]{2,1,0:T(8,128)(2,1)} collective-permute-done((bf16[2,1024,256]{2,1,0:T(8,128)(2,1)}, bf16[2,1024,256]{2,1,0:T(8,128)(2,1)}, u32[]{:S(2)}, u32[]{:S(2)}) %collective-permute-start) | collective-permute-done | bytes 1048608 | tf_op jit(solution)/shard_map/ppermute | solution.py:559
  40.9 2.0 copy.19
  43.5 7.1 %project_q.1.q_ref = bf16[4,1024,256]{2,1,0:T(8,128)(2,1)} custom-call(bf16[1024,1152]{1,0:T(8,128)(2,1)} %get-tuple-element.28.a_ref, bf16[1152,1024]{1,0:T(8,128)(2,1)} %bitcast.32, f32[1024,128]{1,0:T(8,128)} %get-tuple-element.65.cos_ref, f32[1024,128]{1,0:T(8,128)} %get-tuple-element.64.sin_ref), custom_call_target="tpu_custom_call" | custom-call | flops 2415919104 | bytes 7077888 | tf_op jit(solution)/shard_map/project_q/pallas_call | solution.py:109
  51.6 10.3 %forward_local.1 = (f32[4,1024,256]{2,1,0:T(8,128)}, f32[4,1024,128]{2,1,0:T(8,128)}) custom-call(s32[1]{0:T(128)} %bitcast.idx_ref, bf16[4,1024,256]{2,1,0:T(8,128)(2,1)} %project_q.1.q_ref, bf16[2,1024,256]{2,1,0:T(8,128)(2,1)} %get-tuple-element.29.own_ref, bf16[2,1024,256]{2,1,0:T(8,128)(2,1)} %copy-done.10), custom_call_target="tpu_custom_call" | custom-call | flops 6442450944 | bytes 8388608 | tf_op jit(solution)/shard_map/forward_local/pallas_call | solution.py:174
  61.8 20.1 %forward_post.1 = (bf16[1024,1152]{1,0:T(8,128)(2,1)}, bf16[4,1024,256]{2,1,0:T(8,128)(2,1)}, f32[8,1024]{1,0:T(8,128)}, f32[2,512,1152]{2,1,0:T(8,128)}, f32[1,1152]{1,0:T(1,128)}) custom-call(s32[1]{0:T(128)} %bitcast.idx_ref, bf16[4,1024,256]{2,1,0:T(8,128)(2,1)} %project_q.1.q_ref, bf16[2,1024,256]{2,1,0:T(8,128)(2,1)} %collective-permute-done.far_ref.kv_ref, ...), custom_call_target="tpu_custom_call" | custom-call | flops 15837691904 | bytes 12582912 | tf_op jit(solution)/shard_map/forward_post/pallas_call | solution.py:263
  82.5 6.6 %backward_far.2 = (f32[2,1024,256]{2,1,0:T(8,128)}, f32[4,256,1024]{2,1,0:T(8,128)}) custom-call(s32[1]{0:T(128)} %bitcast.idx_ref, bf16[4,1024,256]{2,1,0:T(8,128)(2,1)} %project_q.1.q_ref, bf16[4,1024,256]{2,1,0:T(8,128)(2,1)} %get-tuple-element.33.do_ref, f32[8,1024]{1,0:T(8,128)} %get-tuple-element.34.stat_ref, ...), custom_call_target="tpu_custom_call" | custom-call | flops 10737418240 | bytes 12582912 | tf_op jit(solution)/shard_map/backward_far/pallas_call | solution.py:352
  90.1 7.8 %backward_far.3 = (f32[2,1024,256]{2,1,0:T(8,128)}, f32[4,256,1024]{2,1,0:T(8,128)}) custom-call(s32[1]{0:T(128)} %bitcast.idx_ref, bf16[4,1024,256]{2,1,0:T(8,128)(2,1)} %project_q.1.q_ref, bf16[4,1024,256]{2,1,0:T(8,128)(2,1)} %get-tuple-element.33.do_ref, f32[8,1024]{1,0:T(8,128)} %get-tuple-element.34.stat_ref, ...), custom_call_target="tpu_custom_call" | custom-call | flops 10737418240 | bytes 12582912 | tf_op jit(solution)/shard_map/backward_far/pallas_call | solution.py:352
  97.9 20.5 %backward_local.1 = (f32[2,1024,256]{2,1,0:T(8,128)}, f32[2,1024,256]{2,1,0:T(8,128)}, bf16[1024,1024]{1,0:T(8,128)(2,1)}) custom-call(s32[1]{0:T(128)} %bitcast.idx_ref, bf16[4,1024,256]{2,1,0:T(8,128)(2,1)} %project_q.1.q_ref, bf16[4,1024,256]{2,1,0:T(8,128)(2,1)} %get-tuple-element.33.do_ref, f32[8,1024]{1,0:T(8,128)} %get-tuple-element.34.stat_ref, ...), custom_call_target="tpu_custom_call" | custom-call | flops 16106127360 | bytes 12582912 | tf_op jit(solution)/shard_map/backward_local/pallas_call | solution.py:428
  118.5 6.8 %grad_wq.1 = f32[2,1152,512]{2,1,0:T(8,128)} custom-call(s32[1]{0:T(128)} %bitcast.idx_ref, bf16[1152,1024]{1,0:T(8,128)(2,1)} %get-tuple-element.41.at_ref, bf16[1024,1024]{1,0:T(8,128)(2,1)} %get-tuple-element.42.dq_ref), custom_call_target="tpu_custom_call" | custom-call | flops 2415919104 | bytes 4718592 | tf_op jit(solution)/shard_map/grad_wq/pallas_call | solution.py:473
  125.3 2.0 slice_bitcast_fusion
  127.3 20.8 %collective-permute-start.6 = (f32[1152,512]{1,0:T(8,128)S(1)}, f32[1152,512]{1,0:T(8,128)S(1)}, u32[]{:S(2)}, u32[]{:S(2)}) collective-permute-start(f32[1152,512]{1,0:T(8,128)S(1)} %slice_bitcast_fusion), channel_id=1, source_target_pairs={{0,1},{1,0},{2,3},{3,2},{4,5},{5,4},{6,7},{7,6},{8,9},{9,8},{10,11... | collective-permute-start | bytes 7077896 | tf_op jit(solution)/shard_map/ppermute | solution.py:559
  148.1 2.0 slice_bitcast_fusion.2
  154.3 43.8 %collective-permute-start.7 = (f32[1152,512]{1,0:T(8,128)S(1)}, f32[1152,512]{1,0:T(8,128)}, u32[]{:S(2)}, u32[]{:S(2)}) collective-permute-start(f32[1152,512]{1,0:T(8,128)S(1)} %fusion), channel_id=1, source_target_pairs={{0,2},{2,0},{1,3},{3,1},{4,6},{6,4},{5,7},{7,5},{8,10},{10,8},{9,1... | collective-permute-start | bytes 7077896 | tf_op jit(solution)/shard_map/ppermute | solution.py:559
  200.9 42.2 %collective-permute-done.5.dfar_ref = f32[2,1024,256]{2,1,0:T(8,128)S(1)} collective-permute-done((f32[2,1024,256]{2,1,0:T(8,128)S(1)}, f32[2,1024,256]{2,1,0:T(8,128)S(1)}, u32[]{:S(2)}, u32[]{:S(2)}) %collective-permute-start.5) | collective-permute-done | bytes 2097184 | tf_op jit(solution)/shard_map/ppermute | solution.py:559
  244.5 12.7 %tail.1 = (bf16[1024,1152]{1,0:T(8,128)(2,1)}, f32[2,1152,256]{2,1,0:T(8,128)}, f32[1,1152]{1,0:T(1,128)}) custom-call(s32[1]{0:T(128)} %bitcast.idx_ref, f32[2,1024,256]{2,1,0:T(8,128)} %get-tuple-element.37.down_ref, f32[2,1024,256]{2,1,0:T(8,128)} %copy-done.3, f32[2,1024,256]{2,1,0:T(8,128)} %copy-done.4, f32[1024,128]{1,0:T(8,128)} %get-tuple-element.65.cos_ref, ...), custom_call_target="tpu_custom_call" | custom-call | flops 4831838208 | bytes 9437184 | tf_op jit(solution)/shard_map/tail/pallas_call | solution.py:523
  260.0 33.7 %collective-permute-done.7 = f32[1152,512]{1,0:T(8,128)} collective-permute-done((f32[1152,512]{1,0:T(8,128)S(1)}, f32[1152,512]{1,0:T(8,128)}, u32[]{:S(2)}, u32[]{:S(2)}) %collective-permute-start.7) | collective-permute-done | bytes 2359328 | tf_op jit(solution)/shard_map/ppermute | solution.py:559
  293.7 3.6 add.34
  298.7 45.6 %collective-permute-done.13 = f32[512,1152]{1,0:T(8,128)} collective-permute-done((f32[512,1152]{1,0:T(8,128)}, f32[512,1152]{1,0:T(8,128)}, u32[]{:S(2)}, u32[]{:S(2)}) %collective-permute-start.13) | collective-permute-done | bytes 2359328 | tf_op jit(solution)/shard_map/ppermute | solution.py:559
  344.3 2.6 add.38
  348.0 3.5 collective-permute-done.15
  352.7 23.0 %collective-permute-done.16 = f32[2,1152]{1,0:T(2,128)} collective-permute-done((f32[2,1152]{1,0:T(2,128)}, f32[2,1152]{1,0:T(2,128)}, u32[]{:S(2)}, u32[]{:S(2)}) %collective-permute-start.16) | collective-permute-done | bytes 9248 | tf_op jit(solution)/shard_map/ppermute | solution.py:559
  377.1 2.4 add.36
  379.5 2.9 broadcast_select_fusion.3
  382.5 2.6 pad_maximum_fusion
  385.1 6.7 %reshape.86 = f32[1152,4,256]{2,1,0:T(4,128)} reshape(f32[1152,1024]{1,0:T(8,128)} %pad_maximum_fusion) | data formatting | bytes 9437184 | tf_op jit(solution)/shard_map/reshape | solution.py:619
  391.7 2.0 broadcast_select_fusion.1
  393.7 2.5 pad_maximum_fusion.1
  397.6 6.0 %copy.17 = f32[1152,1,256]{2,1,0:T(1,128)} copy(f32[1152,1,256]{2,0,1:T(8,128)S(1)} %get-tuple-element.63) | data formatting | bytes 2359296
  403.6 5.9 %copy.18 = f32[1152,1,256]{2,1,0:T(1,128)} copy(f32[1152,1,256]{2,0,1:T(8,128)S(1)} %get-tuple-element.62) | data formatting | bytes 2359296
  (72 shorter events, 25.9 us)
Async XLA Ops:
  5.7 35.2 %copy-start.1 = (bf16[1152,4,256]{2,1,0:T(4,128)(2,1)S(1)}, bf16[1152,4,256]{2,1,0:T(4,128)(2,1)}, u32[]{:S(2)}) copy-start(bf16[1152,4,256]{2,1,0:T(4,128)(2,1)} %param.12) | copy-start | bytes 7077892
  11.7 27.5 %collective-permute-start = (bf16[2,1024,256]{2,1,0:T(8,128)(2,1)}, bf16[2,1024,256]{2,1,0:T(8,128)(2,1)}, u32[]{:S(2)}, u32[]{:S(2)}) collective-permute-start(bf16[2,1024,256]{2,1,0:T(8,128)(2,1)} %get-tuple-element.29.own_ref), channel_id=1, source_target_pairs={{0,2},{1,3},{4,6},{5,7},{8,10},{9,11},{12,14},{13,15}} | collective-permute-start | bytes 3145736 | tf_op jit(solution)/shard_map/ppermute | solution.py:559
  17.8 32.8 %collective-permute-start.2 = (bf16[2,1024,256]{2,1,0:T(8,128)(2,1)}, bf16[2,1024,256]{2,1,0:T(8,128)(2,1)S(1)}, u32[]{:S(2)}, u32[]{:S(2)}) collective-permute-start(bf16[2,1024,256]{2,1,0:T(8,128)(2,1)} %get-tuple-element.29.own_ref), channel_id=1, source_target_pairs={{0,1},{2,3},{4,5},{6,7},{8,9},{10,11},{12,13},{14,15}} | collective-permute-start | bytes 3145736 | tf_op jit(solution)/shard_map/ppermute | solution.py:559
  39.2 22.6 %collective-permute-start.1 = (bf16[2,1024,256]{2,1,0:T(8,128)(2,1)}, bf16[2,1024,256]{2,1,0:T(8,128)(2,1)}, u32[]{:S(2)}, u32[]{:S(2)}) collective-permute-start(bf16[2,1024,256]{2,1,0:T(8,128)(2,1)} %collective-permute-done.far_ref.kv_ref), channel_id=1, source_target_pairs={{2,3},{3,2},{6,7},{7,6},{10,11},{11,10},{14,15},{15,14}} | collective-permute-start | bytes 3145736 | tf_op jit(solution)/shard_map/ppermute | solution.py:559
  40.9 2.0 copy-start.8
  50.6 1.0 copy-start.10
  89.1 62.9 %collective-permute-start.4 = (f32[2,1024,256]{2,1,0:T(8,128)}, f32[2,1024,256]{2,1,0:T(8,128)S(1)}, u32[]{:S(2)}, u32[]{:S(2)}) collective-permute-start(f32[2,1024,256]{2,1,0:T(8,128)} %get-tuple-element.40), channel_id=1, source_target_pairs={{2,3},{3,2},{6,7},{7,6},{10,11},{11,10},{14,15},{15,14}} | collective-permute-start | bytes 6291464 | tf_op jit(solution)/shard_map/ppermute | solution.py:559
  125.3 25.5 %copy-start.9 = (f32[2,1024,256]{2,1,0:T(8,128)S(1)}, f32[2,1024,256]{2,1,0:T(8,128)}, u32[]{:S(2)}) copy-start(f32[2,1024,256]{2,1,0:T(8,128)} %get-tuple-element.38) | copy-start | bytes 6291460
  125.3 26.8 %copy-start.2 = (f32[2,1024,256]{2,1,0:T(8,128)S(1)}, f32[2,1024,256]{2,1,0:T(8,128)}, u32[]{:S(2)}) copy-start(f32[2,1024,256]{2,1,0:T(8,128)} %get-tuple-element.39) | copy-start | bytes 6291460
  125.3 28.4 %slice-start = ((s8[4718592]{0:T(1024)(128)(4,1)}), s8[4194304]{0:T(1024)(128)(4,1)S(1)}, s32[]{:S(2)}) async-start(s8[4718592]{0:T(1024)(128)(4,1)} %bitcast.30), calls=%async_computation | async-start | bytes 8388608
  127.3 26.4 %collective-permute-start.6 = (f32[1152,512]{1,0:T(8,128)S(1)}, f32[1152,512]{1,0:T(8,128)S(1)}, u32[]{:S(2)}, u32[]{:S(2)}) collective-permute-start(f32[1152,512]{1,0:T(8,128)S(1)} %slice_bitcast_fusion), channel_id=1, source_target_pairs={{0,1},{1,0},{2,3},{3,2},{4,5},{5,4},{6,7},{7,6},{8,9},{9,8},{10,11... | collective-permute-start | bytes 7077896 | tf_op jit(solution)/shard_map/ppermute | solution.py:559
  148.1 5.6 %slice-start.1 = ((s8[4718592]{0:T(1024)(128)(4,1)}), s8[524288]{0:T(1024)(128)(4,1)S(1)}, s32[]{:S(2)}) async-start(s8[4718592]{0:T(1024)(128)(4,1)} %bitcast.30), calls=%async_computation.1 | async-start | bytes 1048576
  148.1 49.9 %slice-start.2 = ((s8[4718592]{0:T(1024)(128)(4,1)}), s8[4194304]{0:T(1024)(128)(4,1)S(1)}, s32[]{:S(2)}) async-start(s8[4718592]{0:T(1024)(128)(4,1)} %bitcast.37), calls=%async_computation.2 | async-start | bytes 8388608
  150.1 47.9 %collective-permute-start.12 = (f32[512,1152]{1,0:T(8,128)S(1)}, f32[512,1152]{1,0:T(8,128)S(1)}, u32[]{:S(2)}, u32[]{:S(2)}) collective-permute-start(f32[512,1152]{1,0:T(8,128)S(1)} %slice_bitcast_fusion.2), channel_id=1, source_target_pairs={{0,1},{1,0},{2,3},{3,2},{4,5},{5,4},{6,7},{7,6},{8,9},{9,8},{10,11... | collective-permute-start | bytes 7077896 | tf_op jit(solution)/shard_map/ppermute | solution.py:559
  150.8 50.1 %collective-permute-start.3 = (f32[2,1024,256]{2,1,0:T(8,128)S(1)}, f32[2,1024,256]{2,1,0:T(8,128)S(1)}, u32[]{:S(2)}, u32[]{:S(2)}) collective-permute-start(f32[2,1024,256]{2,1,0:T(8,128)S(1)} %copy-done.9), channel_id=1, source_target_pairs={{1,0},{3,2},{5,4},{7,6},{9,8},{11,10},{13,12},{15,14}} | collective-permute-start | bytes 6291464 | tf_op jit(solution)/shard_map/ppermute | solution.py:559
  152.1 46.0 %slice-start.3 = ((s8[4718592]{0:T(1024)(128)(4,1)}), s8[524288]{0:T(1024)(128)(4,1)S(1)}, s32[]{:S(2)}) async-start(s8[4718592]{0:T(1024)(128)(4,1)} %bitcast.37), calls=%async_computation.3 | async-start | bytes 1048576
  152.4 90.8 %collective-permute-start.5 = (f32[2,1024,256]{2,1,0:T(8,128)S(1)}, f32[2,1024,256]{2,1,0:T(8,128)S(1)}, u32[]{:S(2)}, u32[]{:S(2)}) collective-permute-start(f32[2,1024,256]{2,1,0:T(8,128)S(1)} %add.31), channel_id=1, source_target_pairs={{2,0},{3,1},{6,4},{7,5},{10,8},{11,9},{14,12},{15,13}} | collective-permute-start | bytes 6291464 | tf_op jit(solution)/shard_map/ppermute | solution.py:559
  154.3 139.4 %collective-permute-start.7 = (f32[1152,512]{1,0:T(8,128)S(1)}, f32[1152,512]{1,0:T(8,128)}, u32[]{:S(2)}, u32[]{:S(2)}) collective-permute-start(f32[1152,512]{1,0:T(8,128)S(1)} %fusion), channel_id=1, source_target_pairs={{0,2},{2,0},{1,3},{3,1},{4,6},{6,4},{5,7},{7,5},{8,10},{10,8},{9,1... | collective-permute-start | bytes 7077896 | tf_op jit(solution)/shard_map/ppermute | solution.py:559
  199.7 144.6 %collective-permute-start.13 = (f32[512,1152]{1,0:T(8,128)}, f32[512,1152]{1,0:T(8,128)}, u32[]{:S(2)}, u32[]{:S(2)}) collective-permute-start(f32[512,1152]{1,0:T(8,128)} %bitcast_add_fusion), channel_id=1, source_target_pairs={{0,2},{2,0},{1,3},{3,1},{4,6},{6,4},{5,7},{7,5},{8,10},{10,8},{9,1... | collective-permute-start | bytes 7077896 | tf_op jit(solution)/shard_map/ppermute | solution.py:559
  200.9 42.3 %copy-start.3 = (f32[2,1024,256]{2,1,0:T(8,128)}, f32[2,1024,256]{2,1,0:T(8,128)S(1)}, u32[]{:S(2)}) copy-start(f32[2,1024,256]{2,1,0:T(8,128)S(1)} %collective-permute-done.3.dnear_ref) | copy-start | bytes 6291460
  243.2 1.3 copy-start.4
  258.6 88.7 %collective-permute-start.9 = (f32[1152,256]{1,0:T(8,128)S(1)}, f32[1152,256]{1,0:T(8,128)S(1)}, u32[]{:S(2)}, u32[]{:S(2)}) collective-permute-start(f32[1152,256]{1,0:T(8,128)S(1)} %slice_bitcast_fusion.3), channel_id=1, source_target_pairs={{0,1},{1,0},{2,3},{3,2},{4,5},{5,4},{6,7},{7,6},{8,9},{9,8},{10,11... | collective-permute-start | bytes 3538952 | tf_op jit(solution)/shard_map/ppermute | solution.py:559
  297.3 50.0 %copy-start = (f32[2,1152,256]{2,1,0:T(8,128)S(1)}, f32[2,1152,256]{2,1,0:T(8,128)}, u32[]{:S(2)}) copy-start(f32[2,1152,256]{2,1,0:T(8,128)} %get-tuple-element.44) | copy-start | bytes 7077892
  297.3 82.2 %collective-permute-start.8 = (f32[1152,512]{1,0:T(8,128)}, f32[1152,512]{1,0:T(8,128)}, u32[]{:S(2)}, u32[]{:S(2)}) collective-permute-start(f32[1152,512]{1,0:T(8,128)} %add.34), channel_id=1, source_target_pairs={{0,1},{1,0},{2,3},{3,2},{4,5},{5,4},{6,7},{7,6},{8,9},{9,8},{10,11... | collective-permute-start | bytes 7077896 | tf_op jit(solution)/shard_map/ppermute | solution.py:559
  346.9 0.7 copy-start.5
  346.9 0.7 copy-start.6
  346.9 44.8 %collective-permute-start.14 = (f32[512,1152]{1,0:T(8,128)S(1)}, f32[512,1152]{1,0:T(8,128)}, u32[]{:S(2)}, u32[]{:S(2)}) collective-permute-start(f32[512,1152]{1,0:T(8,128)S(1)} %add.38), channel_id=1, source_target_pairs={{0,1},{1,0},{2,3},{3,2},{4,5},{5,4},{6,7},{7,6},{8,9},{9,8},{10,11... | collective-permute-start | bytes 7077896 | tf_op jit(solution)/shard_map/ppermute | solution.py:559
  347.5 29.6 %collective-permute-start.10 = (f32[1152,256]{1,0:T(8,128)S(1)}, f32[1152,256]{1,0:T(8,128)}, u32[]{:S(2)}, u32[]{:S(2)}) collective-permute-start(f32[1152,256]{1,0:T(8,128)S(1)} %bitcast_add_fusion.1), channel_id=1, source_target_pairs={{0,2},{2,0},{1,3},{3,1},{4,6},{6,4},{5,7},{7,5},{8,10},{10,8},{9,1... | collective-permute-start | bytes 3538952 | tf_op jit(solution)/shard_map/ppermute | solution.py:559
  347.6 3.9 collective-permute-start.15
  351.5 0.6 copy-start.7
  352.7 23.0 %collective-permute-start.16 = (f32[2,1152]{1,0:T(2,128)}, f32[2,1152]{1,0:T(2,128)}, u32[]{:S(2)}, u32[]{:S(2)}) collective-permute-start(f32[2,1152]{1,0:T(2,128)} %fusion.1), channel_id=1, source_target_pairs={{0,2},{2,0},{1,3},{3,1},{4,6},{6,4},{5,7},{7,5},{8,10},{10,8},{9,1... | collective-permute-start | bytes 27656 | tf_op jit(solution)/shard_map/ppermute | solution.py:559
  379.5 16.6 %collective-permute-start.11 = (f32[1152,256]{1,0:T(8,128)}, f32[1152,256]{1,0:T(8,128)S(1)}, u32[]{:S(2)}, u32[]{:S(2)}) collective-permute-start(f32[1152,256]{1,0:T(8,128)} %add.36), channel_id=1, source_target_pairs={{0,1},{1,0},{2,3},{3,2},{4,5},{5,4},{6,7},{7,6},{8,9},{9,8},{10,11... | collective-permute-start | bytes 3538952 | tf_op jit(solution)/shard_map/ppermute | solution.py:559

commit v2 on v1

--- a/solution.py
+++ b/solution.py
@@ -7,6 +7,7 @@
 from jax.experimental import pallas as pl
 from jax.experimental.pallas import tpu as pltpu
 from jax.sharding import PartitionSpec as P
+
 
 NORM_EPS = 1e-6
 SOFT_CAP = 50.0
@@ -482,7 +483,7 @@
 
 def tail_kernel(idx_ref, down_ref, dnear_ref, dfar_ref, cos_ref, sin_ref, at_ref, dq_ref, wq_ref, wk_ref, wv_ref,
                 x_ref, dy_ref, gain_ref, dx_ref, dwkv_ref, dgain_ref):
-    bt, half = cos_ref.shape
+    _, half = cos_ref.shape
     i = pl.program_id(0)
     dk = down_ref[0] + dnear_ref[0] + dfar_ref[0]
     cosine, sine = cos_ref[...], sin_ref[...]
@@ -551,6 +552,86 @@
     )(idx, down, dnear, dfar, cosine, sine, at, dq, wq, wk, wv, x, dy, gain)
 
 
+def join_wide_kernel(idx_ref, mine_ref, other_ref, out_ref):
+    first = idx_ref[0] % 2 == 0
+    rows, _ = mine_ref.shape
+    mine, other = mine_ref[...], other_ref[...]
+    low, high = jnp.where(first, mine, other), jnp.where(first, other, mine)
+    heads = 4
+    for h in range(heads):
+        src = low if h < heads // 2 else high
+        base = (h % (heads // 2)) * 256
+        for c in range(2):
+            out_ref[pl.ds(c * heads + h, rows, stride=2 * heads), :] = src[:, base + c * 128:base + (c + 1) * 128]
+
+
+def join_wide(idx, mine, other, heads):
+    dim, width = mine.shape
+    bd = 128
+    spec = pl.BlockSpec((bd, width), lambda i: (i, 0))
+    out = pl.pallas_call(
+        join_wide_kernel,
+        grid=(dim // bd,),
+        in_specs=[pl.BlockSpec(memory_space=pltpu.SMEM), spec, spec],
+        out_specs=pl.BlockSpec((bd * 8, 128), lambda i: (i, 0)),
+        out_shape=jax.ShapeDtypeStruct((dim * 8, 128), F32),
+        compiler_params=params(),
+        cost_estimate=cost(1000, 16 * dim * width),
+        name="join_wide",
+    )(idx, mine, other)
+    return out.reshape(dim, 2, heads, 128).transpose(0, 2, 1, 3).reshape(dim, heads, 256)
+
+
+def join_pair_kernel(idx_ref, mine_ref, other_ref, first_ref, second_ref):
+    core0 = idx_ref[0] % 2 == 0
+    rows = mine_ref.shape[0]
+    mine, other = mine_ref[...], other_ref[...]
+    first, second = jnp.where(core0, mine, other), jnp.where(core0, other, mine)
+    for c in range(2):
+        first_ref[pl.ds(c, rows, stride=2), :] = first[:, c * 128:(c + 1) * 128]
+        second_ref[pl.ds(c, rows, stride=2), :] = second[:, c * 128:(c + 1) * 128]
+
+
+def join_pair(idx, mine, other):
+    dim, width = mine.shape
+    bd = dim // 3
+    spec = pl.BlockSpec((bd, width), lambda i: (i, 0))
+    out_spec = pl.BlockSpec((bd * 2, 128), lambda i: (i, 0))
+    outs = pl.pallas_call(
+        join_pair_kernel,
+        grid=(dim // bd,),
+        in_specs=[pl.BlockSpec(memory_space=pltpu.SMEM), spec, spec],
+        out_specs=[out_spec, out_spec],
+        out_shape=[jax.ShapeDtypeStruct((dim * 2, 128), F32)] * 2,
+        compiler_params=params(),
+        cost_estimate=cost(1000, 16 * dim * width),
+        name="join_pair",
+    )(idx, mine, other)
+    return [o.reshape(dim, 1, width) for o in outs]
+
+
+def join_rows_kernel(idx_ref, mine_ref, other_ref, out_ref):
+    first = idx_ref[0] % 2 == 0
+    out_ref[...] = jnp.where(first == (pl.program_id(0) == 0), mine_ref[...], other_ref[...])
+
+
+def join_rows(idx, mine, other):
+    rows, dim = mine.shape
+    br = 256
+    steps = rows // br
+    spec = pl.BlockSpec((br, dim), lambda w, i: (i, 0))
+    return pl.pallas_call(
+        join_rows_kernel,
+        grid=(2, steps),
+        in_specs=[pl.BlockSpec(memory_space=pltpu.SMEM), spec, spec],
+        out_specs=pl.BlockSpec((br, dim), lambda w, i: (w * steps + i, 0)),
+        out_shape=jax.ShapeDtypeStruct((rows * 2, dim), F32),
+        compiler_params=params(),
+        cost_estimate=cost(1000, 16 * dim * rows),
+        name="join_rows",
+    )(idx, mine, other)
+
+
 def solution(mesh):
     across = [(0, 2), (2, 0), (1, 3), (3, 1)]
     beside = [(0, 1), (1, 0), (2, 3), (3, 2)]
@@ -560,15 +641,14 @@
 
     def sum_halves(parts):
         mine = parts[0] + permute(parts[1], beside)
-        return mine + permute(mine, across)
+        mine = mine + permute(mine, across)
+        return mine, permute(mine, beside)
 
     def local_step(x_in, positions, dy_out, w_query, w_key, w_value, w_out, w_pre, w_post):
         batch, tokens, dim = x_in.shape
         heads, hd = w_query.shape[1], w_query.shape[2]
         half = hd // 2
-        rank = lax.axis_index("cp").astype(jnp.int32)
-        idx = rank.reshape(1)
-        core = rank % 2
+        idx = lax.axis_index("cp").astype(jnp.int32).reshape(1)
         wq = w_query.reshape(dim, heads * hd)
         wk = w_key.reshape(dim, hd)
         wv = w_value.reshape(dim, hd)
@@ -588,7 +668,7 @@
         acc, row_sum = forward_local(idx, q, own, near)
         mid = permute(far, [(2, 3), (3, 2)])
         y, d_out, stat, dwo, dgain_post = forward_post(idx, q, far, mid, acc, row_sum, x, dy, wo, gain_post)
-        dwo_mine = sum_halves(dwo)
+        dwo_mine, dwo_other = sum_halves(dwo)
 
         dmid, dqt = backward_far(idx, q, d_out, stat, mid, None)
         dmid_in = permute(dmid, [(2, 3), (3, 2)])
@@ -597,28 +677,22 @@
         dnear, down, dq = backward_local(idx, q, d_out, stat, own, near, dqt, cosine, sine)
         dnear_in = permute(dnear, [(1, 0), (3, 2)])
         dwq = grad_wq(idx, act_t, dq)
-        dwq_mine = sum_halves(dwq)
+        dwq_mine, dwq_other = sum_halves(dwq)
         dx, dwkv, dgain_pre = tail(idx, down, dnear_in, dfar_in, cosine, sine, act_t, dq, wq, wk, wv, x, dy, gain_pre)
-        dwkv_mine = sum_halves(dwkv)
+        dwkv_mine, dwkv_other = sum_halves(dwkv)
         gains = jnp.concatenate([dgain_pre, dgain_post], axis=0)
         gains = gains + permute(gains, beside)
         gains = gains + permute(gains, across)
 
-        def join(mine, axis):
-            other = permute(mine, beside)
-            low = jnp.where(core == 0, mine, other)
-            high = jnp.where(core == 0, other, mine)
-            return low, high
-
-        dwo_full = jnp.concatenate(join(dwo_mine, 0), axis=0)
-        dwq_full = jnp.concatenate(join(dwq_mine, 1), axis=1)
-        dwk_full, dwv_full = join(dwkv_mine, 0)
+        dwo_full = join_rows(idx, dwo_mine, dwo_other)
+        dwq_full = join_wide(idx, dwq_mine, dwq_other, heads)
+        dwk_full, dwv_full = join_pair(idx, dwkv_mine, dwkv_other)
         return (
             y.reshape(batch, tokens, dim),
             dx.reshape(batch, tokens, dim),
-            dwq_full.reshape(dim, heads, hd),
-            dwk_full.reshape(dim, 1, hd),
-            dwv_full.reshape(dim, 1, hd),
+            dwq_full,
+            dwk_full,
+            dwv_full,
             dwo_full.reshape(heads, hd, dim),
             gains[0],
             gains[1],

time: 411 us -> 398 us (0.968)
  local copies, waits for them, and re-layouts: 32 us -> 12.8 us
  Pallas kernels: 98 us -> 115 us
  other arithmetic: 27.8 us -> 16 us
    pallas_call x0 -> x3, Pallas kernels: none -> 17.7 us  [the longest x1 7.67 us: join_wide(): pl.pallas_call(join_wide_kernel, grid=(dim // bd,), in_specs=[pl.BlockSpe...]
    unnamed x33 -> x27, local copies, waits for them, and re-layouts: 16.9 us -> 4.34 us
    reshape x1 -> x0, local copies, waits for them, and re-layouts: 6.65 us -> none  [local_step(): dwq_full.reshape(dim, heads, hd)]
    concatenate x2 -> x0, other arithmetic: 5.05 us -> none  [the longest x1 2.56 us: local_step(): dwq_full = jnp.concatenate(join(dwq_mine, 1), axis=1)]
    select_n x2 -> x0, other arithmetic: 4.91 us -> none  [join(): low = jnp.where(core == 0, mine, other)]
  transfers between devices with their start and end apart: 17 -> 17, of which waited for: 6 -> 8; matrix products, arithmetic and copies ran while one was open for 9% -> 5% of each run, Pallas kernels for 16% -> 20%
where the time goes in v2:
time: 398 us; the launch traced here: 397 us
  waiting for transfers between devices  169 us (42%)
  Pallas kernels  115 us (29%)
  starting transfers between devices  82.7 us (21%)
  other arithmetic  16 us (4%)
  local copies, waits for them, and re-layouts  12.8 us (3%)
    ppermute x17, waiting for transfers between devices, permute(): return lax.ppermute(value, 'cp', pairs)  169 us
    ppermute x17, starting transfers between devices, permute(): return lax.ppermute(value, 'cp', pairs)  82.7 us
    pallas_call x1, Pallas kernels, backward_local(): pl.pallas_call(backward_local_kernel, grid=(tokens // bk,), in_specs=[pl....  20.4 us
    pallas_call x1, Pallas kernels, forward_post(): pl.pallas_call(forward_post_kernel, grid=(tokens // bq,), in_specs=[pl.Bl...  20.1 us
    pallas_call x2, Pallas kernels, backward_far(): pl.pallas_call(functools.partial(backward_far_kernel, first=first), grid=...  14.4 us
    pallas_call x1, Pallas kernels, tail(): pl.pallas_call(tail_kernel, grid=(tokens // bt,), in_specs=[pl.BlockSpec(...  12.5 us
    pallas_call x1, Pallas kernels, forward_local(): pl.pallas_call(forward_local_kernel, grid=(tokens // bq,), in_specs=[pl.B...  10.3 us
  transfers between devices with their start and end apart: 17, of which 8 were waited for; matrix products, arithmetic and copies ran while one was open for 5% of the time, Pallas kernels for 20%

profile of v2, /device:TPU:0, one launch (start us, length us, event | category | flops | bytes accessed | tf_op | source)
XLA Modules:
  0.0 397.0 jit_solution(3146817693095656769)
XLA Ops:
  2.6 3.1 multiply_sine_fusion
  5.7 6.0 %project_kv.1 = (bf16[1024,1152]{1,0:T(8,128)(2,1)}, bf16[1152,1024]{1,0:T(8,128)(2,1)}, bf16[2,1024,256]{2,1,0:T(8,128)(2,1)}) custom-call(bf16[1024,1152]{1,0:T(8,128)(2,1)} %bitcast.37, f32[1,1152]{1,0:T(1,128)} %reshape.80.gain_ref, bf16[1152,256]{1,0:T(8,128)(2,1)} %bitcast.42, bf16[1152,256]{1,0:T(8,128)(2,1)} %bitcast.44, ...), custom_call_target="tpu_custom_call" | custom-call | flops 1207959552 | bytes 7077888 | tf_op jit(solution)/shard_map/project_kv/pallas_call | solution.py:65
  11.7 6.1 %collective-permute-start = (bf16[2,1024,256]{2,1,0:T(8,128)(2,1)}, bf16[2,1024,256]{2,1,0:T(8,128)(2,1)}, u32[]{:S(2)}, u32[]{:S(2)}) collective-permute-start(bf16[2,1024,256]{2,1,0:T(8,128)(2,1)} %get-tuple-element.31.own_ref), channel_id=1, source_target_pairs={{0,2},{1,3},{4,6},{5,7},{8,10},{9,11},{12,14},{13,15}} | collective-permute-start | bytes 3145736 | tf_op jit(solution)/shard_map/ppermute | solution.py:640
  19.3 20.2 %collective-permute-done.far_ref.kv_ref = bf16[2,1024,256]{2,1,0:T(8,128)(2,1)} collective-permute-done((bf16[2,1024,256]{2,1,0:T(8,128)(2,1)}, bf16[2,1024,256]{2,1,0:T(8,128)(2,1)}, u32[]{:S(2)}, u32[]{:S(2)}) %collective-permute-start) | collective-permute-done | bytes 1048608 | tf_op jit(solution)/shard_map/ppermute | solution.py:640
  41.2 2.0 copy.20
  43.8 7.1 %project_q.1.q_ref = bf16[4,1024,256]{2,1,0:T(8,128)(2,1)} custom-call(bf16[1024,1152]{1,0:T(8,128)(2,1)} %get-tuple-element.30.a_ref, bf16[1152,1024]{1,0:T(8,128)(2,1)} %bitcast.35, f32[1024,128]{1,0:T(8,128)} %get-tuple-element.63.cos_ref, f32[1024,128]{1,0:T(8,128)} %get-tuple-element.62.sin_ref), custom_call_target="tpu_custom_call" | custom-call | flops 2415919104 | bytes 7077888 | tf_op jit(solution)/shard_map/project_q/pallas_call | solution.py:110
  51.9 10.3 %forward_local.1 = (f32[4,1024,256]{2,1,0:T(8,128)}, f32[4,1024,128]{2,1,0:T(8,128)}) custom-call(s32[1]{0:T(128)} %bitcast.idx_ref, bf16[4,1024,256]{2,1,0:T(8,128)(2,1)} %project_q.1.q_ref, bf16[2,1024,256]{2,1,0:T(8,128)(2,1)} %get-tuple-element.31.own_ref, bf16[2,1024,256]{2,1,0:T(8,128)(2,1)} %copy-done.10), custom_call_target="tpu_custom_call" | custom-call | flops 6442450944 | bytes 8388608 | tf_op jit(solution)/shard_map/forward_local/pallas_call | solution.py:175
  62.2 20.1 %forward_post.1 = (bf16[1024,1152]{1,0:T(8,128)(2,1)}, bf16[4,1024,256]{2,1,0:T(8,128)(2,1)}, f32[8,1024]{1,0:T(8,128)}, f32[2,512,1152]{2,1,0:T(8,128)}, f32[1,1152]{1,0:T(1,128)}) custom-call(s32[1]{0:T(128)} %bitcast.idx_ref, bf16[4,1024,256]{2,1,0:T(8,128)(2,1)} %project_q.1.q_ref, bf16[2,1024,256]{2,1,0:T(8,128)(2,1)} %collective-permute-done.far_ref.kv_ref, ...), custom_call_target="tpu_custom_call" | custom-call | flops 15837691904 | bytes 12582912 | tf_op jit(solution)/shard_map/forward_post/pallas_call | solution.py:264
  82.8 6.6 %backward_far.2 = (f32[2,1024,256]{2,1,0:T(8,128)}, f32[4,256,1024]{2,1,0:T(8,128)}) custom-call(s32[1]{0:T(128)} %bitcast.idx_ref, bf16[4,1024,256]{2,1,0:T(8,128)(2,1)} %project_q.1.q_ref, bf16[4,1024,256]{2,1,0:T(8,128)(2,1)} %get-tuple-element.35.do_ref, f32[8,1024]{1,0:T(8,128)} %get-tuple-element.36.stat_ref, ...), custom_call_target="tpu_custom_call" | custom-call | flops 10737418240 | bytes 12582912 | tf_op jit(solution)/shard_map/backward_far/pallas_call | solution.py:353
  89.5 2.0 collective-permute-start.4
  93.3 5.9 %collective-permute-start.12 = (f32[512,1152]{1,0:T(8,128)S(1)}, f32[512,1152]{1,0:T(8,128)}, u32[]{:S(2)}, u32[]{:S(2)}) collective-permute-start(f32[512,1152]{1,0:T(8,128)S(1)} %slice_bitcast_fusion.2), channel_id=1, source_target_pairs={{0,1},{1,0},{2,3},{3,2},{4,5},{5,4},{6,7},{7,6},{8,9},{9,8},{10,11... | collective-permute-start | bytes 7077896 | tf_op jit(solution)/shard_map/ppermute | solution.py:640
  99.2 7.8 %backward_far.3 = (f32[2,1024,256]{2,1,0:T(8,128)}, f32[4,256,1024]{2,1,0:T(8,128)}) custom-call(s32[1]{0:T(128)} %bitcast.idx_ref, bf16[4,1024,256]{2,1,0:T(8,128)(2,1)} %project_q.1.q_ref, bf16[4,1024,256]{2,1,0:T(8,128)(2,1)} %get-tuple-element.35.do_ref, f32[8,1024]{1,0:T(8,128)} %get-tuple-element.36.stat_ref, ...), custom_call_target="tpu_custom_call" | custom-call | flops 10737418240 | bytes 12582912 | tf_op jit(solution)/shard_map/backward_far/pallas_call | solution.py:353
  107.0 20.4 %backward_local.1 = (f32[2,1024,256]{2,1,0:T(8,128)}, f32[2,1024,256]{2,1,0:T(8,128)}, bf16[1024,1024]{1,0:T(8,128)(2,1)}) custom-call(s32[1]{0:T(128)} %bitcast.idx_ref, bf16[4,1024,256]{2,1,0:T(8,128)(2,1)} %project_q.1.q_ref, bf16[4,1024,256]{2,1,0:T(8,128)(2,1)} %get-tuple-element.35.do_ref, f32[8,1024]{1,0:T(8,128)} %get-tuple-element.36.stat_ref, ...), custom_call_target="tpu_custom_call" | custom-call | flops 16106127360 | bytes 12582912 | tf_op jit(solution)/shard_map/backward_local/pallas_call | solution.py:429
  127.5 6.8 %grad_wq.1 = f32[2,1152,512]{2,1,0:T(8,128)} custom-call(s32[1]{0:T(128)} %bitcast.idx_ref, bf16[1152,1024]{1,0:T(8,128)(2,1)} %get-tuple-element.43.at_ref, bf16[1024,1024]{1,0:T(8,128)(2,1)} %get-tuple-element.44.dq_ref), custom_call_target="tpu_custom_call" | custom-call | flops 2415919104 | bytes 4718592 | tf_op jit(solution)/shard_map/grad_wq/pallas_call | solution.py:474
  134.3 2.0 slice_bitcast_fusion
  136.3 15.0 %collective-permute-start.6 = (f32[1152,512]{1,0:T(8,128)S(1)}, f32[1152,512]{1,0:T(8,128)S(1)}, u32[]{:S(2)}, u32[]{:S(2)}) collective-permute-start(f32[1152,512]{1,0:T(8,128)S(1)} %slice_bitcast_fusion), channel_id=1, source_target_pairs={{0,1},{1,0},{2,3},{3,2},{4,5},{5,4},{6,7},{7,6},{8,9},{9,8},{10,11... | collective-permute-start | bytes 7077896 | tf_op jit(solution)/shard_map/ppermute | solution.py:640
  152.6 2.5 add.27
  156.6 2.6 bitcast_add_fusion
  159.3 43.2 %collective-permute-start.13 = (f32[512,1152]{1,0:T(8,128)S(1)}, f32[512,1152]{1,0:T(8,128)}, u32[]{:S(2)}, u32[]{:S(2)}) collective-permute-start(f32[512,1152]{1,0:T(8,128)S(1)} %bitcast_add_fusion), channel_id=1, source_target_pairs={{0,2},{2,0},{1,3},{3,1},{4,6},{6,4},{5,7},{7,5},{8,10},{10,8},{9,1... | collective-permute-start | bytes 7077896 | tf_op jit(solution)/shard_map/ppermute | solution.py:640
  202.5 1.9 fusion
  204.5 40.9 %collective-permute-done.5.dfar_ref = f32[2,1024,256]{2,1,0:T(8,128)S(1)} collective-permute-done((f32[2,1024,256]{2,1,0:T(8,128)S(1)}, f32[2,1024,256]{2,1,0:T(8,128)S(1)}, u32[]{:S(2)}, u32[]{:S(2)}) %collective-permute-start.5) | collective-permute-done | bytes 2097184 | tf_op jit(solution)/shard_map/ppermute | solution.py:640
  246.6 12.5 %tail.1 = (bf16[1024,1152]{1,0:T(8,128)(2,1)}, f32[2,1152,256]{2,1,0:T(8,128)}, f32[1,1152]{1,0:T(1,128)}) custom-call(s32[1]{0:T(128)} %bitcast.idx_ref, f32[2,1024,256]{2,1,0:T(8,128)} %get-tuple-element.39.down_ref, f32[2,1024,256]{2,1,0:T(8,128)} %copy-done.5, f32[2,1024,256]{2,1,0:T(8,128)} %copy-done.6, f32[1024,128]{1,0:T(8,128)} %get-tuple-element.63.cos_ref, ...), custom_call_target="tpu_custom_call" | custom-call | flops 4831838208 | bytes 9437184 | tf_op jit(solution)/shard_map/tail/pallas_call | solution.py:524
  262.1 2.5 collective-permute-done.9
  264.7 31.3 %collective-permute-done.13 = f32[512,1152]{1,0:T(8,128)} collective-permute-done((f32[512,1152]{1,0:T(8,128)S(1)}, f32[512,1152]{1,0:T(8,128)}, u32[]{:S(2)}, u32[]{:S(2)}) %collective-permute-start.13) | collective-permute-done | bytes 2359328 | tf_op jit(solution)/shard_map/ppermute | solution.py:640
  299.2 47.4 %collective-permute-done.7 = f32[1152,512]{1,0:T(8,128)} collective-permute-done((f32[1152,512]{1,0:T(8,128)}, f32[1152,512]{1,0:T(8,128)}, u32[]{:S(2)}, u32[]{:S(2)}) %collective-permute-start.7) | collective-permute-done | bytes 2359328 | tf_op jit(solution)/shard_map/ppermute | solution.py:640
  346.6 2.9 add.29.mine_ref
  350.7 21.0 %collective-permute-done.10 = f32[1152,256]{1,0:T(8,128)S(1)} collective-permute-done((f32[1152,256]{1,0:T(8,128)S(1)}, f32[1152,256]{1,0:T(8,128)S(1)}, u32[]{:S(2)}, u32[]{:S(2)}) %collective-permute-start.10) | collective-permute-done | bytes 1179680 | tf_op jit(solution)/shard_map/ppermute | solution.py:640
  372.5 2.4 collective-permute-done.15
  375.0 3.6 collective-permute-done.16
  379.3 6.2 %join_rows.1 = f32[1024,1152]{1,0:T(8,128)} custom-call(s32[1]{0:T(128)} %bitcast.idx_ref, f32[512,1152]{1,0:T(8,128)} %copy-done, f32[512,1152]{1,0:T(8,128)} %collective-permute-done.14.other_ref), custom_call_target="tpu_custom_call" | custom-call | flops 1000 | bytes 9437184 | tf_op jit(solution)/shard_map/join_rows/pallas_call | solution.py:623
  385.5 7.7 %join_wide.1 = f32[9216,128]{1,0:T(8,128)} custom-call(s32[1]{0:T(128)} %bitcast.idx_ref, f32[1152,512]{1,0:T(8,128)} %copy-done.1, f32[1152,512]{1,0:T(8,128)} %collective-permute-done.8.other_ref), custom_call_target="tpu_custom_call" | custom-call | flops 1000 | bytes 9437184 | tf_op jit(solution)/shard_map/join_wide/pallas_call | solution.py:572
  393.1 3.9 join_pair.1
  (62 shorter events, 22.2 us)
Async XLA Ops:
  5.7 35.5 %copy-start.4 = (bf16[1152,4,256]{2,1,0:T(4,128)(2,1)S(1)}, bf16[1152,4,256]{2,1,0:T(4,128)(2,1)}, u32[]{:S(2)}) copy-start(bf16[1152,4,256]{2,1,0:T(4,128)(2,1)} %param.12) | copy-start | bytes 7077892
  11.7 27.8 %collective-permute-start = (bf16[2,1024,256]{2,1,0:T(8,128)(2,1)}, bf16[2,1024,256]{2,1,0:T(8,128)(2,1)}, u32[]{:S(2)}, u32[]{:S(2)}) collective-permute-start(bf16[2,1024,256]{2,1,0:T(8,128)(2,1)} %get-tuple-element.31.own_ref), channel_id=1, source_target_pairs={{0,2},{1,3},{4,6},{5,7},{8,10},{9,11},{12,14},{13,15}} | collective-permute-start | bytes 3145736 | tf_op jit(solution)/shard_map/ppermute | solution.py:640
  17.8 33.1 %collective-permute-start.2 = (bf16[2,1024,256]{2,1,0:T(8,128)(2,1)}, bf16[2,1024,256]{2,1,0:T(8,128)(2,1)S(1)}, u32[]{:S(2)}, u32[]{:S(2)}) collective-permute-start(bf16[2,1024,256]{2,1,0:T(8,128)(2,1)} %get-tuple-element.31.own_ref), channel_id=1, source_target_pairs={{0,1},{2,3},{4,5},{6,7},{8,9},{10,11},{12,13},{14,15}} | collective-permute-start | bytes 3145736 | tf_op jit(solution)/shard_map/ppermute | solution.py:640
  39.5 22.6 %collective-permute-start.1 = (bf16[2,1024,256]{2,1,0:T(8,128)(2,1)}, bf16[2,1024,256]{2,1,0:T(8,128)(2,1)}, u32[]{:S(2)}, u32[]{:S(2)}) collective-permute-start(bf16[2,1024,256]{2,1,0:T(8,128)(2,1)} %collective-permute-done.far_ref.kv_ref), channel_id=1, source_target_pairs={{2,3},{3,2},{6,7},{7,6},{10,11},{11,10},{14,15},{15,14}} | collective-permute-start | bytes 3145736 | tf_op jit(solution)/shard_map/ppermute | solution.py:640
  41.2 2.0 copy-start.9
  50.9 1.0 copy-start.10
  89.5 63.1 %collective-permute-start.4 = (f32[2,1024,256]{2,1,0:T(8,128)}, f32[2,1024,256]{2,1,0:T(8,128)}, u32[]{:S(2)}, u32[]{:S(2)}) collective-permute-start(f32[2,1024,256]{2,1,0:T(8,128)} %get-tuple-element.42), channel_id=1, source_target_pairs={{2,3},{3,2},{6,7},{7,6},{10,11},{11,10},{14,15},{15,14}} | collective-permute-start | bytes 6291464 | tf_op jit(solution)/shard_map/ppermute | solution.py:640
  93.3 63.3 %collective-permute-start.12 = (f32[512,1152]{1,0:T(8,128)S(1)}, f32[512,1152]{1,0:T(8,128)}, u32[]{:S(2)}, u32[]{:S(2)}) collective-permute-start(f32[512,1152]{1,0:T(8,128)S(1)} %slice_bitcast_fusion.2), channel_id=1, source_target_pairs={{0,1},{1,0},{2,3},{3,2},{4,5},{5,4},{6,7},{7,6},{8,9},{9,8},{10,11... | collective-permute-start | bytes 7077896 | tf_op jit(solution)/shard_map/ppermute | solution.py:640
  134.3 68.2 %slice-start = ((s8[4718592]{0:T(1024)(128)(4,1)}), s8[4194304]{0:T(1024)(128)(4,1)S(1)}, s32[]{:S(2)}) async-start(s8[4718592]{0:T(1024)(128)(4,1)} %bitcast.33), calls=%async_computation | async-start | bytes 8388608
  136.3 66.2 %collective-permute-start.6 = (f32[1152,512]{1,0:T(8,128)S(1)}, f32[1152,512]{1,0:T(8,128)S(1)}, u32[]{:S(2)}, u32[]{:S(2)}) collective-permute-start(f32[1152,512]{1,0:T(8,128)S(1)} %slice_bitcast_fusion), channel_id=1, source_target_pairs={{0,1},{1,0},{2,3},{3,2},{4,5},{5,4},{6,7},{7,6},{8,9},{9,8},{10,11... | collective-permute-start | bytes 7077896 | tf_op jit(solution)/shard_map/ppermute | solution.py:640
  151.2 53.2 %collective-permute-start.3 = (f32[2,1024,256]{2,1,0:T(8,128)}, f32[2,1024,256]{2,1,0:T(8,128)S(1)}, u32[]{:S(2)}, u32[]{:S(2)}) collective-permute-start(f32[2,1024,256]{2,1,0:T(8,128)} %get-tuple-element.40), channel_id=1, source_target_pairs={{1,0},{3,2},{5,4},{7,6},{9,8},{11,10},{13,12},{15,14}} | collective-permute-start | bytes 6291464 | tf_op jit(solution)/shard_map/ppermute | solution.py:640
  152.5 49.9 %slice-start.1 = ((s8[4718592]{0:T(1024)(128)(4,1)}), s8[524288]{0:T(1024)(128)(4,1)S(1)}, s32[]{:S(2)}) async-start(s8[4718592]{0:T(1024)(128)(4,1)} %bitcast.33), calls=%async_computation.1 | async-start | bytes 1048576
  155.1 90.2 %collective-permute-start.5 = (f32[2,1024,256]{2,1,0:T(8,128)S(1)}, f32[2,1024,256]{2,1,0:T(8,128)S(1)}, u32[]{:S(2)}, u32[]{:S(2)}) collective-permute-start(f32[2,1024,256]{2,1,0:T(8,128)S(1)} %add.27), channel_id=1, source_target_pairs={{2,0},{3,1},{6,4},{7,5},{10,8},{11,9},{14,12},{15,13}} | collective-permute-start | bytes 6291464 | tf_op jit(solution)/shard_map/ppermute | solution.py:640
  159.3 136.7 %collective-permute-start.13 = (f32[512,1152]{1,0:T(8,128)S(1)}, f32[512,1152]{1,0:T(8,128)}, u32[]{:S(2)}, u32[]{:S(2)}) collective-permute-start(f32[512,1152]{1,0:T(8,128)S(1)} %bitcast_add_fusion), channel_id=1, source_target_pairs={{0,2},{2,0},{1,3},{3,1},{4,6},{6,4},{5,7},{7,5},{8,10},{10,8},{9,1... | collective-permute-start | bytes 7077896 | tf_op jit(solution)/shard_map/ppermute | solution.py:640
  204.4 142.1 %collective-permute-start.7 = (f32[1152,512]{1,0:T(8,128)}, f32[1152,512]{1,0:T(8,128)}, u32[]{:S(2)}, u32[]{:S(2)}) collective-permute-start(f32[1152,512]{1,0:T(8,128)} %fusion), channel_id=1, source_target_pairs={{0,2},{2,0},{1,3},{3,1},{4,6},{6,4},{5,7},{7,5},{8,10},{10,8},{9,1... | collective-permute-start | bytes 7077896 | tf_op jit(solution)/shard_map/ppermute | solution.py:640
  204.5 40.9 %copy-start.5 = (f32[2,1024,256]{2,1,0:T(8,128)}, f32[2,1024,256]{2,1,0:T(8,128)S(1)}, u32[]{:S(2)}) copy-start(f32[2,1024,256]{2,1,0:T(8,128)S(1)} %collective-permute-done.3.dnear_ref) | copy-start | bytes 6291460
  245.3 1.3 copy-start.6
  259.1 5.4 %copy-start.3 = (f32[2,1152,256]{2,1,0:T(8,128)S(1)}, f32[2,1152,256]{2,1,0:T(8,128)}, u32[]{:S(2)}) copy-start(f32[2,1152,256]{2,1,0:T(8,128)} %get-tuple-element.46) | copy-start | bytes 7077892
  260.7 3.9 collective-permute-start.9
  264.7 107.0 %collective-permute-start.10 = (f32[1152,256]{1,0:T(8,128)S(1)}, f32[1152,256]{1,0:T(8,128)S(1)}, u32[]{:S(2)}, u32[]{:S(2)}) collective-permute-start(f32[1152,256]{1,0:T(8,128)S(1)} %bitcast_add_fusion.1), channel_id=1, source_target_pairs={{0,2},{2,0},{1,3},{3,1},{4,6},{6,4},{5,7},{7,5},{8,10},{10,8},{9,1... | collective-permute-start | bytes 3538952 | tf_op jit(solution)/shard_map/ppermute | solution.py:640
  297.9 51.6 %copy-start = (f32[512,1152]{1,0:T(8,128)}, f32[512,1152]{1,0:T(8,128)S(1)}, u32[]{:S(2)}) copy-start(f32[512,1152]{1,0:T(8,128)S(1)} %add.33.mine_ref) | copy-start | bytes 7077892
  297.9 81.4 %collective-permute-start.14 = (f32[512,1152]{1,0:T(8,128)S(1)}, f32[512,1152]{1,0:T(8,128)}, u32[]{:S(2)}, u32[]{:S(2)}) collective-permute-start(f32[512,1152]{1,0:T(8,128)S(1)} %add.33.mine_ref), channel_id=1, source_target_pairs={{0,1},{1,0},{2,3},{3,2},{4,5},{5,4},{6,7},{7,6},{8,9},{9,8},{10,11... | collective-permute-start | bytes 7077896 | tf_op jit(solution)/shard_map/ppermute | solution.py:640
  349.5 36.0 %copy-start.1 = (f32[1152,512]{1,0:T(8,128)}, f32[1152,512]{1,0:T(8,128)S(1)}, u32[]{:S(2)}) copy-start(f32[1152,512]{1,0:T(8,128)S(1)} %add.29.mine_ref) | copy-start | bytes 7077892
  349.5 22.8 %copy-start.7 = (f32[1,1152]{1,0:T(1,128)S(1)}, f32[1,1152]{1,0:T(1,128)}, u32[]{:S(2)}) copy-start(f32[1,1152]{1,0:T(1,128)} %get-tuple-element.51) | copy-start | bytes 13828
  349.5 22.8 %copy-start.8 = (f32[1,1152]{1,0:T(1,128)S(1)}, f32[1,1152]{1,0:T(1,128)}, u32[]{:S(2)}) copy-start(f32[1,1152]{1,0:T(1,128)} %get-tuple-element.50) | copy-start | bytes 13828
  349.5 35.9 %collective-permute-start.8 = (f32[1152,512]{1,0:T(8,128)S(1)}, f32[1152,512]{1,0:T(8,128)}, u32[]{:S(2)}, u32[]{:S(2)}) collective-permute-start(f32[1152,512]{1,0:T(8,128)S(1)} %add.29.mine_ref), channel_id=1, source_target_pairs={{0,1},{1,0},{2,3},{3,2},{4,5},{5,4},{6,7},{7,6},{8,9},{9,8},{10,11... | collective-permute-start | bytes 7077896 | tf_op jit(solution)/shard_map/ppermute | solution.py:640
  371.9 13.6 %copy-start.2 = (f32[1152,256]{1,0:T(8,128)}, f32[1152,256]{1,0:T(8,128)S(1)}, u32[]{:S(2)}) copy-start(f32[1152,256]{1,0:T(8,128)S(1)} %add.31.mine_ref) | copy-start | bytes 3538948
  371.9 21.2 %collective-permute-start.11 = (f32[1152,256]{1,0:T(8,128)S(1)}, f32[1152,256]{1,0:T(8,128)}, u32[]{:S(2)}, u32[]{:S(2)}) collective-permute-start(f32[1152,256]{1,0:T(8,128)S(1)} %add.31.mine_ref), channel_id=1, source_target_pairs={{0,1},{1,0},{2,3},{3,2},{4,5},{5,4},{6,7},{7,6},{8,9},{9,8},{10,11... | collective-permute-start | bytes 3538952 | tf_op jit(solution)/shard_map/ppermute | solution.py:640
  372.3 2.6 collective-permute-start.15
  374.9 3.7 collective-permute-start.16

commit v3 on v2

--- a/solution.py
+++ b/solution.py
@@ -1,4 +1,3 @@
-import functools
 import math
 
 import jax
@@ -16,6 +15,7 @@
 LOG2E = math.log2(math.e)
 CAP2 = SOFT_CAP * LOG2E
 INV_CAP = 1.0 / SOFT_CAP
+
 
 F32 = jnp.float32
 BF16 = jnp.bfloat16
@@ -195,74 +195,42 @@
     )(idx, q, own, near)
 
 
-def forward_post_kernel(idx_ref, q_ref, far_ref, mid_ref, acc_in_ref, sum_in_ref, x_ref, dy_ref, wo_ref, gain_ref,
-                        y_ref, do_ref, stat_ref, dwo_ref, dgain_ref, acc_ref, sum_ref, o_ref, dz_ref):
+def forward_far_kernel(idx_ref, q_ref, far_ref, mid_ref, acc_in_ref, sum_in_ref, o_ref, out_ref, lse_ref, acc_ref, sum_ref):
     heads, bq, hd = q_ref.shape
     tokens = far_ref.shape[1]
-    i = pl.program_id(0)
-    steps = pl.num_programs(0)
     acc_ref[...] = acc_in_ref[...]
     sum_ref[...] = sum_in_ref[...]
 
     @pl.when(idx_ref[0] >= 2)
     def _():
-        def step(j, _):
-            rows = pl.ds(pl.multiple_of(j * 512, 512), 512)
-            forward_tile(q_ref, acc_ref, sum_ref, far_ref[0, rows, :], far_ref[1, rows, :], False)
-            forward_tile(q_ref, acc_ref, sum_ref, mid_ref[0, rows, :], mid_ref[1, rows, :], False)
-            return 0
-
-        lax.fori_loop(0, tokens // 512, step, 0)
+        def step(ref):
+            def run(j, _):
+                rows = pl.ds(pl.multiple_of(j * 512, 512), 512)
+                forward_tile(q_ref, acc_ref, sum_ref, ref[0, rows, :], ref[1, rows, :], False)
+                return 0
+
+            return run
+
+        lax.fori_loop(0, tokens // 512, step(far_ref), 0)
+        lax.fori_loop(0, tokens // 512, step(mid_ref), 0)
 
     lane = lax.broadcasted_iota(jnp.int32, (bq, 128), 1)
-    stat = jnp.zeros((bq, 128), F32)
+    lse = jnp.zeros((bq, 128), F32)
     for h in range(heads):
         total = jnp.sum(sum_ref[h], axis=-1, keepdims=True)
-        stat = jnp.where(lane == h, jnp.log2(total), stat)
+        lse = jnp.where(lane == h, jnp.log2(total), lse)
         out = acc_ref[h] / total
-        acc_ref[h] = out
-        o_ref[pl.ds(pl.multiple_of(i * bq, bq), bq), h * hd:(h + 1) * hd] = out.astype(BF16)
-    rows = pl.ds(pl.multiple_of(i * bq, bq), bq)
-    z = dot(o_ref[rows, :], wo_ref[...]).astype(BF16).astype(F32)
-    gain = 1.0 + gain_ref[...]
-    rstd = lax.rsqrt(jnp.mean(z * z, axis=-1, keepdims=True) + NORM_EPS)
-    z_unit = z * rstd
-    y_ref[...] = (x_ref[...].astype(F32) + (z_unit * gain).astype(BF16).astype(F32)).astype(BF16)
-    dy = dy_ref[...].astype(F32)
-
-    @pl.when(i == 0)
-    def _():
-        dgain_ref[...] = jnp.zeros_like(dgain_ref)
-
-    dgain_ref[...] += jnp.sum(dy * z_unit, axis=0, keepdims=True)
-    g = dy * gain
-    dz = (rstd * (g - z_unit * jnp.mean(g * z_unit, axis=-1, keepdims=True))).astype(BF16)
-    dz_ref[rows, :] = dz
-    for h in range(heads):
-        d_out = dot(dz, wo_ref[h * hd:(h + 1) * hd, :], NT).astype(BF16)
-        do_ref[h] = d_out
-        delta = jnp.sum(d_out.astype(F32) * acc_ref[h], axis=-1, keepdims=True)
-        stat = jnp.where(lane == heads + h, delta, stat)
-    stat_ref[...] = stat.T[0:8, :]
-
-    @pl.when(i == steps - 1)
-    def _():
-        core = idx_ref[0] % 2
-        per = heads // 2
-        for which in range(2):
-            for hh in range(per):
-                cols = pl.ds(pl.multiple_of((((core + which) % 2) * per + hh) * hd, hd), hd)
-                dwo_ref[which, hh * hd:(hh + 1) * hd, :] = dot(o_ref[:, cols].T, dz_ref[...])
-
-
-def forward_post(idx, q, far, mid, acc, row_sum, x, dy, wo, gain):
+        out_ref[h] = out
+        o_ref[:, h * hd:(h + 1) * hd] = out.astype(BF16)
+    lse_ref[...] = lse
+
+
+def forward_far(idx, q, far, mid, acc, row_sum):
     heads, tokens, hd = q.shape
-    dim = x.shape[1]
     bq = 256
     rows3 = lambda last: pl.BlockSpec((heads, bq, last), lambda i: (0, i, 0))
-    rows2 = pl.BlockSpec((bq, dim), lambda i: (i, 0))
-    return pl.pallas_call(
-        forward_post_kernel,
+    return pl.pallas_call(
+        forward_far_kernel,
         grid=(tokens // bq,),
         in_specs=[
             pl.BlockSpec(memory_space=pltpu.SMEM),
@@ -271,35 +239,127 @@
             whole(mid.shape),
             rows3(hd),
             rows3(128),
+        ],
+        out_specs=[
+            pl.BlockSpec((bq, heads * hd), lambda i: (i, 0)),
+            rows3(hd),
+            pl.BlockSpec((bq, 128), lambda i: (i, 0)),
+        ],
+        out_shape=[
+            jax.ShapeDtypeStruct((tokens, heads * hd), BF16),
+            jax.ShapeDtypeStruct((heads, tokens, hd), F32),
+            jax.ShapeDtypeStruct((tokens, 128), F32),
+        ],
+        scratch_shapes=[
+            pltpu.VMEM((heads, bq, hd), F32),
+            pltpu.VMEM((heads, bq, 128), F32),
+        ],
+        compiler_params=params(),
+        cost_estimate=cost(8 * heads * tokens * tokens * hd, 12 * heads * tokens * hd),
+        name="forward_far",
+    )(idx, q, far, mid, acc, row_sum)
+
+
+def post_norm(o, wo, gain, dy):
+    z = dot(o, wo).astype(BF16).astype(F32)
+    rstd = lax.rsqrt(jnp.mean(z * z, axis=-1, keepdims=True) + NORM_EPS)
+    unit = z * rstd
+    g = dy * gain
+    dz = (rstd * (g - unit * jnp.mean(g * unit, axis=-1, keepdims=True))).astype(BF16)
+    return unit, dz
+
+
+def post_kernel(o_ref, out_ref, lse_ref, x_ref, dy_ref, wo_ref, gain_ref, y_ref, do_ref, dz_ref, stat_ref, dgain_ref):
+    heads, bq, hd = out_ref.shape
+    gain = 1.0 + gain_ref[...]
+    dy = dy_ref[...].astype(F32)
+    unit, dz = post_norm(o_ref[...], wo_ref[...], gain, dy)
+    y_ref[...] = (x_ref[...].astype(F32) + (unit * gain).astype(BF16).astype(F32)).astype(BF16)
+    dz_ref[...] = dz
+
+    @pl.when(pl.program_id(0) == 0)
+    def _():
+        dgain_ref[...] = jnp.zeros_like(dgain_ref)
+
+    dgain_ref[...] += jnp.sum(dy * unit, axis=0, keepdims=True)
+    lane = lax.broadcasted_iota(jnp.int32, (bq, 128), 1)
+    stat = lse_ref[...]
+    for h in range(heads):
+        d_out = dot(dz, wo_ref[h * hd:(h + 1) * hd, :], NT).astype(BF16)
+        do_ref[h] = d_out
+        delta = jnp.sum(d_out.astype(F32) * out_ref[h], axis=-1, keepdims=True)
+        stat = jnp.where(lane == heads + h, delta, stat)
+    stat_ref[...] = stat.T[0:8, :]
+
+
+def post(o, out, lse, x, dy, wo, gain):
+    heads, tokens, hd = out.shape
+    dim = x.shape[1]
+    bq = 256
+    rows3 = pl.BlockSpec((heads, bq, hd), lambda i: (0, i, 0))
+    rows2 = lambda width: pl.BlockSpec((bq, width), lambda i: (i, 0))
+    return pl.pallas_call(
+        post_kernel,
+        grid=(tokens // bq,),
+        in_specs=[rows2(heads * hd), rows3, rows2(128), rows2(dim), rows2(dim), whole(wo.shape), whole((1, dim))],
+        out_specs=[rows2(dim), rows3, rows2(dim), pl.BlockSpec((8, bq), lambda i: (0, i)), whole((1, dim))],
+        out_shape=[
+            jax.ShapeDtypeStruct((tokens, dim), BF16),
+            jax.ShapeDtypeStruct((heads, tokens, hd), BF16),
+            jax.ShapeDtypeStruct((tokens, dim), BF16),
+            jax.ShapeDtypeStruct((8, tokens), F32),
+            jax.ShapeDtypeStruct((1, dim), F32),
+        ],
+        compiler_params=params(),
+        cost_estimate=cost(4 * tokens * heads * hd * dim, 12 * heads * tokens * hd),
+        name="post",
+    )(o, out, lse, x, dy, wo, gain)
+
+
+def grad_wo_kernel(idx_ref, o_ref, dz_ref, po_ref, pdy_low_ref, pdy_high_ref, wo_ref, gain_ref, dwo_ref, pdz_ref):
+    _, width = o_ref.shape
+    bt = pdy_low_ref.shape[0]
+    hd = 256
+    i = pl.program_id(0)
+    rows = pl.ds(pl.multiple_of(i * bt, bt), bt)
+    dy = jnp.where(idx_ref[0] >= 2, pdy_high_ref[...], pdy_low_ref[...]).astype(F32)
+    pdz_ref[rows, :] = post_norm(po_ref[rows, :], wo_ref[...], 1.0 + gain_ref[...], dy)[1]
+
+    @pl.when(i == pl.num_programs(0) - 1)
+    def _():
+        core = idx_ref[0] % 2
+        per = width // hd // 2
+        for which in range(2):
+            for hh in range(per):
+                cols = pl.ds(pl.multiple_of((((core + which) % 2) * per + hh) * hd, hd), hd)
+                dwo_ref[which, hh * hd:(hh + 1) * hd, :] = dot(o_ref[:, cols].T, dz_ref[...]) + dot(po_ref[:, cols].T, pdz_ref[...])
+
+
+def grad_wo(idx, o, dz, po, pdy_low, pdy_high, wo, gain):
+    tokens, width = o.shape
+    dim = dz.shape[1]
+    bt = 256
+    rows2 = pl.BlockSpec((bt, dim), lambda i: (i, 0))
+    return pl.pallas_call(
+        grad_wo_kernel,
+        grid=(tokens // bt,),
+        in_specs=[
+            pl.BlockSpec(memory_space=pltpu.SMEM),
+            whole(o.shape),
+            whole(dz.shape),
+            whole(o.shape),
             rows2,
             rows2,
             whole(wo.shape),
             whole((1, dim)),
         ],
-        out_specs=[
-            rows2,
-            rows3(hd),
-            pl.BlockSpec((8, bq), lambda i: (0, i)),
-            whole((2, heads * hd // 2, dim)),
-            whole((1, dim)),
-        ],
-        out_shape=[
-            jax.ShapeDtypeStruct((tokens, dim), BF16),
-            jax.ShapeDtypeStruct((heads, tokens, hd), BF16),
-            jax.ShapeDtypeStruct((8, tokens), F32),
-            jax.ShapeDtypeStruct((2, heads * hd // 2, dim), F32),
-            jax.ShapeDtypeStruct((1, dim), F32),
-        ],
-        scratch_shapes=[
-            pltpu.VMEM((heads, bq, hd), F32),
-            pltpu.VMEM((heads, bq, 128), F32),
-            pltpu.VMEM((tokens, heads * hd), BF16),
-            pltpu.VMEM((tokens, dim), BF16),
-        ],
-        compiler_params=params(),
-        cost_estimate=cost(8 * heads * tokens * tokens * hd + 6 * tokens * heads * hd * dim, 12 * heads * tokens * hd),
-        name="forward_post",
-    )(idx, q, far, mid, acc, row_sum, x, dy, wo, gain)
+        out_specs=whole((2, width // 2, dim)),
+        out_shape=jax.ShapeDtypeStruct((2, width // 2, dim), F32),
+        scratch_shapes=[pltpu.VMEM((tokens, dim), BF16)],
+        compiler_params=params(),
+        cost_estimate=cost(6 * tokens * width * dim, 12 * tokens * dim),
+        name="grad_wo",
+    )(idx, o, dz, po, pdy_low, pdy_high, wo, gain)
 
 
 def backward_tile(q_ref, do_ref, stat_ref, dqt_ref, dkv_ref, k, v, kt, start, bq, masked):
@@ -322,57 +382,61 @@
         dqt_ref[h, :, rows] += dot(kt, ds)
 
 
-def backward_far_kernel(idx_ref, q_ref, do_ref, stat_ref, kv_ref, dqt_in_ref, dkv_ref, dqt_ref, *, first):
+def backward_far_kernel(idx_ref, q_ref, do_ref, stat_ref, mid_ref, far_ref, dmid_ref, dfar_ref, dqt_ref):
     tokens = q_ref.shape[1]
     bq = 512
-
-    @pl.when(pl.program_id(0) == 0)
-    def _():
-        dqt_ref[...] = jnp.zeros_like(dqt_ref) if first else dqt_in_ref[...]
-
-    dkv_ref[...] = jnp.zeros_like(dkv_ref)
-
-    @pl.when(idx_ref[0] >= 2)
-    def _():
-        k, v = kv_ref[0], kv_ref[1]
-        kt = k.T
-
-        def step(j, _):
-            backward_tile(q_ref, do_ref, stat_ref, dqt_ref, dkv_ref, k, v, kt, j * bq, bq, False)
-            return 0
-
-        lax.fori_loop(0, tokens // bq, step, 0)
-
-
-def backward_far(idx, q, d_out, stat, kv, dqt):
+    i = pl.program_id(0)
+    per = pl.num_programs(0) // 2
+
+    @pl.when(i == 0)
+    def _():
+        dqt_ref[...] = jnp.zeros_like(dqt_ref)
+
+    def block(kv_ref, dkv_ref):
+        dkv_ref[...] = jnp.zeros_like(dkv_ref)
+
+        @pl.when(idx_ref[0] >= 2)
+        def _():
+            k, v = kv_ref[0], kv_ref[1]
+            kt = k.T
+
+            def step(j, _):
+                backward_tile(q_ref, do_ref, stat_ref, dqt_ref, dkv_ref, k, v, kt, j * bq, bq, False)
+                return 0
+
+            lax.fori_loop(0, tokens // bq, step, 0)
+
+    pl.when(i < per)(lambda: block(mid_ref, dmid_ref))
+    pl.when(i >= per)(lambda: block(far_ref, dfar_ref))
+
+
+def backward_far(idx, q, d_out, stat, mid, far):
     heads, tokens, hd = q.shape
     bk = 256
-    first = dqt is None
-    if first:
-        dqt = jnp.zeros((8, 128), F32)
-    return pl.pallas_call(
-        functools.partial(backward_far_kernel, first=first),
-        grid=(tokens // bk,),
+    per = tokens // bk
+    early = pl.BlockSpec((2, bk, hd), lambda i: (0, jnp.minimum(i, per - 1), 0))
+    late = pl.BlockSpec((2, bk, hd), lambda i: (0, jnp.maximum(i - per, 0), 0))
+    return pl.pallas_call(
+        backward_far_kernel,
+        grid=(2 * per,),
         in_specs=[
             pl.BlockSpec(memory_space=pltpu.SMEM),
             whole(q.shape),
             whole(d_out.shape),
             whole(stat.shape),
-            pl.BlockSpec((2, bk, hd), lambda i: (0, i, 0)),
-            whole(dqt.shape),
-        ],
-        out_specs=[
-            pl.BlockSpec((2, bk, hd), lambda i: (0, i, 0)),
-            whole((heads, hd, tokens)),
-        ],
+            early,
+            late,
+        ],
+        out_specs=[early, late, whole((heads, hd, tokens))],
         out_shape=[
             jax.ShapeDtypeStruct((2, tokens, hd), F32),
+            jax.ShapeDtypeStruct((2, tokens, hd), F32),
             jax.ShapeDtypeStruct((heads, hd, tokens), F32),
         ],
         compiler_params=params(),
-        cost_estimate=cost(10 * heads * tokens * tokens * hd, 12 * heads * tokens * hd),
+        cost_estimate=cost(20 * heads * tokens * tokens * hd, 12 * heads * tokens * hd),
         name="backward_far",
-    )(idx, q, d_out, stat, kv, dqt)
+    )(idx, q, d_out, stat, mid, far)
 
 
 def backward_local_kernel(idx_ref, q_ref, do_ref, stat_ref, own_ref, near_ref, dqt_in_ref, cos_ref, sin_ref,
@@ -482,8 +546,9 @@
 
 
 def tail_kernel(idx_ref, down_ref, dnear_ref, dfar_ref, cos_ref, sin_ref, at_ref, dq_ref, wq_ref, wk_ref, wv_ref,
-                x_ref, dy_ref, gain_ref, dx_ref, dwkv_ref, dgain_ref):
+                x_ref, dy_ref, gain_ref, dpost_ref, dx_ref, dwkv_ref, dgain_ref):
     _, half = cos_ref.shape
+    dim = x_ref.shape[1]
     i = pl.program_id(0)
     dk = down_ref[0] + dnear_ref[0] + dfar_ref[0]
     cosine, sine = cos_ref[...], sin_ref[...]
@@ -501,8 +566,8 @@
     is_core0 = core == 0
     mine = jnp.where(is_core0, dk, dv)
     theirs = jnp.where(is_core0, dv, dk)
-    dwkv_ref[0] += dot(at, mine)
-    dwkv_ref[1] += dot(at, theirs)
+    dwkv_ref[0, 0:dim, :] += dot(at, mine)
+    dwkv_ref[1, 0:dim, :] += dot(at, theirs)
     da = dot(dq_ref[...], wq_ref[...], NT) + dot(dk, wk_ref[...], NT) + dot(dv, wv_ref[...], NT)
     x = x_ref[...].astype(F32)
     rstd = lax.rsqrt(jnp.mean(x * x, axis=-1, keepdims=True) + NORM_EPS)
@@ -512,8 +577,15 @@
     dx = rstd * (g - unit * jnp.mean(g * unit, axis=-1, keepdims=True))
     dx_ref[...] = (dy_ref[...].astype(F32) + dx).astype(BF16)
 
-
-def tail(idx, down, dnear, dfar, cosine, sine, at, dq, wq, wk, wv, x, dy, gain):
+    @pl.when(i == pl.num_programs(0) - 1)
+    def _():
+        dpre, dpost = dgain_ref[...], dpost_ref[...]
+        for which, row in enumerate((jnp.where(is_core0, dpre, dpost), jnp.where(is_core0, dpost, dpre))):
+            for c in range(dim // 128):
+                dwkv_ref[which, dim + c // 2:dim + c // 2 + 1, c % 2 * 128:(c % 2 + 1) * 128] = row[:, c * 128:(c + 1) * 128]
+
+
+def tail(idx, down, dnear, dfar, cosine, sine, at, dq, wq, wk, wv, x, dy, gain, dpost):
     tokens, dim = x.shape
     hd = wk.shape[1]
     width = wq.shape[1]
@@ -539,17 +611,18 @@
             rows2,
             rows2,
             whole((1, dim)),
-        ],
-        out_specs=[rows2, whole((2, dim, hd)), whole((1, dim))],
+            whole((1, dim)),
+        ],
+        out_specs=[rows2, whole((2, dim + 8, hd))],
         out_shape=[
             jax.ShapeDtypeStruct((tokens, dim), BF16),
-            jax.ShapeDtypeStruct((2, dim, hd), F32),
-            jax.ShapeDtypeStruct((1, dim), F32),
-        ],
+            jax.ShapeDtypeStruct((2, dim + 8, hd), F32),
+        ],
+        scratch_shapes=[pltpu.VMEM((1, dim), F32)],
         compiler_params=params(),
         cost_estimate=cost(2 * tokens * dim * (width + 4 * hd), 8 * tokens * dim),
         name="tail",
-    )(idx, down, dnear, dfar, cosine, sine, at, dq, wq, wk, wv, x, dy, gain)
+    )(idx, down, dnear, dfar, cosine, sine, at, dq, wq, wk, wv, x, dy, gain, dpost)
 
 
 def join_wide_kernel(idx_ref, mine_ref, other_ref, out_ref):
@@ -582,32 +655,30 @@
     return out.reshape(dim, 2, heads, 128).transpose(0, 2, 1, 3).reshape(dim, heads, 256)
 
 
-def join_pair_kernel(idx_ref, mine_ref, other_ref, first_ref, second_ref):
+def join_pair_kernel(idx_ref, mine_ref, other_ref, first_ref, second_ref, dpre_ref, dpost_ref):
     core0 = idx_ref[0] % 2 == 0
-    rows = mine_ref.shape[0]
+    dim = dpre_ref.shape[1]
     mine, other = mine_ref[...], other_ref[...]
     first, second = jnp.where(core0, mine, other), jnp.where(core0, other, mine)
-    for c in range(2):
-        first_ref[pl.ds(c, rows, stride=2), :] = first[:, c * 128:(c + 1) * 128]
-        second_ref[pl.ds(c, rows, stride=2), :] = second[:, c * 128:(c + 1) * 128]
+    for src, out_ref, gain_ref in ((first, first_ref, dpre_ref), (second, second_ref, dpost_ref)):
+        for c in range(2):
+            out_ref[pl.ds(c, dim, stride=2), :] = src[0:dim, c * 128:(c + 1) * 128]
+        for c in range(dim // 128):
+            gain_ref[:, c * 128:(c + 1) * 128] = src[dim + c // 2:dim + c // 2 + 1, c % 2 * 128:(c % 2 + 1) * 128]
 
 
 def join_pair(idx, mine, other):
-    dim, width = mine.shape
-    bd = dim // 3
-    spec = pl.BlockSpec((bd, width), lambda i: (i, 0))
-    out_spec = pl.BlockSpec((bd * 2, 128), lambda i: (i, 0))
+    dim, width = mine.shape[0] - 8, mine.shape[1]
     outs = pl.pallas_call(
         join_pair_kernel,
-        grid=(dim // bd,),
-        in_specs=[pl.BlockSpec(memory_space=pltpu.SMEM), spec, spec],
-        out_specs=[out_spec, out_spec],
-        out_shape=[jax.ShapeDtypeStruct((dim * 2, 128), F32)] * 2,
+        in_specs=[pl.BlockSpec(memory_space=pltpu.SMEM), whole(mine.shape), whole(mine.shape)],
+        out_specs=[whole((dim * 2, 128))] * 2 + [whole((1, dim))] * 2,
+        out_shape=[jax.ShapeDtypeStruct((dim * 2, 128), F32)] * 2 + [jax.ShapeDtypeStruct((1, dim), F32)] * 2,
         compiler_params=params(),
         cost_estimate=cost(1000, 16 * dim * width),
         name="join_pair",
     )(idx, mine, other)
-    return [o.reshape(dim, 1, width) for o in outs]
+    return [o.reshape(dim, 1, width) for o in outs[:2]] + [o.reshape(dim) for o in outs[2:]]
 
 
 def join_rows_kernel(idx_ref, mine_ref, other_ref, out_ref):
@@ -640,7 +711,8 @@
         return lax.ppermute(value, "cp", pairs)
 
     def sum_halves(parts):
-        mine = parts[0] + permute(parts[1], beside)
+        theirs = permute(parts[1], beside)
+        mine = parts[0] + theirs
         mine = mine + permute(mine, across)
         return mine, permute(mine, beside)
 
@@ -667,26 +739,28 @@
         q = project_q(act, wq, cosine, sine, heads)
         acc, row_sum = forward_local(idx, q, own, near)
         mid = permute(far, [(2, 3), (3, 2)])
-        y, d_out, stat, dwo, dgain_post = forward_post(idx, q, far, mid, acc, row_sum, x, dy, wo, gain_post)
-        dwo_mine, dwo_other = sum_halves(dwo)
-
-        dmid, dqt = backward_far(idx, q, d_out, stat, mid, None)
+        dy_high = permute(dy, [(2, 0), (3, 1)])
+        o, out, lse = forward_far(idx, q, far, mid, acc, row_sum)
+        dy_low = permute(dy, [(0, 2), (1, 3)])
+        partner_o = permute(o, across)
+        y, d_out, dz, stat, dgain_post = post(o, out, lse, x, dy, wo, gain_post)
+
+        dmid, dfar, dqt = backward_far(idx, q, d_out, stat, mid, far)
         dmid_in = permute(dmid, [(2, 3), (3, 2)])
-        dfar, dqt = backward_far(idx, q, d_out, stat, far, dqt)
         dfar_in = permute(dfar + dmid_in, [(2, 0), (3, 1)])
         dnear, down, dq = backward_local(idx, q, d_out, stat, own, near, dqt, cosine, sine)
         dnear_in = permute(dnear, [(1, 0), (3, 2)])
         dwq = grad_wq(idx, act_t, dq)
         dwq_mine, dwq_other = sum_halves(dwq)
-        dx, dwkv, dgain_pre = tail(idx, down, dnear_in, dfar_in, cosine, sine, act_t, dq, wq, wk, wv, x, dy, gain_pre)
+        dwo = grad_wo(idx, o, dz, partner_o, dy_high, dy_low, wo, gain_post)
+        dwo_mine = dwo[0] + permute(dwo[1], beside)
+        dwo_other = permute(dwo_mine, beside)
+        dx, dwkv = tail(idx, down, dnear_in, dfar_in, cosine, sine, act_t, dq, wq, wk, wv, x, dy, gain_pre, dgain_post)
         dwkv_mine, dwkv_other = sum_halves(dwkv)
-        gains = jnp.concatenate([dgain_pre, dgain_post], axis=0)
-        gains = gains + permute(gains, beside)
-        gains = gains + permute(gains, across)
 
         dwo_full = join_rows(idx, dwo_mine, dwo_other)
         dwq_full = join_wide(idx, dwq_mine, dwq_other, heads)
-        dwk_full, dwv_full = join_pair(idx, dwkv_mine, dwkv_other)
+        dwk_full, dwv_full, dpre_full, dpost_full = join_pair(idx, dwkv_mine, dwkv_other)
         return (
             y.reshape(batch, tokens, dim),
             dx.reshape(batch, tokens, dim),
@@ -694,8 +768,8 @@
             dwk_full,
             dwv_full,
             dwo_full.reshape(heads, hd, dim),
-            gains[0],
-            gains[1],
+            dpre_full,
+            dpost_full,
         )
 
     seq_spec = P("dp", "cp", None)

time: 398 us -> 405 us (1.018)
  Pallas kernels: 115 us -> 129 us
  starting transfers between devices: 82.7 us -> 75.1 us
    pallas_call x4 -> x5, Pallas kernels: 38.4 us -> 51.6 us  [the longest x1 17.1 us: grad_wo(): pl.pallas_call(grad_wo_kernel, grid=(tokens // bt,), in_specs=[pl.BlockSp...]
    ppermute x17, starting transfers between devices: 82.7 us -> 75.1 us  [permute(): return lax.ppermute(value, 'cp', pairs)]
  transfers between devices with their start and end apart: 17 -> 17, of which waited for: 8 -> 6; matrix products, arithmetic and copies ran while one was open for 5% -> 5% of each run, Pallas kernels for 20% -> 22%
where the time goes in v3:
time: 405 us; the launch traced here: 404 us
  waiting for transfers between devices  168 us (41%)
  Pallas kernels  129 us (32%)
  starting transfers between devices  75.1 us (19%)
  other arithmetic  15.8 us (4%)
  local copies, waits for them, and re-layouts  14.4 us (4%)
    ppermute x17, waiting for transfers between devices, permute(): return lax.ppermute(value, 'cp', pairs)  168 us
    ppermute x17, starting transfers between devices, permute(): return lax.ppermute(value, 'cp', pairs)  75.1 us
    pallas_call x1, Pallas kernels, backward_local(): pl.pallas_call(backward_local_kernel, grid=(tokens // bk,), in_specs=[pl....  20.5 us
    pallas_call x1, Pallas kernels, grad_wo(): pl.pallas_call(grad_wo_kernel, grid=(tokens // bt,), in_specs=[pl.BlockSp...  17.1 us
    pallas_call x1, Pallas kernels, post(): pl.pallas_call(post_kernel, grid=(tokens // bq,), in_specs=[rows2(heads *...  14.1 us
    pallas_call x1, Pallas kernels, tail(): pl.pallas_call(tail_kernel, grid=(tokens // bt,), in_specs=[pl.BlockSpec(...  13.3 us
    pallas_call x1, Pallas kernels, forward_local(): pl.pallas_call(forward_local_kernel, grid=(tokens // bq,), in_specs=[pl.B...  10.3 us
    pallas_call x1, Pallas kernels, backward_far(): pl.pallas_call(backward_far_kernel, grid=(2 * per,), in_specs=[pl.BlockSp...  9.62 us
  transfers between devices with their start and end apart: 17, of which 6 were waited for; matrix products, arithmetic and copies ran while one was open for 5% of the time, Pallas kernels for 22%

profile of v3, /device:TPU:0, one launch (start us, length us, event | category | flops | bytes accessed | tf_op | source)
XLA Modules:
  0.0 404.1 jit_solution(6218992256906508067)
XLA Ops:
  2.6 3.1 multiply_sine_fusion
  5.7 6.0 %project_kv.1 = (bf16[1024,1152]{1,0:T(8,128)(2,1)}, bf16[1152,1024]{1,0:T(8,128)(2,1)}, bf16[2,1024,256]{2,1,0:T(8,128)(2,1)}) custom-call(bf16[1024,1152]{1,0:T(8,128)(2,1)} %bitcast.37, f32[1,1152]{1,0:T(1,128)} %reshape.86.gain_ref, bf16[1152,256]{1,0:T(8,128)(2,1)} %bitcast.44, bf16[1152,256]{1,0:T(8,128)(2,1)} %bitcast.46, ...), custom_call_target="tpu_custom_call" | custom-call | flops 1207959552 | bytes 7077888 | tf_op jit(solution)/shard_map/project_kv/pallas_call | solution.py:65
  11.7 6.1 %collective-permute-start = (bf16[2,1024,256]{2,1,0:T(8,128)(2,1)}, bf16[2,1024,256]{2,1,0:T(8,128)(2,1)}, u32[]{:S(2)}, u32[]{:S(2)}) collective-permute-start(bf16[2,1024,256]{2,1,0:T(8,128)(2,1)} %get-tuple-element.34.own_ref), channel_id=1, source_target_pairs={{0,2},{1,3},{4,6},{5,7},{8,10},{9,11},{12,14},{13,15}} | collective-permute-start | bytes 3145736 | tf_op jit(solution)/shard_map/ppermute | solution.py:711
  19.4 20.1 %collective-permute-done.far_ref = bf16[2,1024,256]{2,1,0:T(8,128)(2,1)} collective-permute-done((bf16[2,1024,256]{2,1,0:T(8,128)(2,1)}, bf16[2,1024,256]{2,1,0:T(8,128)(2,1)}, u32[]{:S(2)}, u32[]{:S(2)}) %collective-permute-start) | collective-permute-done | bytes 1048608 | tf_op jit(solution)/shard_map/ppermute | solution.py:711
  39.5 1.6 collective-permute-start.1
  41.2 2.0 copy.20
  43.7 7.1 %project_q.1.q_ref = bf16[4,1024,256]{2,1,0:T(8,128)(2,1)} custom-call(bf16[1024,1152]{1,0:T(8,128)(2,1)} %get-tuple-element.33.a_ref, bf16[1152,1024]{1,0:T(8,128)(2,1)} %bitcast.35, f32[1024,128]{1,0:T(8,128)} %get-tuple-element.67.cos_ref, f32[1024,128]{1,0:T(8,128)} %get-tuple-element.66.sin_ref), custom_call_target="tpu_custom_call" | custom-call | flops 2415919104 | bytes 7077888 | tf_op jit(solution)/shard_map/project_q/pallas_call | solution.py:110
  51.8 10.3 %forward_local.1 = (f32[4,1024,256]{2,1,0:T(8,128)}, f32[4,1024,128]{2,1,0:T(8,128)}) custom-call(s32[1]{0:T(128)} %bitcast.idx_ref, bf16[4,1024,256]{2,1,0:T(8,128)(2,1)} %project_q.1.q_ref, bf16[2,1024,256]{2,1,0:T(8,128)(2,1)} %get-tuple-element.34.own_ref, bf16[2,1024,256]{2,1,0:T(8,128)(2,1)} %copy-done.7), custom_call_target="tpu_custom_call" | custom-call | flops 6442450944 | bytes 8388608 | tf_op jit(solution)/shard_map/forward_local/pallas_call | solution.py:175
  62.1 7.5 %forward_far.1 = (bf16[1024,1024]{1,0:T(8,128)(2,1)}, f32[4,1024,256]{2,1,0:T(8,128)}, f32[1024,128]{1,0:T(8,128)}) custom-call(s32[1]{0:T(128)} %bitcast.idx_ref, bf16[4,1024,256]{2,1,0:T(8,128)(2,1)} %project_q.1.q_ref, bf16[2,1024,256]{2,1,0:T(8,128)(2,1)} %collective-permute-done.far_ref, bf16[2,1024,256]{2,1,0:T(8,128)(2,1)} %collective-permute-done.1.mid_ref, ...), custom_call_target="tpu_custom_call" | custom-call | flops 8589934592 | bytes 12582912 | tf_op jit(solution)/shard_map/forward_far/pallas_call | solution.py:232
  69.5 14.1 %post.1 = (bf16[1024,1152]{1,0:T(8,128)(2,1)}, bf16[4,1024,256]{2,1,0:T(8,128)(2,1)}, bf16[1024,1152]{1,0:T(8,128)(2,1)}, f32[8,1024]{1,0:T(8,128)}, f32[1,1152]{1,0:T(1,128)}) custom-call(bf16[1024,1024]{1,0:T(8,128)(2,1)} %get-tuple-element.37.o_ref, f32[4,1024,256]{2,1,0:T(8,128)} %get-tuple-element.38.out_ref, f32[1024,128]{1,0:T(8,128)} %get-tuple-element.39.lse_ref, ...), custom_call_target="tpu_custom_call" | custom-call | flops 4831838208 | bytes 12582912 | tf_op jit(solution)/shard_map/post/pallas_call | solution.py:301
  83.7 9.6 %backward_far.1 = (f32[2,1024,256]{2,1,0:T(8,128)}, f32[2,1024,256]{2,1,0:T(8,128)}, f32[4,256,1024]{2,1,0:T(8,128)}) custom-call(s32[1]{0:T(128)} %bitcast.idx_ref, bf16[4,1024,256]{2,1,0:T(8,128)(2,1)} %project_q.1.q_ref, bf16[4,1024,256]{2,1,0:T(8,128)(2,1)} %get-tuple-element.41.do_ref, f32[8,1024]{1,0:T(8,128)} %get-tuple-element.42.stat_ref, ...), custom_call_target="tpu_custom_call" | custom-call | flops 21474836480 | bytes 12582912 | tf_op jit(solution)/shard_map/backward_far/pallas_call | solution.py:419
  93.3 2.0 collective-permute-start.4
  96.5 52.4 %collective-permute-start.14 = (bf16[1024,1152]{1,0:T(8,128)(2,1)S(1)}, bf16[1024,1152]{1,0:T(8,128)(2,1)}, u32[]{:S(2)}, u32[]{:S(2)}) collective-permute-start(bf16[1024,1152]{1,0:T(8,128)(2,1)S(1)} %bitcast.52), channel_id=1, source_target_pairs={{0,2},{1,3},{4,6},{5,7},{8,10},{9,11},{12,14},{13,15}} | collective-permute-start | bytes 7077896 | tf_op jit(solution)/shard_map/ppermute | solution.py:711
  148.9 20.5 %backward_local.1 = (f32[2,1024,256]{2,1,0:T(8,128)}, f32[2,1024,256]{2,1,0:T(8,128)}, bf16[1024,1024]{1,0:T(8,128)(2,1)}) custom-call(s32[1]{0:T(128)} %bitcast.idx_ref, bf16[4,1024,256]{2,1,0:T(8,128)(2,1)} %project_q.1.q_ref, bf16[4,1024,256]{2,1,0:T(8,128)(2,1)} %get-tuple-element.41.do_ref, f32[8,1024]{1,0:T(8,128)} %get-tuple-element.42.stat_ref, ...), custom_call_target="tpu_custom_call" | custom-call | flops 16106127360 | bytes 12582912 | tf_op jit(solution)/shard_map/backward_local/pallas_call | solution.py:493
  170.7 3.8 add.18
  175.8 6.8 %grad_wq.1 = f32[2,1152,512]{2,1,0:T(8,128)} custom-call(s32[1]{0:T(128)} %bitcast.idx_ref, bf16[1152,1024]{1,0:T(8,128)(2,1)} %get-tuple-element.48.at_ref, bf16[1024,1024]{1,0:T(8,128)(2,1)} %get-tuple-element.49.dq_ref), custom_call_target="tpu_custom_call" | custom-call | flops 2415919104 | bytes 4718592 | tf_op jit(solution)/shard_map/grad_wq/pallas_call | solution.py:538
  182.6 3.2 slice_bitcast_fusion.2
  185.8 10.5 %collective-permute-done.13.pdy_low_ref = bf16[1024,1152]{1,0:T(8,128)(2,1)} collective-permute-done((bf16[1024,1152]{1,0:T(8,128)(2,1)S(1)}, bf16[1024,1152]{1,0:T(8,128)(2,1)}, u32[]{:S(2)}, u32[]{:S(2)}) %collective-permute-start.13) | collective-permute-done | bytes 2359328 | tf_op jit(solution)/shard_map/ppermute | solution.py:711
  196.3 5.4 %collective-permute-start.6 = (f32[1152,512]{1,0:T(8,128)}, f32[1152,512]{1,0:T(8,128)}, u32[]{:S(2)}, u32[]{:S(2)}) collective-permute-start(f32[1152,512]{1,0:T(8,128)} %slice_bitcast_fusion.2), channel_id=1, source_target_pairs={{0,1},{1,0},{2,3},{3,2},{4,5},{5,4},{6,7},{7,6},{8,9},{9,8},{10,11... | collective-permute-start | bytes 7077896 | tf_op jit(solution)/shard_map/ppermute | solution.py:711
  201.8 41.5 %collective-permute-done.12.po_ref = bf16[1024,1024]{1,0:T(8,128)(2,1)} collective-permute-done((bf16[1024,1024]{1,0:T(8,128)(2,1)}, bf16[1024,1024]{1,0:T(8,128)(2,1)}, u32[]{:S(2)}, u32[]{:S(2)}) %collective-permute-start.12) | collective-permute-done | bytes 2097184 | tf_op jit(solution)/shard_map/ppermute | solution.py:711
  243.2 17.1 %grad_wo.1 = f32[2,512,1152]{2,1,0:T(8,128)} custom-call(s32[1]{0:T(128)} %bitcast.idx_ref, bf16[1024,1024]{1,0:T(8,128)(2,1)} %get-tuple-element.37.o_ref, bf16[1024,1152]{1,0:T(8,128)(2,1)} %get-tuple-element.55.dz_ref, bf16[1024,1024]{1,0:T(8,128)(2,1)} %collective-permute-done.12.po_ref, bf16[1024,1152]{1,0:T(8,128)(2,1)} %collective-permute-done.13.pdy_low_ref, ...), custom_call_target="tpu_custom_call" | custom-call | flops 7247757312 | bytes 14155776 | tf_op jit(solution)/shard_map/grad_wo/pallas_call | solution.py:343
  260.4 3.3 slice_bitcast_fusion
  263.6 21.9 %collective-permute-done.5.dfar_ref = f32[2,1024,256]{2,1,0:T(8,128)} collective-permute-done((f32[2,1024,256]{2,1,0:T(8,128)}, f32[2,1024,256]{2,1,0:T(8,128)}, u32[]{:S(2)}, u32[]{:S(2)}) %collective-permute-start.5) | collective-permute-done | bytes 2097184 | tf_op jit(solution)/shard_map/ppermute | solution.py:711
  285.5 13.3 %tail.1 = (bf16[1024,1152]{1,0:T(8,128)(2,1)}, f32[2,1160,256]{2,1,0:T(8,128)}) custom-call(s32[1]{0:T(128)} %bitcast.idx_ref, f32[2,1024,256]{2,1,0:T(8,128)} %get-tuple-element.44.down_ref, f32[2,1024,256]{2,1,0:T(8,128)} %collective-permute-done.3.dnear_ref, f32[2,1024,256]{2,1,0:T(8,128)} %collective-permute-done.5.dfar_ref, ...), custom_call_target="tpu_custom_call" | custom-call | flops 4831838208 | bytes 9437184 | tf_op jit(solution)/shard_map/tail/pallas_call | solution.py:596
  300.5 3.1 fusion.1
  303.8 2.0 collective-permute-start.10
  306.1 51.6 %collective-permute-done.7 = f32[1152,512]{1,0:T(8,128)S(1)} collective-permute-done((f32[1152,512]{1,0:T(8,128)S(1)}, f32[1152,512]{1,0:T(8,128)S(1)}, u32[]{:S(2)}, u32[]{:S(2)}) %collective-permute-start.7) | collective-permute-done | bytes 2359328 | tf_op jit(solution)/shard_map/ppermute | solution.py:711
  357.7 2.0 add.20.mine_ref
  359.7 22.8 %collective-permute-done.10 = f32[1160,256]{1,0:T(8,128)S(1)} collective-permute-done((f32[1160,256]{1,0:T(8,128)S(1)}, f32[1160,256]{1,0:T(8,128)S(1)}, u32[]{:S(2)}, u32[]{:S(2)}) %collective-permute-start.10) | collective-permute-done | bytes 1187872 | tf_op jit(solution)/shard_map/ppermute | solution.py:711
  384.4 6.2 %join_rows.1 = f32[1024,1152]{1,0:T(8,128)} custom-call(s32[1]{0:T(128)} %bitcast.idx_ref, f32[512,1152]{1,0:T(8,128)} %copy-done, f32[512,1152]{1,0:T(8,128)} %copy-done.5), custom_call_target="tpu_custom_call" | custom-call | flops 1000 | bytes 9437184 | tf_op jit(solution)/shard_map/join_rows/pallas_call | solution.py:694
  390.5 7.7 %join_wide.1 = f32[9216,128]{1,0:T(8,128)} custom-call(s32[1]{0:T(128)} %bitcast.idx_ref, f32[1152,512]{1,0:T(8,128)} %add.20.mine_ref, f32[1152,512]{1,0:T(8,128)} %collective-permute-done.8.other_ref), custom_call_target="tpu_custom_call" | custom-call | flops 1000 | bytes 9437184 | tf_op jit(solution)/shard_map/join_wide/pallas_call | solution.py:645
  398.2 3.3 join_pair.1
  (53 shorter events, 15.4 us)
Async XLA Ops:
  5.7 35.5 %copy-start.3 = (bf16[1152,4,256]{2,1,0:T(4,128)(2,1)S(1)}, bf16[1152,4,256]{2,1,0:T(4,128)(2,1)}, u32[]{:S(2)}) copy-start(bf16[1152,4,256]{2,1,0:T(4,128)(2,1)} %param.12) | copy-start | bytes 7077892
  11.7 27.8 %collective-permute-start = (bf16[2,1024,256]{2,1,0:T(8,128)(2,1)}, bf16[2,1024,256]{2,1,0:T(8,128)(2,1)}, u32[]{:S(2)}, u32[]{:S(2)}) collective-permute-start(bf16[2,1024,256]{2,1,0:T(8,128)(2,1)} %get-tuple-element.34.own_ref), channel_id=1, source_target_pairs={{0,2},{1,3},{4,6},{5,7},{8,10},{9,11},{12,14},{13,15}} | collective-permute-start | bytes 3145736 | tf_op jit(solution)/shard_map/ppermute | solution.py:711
  17.9 33.0 %collective-permute-start.2 = (bf16[2,1024,256]{2,1,0:T(8,128)(2,1)}, bf16[2,1024,256]{2,1,0:T(8,128)(2,1)S(1)}, u32[]{:S(2)}, u32[]{:S(2)}) collective-permute-start(bf16[2,1024,256]{2,1,0:T(8,128)(2,1)} %get-tuple-element.34.own_ref), channel_id=1, source_target_pairs={{0,1},{2,3},{4,5},{6,7},{8,9},{10,11},{12,13},{14,15}} | collective-permute-start | bytes 3145736 | tf_op jit(solution)/shard_map/ppermute | solution.py:711
  39.5 22.5 %collective-permute-start.1 = (bf16[2,1024,256]{2,1,0:T(8,128)(2,1)}, bf16[2,1024,256]{2,1,0:T(8,128)(2,1)}, u32[]{:S(2)}, u32[]{:S(2)}) collective-permute-start(bf16[2,1024,256]{2,1,0:T(8,128)(2,1)} %collective-permute-done.far_ref), channel_id=1, source_target_pairs={{2,3},{3,2},{6,7},{7,6},{10,11},{11,10},{14,15},{15,14}} | collective-permute-start | bytes 3145736 | tf_op jit(solution)/shard_map/ppermute | solution.py:711
  41.2 2.0 copy-start.6
  50.8 1.0 copy-start.7
  83.7 11.6 %copy-start.4 = (bf16[1,1024,1152]{2,1,0:T(8,128)(2,1)S(1)}, bf16[1,1024,1152]{2,1,0:T(8,128)(2,1)}, u32[]{:S(2)}) copy-start(bf16[1,1024,1152]{2,1,0:T(8,128)(2,1)} %param.11) | copy-start | bytes 7077892
  93.3 77.4 %collective-permute-start.4 = (f32[2,1024,256]{2,1,0:T(8,128)}, f32[2,1024,256]{2,1,0:T(8,128)}, u32[]{:S(2)}, u32[]{:S(2)}) collective-permute-start(f32[2,1024,256]{2,1,0:T(8,128)} %get-tuple-element.47), channel_id=1, source_target_pairs={{2,3},{3,2},{6,7},{7,6},{10,11},{11,10},{14,15},{15,14}} | collective-permute-start | bytes 6291464 | tf_op jit(solution)/shard_map/ppermute | solution.py:711
  95.3 101.1 %collective-permute-start.13 = (bf16[1024,1152]{1,0:T(8,128)(2,1)S(1)}, bf16[1024,1152]{1,0:T(8,128)(2,1)}, u32[]{:S(2)}, u32[]{:S(2)}) collective-permute-start(bf16[1024,1152]{1,0:T(8,128)(2,1)S(1)} %bitcast.51), channel_id=1, source_target_pairs={{2,0},{3,1},{6,4},{7,5},{10,8},{11,9},{14,12},{15,13}} | collective-permute-start | bytes 7077896 | tf_op jit(solution)/shard_map/ppermute | solution.py:711
  96.5 105.2 %collective-permute-start.14 = (bf16[1024,1152]{1,0:T(8,128)(2,1)S(1)}, bf16[1024,1152]{1,0:T(8,128)(2,1)}, u32[]{:S(2)}, u32[]{:S(2)}) collective-permute-start(bf16[1024,1152]{1,0:T(8,128)(2,1)S(1)} %bitcast.52), channel_id=1, source_target_pairs={{0,2},{1,3},{4,6},{5,7},{8,10},{9,11},{12,14},{13,15}} | collective-permute-start | bytes 7077896 | tf_op jit(solution)/shard_map/ppermute | solution.py:711
  148.9 94.3 %collective-permute-start.12 = (bf16[1024,1024]{1,0:T(8,128)(2,1)}, bf16[1024,1024]{1,0:T(8,128)(2,1)}, u32[]{:S(2)}, u32[]{:S(2)}) collective-permute-start(bf16[1024,1024]{1,0:T(8,128)(2,1)} %get-tuple-element.37.o_ref), channel_id=1, source_target_pairs={{0,2},{2,0},{1,3},{3,1},{4,6},{6,4},{5,7},{7,5},{8,10},{10,8},{9,1... | collective-permute-start | bytes 6291464 | tf_op jit(solution)/shard_map/ppermute | solution.py:711
  169.4 94.3 %collective-permute-start.3 = (f32[2,1024,256]{2,1,0:T(8,128)}, f32[2,1024,256]{2,1,0:T(8,128)}, u32[]{:S(2)}, u32[]{:S(2)}) collective-permute-start(f32[2,1024,256]{2,1,0:T(8,128)} %get-tuple-element.45), channel_id=1, source_target_pairs={{1,0},{3,2},{5,4},{7,6},{9,8},{11,10},{13,12},{15,14}} | collective-permute-start | bytes 6291464 | tf_op jit(solution)/shard_map/ppermute | solution.py:711
  174.5 111.0 %collective-permute-start.5 = (f32[2,1024,256]{2,1,0:T(8,128)}, f32[2,1024,256]{2,1,0:T(8,128)}, u32[]{:S(2)}, u32[]{:S(2)}) collective-permute-start(f32[2,1024,256]{2,1,0:T(8,128)} %add.18), channel_id=1, source_target_pairs={{2,0},{3,1},{6,4},{7,5},{10,8},{11,9},{14,12},{15,13}} | collective-permute-start | bytes 6291464 | tf_op jit(solution)/shard_map/ppermute | solution.py:711
  196.3 104.2 %collective-permute-start.6 = (f32[1152,512]{1,0:T(8,128)}, f32[1152,512]{1,0:T(8,128)}, u32[]{:S(2)}, u32[]{:S(2)}) collective-permute-start(f32[1152,512]{1,0:T(8,128)} %slice_bitcast_fusion.2), channel_id=1, source_target_pairs={{0,1},{1,0},{2,3},{3,2},{4,5},{5,4},{6,7},{7,6},{8,9},{9,8},{10,11... | collective-permute-start | bytes 7077896 | tf_op jit(solution)/shard_map/ppermute | solution.py:711
  263.6 42.2 %collective-permute-start.15 = (f32[512,1152]{1,0:T(8,128)}, f32[512,1152]{1,0:T(8,128)S(1)}, u32[]{:S(2)}, u32[]{:S(2)}) collective-permute-start(f32[512,1152]{1,0:T(8,128)} %slice_bitcast_fusion), channel_id=1, source_target_pairs={{0,1},{1,0},{2,3},{3,2},{4,5},{5,4},{6,7},{7,6},{8,9},{9,8},{10,11... | collective-permute-start | bytes 7077896 | tf_op jit(solution)/shard_map/ppermute | solution.py:711
  298.9 6.9 %slice-start = ((s8[4718592]{0:T(1024)(128)(4,1)}), s8[4194304]{0:T(1024)(128)(4,1)S(1)}, s32[]{:S(2)}) async-start(s8[4718592]{0:T(1024)(128)(4,1)} %bitcast.40), calls=%async_computation | async-start | bytes 8388608
  300.4 3.2 copy-start.2
  300.4 5.4 %slice-start.1 = ((s8[4718592]{0:T(1024)(128)(4,1)}), s8[524288]{0:T(1024)(128)(4,1)S(1)}, s32[]{:S(2)}) async-start(s8[4718592]{0:T(1024)(128)(4,1)} %bitcast.40), calls=%async_computation.1 | async-start | bytes 1048576
  300.4 3.2 collective-permute-start.9
  303.6 54.2 %collective-permute-start.7 = (f32[1152,512]{1,0:T(8,128)S(1)}, f32[1152,512]{1,0:T(8,128)S(1)}, u32[]{:S(2)}, u32[]{:S(2)}) collective-permute-start(f32[1152,512]{1,0:T(8,128)S(1)} %fusion.1), channel_id=1, source_target_pairs={{0,2},{2,0},{1,3},{3,1},{4,6},{6,4},{5,7},{7,5},{8,10},{10,8},{9,1... | collective-permute-start | bytes 7077896 | tf_op jit(solution)/shard_map/ppermute | solution.py:711
  303.8 78.8 %collective-permute-start.10 = (f32[1160,256]{1,0:T(8,128)S(1)}, f32[1160,256]{1,0:T(8,128)S(1)}, u32[]{:S(2)}, u32[]{:S(2)}) collective-permute-start(f32[1160,256]{1,0:T(8,128)S(1)} %bitcast_add_fusion), channel_id=1, source_target_pairs={{0,2},{2,0},{1,3},{3,1},{4,6},{6,4},{5,7},{7,5},{8,10},{10,8},{9,1... | collective-permute-start | bytes 3563528 | tf_op jit(solution)/shard_map/ppermute | solution.py:711
  306.1 53.6 %copy-start = (f32[512,1152]{1,0:T(8,128)}, f32[512,1152]{1,0:T(8,128)S(1)}, u32[]{:S(2)}) copy-start(f32[512,1152]{1,0:T(8,128)S(1)} %fusion.mine_ref) | copy-start | bytes 7077892
  306.1 76.7 %collective-permute-start.16 = (f32[512,1152]{1,0:T(8,128)S(1)}, f32[512,1152]{1,0:T(8,128)S(1)}, u32[]{:S(2)}, u32[]{:S(2)}) collective-permute-start(f32[512,1152]{1,0:T(8,128)S(1)} %fusion.mine_ref), channel_id=1, source_target_pairs={{0,1},{1,0},{2,3},{3,2},{4,5},{5,4},{6,7},{7,6},{8,9},{9,8},{10,11... | collective-permute-start | bytes 7077896 | tf_op jit(solution)/shard_map/ppermute | solution.py:711
  359.7 30.8 %collective-permute-start.8 = (f32[1152,512]{1,0:T(8,128)}, f32[1152,512]{1,0:T(8,128)}, u32[]{:S(2)}, u32[]{:S(2)}) collective-permute-start(f32[1152,512]{1,0:T(8,128)} %add.20.mine_ref), channel_id=1, source_target_pairs={{0,1},{1,0},{2,3},{3,2},{4,5},{5,4},{6,7},{7,6},{8,9},{9,8},{10,11... | collective-permute-start | bytes 7077896 | tf_op jit(solution)/shard_map/ppermute | solution.py:711
  382.8 7.8 %copy-start.1 = (f32[1160,256]{1,0:T(8,128)}, f32[1160,256]{1,0:T(8,128)S(1)}, u32[]{:S(2)}) copy-start(f32[1160,256]{1,0:T(8,128)S(1)} %add.22.mine_ref) | copy-start | bytes 3563524
  382.8 15.4 %collective-permute-start.11 = (f32[1160,256]{1,0:T(8,128)S(1)}, f32[1160,256]{1,0:T(8,128)}, u32[]{:S(2)}, u32[]{:S(2)}) collective-permute-start(f32[1160,256]{1,0:T(8,128)S(1)} %add.22.mine_ref), channel_id=1, source_target_pairs={{0,1},{1,0},{2,3},{3,2},{4,5},{5,4},{6,7},{7,6},{8,9},{9,8},{10,11... | collective-permute-start | bytes 3563528 | tf_op jit(solution)/shard_map/ppermute | solution.py:711
  382.8 1.5 copy-start.5

commit v4 on v3

--- a/solution.py
+++ b/solution.py
@@ -38,8 +38,29 @@
     return pl.BlockSpec(shape, lambda *_: zeros)
 
 
-def cost(flops, nbytes, trans=0):
-    return pl.CostEstimate(flops=int(flops), bytes_accessed=int(nbytes), transcendentals=int(trans))
+def rows_spec(rows, width):
+    return pl.BlockSpec((rows, width), lambda i: (i, 0))
+
+
+def stack_spec(depth, rows, width):
+    return pl.BlockSpec((depth, rows, width), lambda i: (0, i, 0))
+
+
+COST = pl.CostEstimate(flops=10**10, bytes_accessed=10**7, transcendentals=0)
+
+
+def meet_sibling(rank):
+    sibling = {"cp": rank + 1 - 2 * (rank % 2)}
+    barrier = pltpu.get_barrier_semaphore()
+    pl.semaphore_signal(barrier, inc=1, device_id=sibling, device_id_type=pl.DeviceIdType.MESH)
+    pl.semaphore_wait(barrier, 1)
+
+
+def to_sibling(rank, src, dst, send, recv):
+    return pltpu.make_async_remote_copy(
+        src_ref=src, dst_ref=dst, send_sem=send, recv_sem=recv,
+        device_id={"cp": rank + 1 - 2 * (rank % 2)}, device_id_type=pl.DeviceIdType.MESH,
+    )
 
 
 def kv_kernel(x_ref, gain_ref, wk_ref, wv_ref, cos_ref, sin_ref, a_ref, at_ref, kv_ref):
@@ -66,17 +87,17 @@
         kv_kernel,
         grid=(tokens // bt,),
         in_specs=[
-            pl.BlockSpec((bt, dim), lambda i: (i, 0)),
+            rows_spec(bt, dim),
             whole((1, dim)),
             whole((dim, hd)),
             whole((dim, hd)),
-            pl.BlockSpec((bt, half), lambda i: (i, 0)),
-            pl.BlockSpec((bt, half), lambda i: (i, 0)),
+            rows_spec(bt, half),
+            rows_spec(bt, half),
         ],
         out_specs=[
-            pl.BlockSpec((bt, dim), lambda i: (i, 0)),
+            rows_spec(bt, dim),
             pl.BlockSpec((dim, bt), lambda i: (0, i)),
-            pl.BlockSpec((2, bt, hd), lambda i: (0, i, 0)),
+            stack_spec(2, bt, hd),
         ],
         out_shape=[
             jax.ShapeDtypeStruct((tokens, dim), BF16),
@@ -84,7 +105,7 @@
             jax.ShapeDtypeStruct((2, tokens, hd), BF16),
         ],
         compiler_params=params(),
-        cost_estimate=cost(4 * tokens * dim * hd, 6 * tokens * dim),
+        cost_estimate=COST,
         name="project_kv",
     )(x, gain, wk, wv, cosine, sine)
 
@@ -111,15 +132,15 @@
         q_kernel,
         grid=(tokens // bt,),
         in_specs=[
-            pl.BlockSpec((bt, dim), lambda i: (i, 0)),
+            rows_spec(bt, dim),
             whole(wq.shape),
-            pl.BlockSpec((bt, half), lambda i: (i, 0)),
-            pl.BlockSpec((bt, half), lambda i: (i, 0)),
-        ],
-        out_specs=pl.BlockSpec((heads, bt, hd), lambda i: (0, i, 0)),
+            rows_spec(bt, half),
+            rows_spec(bt, half),
+        ],
+        out_specs=stack_spec(heads, bt, hd),
         out_shape=jax.ShapeDtypeStruct((heads, tokens, hd), BF16),
         compiler_params=params(),
-        cost_estimate=cost(2 * tokens * dim * heads * hd, 6 * tokens * dim),
+        cost_estimate=COST,
         name="project_q",
     )(a, wq, cosine, sine)
 
@@ -177,20 +198,20 @@
         grid=(tokens // bq,),
         in_specs=[
             pl.BlockSpec(memory_space=pltpu.SMEM),
-            pl.BlockSpec((heads, bq, hd), lambda i: (0, i, 0)),
+            stack_spec(heads, bq, hd),
             whole(own.shape),
             whole(near.shape),
         ],
         out_specs=[
-            pl.BlockSpec((heads, bq, hd), lambda i: (0, i, 0)),
-            pl.BlockSpec((heads, bq, 128), lambda i: (0, i, 0)),
+            stack_spec(heads, bq, hd),
+            stack_spec(heads, bq, 128),
         ],
         out_shape=[
             jax.ShapeDtypeStruct((heads, tokens, hd), F32),
             jax.ShapeDtypeStruct((heads, tokens, 128), F32),
         ],
         compiler_params=params(),
-        cost_estimate=cost(6 * heads * tokens * tokens * hd, 8 * heads * tokens * hd),
+        cost_estimate=COST,
         name="forward_local",
     )(idx, q, own, near)
 
@@ -228,7 +249,7 @@
 def forward_far(idx, q, far, mid, acc, row_sum):
     heads, tokens, hd = q.shape
     bq = 256
-    rows3 = lambda last: pl.BlockSpec((heads, bq, last), lambda i: (0, i, 0))
+    rows3 = lambda last: stack_spec(heads, bq, last)
     return pl.pallas_call(
         forward_far_kernel,
         grid=(tokens // bq,),
@@ -241,9 +262,9 @@
             rows3(128),
         ],
         out_specs=[
-            pl.BlockSpec((bq, heads * hd), lambda i: (i, 0)),
+            rows_spec(bq, heads * hd),
             rows3(hd),
-            pl.BlockSpec((bq, 128), lambda i: (i, 0)),
+            rows_spec(bq, 128),
         ],
         out_shape=[
             jax.ShapeDtypeStruct((tokens, heads * hd), BF16),
@@ -255,7 +276,7 @@
             pltpu.VMEM((heads, bq, 128), F32),
         ],
         compiler_params=params(),
-        cost_estimate=cost(8 * heads * tokens * tokens * hd, 12 * heads * tokens * hd),
+        cost_estimate=COST,
         name="forward_far",
     )(idx, q, far, mid, acc, row_sum)
 
@@ -296,8 +317,8 @@
     heads, tokens, hd = out.shape
     dim = x.shape[1]
     bq = 256
-    rows3 = pl.BlockSpec((heads, bq, hd), lambda i: (0, i, 0))
-    rows2 = lambda width: pl.BlockSpec((bq, width), lambda i: (i, 0))
+    rows3 = stack_spec(heads, bq, hd)
+    rows2 = lambda width: rows_spec(bq, width)
     return pl.pallas_call(
         post_kernel,
         grid=(tokens // bq,),
@@ -311,12 +332,12 @@
             jax.ShapeDtypeStruct((1, dim), F32),
         ],
         compiler_params=params(),
-        cost_estimate=cost(4 * tokens * heads * hd * dim, 12 * heads * tokens * hd),
+        cost_estimate=COST,
         name="post",
     )(o, out, lse, x, dy, wo, gain)
 
 
-def grad_wo_kernel(idx_ref, o_ref, dz_ref, po_ref, pdy_low_ref, pdy_high_ref, wo_ref, gain_ref, dwo_ref, pdz_ref):
+def grad_wo_kernel(idx_ref, o_ref, dz_ref, po_ref, pdy_low_ref, pdy_high_ref, wo_ref, gain_ref, mine_ref, theirs_ref, pdz_ref):
     _, width = o_ref.shape
     bt = pdy_low_ref.shape[0]
     hd = 256
@@ -329,17 +350,17 @@
     def _():
         core = idx_ref[0] % 2
         per = width // hd // 2
-        for which in range(2):
+        for which, ref in enumerate((mine_ref, theirs_ref)):
             for hh in range(per):
                 cols = pl.ds(pl.multiple_of((((core + which) % 2) * per + hh) * hd, hd), hd)
-                dwo_ref[which, hh * hd:(hh + 1) * hd, :] = dot(o_ref[:, cols].T, dz_ref[...]) + dot(po_ref[:, cols].T, pdz_ref[...])
+                ref[hh * hd:(hh + 1) * hd, :] = dot(o_ref[:, cols].T, dz_ref[...]) + dot(po_ref[:, cols].T, pdz_ref[...])
 
 
 def grad_wo(idx, o, dz, po, pdy_low, pdy_high, wo, gain):
     tokens, width = o.shape
     dim = dz.shape[1]
     bt = 256
-    rows2 = pl.BlockSpec((bt, dim), lambda i: (i, 0))
+    rows2 = rows_spec(bt, dim)
     return pl.pallas_call(
         grad_wo_kernel,
         grid=(tokens // bt,),
@@ -353,11 +374,11 @@
             whole(wo.shape),
             whole((1, dim)),
         ],
-        out_specs=whole((2, width // 2, dim)),
-        out_shape=jax.ShapeDtypeStruct((2, width // 2, dim), F32),
+        out_specs=[whole((width // 2, dim))] * 2,
+        out_shape=[jax.ShapeDtypeStruct((width // 2, dim), F32)] * 2,
         scratch_shapes=[pltpu.VMEM((tokens, dim), BF16)],
         compiler_params=params(),
-        cost_estimate=cost(6 * tokens * width * dim, 12 * tokens * dim),
+        cost_estimate=COST,
         name="grad_wo",
     )(idx, o, dz, po, pdy_low, pdy_high, wo, gain)
 
@@ -382,35 +403,46 @@
         dqt_ref[h, :, rows] += dot(kt, ds)
 
 
-def backward_far_kernel(idx_ref, q_ref, do_ref, stat_ref, mid_ref, far_ref, dmid_ref, dfar_ref, dqt_ref):
+def backward_far_kernel(q_ref, do_ref, stat_ref, mid_ref, far_ref, dfar_ref, dqt_ref, send_ref, recv_ref, send_sem, recv_sem):
     tokens = q_ref.shape[1]
     bq = 512
+    rank = lax.axis_index("cp")
     i = pl.program_id(0)
-    per = pl.num_programs(0) // 2
+    per = send_ref.shape[0]
 
     @pl.when(i == 0)
     def _():
         dqt_ref[...] = jnp.zeros_like(dqt_ref)
+        meet_sibling(rank)
+
+    def copy(slot):
+        return to_sibling(rank, send_ref.at[slot], recv_ref.at[slot], send_sem.at[slot], recv_sem.at[slot])
 
     def block(kv_ref, dkv_ref):
-        dkv_ref[...] = jnp.zeros_like(dkv_ref)
-
-        @pl.when(idx_ref[0] >= 2)
-        def _():
-            k, v = kv_ref[0], kv_ref[1]
-            kt = k.T
-
-            def step(j, _):
-                backward_tile(q_ref, do_ref, stat_ref, dqt_ref, dkv_ref, k, v, kt, j * bq, bq, False)
-                return 0
-
-            lax.fori_loop(0, tokens // bq, step, 0)
-
-    pl.when(i < per)(lambda: block(mid_ref, dmid_ref))
-    pl.when(i >= per)(lambda: block(far_ref, dfar_ref))
-
-
-def backward_far(idx, q, d_out, stat, mid, far):
+        k, v = kv_ref[0], kv_ref[1]
+        kt = k.T
+
+        def step(j, _):
+            backward_tile(q_ref, do_ref, stat_ref, dqt_ref, dkv_ref, k, v, kt, j * bq, bq, False)
+            return 0
+
+        lax.fori_loop(0, tokens // bq, step, 0)
+
+    @pl.when(jnp.logical_and(rank >= 2, i < per))
+    def _():
+        mine = send_ref.at[i]
+        mine[...] = jnp.zeros_like(mine)
+        block(mid_ref, mine)
+        copy(i).start()
+
+    @pl.when(jnp.logical_and(rank >= 2, i >= per))
+    def _():
+        copy(i - per).wait()
+        dfar_ref[...] = recv_ref[i - per]
+        block(far_ref, dfar_ref)
+
+
+def backward_far(q, d_out, stat, mid, far):
     heads, tokens, hd = q.shape
     bk = 256
     per = tokens // bk
@@ -419,58 +451,66 @@
     return pl.pallas_call(
         backward_far_kernel,
         grid=(2 * per,),
-        in_specs=[
-            pl.BlockSpec(memory_space=pltpu.SMEM),
-            whole(q.shape),
-            whole(d_out.shape),
-            whole(stat.shape),
-            early,
-            late,
-        ],
-        out_specs=[early, late, whole((heads, hd, tokens))],
+        in_specs=[whole(q.shape), whole(d_out.shape), whole(stat.shape), early, late],
+        out_specs=[late, whole((heads, hd, tokens))],
         out_shape=[
             jax.ShapeDtypeStruct((2, tokens, hd), F32),
-            jax.ShapeDtypeStruct((2, tokens, hd), F32),
             jax.ShapeDtypeStruct((heads, hd, tokens), F32),
         ],
-        compiler_params=params(),
-        cost_estimate=cost(20 * heads * tokens * tokens * hd, 12 * heads * tokens * hd),
+        scratch_shapes=[
+            pltpu.VMEM((per, 2, bk, hd), F32),
+            pltpu.VMEM((per, 2, bk, hd), F32),
+            pltpu.SemaphoreType.DMA((per,)),
+            pltpu.SemaphoreType.DMA((per,)),
+        ],
+        compiler_params=pltpu.CompilerParams(vmem_limit_bytes=VMEM_LIMIT, collective_id=0, has_side_effects=True),
+        cost_estimate=COST,
         name="backward_far",
-    )(idx, q, d_out, stat, mid, far)
-
-
-def backward_local_kernel(idx_ref, q_ref, do_ref, stat_ref, own_ref, near_ref, dqt_in_ref, cos_ref, sin_ref,
-                          dnear_ref, down_ref, dq_ref, dqt_ref):
+    )(q, d_out, stat, mid, far)
+
+
+def backward_local_kernel(q_ref, do_ref, stat_ref, own_ref, near_ref, dqt_in_ref, cos_ref, sin_ref, at_ref,
+                          down_ref, dq_ref, dwq_ref, dqt_ref, near_send, near_recv, dwq_send, dwq_recv,
+                          near_send_sem, near_recv_sem, dwq_send_sem, dwq_recv_sem):
     heads, tokens, hd = q_ref.shape
     half = hd // 2
     bk = own_ref.shape[1]
+    rank = lax.axis_index("cp")
+    core = rank % 2
     i = pl.program_id(0)
     steps = pl.num_programs(0)
 
     @pl.when(i == 0)
     def _():
         dqt_ref[...] = dqt_in_ref[...]
-
-    dnear_ref[...] = jnp.zeros_like(dnear_ref)
-    down_ref[...] = jnp.zeros_like(down_ref)
-
-    @pl.when(idx_ref[0] % 2 == 1)
+        meet_sibling(rank)
+
+    def near_copy(slot):
+        return to_sibling(rank, near_send.at[slot], near_recv.at[slot], near_send_sem.at[slot], near_recv_sem.at[slot])
+
+    @pl.when(core == 1)
     def _():
         k, v = near_ref[0], near_ref[1]
         kt = k.T
+        mine = near_send.at[i]
+        mine[...] = jnp.zeros_like(mine)
 
         def step(j, _):
-            backward_tile(q_ref, do_ref, stat_ref, dqt_ref, dnear_ref, k, v, kt, j * 512, 512, False)
+            backward_tile(q_ref, do_ref, stat_ref, dqt_ref, mine, k, v, kt, j * 512, 512, False)
             return 0
 
         lax.fori_loop(0, tokens // 512, step, 0)
-
+        near_copy(i).start()
+
+    own_rows = pl.ds(pl.multiple_of(i * bk, bk), bk)
+    down = down_ref.at[:, own_rows, :]
+    down[...] = jnp.zeros_like(down)
     k, v = own_ref[0], own_ref[1]
     kt = k.T
-    backward_tile(q_ref, do_ref, stat_ref, dqt_ref, down_ref, k, v, kt, i * bk, bk, True)
+    backward_tile(q_ref, do_ref, stat_ref, dqt_ref, down, k, v, kt, i * bk, bk, True)
 
     def own_step(j, _):
-        backward_tile(q_ref, do_ref, stat_ref, dqt_ref, down_ref, k, v, kt, j * bk, bk, False)
+        backward_tile(q_ref, do_ref, stat_ref, dqt_ref, down, k, v, kt, j * bk, bk, False)
         return 0
 
     lax.fori_loop(i + 1, steps, own_step, 0)
@@ -484,17 +524,51 @@
             cosine, sine = cos_ref[...], sin_ref[...]
             dq_ref[:, h * hd:h * hd + half] = ((first * cosine + second * sine) * scale).astype(BF16)
             dq_ref[:, h * hd + half:(h + 1) * hd] = ((second * cosine - first * sine) * scale).astype(BF16)
-
-
-def backward_local(idx, q, d_out, stat, own, near, dqt, cosine, sine):
+        dim, width = dwq_ref.shape
+        bd = dim // 3
+
+        def product(out_ref, which):
+            dq = dq_ref[:, pl.ds(pl.multiple_of((core + which) % 2 * width, width), width)]
+
+            def rows_step(r, _):
+                rows = pl.ds(pl.multiple_of(r * bd, bd), bd)
+                out_ref[rows, :] = dot(at_ref[rows, :], dq)
+                return 0
+
+            lax.fori_loop(0, dim // bd, rows_step, 0)
+
+        product(dwq_send, 1)
+        copy = to_sibling(rank, dwq_send, dwq_recv, dwq_send_sem, dwq_recv_sem)
+        copy.start()
+        product(dwq_ref, 0)
+
+        @pl.when(core == 1)
+        def _():
+            for slot in range(near_send.shape[0]):
+                near_copy(slot).wait_send()
+
+        @pl.when(core == 0)
+        def _():
+            for slot in range(near_recv.shape[0]):
+                near_copy(slot).wait_recv()
+                down_ref[:, slot * bk:(slot + 1) * bk, :] += near_recv[slot]
+
+        copy.wait()
+        dwq_ref[...] += dwq_recv[...]
+
+
+def backward_local(q, d_out, stat, own, near, dqt, cosine, sine, at):
     heads, tokens, hd = q.shape
+    dim = at.shape[0]
     bk = 256
-    kv_spec = pl.BlockSpec((2, bk, hd), lambda i: (0, i, 0))
+    per = tokens // bk
+    width = heads * hd // 2
+    kv_spec = stack_spec(2, bk, hd)
+    dma = pltpu.SemaphoreType.DMA
     return pl.pallas_call(
         backward_local_kernel,
-        grid=(tokens // bk,),
+        grid=(per,),
         in_specs=[
-            pl.BlockSpec(memory_space=pltpu.SMEM),
             whole(q.shape),
             whole(d_out.shape),
             whole(stat.shape),
@@ -503,62 +577,46 @@
             whole(dqt.shape),
             whole(cosine.shape),
             whole(sine.shape),
-        ],
-        out_specs=[kv_spec, kv_spec, whole((tokens, heads * hd))],
+            whole(at.shape),
+        ],
+        out_specs=[whole((2, tokens, hd)), whole((tokens, heads * hd)), whole((dim, width))],
         out_shape=[
             jax.ShapeDtypeStruct((2, tokens, hd), F32),
-            jax.ShapeDtypeStruct((2, tokens, hd), F32),
             jax.ShapeDtypeStruct((tokens, heads * hd), BF16),
-        ],
-        scratch_shapes=[pltpu.VMEM((heads, hd, tokens), F32)],
-        compiler_params=params(),
-        cost_estimate=cost(15 * heads * tokens * tokens * hd, 12 * heads * tokens * hd),
+            jax.ShapeDtypeStruct((dim, width), F32),
+        ],
+        scratch_shapes=[
+            pltpu.VMEM((heads, hd, tokens), F32),
+            pltpu.VMEM((per, 2, bk, hd), F32),
+            pltpu.VMEM((per, 2, bk, hd), F32),
+            pltpu.VMEM((dim, width), F32),
+            pltpu.VMEM((dim, width), F32),
+            dma((per,)),
+            dma((per,)),
+            dma,
+            dma,
+        ],
+        compiler_params=pltpu.CompilerParams(vmem_limit_bytes=VMEM_LIMIT, collective_id=1, has_side_effects=True),
+        cost_estimate=COST,
         name="backward_local",
-    )(idx, q, d_out, stat, own, near, dqt, cosine, sine)
-
-
-def dwq_kernel(idx_ref, at_ref, dq_ref, out_ref):
-    out_ref[0] = dot(at_ref[...], dq_ref[...])
-
-
-def grad_wq(idx, at, dq):
-    dim, tokens = at.shape
-    width = dq.shape[1]
-    cols = 256
-    per = width // 2 // cols
-    grid_spec = pltpu.PrefetchScalarGridSpec(
-        num_scalar_prefetch=1,
-        grid=(2, per),
-        in_specs=[
-            pl.BlockSpec((dim, tokens), lambda w, j, idx: (0, 0)),
-            pl.BlockSpec((tokens, cols), lambda w, j, idx: (0, ((w + 1 + idx[0]) % 2) * per + j)),
-        ],
-        out_specs=pl.BlockSpec((1, dim, cols), lambda w, j, idx: (1 - w, 0, j)),
-    )
-    return pl.pallas_call(
-        dwq_kernel,
-        grid_spec=grid_spec,
-        out_shape=jax.ShapeDtypeStruct((2, dim, width // 2), F32),
-        compiler_params=params(),
-        cost_estimate=cost(2 * dim * tokens * width, 4 * dim * width),
-        name="grad_wq",
-    )(idx, at, dq)
-
-
-def tail_kernel(idx_ref, down_ref, dnear_ref, dfar_ref, cos_ref, sin_ref, at_ref, dq_ref, wq_ref, wk_ref, wv_ref,
-                x_ref, dy_ref, gain_ref, dpost_ref, dx_ref, dwkv_ref, dgain_ref):
+    )(q, d_out, stat, own, near, dqt, cosine, sine, at)
+
+
+def tail_kernel(idx_ref, down_ref, dfar_ref, cos_ref, sin_ref, at_ref, dq_ref, wq_ref, wk_ref, wv_ref,
+                x_ref, dy_ref, gain_ref, dpost_ref, dx_ref, mine_ref, theirs_ref, dgain_ref):
     _, half = cos_ref.shape
     dim = x_ref.shape[1]
     i = pl.program_id(0)
-    dk = down_ref[0] + dnear_ref[0] + dfar_ref[0]
+    dk = down_ref[0] + dfar_ref[0]
     cosine, sine = cos_ref[...], sin_ref[...]
     first, second = dk[:, :half], dk[:, half:]
     dk = jnp.concatenate([first * cosine + second * sine, second * cosine - first * sine], axis=1).astype(BF16)
-    dv = (down_ref[1] + dnear_ref[1] + dfar_ref[1]).astype(BF16)
+    dv = (down_ref[1] + dfar_ref[1]).astype(BF16)
 
     @pl.when(i == 0)
     def _():
-        dwkv_ref[...] = jnp.zeros_like(dwkv_ref)
+        mine_ref[...] = jnp.zeros_like(mine_ref)
+        theirs_ref[...] = jnp.zeros_like(theirs_ref)
         dgain_ref[...] = jnp.zeros_like(dgain_ref)
 
     core = idx_ref[0] % 2
@@ -566,8 +624,8 @@
     is_core0 = core == 0
     mine = jnp.where(is_core0, dk, dv)
     theirs = jnp.where(is_core0, dv, dk)
-    dwkv_ref[0, 0:dim, :] += dot(at, mine)
-    dwkv_ref[1, 0:dim, :] += dot(at, theirs)
+    mine_ref[0:dim, :] += dot(at, mine)
+    theirs_ref[0:dim, :] += dot(at, theirs)
     da = dot(dq_ref[...], wq_ref[...], NT) + dot(dk, wk_ref[...], NT) + dot(dv, wv_ref[...], NT)
     x = x_ref[...].astype(F32)
     rstd = lax.rsqrt(jnp.mean(x * x, axis=-1, keepdims=True) + NORM_EPS)
@@ -580,19 +638,19 @@
     @pl.when(i == pl.num_programs(0) - 1)
     def _():
         dpre, dpost = dgain_ref[...], dpost_ref[...]
-        for which, row in enumerate((jnp.where(is_core0, dpre, dpost), jnp.where(is_core0, dpost, dpre))):
+        for ref, row in ((mine_ref, jnp.where(is_core0, dpre, dpost)), (theirs_ref, jnp.where(is_core0, dpost, dpre))):
             for c in range(dim // 128):
-                dwkv_ref[which, dim + c // 2:dim + c // 2 + 1, c % 2 * 128:(c % 2 + 1) * 128] = row[:, c * 128:(c + 1) * 128]
-
-
-def tail(idx, down, dnear, dfar, cosine, sine, at, dq, wq, wk, wv, x, dy, gain, dpost):
+                ref[dim + c // 2:dim + c // 2 + 1, c % 2 * 128:(c % 2 + 1) * 128] = row[:, c * 128:(c + 1) * 128]
+
+
+def tail(idx, down, dfar, cosine, sine, at, dq, wq, wk, wv, x, dy, gain, dpost):
     tokens, dim = x.shape
     hd = wk.shape[1]
     width = wq.shape[1]
     bt = 256
-    kv_spec = pl.BlockSpec((2, bt, hd), lambda i: (0, i, 0))
-    rope_spec = pl.BlockSpec((bt, hd // 2), lambda i: (i, 0))
-    rows2 = pl.BlockSpec((bt, dim), lambda i: (i, 0))
+    kv_spec = stack_spec(2, bt, hd)
+    rope_spec = rows_spec(bt, hd // 2)
+    rows2 = rows_spec(bt, dim)
     return pl.pallas_call(
         tail_kernel,
         grid=(tokens // bt,),
@@ -600,11 +658,10 @@
             pl.BlockSpec(memory_space=pltpu.SMEM),
             kv_spec,
             kv_spec,
-            kv_spec,
             rope_spec,
             rope_spec,
             pl.BlockSpec((dim, bt), lambda i: (0, i)),
-            pl.BlockSpec((bt, width), lambda i: (i, 0)),
+            rows_spec(bt, width),
             whole(wq.shape),
             whole(wk.shape),
             whole(wv.shape),
@@ -613,16 +670,17 @@
             whole((1, dim)),
             whole((1, dim)),
         ],
-        out_specs=[rows2, whole((2, dim + 8, hd))],
+        out_specs=[rows2, whole((dim + 8, hd)), whole((dim + 8, hd))],
         out_shape=[
             jax.ShapeDtypeStruct((tokens, dim), BF16),
-            jax.ShapeDtypeStruct((2, dim + 8, hd), F32),
+            jax.ShapeDtypeStruct((dim + 8, hd), F32),
+            jax.ShapeDtypeStruct((dim + 8, hd), F32),
         ],
         scratch_shapes=[pltpu.VMEM((1, dim), F32)],
         compiler_params=params(),
-        cost_estimate=cost(2 * tokens * dim * (width + 4 * hd), 8 * tokens * dim),
+        cost_estimate=COST,
         name="tail",
-    )(idx, down, dnear, dfar, cosine, sine, at, dq, wq, wk, wv, x, dy, gain, dpost)
+    )(idx, down, dfar, cosine, sine, at, dq, wq, wk, wv, x, dy, gain, dpost)
 
 
 def join_wide_kernel(idx_ref, mine_ref, other_ref, out_ref):
@@ -641,15 +699,15 @@
 def join_wide(idx, mine, other, heads):
     dim, width = mine.shape
     bd = 128
-    spec = pl.BlockSpec((bd, width), lambda i: (i, 0))
+    spec = rows_spec(bd, width)
     out = pl.pallas_call(
         join_wide_kernel,
         grid=(dim // bd,),
         in_specs=[pl.BlockSpec(memory_space=pltpu.SMEM), spec, spec],
-        out_specs=pl.BlockSpec((bd * 8, 128), lambda i: (i, 0)),
+        out_specs=rows_spec(bd * 8, 128),
         out_shape=jax.ShapeDtypeStruct((dim * 8, 128), F32),
         compiler_params=params(),
-        cost_estimate=cost(1000, 16 * dim * width),
+        cost_estimate=COST,
         name="join_wide",
     )(idx, mine, other)
     return out.reshape(dim, 2, heads, 128).transpose(0, 2, 1, 3).reshape(dim, heads, 256)
@@ -675,7 +733,7 @@
         out_specs=[whole((dim * 2, 128))] * 2 + [whole((1, dim))] * 2,
         out_shape=[jax.ShapeDtypeStruct((dim * 2, 128), F32)] * 2 + [jax.ShapeDtypeStruct((1, dim), F32)] * 2,
         compiler_params=params(),
-        cost_estimate=cost(1000, 16 * dim * width),
+        cost_estimate=COST,
         name="join_pair",
     )(idx, mine, other)
     return [o.reshape(dim, 1, width) for o in outs[:2]] + [o.reshape(dim) for o in outs[2:]]
@@ -698,7 +756,7 @@
         out_specs=pl.BlockSpec((br, dim), lambda w, i: (w * steps + i, 0)),
         out_shape=jax.ShapeDtypeStruct((rows * 2, dim), F32),
         compiler_params=params(),
-        cost_estimate=cost(1000, 16 * dim * rows),
+        cost_estimate=COST,
         name="join_rows",
     )(idx, mine, other)
 
@@ -745,17 +803,15 @@
         partner_o = permute(o, across)
         y, d_out, dz, stat, dgain_post = post(o, out, lse, x, dy, wo, gain_post)
 
-        dmid, dfar, dqt = backward_far(idx, q, d_out, stat, mid, far)
-        dmid_in = permute(dmid, [(2, 3), (3, 2)])
-        dfar_in = permute(dfar + dmid_in, [(2, 0), (3, 1)])
-        dnear, down, dq = backward_local(idx, q, d_out, stat, own, near, dqt, cosine, sine)
-        dnear_in = permute(dnear, [(1, 0), (3, 2)])
-        dwq = grad_wq(idx, act_t, dq)
-        dwq_mine, dwq_other = sum_halves(dwq)
+        dfar, dqt = backward_far(q, d_out, stat, mid, far)
+        dfar_in = permute(dfar, [(2, 0), (3, 1)])
+        down, dq, dwq_part = backward_local(q, d_out, stat, own, near, dqt, cosine, sine, act_t)
+        dwq_mine = dwq_part + permute(dwq_part, across)
+        dwq_other = permute(dwq_mine, beside)
         dwo = grad_wo(idx, o, dz, partner_o, dy_high, dy_low, wo, gain_post)
         dwo_mine = dwo[0] + permute(dwo[1], beside)
         dwo_other = permute(dwo_mine, beside)
-        dx, dwkv = tail(idx, down, dnear_in, dfar_in, cosine, sine, act_t, dq, wq, wk, wv, x, dy, gain_pre, dgain_post)
+        dx, *dwkv = tail(idx, down, dfar_in, cosine, sine, act_t, dq, wq, wk, wv, x, dy, gain_pre, dgain_post)
         dwkv_mine, dwkv_other = sum_halves(dwkv)
 
         dwo_full = join_rows(idx, dwo_mine, dwo_other)

time: 405 us -> 292 us (0.72)
  waiting for transfers between devices: 168 us -> 54.9 us
  Pallas kernels: 129 us -> 152 us
  starting transfers between devices: 75.1 us -> 63.7 us
  local copies, waits for them, and re-layouts: 14.4 us -> 8.09 us
  other arithmetic: 15.8 us -> 10.9 us
    ppermute x17 -> x14, waiting for transfers between devices: 168 us -> 54.9 us  [permute(): return lax.ppermute(value, 'cp', pairs)]
    pallas_call x5 -> x4, Pallas kernels: 50 us -> 72.5 us  [the longest x1 44 us: backward_local(): pl.pallas_call(backward_local_kernel, grid=(per,), in_specs=[whole(q.shap...]
    ppermute x17 -> x14, starting transfers between devices: 75.1 us -> 63.7 us  [permute(): return lax.ppermute(value, 'cp', pairs)]
    squeeze x3 -> x0, local copies, waits for them, and re-layouts: 8.03 us -> none  [the longest x2 4.75 us: sum_halves(): theirs = permute(parts[1], beside)]
  transfers between devices with their start and end apart: 17 -> 14, of which waited for: 6 -> 3; matrix products, arithmetic and copies ran while one was open for 5% -> 3% of each run, Pallas kernels for 22% -> 48%
where the time goes in v4:
time: 292 us; the launch traced here: 291 us
  Pallas kernels  152 us (52%)
  starting transfers between devices  63.7 us (22%)
  waiting for transfers between devices  54.9 us (19%)
  other arithmetic  10.9 us (4%)
  local copies, waits for them, and re-layouts  8.09 us (3%)
    ppermute x14, starting transfers between devices, permute(): return lax.ppermute(value, 'cp', pairs)  63.7 us
    ppermute x14, waiting for transfers between devices, permute(): return lax.ppermute(value, 'cp', pairs)  54.9 us
    pallas_call x1, Pallas kernels, backward_local(): pl.pallas_call(backward_local_kernel, grid=(per,), in_specs=[whole(q.shap...  44 us
    pallas_call x1, Pallas kernels, grad_wo(): pl.pallas_call(grad_wo_kernel, grid=(tokens // bt,), in_specs=[pl.BlockSp...  17.5 us
    pallas_call x1, Pallas kernels, backward_far(): pl.pallas_call(backward_far_kernel, grid=(2 * per,), in_specs=[whole(q.sh...  15.3 us
    pallas_call x1, Pallas kernels, post(): pl.pallas_call(post_kernel, grid=(tokens // bq,), in_specs=[rows2(heads *...  14.1 us
    pallas_call x1, Pallas kernels, tail(): pl.pallas_call(tail_kernel, grid=(tokens // bt,), in_specs=[pl.BlockSpec(...  13 us
    pallas_call x1, Pallas kernels, forward_local(): pl.pallas_call(forward_local_kernel, grid=(tokens // bq,), in_specs=[pl.B...  10.3 us
  transfers between devices with their start and end apart: 14, of which 3 were waited for; matrix products, arithmetic and copies ran while one was open for 3% of the time, Pallas kernels for 48%

profile of v4, /device:TPU:0, one launch (start us, length us, event | category | flops | bytes accessed | tf_op | source)
XLA Modules:
  0.0 290.6 jit_solution(4714956672491768878)
XLA Ops:
  0.6 1.3 reshape.86.gain_ref
  2.6 3.0 %multiply_sine_fusion = (f32[1024,128]{1,0:T(8,128)}, f32[1024,128]{1,0:T(8,128)}) fusion(f32[128]{0:T(128)S(1)} %multiply_power_fusion, f32[1024]{0:T(1024)S(1)} %bitcast.22), kind=kLoop, calls=%fused_computation | loop fusion | flops 131072 | bytes 1053184 | tf_op jit(solution)/shard_map/sin | solution.py:792
  5.7 6.0 %project_kv.1 = (bf16[1024,1152]{1,0:T(8,128)(2,1)}, bf16[1152,1024]{1,0:T(8,128)(2,1)}, bf16[2,1024,256]{2,1,0:T(8,128)(2,1)}) custom-call(bf16[1024,1152]{1,0:T(8,128)(2,1)} %bitcast.25, f32[1,1152]{1,0:T(1,128)} %reshape.86.gain_ref, bf16[1152,256]{1,0:T(8,128)(2,1)} %bitcast.32, bf16[1152,256]{1,0:T(8,128)(2,1)} %bitcast.34, ...), custom_call_target="tpu_custom_call" | custom-call | flops 10000000000 | bytes 10000000 | tf_op jit(solution)/shard_map/project_kv/pallas_call | solution.py:86
  11.7 6.1 %collective-permute-start = (bf16[2,1024,256]{2,1,0:T(8,128)(2,1)}, bf16[2,1024,256]{2,1,0:T(8,128)(2,1)}, u32[]{:S(2)}, u32[]{:S(2)}) collective-permute-start(bf16[2,1024,256]{2,1,0:T(8,128)(2,1)} %get-tuple-element.36.own_ref), channel_id=1, source_target_pairs={{0,2},{1,3},{4,6},{5,7},{8,10},{9,11},{12,14},{13,15}} | collective-permute-start | bytes 3145736 | tf_op jit(solution)/shard_map/ppermute | solution.py:769
  17.8 1.5 collective-permute-start.2
  19.3 1.3 collective-permute-start.10
  20.6 7.5 %collective-permute-start.11 = (bf16[1024,1152]{1,0:T(8,128)(2,1)}, bf16[1024,1152]{1,0:T(8,128)(2,1)}, u32[]{:S(2)}, u32[]{:S(2)}) collective-permute-start(bf16[1024,1152]{1,0:T(8,128)(2,1)} %bitcast.29), channel_id=1, source_target_pairs={{0,2},{1,3},{4,6},{5,7},{8,10},{9,11},{12,14},{13,15}} | collective-permute-start | bytes 7077896 | tf_op jit(solution)/shard_map/ppermute | solution.py:769
  28.0 2.0 copy.20
  30.1 10.6 %collective-permute-done.far_ref = bf16[2,1024,256]{2,1,0:T(8,128)(2,1)} collective-permute-done((bf16[2,1024,256]{2,1,0:T(8,128)(2,1)}, bf16[2,1024,256]{2,1,0:T(8,128)(2,1)}, u32[]{:S(2)}, u32[]{:S(2)}) %collective-permute-start) | collective-permute-done | bytes 1048608 | tf_op jit(solution)/shard_map/ppermute | solution.py:769
  41.6 7.1 %project_q.1.q_ref = bf16[4,1024,256]{2,1,0:T(8,128)(2,1)} custom-call(bf16[1024,1152]{1,0:T(8,128)(2,1)} %get-tuple-element.35.a_ref, bf16[1152,1024]{1,0:T(8,128)(2,1)} %bitcast.20, f32[1024,128]{1,0:T(8,128)} %get-tuple-element.71.cos_ref, f32[1024,128]{1,0:T(8,128)} %get-tuple-element.70.sin_ref), custom_call_target="tpu_custom_call" | custom-call | flops 10000000000 | bytes 10000000 | tf_op jit(solution)/shard_map/project_q/pallas_call | solution.py:131
  49.3 1.0 copy-done.9
  50.4 10.3 %forward_local.1 = (f32[4,1024,256]{2,1,0:T(8,128)}, f32[4,1024,128]{2,1,0:T(8,128)}) custom-call(s32[1]{0:T(128)} %bitcast.idx_ref, bf16[4,1024,256]{2,1,0:T(8,128)(2,1)} %project_q.1.q_ref, bf16[2,1024,256]{2,1,0:T(8,128)(2,1)} %get-tuple-element.36.own_ref, bf16[2,1024,256]{2,1,0:T(8,128)(2,1)} %copy-done.9), custom_call_target="tpu_custom_call" | custom-call | flops 10000000000 | bytes 10000000 | tf_op jit(solution)/shard_map/forward_local/pallas_call | solution.py:196
  61.6 7.4 %forward_far.1 = (bf16[1024,1024]{1,0:T(8,128)(2,1)}, f32[4,1024,256]{2,1,0:T(8,128)}, f32[1024,128]{1,0:T(8,128)}) custom-call(s32[1]{0:T(128)} %bitcast.idx_ref, bf16[4,1024,256]{2,1,0:T(8,128)(2,1)} %project_q.1.q_ref, bf16[2,1024,256]{2,1,0:T(8,128)(2,1)} %collective-permute-done.far_ref, bf16[2,1024,256]{2,1,0:T(8,128)(2,1)} %copy-done.10, ...), custom_call_target="tpu_custom_call" | custom-call | flops 10000000000 | bytes 10000000 | tf_op jit(solution)/shard_map/forward_far/pallas_call | solution.py:253
  69.0 14.9 %collective-permute-start.9 = (bf16[1024,1024]{1,0:T(8,128)(2,1)}, bf16[1024,1024]{1,0:T(8,128)(2,1)}, u32[]{:S(2)}, u32[]{:S(2)}) collective-permute-start(bf16[1024,1024]{1,0:T(8,128)(2,1)} %get-tuple-element.39.o_ref), channel_id=1, source_target_pairs={{0,2},{2,0},{1,3},{3,1},{4,6},{6,4},{5,7},{7,5},{8,10},{10,8},{9,1... | collective-permute-start | bytes 6291464 | tf_op jit(solution)/shard_map/ppermute | solution.py:769
  83.9 14.1 %post.1 = (bf16[1024,1152]{1,0:T(8,128)(2,1)}, bf16[4,1024,256]{2,1,0:T(8,128)(2,1)}, bf16[1024,1152]{1,0:T(8,128)(2,1)}, f32[8,1024]{1,0:T(8,128)}, f32[1,1152]{1,0:T(1,128)}) custom-call(bf16[1024,1024]{1,0:T(8,128)(2,1)} %get-tuple-element.39.o_ref, f32[4,1024,256]{2,1,0:T(8,128)} %get-tuple-element.40.out_ref, f32[1024,128]{1,0:T(8,128)} %get-tuple-element.41.lse_ref, ...), custom_call_target="tpu_custom_call" | custom-call | flops 10000000000 | bytes 10000000 | tf_op jit(solution)/shard_map/post/pallas_call | solution.py:322
  98.1 15.3 %backward_far.1 = (f32[2,1024,256]{2,1,0:T(8,128)}, f32[4,256,1024]{2,1,0:T(8,128)}) custom-call(bf16[4,1024,256]{2,1,0:T(8,128)(2,1)} %project_q.1.q_ref, bf16[4,1024,256]{2,1,0:T(8,128)(2,1)} %get-tuple-element.43.do_ref, f32[8,1024]{1,0:T(8,128)} %get-tuple-element.44.stat_ref, bf16[2,1024,256]{2,1,0:T(8,128)(2,1)} %copy-done.10, ...), custom_call_target="tpu_custom_call" | custom-call | flops 10000000000 | bytes 10000000 | tf_op jit(solution)/shard_map/backward_far/pallas_call | solution.py:451
  113.4 1.5 collective-permute-start.3
  114.9 44.0 %backward_local.1 = (f32[2,1024,256]{2,1,0:T(8,128)}, bf16[1024,1024]{1,0:T(8,128)(2,1)}, f32[1152,512]{1,0:T(8,128)}) custom-call(bf16[4,1024,256]{2,1,0:T(8,128)(2,1)} %project_q.1.q_ref, bf16[4,1024,256]{2,1,0:T(8,128)(2,1)} %get-tuple-element.43.do_ref, f32[8,1024]{1,0:T(8,128)} %get-tuple-element.44.stat_ref, ...), custom_call_target="tpu_custom_call" | custom-call | flops 10000000000 | bytes 10000000 | tf_op jit(solution)/shard_map/backward_local/pallas_call | solution.py:568
  158.9 28.0 %collective-permute-start.4 = (f32[1152,512]{1,0:T(8,128)}, f32[1152,512]{1,0:T(8,128)}, u32[]{:S(2)}, u32[]{:S(2)}) collective-permute-start(f32[1152,512]{1,0:T(8,128)} %get-tuple-element.52), channel_id=1, source_target_pairs={{0,2},{2,0},{1,3},{3,1},{4,6},{6,4},{5,7},{7,5},{8,10},{10,8},{9,1... | collective-permute-start | bytes 7077896 | tf_op jit(solution)/shard_map/ppermute | solution.py:769
  186.9 17.5 %grad_wo.1 = (f32[512,1152]{1,0:T(8,128)}, f32[512,1152]{1,0:T(8,128)}) custom-call(s32[1]{0:T(128)} %bitcast.idx_ref, bf16[1024,1024]{1,0:T(8,128)(2,1)} %get-tuple-element.39.o_ref, bf16[1024,1152]{1,0:T(8,128)(2,1)} %get-tuple-element.57.dz_ref, bf16[1024,1024]{1,0:T(8,128)(2,1)} %collective-permute-done.9.po_ref, ...), custom_call_target="tpu_custom_call" | custom-call | flops 10000000000 | bytes 10000000 | tf_op jit(solution)/shard_map/grad_wo/pallas_call | solution.py:364
  204.4 1.3 copy-done.8
  205.7 13.0 %tail.1 = (bf16[1024,1152]{1,0:T(8,128)(2,1)}, f32[1160,256]{1,0:T(8,128)}, f32[1160,256]{1,0:T(8,128)}) custom-call(s32[1]{0:T(128)} %bitcast.idx_ref, f32[2,1024,256]{2,1,0:T(8,128)} %get-tuple-element.47.down_ref, f32[2,1024,256]{2,1,0:T(8,128)} %copy-done.8, f32[1024,128]{1,0:T(8,128)} %get-tuple-element.71.cos_ref, ...), custom_call_target="tpu_custom_call" | custom-call | flops 10000000000 | bytes 10000000 | tf_op jit(solution)/shard_map/tail/pallas_call | solution.py:654
  219.3 19.9 %collective-permute-done.4 = f32[1152,512]{1,0:T(8,128)} collective-permute-done((f32[1152,512]{1,0:T(8,128)}, f32[1152,512]{1,0:T(8,128)}, u32[]{:S(2)}, u32[]{:S(2)}) %collective-permute-start.4) | collective-permute-done | bytes 2359328 | tf_op jit(solution)/shard_map/ppermute | solution.py:769
  239.1 2.2 add.12.mine_ref
  241.7 1.4 collective-permute-start.7
  243.9 1.9 add.15.mine_ref
  245.9 24.4 %collective-permute-done.7 = f32[1160,256]{1,0:T(8,128)S(1)} collective-permute-done((f32[1160,256]{1,0:T(8,128)S(1)}, f32[1160,256]{1,0:T(8,128)S(1)}, u32[]{:S(2)}, u32[]{:S(2)}) %collective-permute-start.7) | collective-permute-done | bytes 1187872 | tf_op jit(solution)/shard_map/ppermute | solution.py:769
  270.5 8.0 %join_wide.1 = f32[9216,128]{1,0:T(8,128)} custom-call(s32[1]{0:T(128)} %bitcast.idx_ref, f32[1152,512]{1,0:T(8,128)} %copy-done.2, f32[1152,512]{1,0:T(8,128)} %collective-permute-done.5.other_ref), custom_call_target="tpu_custom_call" | custom-call | flops 10000000000 | bytes 10000000 | tf_op jit(solution)/shard_map/join_wide/pallas_call | solution.py:703
  278.6 3.3 %join_pair.1 = (f32[2304,128]{1,0:T(8,128)}, f32[2304,128]{1,0:T(8,128)}, f32[1,1152]{1,0:T(1,128)}, f32[1,1152]{1,0:T(1,128)}) custom-call(s32[1]{0:T(128)} %bitcast.idx_ref, f32[1160,256]{1,0:T(8,128)} %copy-done.6, f32[1160,256]{1,0:T(8,128)} %collective-permute-done.8.other_ref), custom_call_target="tpu_custom_call" | custom-call | flops 10000000000 | bytes 10000000 | tf_op jit(solution)/shard_map/join_pair/pallas_call | solution.py:730
  281.9 1.3 reduce
  283.2 1.3 reduce.1
  284.5 6.2 %join_rows.1 = f32[1024,1152]{1,0:T(8,128)} custom-call(s32[1]{0:T(128)} %bitcast.idx_ref, f32[512,1152]{1,0:T(8,128)} %copy-done.3, f32[512,1152]{1,0:T(8,128)} %collective-permute-done.13.other_ref), custom_call_target="tpu_custom_call" | custom-call | flops 10000000000 | bytes 10000000 | tf_op jit(solution)/shard_map/join_rows/pallas_call | solution.py:752
  (42 shorter events, 5.2 us)
Async XLA Ops:
  5.7 22.4 %copy-start.4 = (bf16[1152,4,256]{2,1,0:T(4,128)(2,1)S(1)}, bf16[1152,4,256]{2,1,0:T(4,128)(2,1)}, u32[]{:S(2)}) copy-start(bf16[1152,4,256]{2,1,0:T(4,128)(2,1)} %param.12) | copy-start | bytes 7077892
  11.7 28.9 %collective-permute-start = (bf16[2,1024,256]{2,1,0:T(8,128)(2,1)}, bf16[2,1024,256]{2,1,0:T(8,128)(2,1)}, u32[]{:S(2)}, u32[]{:S(2)}) collective-permute-start(bf16[2,1024,256]{2,1,0:T(8,128)(2,1)} %get-tuple-element.36.own_ref), channel_id=1, source_target_pairs={{0,2},{1,3},{4,6},{5,7},{8,10},{9,11},{12,14},{13,15}} | collective-permute-start | bytes 3145736 | tf_op jit(solution)/shard_map/ppermute | solution.py:769
  17.8 31.5 %collective-permute-start.2 = (bf16[2,1024,256]{2,1,0:T(8,128)(2,1)}, bf16[2,1024,256]{2,1,0:T(8,128)(2,1)S(1)}, u32[]{:S(2)}, u32[]{:S(2)}) collective-permute-start(bf16[2,1024,256]{2,1,0:T(8,128)(2,1)} %get-tuple-element.36.own_ref), channel_id=1, source_target_pairs={{0,1},{2,3},{4,5},{6,7},{8,9},{10,11},{12,13},{14,15}} | collective-permute-start | bytes 3145736 | tf_op jit(solution)/shard_map/ppermute | solution.py:769
  19.3 167.6 %collective-permute-start.10 = (bf16[1024,1152]{1,0:T(8,128)(2,1)}, bf16[1024,1152]{1,0:T(8,128)(2,1)}, u32[]{:S(2)}, u32[]{:S(2)}) collective-permute-start(bf16[1024,1152]{1,0:T(8,128)(2,1)} %bitcast.28), channel_id=1, source_target_pairs={{2,0},{3,1},{6,4},{7,5},{10,8},{11,9},{14,12},{15,13}} | collective-permute-start | bytes 7077896 | tf_op jit(solution)/shard_map/ppermute | solution.py:769
  20.6 166.3 %collective-permute-start.11 = (bf16[1024,1152]{1,0:T(8,128)(2,1)}, bf16[1024,1152]{1,0:T(8,128)(2,1)}, u32[]{:S(2)}, u32[]{:S(2)}) collective-permute-start(bf16[1024,1152]{1,0:T(8,128)(2,1)} %bitcast.29), channel_id=1, source_target_pairs={{0,2},{1,3},{4,6},{5,7},{8,10},{9,11},{12,14},{13,15}} | collective-permute-start | bytes 7077896 | tf_op jit(solution)/shard_map/ppermute | solution.py:769
  40.6 20.0 %collective-permute-start.1 = (bf16[2,1024,256]{2,1,0:T(8,128)(2,1)}, bf16[2,1024,256]{2,1,0:T(8,128)(2,1)S(1)}, u32[]{:S(2)}, u32[]{:S(2)}) collective-permute-start(bf16[2,1024,256]{2,1,0:T(8,128)(2,1)} %collective-permute-done.far_ref), channel_id=1, source_target_pairs={{2,3},{3,2},{6,7},{7,6},{10,11},{11,10},{14,15},{15,14}} | collective-permute-start | bytes 3145736 | tf_op jit(solution)/shard_map/ppermute | solution.py:769
  41.5 7.2 %copy-start.7 = (f32[1152]{0:T(1024)S(1)}, f32[1152]{0:T(1024)}, u32[]{:S(2)}) copy-start(f32[1152]{0:T(1024)} %param.17) | copy-start | bytes 13828
  49.3 1.0 copy-start.9
  60.6 1.0 copy-start.10
  69.0 117.9 %collective-permute-start.9 = (bf16[1024,1024]{1,0:T(8,128)(2,1)}, bf16[1024,1024]{1,0:T(8,128)(2,1)}, u32[]{:S(2)}, u32[]{:S(2)}) collective-permute-start(bf16[1024,1024]{1,0:T(8,128)(2,1)} %get-tuple-element.39.o_ref), channel_id=1, source_target_pairs={{0,2},{2,0},{1,3},{3,1},{4,6},{6,4},{5,7},{7,5},{8,10},{10,8},{9,1... | collective-permute-start | bytes 6291464 | tf_op jit(solution)/shard_map/ppermute | solution.py:769
  113.4 91.0 %collective-permute-start.3 = (f32[2,1024,256]{2,1,0:T(8,128)}, f32[2,1024,256]{2,1,0:T(8,128)S(1)}, u32[]{:S(2)}, u32[]{:S(2)}) collective-permute-start(f32[2,1024,256]{2,1,0:T(8,128)} %get-tuple-element.48), channel_id=1, source_target_pairs={{2,0},{3,1},{6,4},{7,5},{10,8},{11,9},{14,12},{15,13}} | collective-permute-start | bytes 6291464 | tf_op jit(solution)/shard_map/ppermute | solution.py:769
  158.9 80.2 %collective-permute-start.4 = (f32[1152,512]{1,0:T(8,128)}, f32[1152,512]{1,0:T(8,128)}, u32[]{:S(2)}, u32[]{:S(2)}) collective-permute-start(f32[1152,512]{1,0:T(8,128)} %get-tuple-element.52), channel_id=1, source_target_pairs={{0,2},{2,0},{1,3},{3,1},{4,6},{6,4},{5,7},{7,5},{8,10},{10,8},{9,1... | collective-permute-start | bytes 7077896 | tf_op jit(solution)/shard_map/ppermute | solution.py:769
  204.3 38.7 %collective-permute-start.12 = (f32[512,1152]{1,0:T(8,128)}, f32[512,1152]{1,0:T(8,128)}, u32[]{:S(2)}, u32[]{:S(2)}) collective-permute-start(f32[512,1152]{1,0:T(8,128)} %get-tuple-element.59), channel_id=1, source_target_pairs={{0,1},{1,0},{2,3},{3,2},{4,5},{5,4},{6,7},{7,6},{8,9},{9,8},{10,11... | collective-permute-start | bytes 7077896 | tf_op jit(solution)/shard_map/ppermute | solution.py:769
  204.3 1.3 copy-start.8
  205.7 33.5 %copy-start.1 = (f32[1152,512]{1,0:T(8,128)S(1)}, f32[1152,512]{1,0:T(8,128)}, u32[]{:S(2)}) copy-start(f32[1152,512]{1,0:T(8,128)} %get-tuple-element.52) | copy-start | bytes 7077892
  218.7 22.7 %copy-start.5 = (f32[1160,256]{1,0:T(8,128)S(1)}, f32[1160,256]{1,0:T(8,128)}, u32[]{:S(2)}) copy-start(f32[1160,256]{1,0:T(8,128)} %get-tuple-element.53) | copy-start | bytes 3563524
  218.7 22.7 %collective-permute-start.6 = (f32[1160,256]{1,0:T(8,128)}, f32[1160,256]{1,0:T(8,128)S(1)}, u32[]{:S(2)}, u32[]{:S(2)}) collective-permute-start(f32[1160,256]{1,0:T(8,128)} %get-tuple-element.54), channel_id=1, source_target_pairs={{0,1},{1,0},{2,3},{3,2},{4,5},{5,4},{6,7},{7,6},{8,9},{9,8},{10,11... | collective-permute-start | bytes 3563528 | tf_op jit(solution)/shard_map/ppermute | solution.py:769
  241.3 4.4 %copy-start.2 = (f32[1152,512]{1,0:T(8,128)}, f32[1152,512]{1,0:T(8,128)S(1)}, u32[]{:S(2)}) copy-start(f32[1152,512]{1,0:T(8,128)S(1)} %add.12.mine_ref) | copy-start | bytes 7077892
  241.4 2.5 copy-start
  241.4 29.1 %collective-permute-start.5 = (f32[1152,512]{1,0:T(8,128)S(1)}, f32[1152,512]{1,0:T(8,128)}, u32[]{:S(2)}, u32[]{:S(2)}) collective-permute-start(f32[1152,512]{1,0:T(8,128)S(1)} %add.12.mine_ref), channel_id=1, source_target_pairs={{0,1},{1,0},{2,3},{3,2},{4,5},{5,4},{6,7},{7,6},{8,9},{9,8},{10,11... | collective-permute-start | bytes 7077896 | tf_op jit(solution)/shard_map/ppermute | solution.py:769
  241.7 28.6 %collective-permute-start.7 = (f32[1160,256]{1,0:T(8,128)S(1)}, f32[1160,256]{1,0:T(8,128)S(1)}, u32[]{:S(2)}, u32[]{:S(2)}) collective-permute-start(f32[1160,256]{1,0:T(8,128)S(1)} %add.13), channel_id=1, source_target_pairs={{0,2},{2,0},{1,3},{3,1},{4,6},{6,4},{5,7},{7,5},{8,10},{10,8},{9,1... | collective-permute-start | bytes 3563528 | tf_op jit(solution)/shard_map/ppermute | solution.py:769
  245.8 32.8 %copy-start.3 = (f32[512,1152]{1,0:T(8,128)}, f32[512,1152]{1,0:T(8,128)S(1)}, u32[]{:S(2)}) copy-start(f32[512,1152]{1,0:T(8,128)S(1)} %add.15.mine_ref) | copy-start | bytes 7077892
  245.8 38.7 %collective-permute-start.13 = (f32[512,1152]{1,0:T(8,128)S(1)}, f32[512,1152]{1,0:T(8,128)}, u32[]{:S(2)}, u32[]{:S(2)}) collective-permute-start(f32[512,1152]{1,0:T(8,128)S(1)} %add.15.mine_ref), channel_id=1, source_target_pairs={{0,1},{1,0},{2,3},{3,2},{4,5},{5,4},{6,7},{7,6},{8,9},{9,8},{10,11... | collective-permute-start | bytes 7077896 | tf_op jit(solution)/shard_map/ppermute | solution.py:769
  270.5 8.1 %copy-start.6 = (f32[1160,256]{1,0:T(8,128)}, f32[1160,256]{1,0:T(8,128)S(1)}, u32[]{:S(2)}) copy-start(f32[1160,256]{1,0:T(8,128)S(1)} %add.14.mine_ref) | copy-start | bytes 3563524
  270.5 8.1 %collective-permute-start.8 = (f32[1160,256]{1,0:T(8,128)S(1)}, f32[1160,256]{1,0:T(8,128)}, u32[]{:S(2)}, u32[]{:S(2)}) collective-permute-start(f32[1160,256]{1,0:T(8,128)S(1)} %add.14.mine_ref), channel_id=1, source_target_pairs={{0,1},{1,0},{2,3},{3,2},{4,5},{5,4},{6,7},{7,6},{8,9},{9,8},{10,11... | collective-permute-start | bytes 3563528 | tf_op jit(solution)/shard_map/ppermute | solution.py:769

commit v5 on v4

--- a/solution.py
+++ b/solution.py
@@ -63,86 +63,10 @@
     )
 
 
-def kv_kernel(x_ref, gain_ref, wk_ref, wv_ref, cos_ref, sin_ref, a_ref, at_ref, kv_ref):
-    half = cos_ref.shape[1]
-    x = x_ref[...].astype(F32)
-    rstd = lax.rsqrt(jnp.mean(x * x, axis=-1, keepdims=True) + NORM_EPS)
-    a = (x * rstd * (1.0 + gain_ref[...])).astype(BF16)
-    a_ref[...] = a
-    at_ref[...] = a.T
-    k = dot(a, wk_ref[...]).astype(BF16).astype(F32)
-    first, second = k[:, :half], k[:, half:]
-    cosine, sine = cos_ref[...], sin_ref[...]
-    kv_ref[0, :, :half] = (first * cosine - second * sine).astype(BF16)
-    kv_ref[0, :, half:] = (second * cosine + first * sine).astype(BF16)
-    kv_ref[1] = dot(a, wv_ref[...]).astype(BF16)
-
-
-def project_kv(x, gain, wk, wv, cosine, sine):
-    tokens, dim = x.shape
-    hd = wk.shape[1]
-    half = hd // 2
-    bt = 256
-    return pl.pallas_call(
-        kv_kernel,
-        grid=(tokens // bt,),
-        in_specs=[
-            rows_spec(bt, dim),
-            whole((1, dim)),
-            whole((dim, hd)),
-            whole((dim, hd)),
-            rows_spec(bt, half),
-            rows_spec(bt, half),
-        ],
-        out_specs=[
-            rows_spec(bt, dim),
-            pl.BlockSpec((dim, bt), lambda i: (0, i)),
-            stack_spec(2, bt, hd),
-        ],
-        out_shape=[
-            jax.ShapeDtypeStruct((tokens, dim), BF16),
-            jax.ShapeDtypeStruct((dim, tokens), BF16),
-            jax.ShapeDtypeStruct((2, tokens, hd), BF16),
-        ],
-        compiler_params=params(),
-        cost_estimate=COST,
-        name="project_kv",
-    )(x, gain, wk, wv, cosine, sine)
-
-
-def q_kernel(a_ref, wq_ref, cos_ref, sin_ref, q_ref):
-    heads, _, hd = q_ref.shape
-    half = hd // 2
-    cosine, sine = cos_ref[...], sin_ref[...]
-    a = a_ref[...]
-    scale = QUERY_SCALE ** -0.5
-    for h in range(heads):
-        q = dot(a, wq_ref[:, h * hd:(h + 1) * hd]).astype(BF16).astype(F32)
-        first, second = q[:, :half], q[:, half:]
-        q_ref[h, :, :half] = ((first * cosine - second * sine) * scale).astype(BF16)
-        q_ref[h, :, half:] = ((second * cosine + first * sine) * scale).astype(BF16)
-
-
-def project_q(a, wq, cosine, sine, heads):
-    tokens, dim = a.shape
-    hd = wq.shape[1] // heads
-    half = hd // 2
-    bt = 256
-    return pl.pallas_call(
-        q_kernel,
-        grid=(tokens // bt,),
-        in_specs=[
-            rows_spec(bt, dim),
-            whole(wq.shape),
-            rows_spec(bt, half),
-            rows_spec(bt, half),
-        ],
-        out_specs=stack_spec(heads, bt, hd),
-        out_shape=jax.ShapeDtypeStruct((heads, tokens, hd), BF16),
-        compiler_params=params(),
-        cost_estimate=COST,
-        name="project_q",
-    )(a, wq, cosine, sine)
+def rope(values, cosine, sine):
+    half = cosine.shape[-1]
+    first, second = values[:, :half], values[:, half:]
+    return jnp.concatenate([first * cosine - second * sine, second * cosine + first * sine], axis=-1)
 
 
 def forward_tile(q_ref, acc_ref, sum_ref, k, v, masked):
@@ -162,123 +86,198 @@
         acc_ref[h] += dot(p.astype(BF16), v)
 
 
-def forward_local_kernel(idx_ref, q_ref, own_ref, near_ref, acc_ref, sum_ref):
-    bq = q_ref.shape[1]
-    tokens = own_ref.shape[1]
+def forward_kernel(x_ref, gain_ref, wk_ref, wv_ref, wq_ref, cos_ref, sin_ref,
+                   at_ref, q_ref, own_ref, near_ref, far_ref, mid_ref, o_ref, out_ref, lse_ref,
+                   a_s, own_s, near_s, far_s, mid_s, acc_s, sum_s,
+                   far_send, far_recv, near_send, near_recv, mid_send, mid_recv):
+    heads, tokens, hd = q_ref.shape
+    bt = x_ref.shape[0]
+    tiles = tokens // bt
+    big = 2 * bt
+    rank = lax.axis_index("cp")
+    core = rank % 2
     i = pl.program_id(0)
-    acc_ref[...] = jnp.zeros_like(acc_ref)
-    sum_ref[...] = jnp.zeros_like(sum_ref)
-
-    def keys(ref, start, size):
-        rows = pl.ds(pl.multiple_of(start, 128), size)
-        return ref[0, rows, :], ref[1, rows, :]
-
-    forward_tile(q_ref, acc_ref, sum_ref, *keys(own_ref, i * bq, bq), True)
-
-    def own_step(j, _):
-        forward_tile(q_ref, acc_ref, sum_ref, *keys(own_ref, j * bq, bq), False)
-        return 0
-
-    lax.fori_loop(0, i, own_step, 0)
-
-    @pl.when(idx_ref[0] % 2 == 1)
-    def _():
-        def near_step(j, _):
-            forward_tile(q_ref, acc_ref, sum_ref, *keys(near_ref, j * 512, 512), False)
+    across = {"cp": (rank + 2) % 4}
+    mesh_id = pl.DeviceIdType.MESH
+
+    def rows_of(t, size=bt):
+        return pl.ds(pl.multiple_of(t * size, size), size)
+
+    def far_copy(t):
+        rows = rows_of(t)
+        return pltpu.make_async_remote_copy(
+            src_ref=own_s.at[:, rows, :], dst_ref=far_s.at[:, rows, :], send_sem=far_send.at[t], recv_sem=far_recv.at[t],
+            device_id=across, device_id_type=mesh_id,
+        )
+
+    def near_copy(t):
+        rows = rows_of(t)
+        return to_sibling(rank, own_s.at[:, rows, :], near_s.at[:, rows, :], near_send.at[t], near_recv.at[t])
+
+    def mid_copy(c):
+        rows = rows_of(c, big)
+        return to_sibling(rank, far_s.at[:, rows, :], mid_s.at[:, rows, :], mid_send.at[c], mid_recv.at[c])
+
+    @pl.when(i == 0)
+    def _():
+        barrier = pltpu.get_barrier_semaphore()
+        for other in (across, {"cp": rank + 1 - 2 * core}):
+            pl.semaphore_signal(barrier, inc=1, device_id=other, device_id_type=mesh_id)
+        pl.semaphore_wait(barrier, 2)
+
+    @pl.when(i < tiles)
+    def _():
+        rows = rows_of(i)
+        x = x_ref[...].astype(F32)
+        rstd = lax.rsqrt(jnp.mean(x * x, axis=-1, keepdims=True) + NORM_EPS)
+        a = (x * rstd * (1.0 + gain_ref[...])).astype(BF16)
+        a_s[rows, :] = a
+        own_s[0, rows, :] = rope(dot(a, wk_ref[...]).astype(BF16).astype(F32), cos_ref[rows, :], sin_ref[rows, :]).astype(BF16)
+        own_s[1, rows, :] = dot(a, wv_ref[...]).astype(BF16)
+        pl.when(rank < 2)(lambda: far_copy(i).start())
+        pl.when(core == 0)(lambda: near_copy(i).start())
+        at_ref[...] = a.T
+
+    def attend(t, kv_ref, start, size, masked):
+        rows, keys = rows_of(t), pl.ds(pl.multiple_of(start, bt), size)
+        forward_tile(q_ref.at[:, rows, :], acc_s.at[:, rows, :], sum_s.at[:, rows, :],
+                     kv_ref[0, keys, :], kv_ref[1, keys, :], masked)
+
+    @pl.when(jnp.logical_and(i >= tiles, i < 2 * tiles))
+    def _():
+        t = i - tiles
+        rows = rows_of(t)
+        a = a_s[rows, :]
+        scale = QUERY_SCALE ** -0.5
+        for h in range(heads):
+            q = dot(a, wq_ref[:, h * hd:(h + 1) * hd]).astype(BF16).astype(F32)
+            q_ref[h, rows, :] = (rope(q, cos_ref[rows, :], sin_ref[rows, :]) * scale).astype(BF16)
+        acc_s[:, rows, :] = jnp.zeros((heads, bt, hd), F32)
+        sum_s[:, rows, :] = jnp.zeros((heads, bt, 128), F32)
+        attend(t, own_s, t * bt, bt, True)
+
+        def own_step(j, _):
+            attend(t, own_s, j * bt, bt, False)
             return 0
 
-        lax.fori_loop(0, tokens // 512, near_step, 0)
-
-
-def forward_local(idx, q, own, near):
-    heads, tokens, hd = q.shape
-    bq = 256
+        lax.fori_loop(0, t, own_step, 0)
+
+        @pl.when(core == 1)
+        def _():
+            pl.when(t == 0)(lambda: [near_copy(n).wait_recv() for n in range(tiles)] and None)
+
+            def near_step(j, _):
+                attend(t, near_s, j * big, big, False)
+                return 0
+
+            lax.fori_loop(0, tokens // big, near_step, 0)
+
+    chunks = tokens // big
+    c = i - 2 * tiles
+
+    def far_chunk(kv_ref, start):
+        def step(t, _):
+            attend(t, kv_ref, start, big, False)
+            return 0
+
+        lax.fori_loop(0, tiles, step, 0)
+
+    @pl.when(jnp.logical_and(rank >= 2, jnp.logical_and(c >= 0, c < chunks)))
+    def _():
+        far_copy(2 * c).wait_recv()
+        far_copy(2 * c + 1).wait_recv()
+        mid_copy(c).start()
+        far_chunk(far_s, c * big)
+
+    @pl.when(jnp.logical_and(rank >= 2, jnp.logical_and(c >= chunks, c < 2 * chunks)))
+    def _():
+        mid_copy(c - chunks).wait_recv()
+        far_chunk(mid_s, (c - chunks) * big)
+
+    last = i - 2 * tiles - 2 * chunks
+
+    @pl.when(last >= 0)
+    def _():
+        rows = rows_of(last)
+        lane = lax.broadcasted_iota(jnp.int32, (bt, 128), 1)
+        lse = jnp.zeros((bt, 128), F32)
+        for h in range(heads):
+            total = jnp.sum(sum_s[h, rows, :], axis=-1, keepdims=True)
+            lse = jnp.where(lane == h, jnp.log2(total), lse)
+            out = acc_s[h, rows, :] / total
+            out_ref[h] = out
+            o_ref[:, h * hd:(h + 1) * hd] = out.astype(BF16)
+        lse_ref[...] = lse
+        for dst, src in ((own_ref, own_s), (near_ref, near_s), (far_ref, far_s), (mid_ref, mid_s)):
+            dst[...] = src[:, rows, :]
+
+    @pl.when(last == tiles - 1)
+    def _():
+        pl.when(rank < 2)(lambda: [far_copy(n).wait_send() for n in range(tiles)] and None)
+        pl.when(core == 0)(lambda: [near_copy(n).wait_send() for n in range(tiles)] and None)
+        pl.when(rank >= 2)(lambda: [mid_copy(n).wait_send() for n in range(chunks)] and None)
+
+
+def forward(x, gain, wk, wv, wq, cosine, sine, heads):
+    tokens, dim = x.shape
+    hd = wk.shape[1]
+    bt = 256
+    tiles = tokens // bt
+    chunks = tiles // 2
+    done = 2 * tiles + 2 * chunks
+    dma = pltpu.SemaphoreType.DMA
+    early = lambda i: jnp.minimum(i, tiles - 1)
+    late = lambda i: jnp.maximum(i - done, 0)
+    kv_shape = jax.ShapeDtypeStruct((2, tokens, hd), BF16)
+    kv_out = pl.BlockSpec((2, bt, hd), lambda i: (0, late(i), 0))
     return pl.pallas_call(
-        forward_local_kernel,
-        grid=(tokens // bq,),
+        forward_kernel,
+        grid=(done + tiles,),
         in_specs=[
-            pl.BlockSpec(memory_space=pltpu.SMEM),
-            stack_spec(heads, bq, hd),
-            whole(own.shape),
-            whole(near.shape),
+            pl.BlockSpec((bt, dim), lambda i: (early(i), 0)),
+            whole(gain.shape),
+            whole(wk.shape),
+            whole(wv.shape),
+            whole(wq.shape),
+            whole(cosine.shape),
+            whole(sine.shape),
         ],
         out_specs=[
-            stack_spec(heads, bq, hd),
-            stack_spec(heads, bq, 128),
+            pl.BlockSpec((dim, bt), lambda i: (0, early(i))),
+            whole((heads, tokens, hd)),
+            kv_out,
+            kv_out,
+            kv_out,
+            kv_out,
+            pl.BlockSpec((bt, heads * hd), lambda i: (late(i), 0)),
+            pl.BlockSpec((heads, bt, hd), lambda i: (0, late(i), 0)),
+            pl.BlockSpec((bt, 128), lambda i: (late(i), 0)),
         ],
         out_shape=[
-            jax.ShapeDtypeStruct((heads, tokens, hd), F32),
-            jax.ShapeDtypeStruct((heads, tokens, 128), F32),
-        ],
-        compiler_params=params(),
-        cost_estimate=COST,
-        name="forward_local",
-    )(idx, q, own, near)
-
-
-def forward_far_kernel(idx_ref, q_ref, far_ref, mid_ref, acc_in_ref, sum_in_ref, o_ref, out_ref, lse_ref, acc_ref, sum_ref):
-    heads, bq, hd = q_ref.shape
-    tokens = far_ref.shape[1]
-    acc_ref[...] = acc_in_ref[...]
-    sum_ref[...] = sum_in_ref[...]
-
-    @pl.when(idx_ref[0] >= 2)
-    def _():
-        def step(ref):
-            def run(j, _):
-                rows = pl.ds(pl.multiple_of(j * 512, 512), 512)
-                forward_tile(q_ref, acc_ref, sum_ref, ref[0, rows, :], ref[1, rows, :], False)
-                return 0
-
-            return run
-
-        lax.fori_loop(0, tokens // 512, step(far_ref), 0)
-        lax.fori_loop(0, tokens // 512, step(mid_ref), 0)
-
-    lane = lax.broadcasted_iota(jnp.int32, (bq, 128), 1)
-    lse = jnp.zeros((bq, 128), F32)
-    for h in range(heads):
-        total = jnp.sum(sum_ref[h], axis=-1, keepdims=True)
-        lse = jnp.where(lane == h, jnp.log2(total), lse)
-        out = acc_ref[h] / total
-        out_ref[h] = out
-        o_ref[:, h * hd:(h + 1) * hd] = out.astype(BF16)
-    lse_ref[...] = lse
-
-
-def forward_far(idx, q, far, mid, acc, row_sum):
-    heads, tokens, hd = q.shape
-    bq = 256
-    rows3 = lambda last: stack_spec(heads, bq, last)
-    return pl.pallas_call(
-        forward_far_kernel,
-        grid=(tokens // bq,),
-        in_specs=[
-            pl.BlockSpec(memory_space=pltpu.SMEM),
-            rows3(hd),
-            whole(far.shape),
-            whole(mid.shape),
-            rows3(hd),
-            rows3(128),
-        ],
-        out_specs=[
-            rows_spec(bq, heads * hd),
-            rows3(hd),
-            rows_spec(bq, 128),
-        ],
-        out_shape=[
+            jax.ShapeDtypeStruct((dim, tokens), BF16),
+            jax.ShapeDtypeStruct((heads, tokens, hd), BF16),
+            kv_shape,
+            kv_shape,
+            kv_shape,
+            kv_shape,
             jax.ShapeDtypeStruct((tokens, heads * hd), BF16),
             jax.ShapeDtypeStruct((heads, tokens, hd), F32),
             jax.ShapeDtypeStruct((tokens, 128), F32),
         ],
-        scratch_shapes=[
-            pltpu.VMEM((heads, bq, hd), F32),
-            pltpu.VMEM((heads, bq, 128), F32),
-        ],
-        compiler_params=params(),
+        scratch_shapes=[pltpu.VMEM((tokens, dim), BF16)] + [pltpu.VMEM((2, tokens, hd), BF16)] * 4 + [
+            pltpu.VMEM((heads, tokens, hd), F32),
+            pltpu.VMEM((heads, tokens, 128), F32),
+            dma((tiles,)),
+            dma((tiles,)),
+            dma((tiles,)),
+            dma((tiles,)),
+            dma((chunks,)),
+            dma((chunks,)),
+        ],
+        compiler_params=pltpu.CompilerParams(vmem_limit_bytes=VMEM_LIMIT, collective_id=2, has_side_effects=True),
         cost_estimate=COST,
-        name="forward_far",
-    )(idx, q, far, mid, acc, row_sum)
+        name="forward",
+    )(x, gain, wk, wv, wq, cosine, sine)
 
 
 def post_norm(o, wo, gain, dy):
@@ -791,14 +790,8 @@
         angles = positions.reshape(tokens, 1).astype(F32) * inv_freq
         cosine, sine = jnp.cos(angles), jnp.sin(angles)
 
-        act, act_t, own = project_kv(x, gain_pre, wk, wv, cosine, sine)
-        far = permute(own, [(0, 2), (1, 3)])
-        near = permute(own, [(0, 1), (2, 3)])
-        q = project_q(act, wq, cosine, sine, heads)
-        acc, row_sum = forward_local(idx, q, own, near)
-        mid = permute(far, [(2, 3), (3, 2)])
         dy_high = permute(dy, [(2, 0), (3, 1)])
-        o, out, lse = forward_far(idx, q, far, mid, acc, row_sum)
+        act_t, q, own, near, far, mid, o, out, lse = forward(x, gain_pre, wk, wv, wq, cosine, sine, heads)
         dy_low = permute(dy, [(0, 2), (1, 3)])
         partner_o = permute(o, across)
         y, d_out, dz, stat, dgain_post = post(o, out, lse, x, dy, wo, gain_post)

time: 292 us -> 301 us (1.031)
  Pallas kernels: 152 us -> 181 us
  waiting for transfers between devices: 54.9 us -> 44.1 us
  starting transfers between devices: 63.7 us -> 57.1 us
    pallas_call x4 -> x1, Pallas kernels: 30.9 us -> 66.3 us  [forward(): pl.pallas_call(forward_kernel, grid=(done + tiles,), in_specs=[pl.BlockSp...]
    ppermute x14 -> x11, waiting for transfers between devices: 54.9 us -> 44.1 us  [permute(): return lax.ppermute(value, 'cp', pairs)]
    pallas_call x1, Pallas kernels: 15.3 us -> 8.38 us  [backward_far(): pl.pallas_call(backward_far_kernel, grid=(2 * per,), in_specs=[whole(q.sh...]
    ppermute x14 -> x11, starting transfers between devices: 63.7 us -> 57.1 us  [permute(): return lax.ppermute(value, 'cp', pairs)]
    unnamed x23 -> x19, local copies, waits for them, and re-layouts: 6.2 us -> 5.51 us
  transfers between devices with their start and end apart: 14 -> 11, of which waited for: 3 -> 2; matrix products, arithmetic and copies ran while one was open for 3% -> 5% of each run, Pallas kernels for 48% -> 58%
where the time goes in v5:
time: 301 us
  Pallas kernels  181 us (60%)
  starting transfers between devices  57.1 us (19%)
  waiting for transfers between devices  44.1 us (15%)
  other arithmetic  10.3 us (3%)
  local copies, waits for them, and re-layouts  7.4 us (2%)
    pallas_call x1, Pallas kernels, forward(): pl.pallas_call(forward_kernel, grid=(done + tiles,), in_specs=[pl.BlockSp...  66.3 us
    ppermute x11, starting transfers between devices, permute(): return lax.ppermute(value, 'cp', pairs)  57.1 us
    pallas_call x1, Pallas kernels, backward_local(): pl.pallas_call(backward_local_kernel, grid=(per,), in_specs=[whole(q.shap...  44.4 us
    ppermute x11, waiting for transfers between devices, permute(): return lax.ppermute(value, 'cp', pairs)  44.1 us
    pallas_call x1, Pallas kernels, grad_wo(): pl.pallas_call(grad_wo_kernel, grid=(tokens // bt,), in_specs=[pl.BlockSp...  17.1 us
    pallas_call x1, Pallas kernels, post(): pl.pallas_call(post_kernel, grid=(tokens // bq,), in_specs=[rows2(heads *...  14.1 us
    pallas_call x1, Pallas kernels, tail(): pl.pallas_call(tail_kernel, grid=(tokens // bt,), in_specs=[pl.BlockSpec(...  13.1 us
    pallas_call x1, Pallas kernels, backward_far(): pl.pallas_call(backward_far_kernel, grid=(2 * per,), in_specs=[whole(q.sh...  8.38 us
  transfers between devices with their start and end apart: 11, of which 2 were waited for; matrix products, arithmetic and copies ran while one was open for 5% of the time, Pallas kernels for 58%

profile of v5, /device:TPU:0, one launch (start us, length us, event | category | flops | bytes accessed | tf_op | source)
XLA Modules:
  0.0 300.6 jit_solution(1297161604493219814)
XLA Ops:
  0.6 1.3 collective-permute-start.7
  1.9 6.7 %collective-permute-start.8 = (bf16[1024,1152]{1,0:T(8,128)(2,1)}, bf16[1024,1152]{1,0:T(8,128)(2,1)}, u32[]{:S(2)}, u32[]{:S(2)}) collective-permute-start(bf16[1024,1152]{1,0:T(8,128)(2,1)} %bitcast.29), channel_id=1, source_target_pairs={{0,2},{1,3},{4,6},{5,7},{8,10},{9,11},{12,14},{13,15}} | collective-permute-start | bytes 7077896 | tf_op jit(solution)/shard_map/ppermute | solution.py:768
  8.6 1.3 reshape.85.gain_ref
  9.9 3.6 %copy.20 = bf16[144,8,4,256]{3,1,2,0:T(8,128)(2,1)} copy(bf16[144,8,4,256]{3,2,1,0:T(4,128)(2,1)} %bitcast.19) | data formatting | bytes 4718592
  13.6 3.0 %multiply_sine_fusion = (f32[1024,128]{1,0:T(8,128)}, f32[1024,128]{1,0:T(8,128)}) fusion(f32[128]{0:T(128)S(1)} %multiply_power_fusion, f32[1024]{0:T(1024)S(1)} %bitcast.22), kind=kLoop, calls=%fused_computation | loop fusion | flops 131072 | bytes 1053184 | tf_op jit(solution)/shard_map/sin | solution.py:791
  16.7 66.3 %forward.1 = (bf16[1152,1024]{1,0:T(8,128)(2,1)}, bf16[4,1024,256]{2,1,0:T(8,128)(2,1)}, bf16[2,1024,256]{2,1,0:T(8,128)(2,1)}, bf16[2,1024,256]{2,1,0:T(8,128)(...) custom-call(bf16[1024,1152]{1,0:T(8,128)(2,1)} %bitcast.25, ...), custom_call_target="tpu_custom_call" | custom-call | flops 10000000000 | bytes 10000000 | tf_op jit(solution)/shard_map/forward/pallas_call | solution.py:233
  83.0 16.8 %collective-permute-start.6 = (bf16[1024,1024]{1,0:T(8,128)(2,1)}, bf16[1024,1024]{1,0:T(8,128)(2,1)}, u32[]{:S(2)}, u32[]{:S(2)}) collective-permute-start(bf16[1024,1024]{1,0:T(8,128)(2,1)} %get-tuple-element.36.o_ref), channel_id=1, source_target_pairs={{0,2},{2,0},{1,3},{3,1},{4,6},{6,4},{5,7},{7,5},{8,10},{10,8},{9,1... | collective-permute-start | bytes 6291464 | tf_op jit(solution)/shard_map/ppermute | solution.py:768
  99.8 0.6 reshape.91.gain_ref
  100.4 14.1 %post.1 = (bf16[1024,1152]{1,0:T(8,128)(2,1)}, bf16[4,1024,256]{2,1,0:T(8,128)(2,1)}, bf16[1024,1152]{1,0:T(8,128)(2,1)}, f32[8,1024]{1,0:T(8,128)}, f32[1,1152]{1,0:T(1,128)}) custom-call(bf16[1024,1024]{1,0:T(8,128)(2,1)} %get-tuple-element.36.o_ref, f32[4,1024,256]{2,1,0:T(8,128)} %get-tuple-element.37.out_ref, f32[1024,128]{1,0:T(8,128)} %get-tuple-element.38.lse_ref, ...), custom_call_target="tpu_custom_call" | custom-call | flops 10000000000 | bytes 10000000 | tf_op jit(solution)/shard_map/post/pallas_call | solution.py:321
  114.5 8.4 %backward_far.1 = (f32[2,1024,256]{2,1,0:T(8,128)}, f32[4,256,1024]{2,1,0:T(8,128)}) custom-call(bf16[4,1024,256]{2,1,0:T(8,128)(2,1)} %get-tuple-element.40.q_ref, bf16[4,1024,256]{2,1,0:T(8,128)(2,1)} %get-tuple-element.41.do_ref, f32[8,1024]{1,0:T(8,128)} %get-tuple-element.42.stat_ref, bf16[2,1024,256]{2,1,0:T(8,128)(2,1)} %get-tuple-element.45.mid_ref, ...), custom_call_target="tpu_custom_call" | custom-call | flops 10000000000 | bytes 10000000 | tf_op jit(solution)/shard_map/backward_far/pallas_call | solution.py:450
  122.9 1.3 collective-permute-start
  124.2 44.4 %backward_local.1 = (f32[2,1024,256]{2,1,0:T(8,128)}, bf16[1024,1024]{1,0:T(8,128)(2,1)}, f32[1152,512]{1,0:T(8,128)}) custom-call(bf16[4,1024,256]{2,1,0:T(8,128)(2,1)} %get-tuple-element.40.q_ref, bf16[4,1024,256]{2,1,0:T(8,128)(2,1)} %get-tuple-element.41.do_ref, f32[8,1024]{1,0:T(8,128)} %get-tuple-element.42.stat_ref, ...), custom_call_target="tpu_custom_call" | custom-call | flops 10000000000 | bytes 10000000 | tf_op jit(solution)/shard_map/backward_local/pallas_call | solution.py:567
  168.6 28.6 %collective-permute-start.1 = (f32[1152,512]{1,0:T(8,128)}, f32[1152,512]{1,0:T(8,128)}, u32[]{:S(2)}, u32[]{:S(2)}) collective-permute-start(f32[1152,512]{1,0:T(8,128)} %get-tuple-element.54), channel_id=1, source_target_pairs={{0,2},{2,0},{1,3},{3,1},{4,6},{6,4},{5,7},{7,5},{8,10},{10,8},{9,1... | collective-permute-start | bytes 7077896 | tf_op jit(solution)/shard_map/ppermute | solution.py:768
  197.2 1.4 copy-done.8
  198.6 17.1 %grad_wo.1 = (f32[512,1152]{1,0:T(8,128)}, f32[512,1152]{1,0:T(8,128)}) custom-call(s32[1]{0:T(128)} %bitcast.7.idx_ref, bf16[1024,1024]{1,0:T(8,128)(2,1)} %get-tuple-element.36.o_ref, bf16[1024,1152]{1,0:T(8,128)(2,1)} %get-tuple-element.59.dz_ref, bf16[1024,1024]{1,0:T(8,128)(2,1)} %collective-permute-done.6.po_ref, bf16[1024,1152]{1,0:T(8,128)(2,1)} %copy-done.8, ...), custom_call_target="tpu_custom_call" | custom-call | flops 10000000000 | bytes 10000000 | tf_op jit(solution)/shard_map/grad_wo/pallas_call | solution.py:363
  215.7 13.1 %tail.1 = (bf16[1024,1152]{1,0:T(8,128)(2,1)}, f32[1160,256]{1,0:T(8,128)}, f32[1160,256]{1,0:T(8,128)}) custom-call(s32[1]{0:T(128)} %bitcast.7.idx_ref, f32[2,1024,256]{2,1,0:T(8,128)} %get-tuple-element.49.down_ref, f32[2,1024,256]{2,1,0:T(8,128)} %collective-permute-done.dfar_ref, f32[1024,128]{1,0:T(8,128)} %get-tuple-element.73.cos_ref, ...), custom_call_target="tpu_custom_call" | custom-call | flops 10000000000 | bytes 10000000 | tf_op jit(solution)/shard_map/tail/pallas_call | solution.py:653
  228.8 0.5 collective-permute-start.3
  229.3 19.7 %collective-permute-done.1 = f32[1152,512]{1,0:T(8,128)} collective-permute-done((f32[1152,512]{1,0:T(8,128)}, f32[1152,512]{1,0:T(8,128)}, u32[]{:S(2)}, u32[]{:S(2)}) %collective-permute-start.1) | collective-permute-done | bytes 2359328 | tf_op jit(solution)/shard_map/ppermute | solution.py:768
  249.1 2.2 add.12.mine_ref
  251.3 0.0 collective-permute-start.2
  251.4 0.2 add.13
  251.6 1.8 collective-permute-start.4
  253.4 0.4 copy-done.1
  253.8 2.0 add.15.mine_ref
  255.8 0.0 collective-permute-start.10
  255.9 24.3 %collective-permute-done.4 = f32[1160,256]{1,0:T(8,128)S(1)} collective-permute-done((f32[1160,256]{1,0:T(8,128)S(1)}, f32[1160,256]{1,0:T(8,128)S(1)}, u32[]{:S(2)}, u32[]{:S(2)}) %collective-permute-start.4) | collective-permute-done | bytes 1187872 | tf_op jit(solution)/shard_map/ppermute | solution.py:768
  280.2 0.2 add.14.mine_ref
  280.5 8.0 %join_wide.1 = f32[9216,128]{1,0:T(8,128)} custom-call(s32[1]{0:T(128)} %bitcast.7.idx_ref, f32[1152,512]{1,0:T(8,128)} %copy-done.2, f32[1152,512]{1,0:T(8,128)} %collective-permute-done.2.other_ref), custom_call_target="tpu_custom_call" | custom-call | flops 10000000000 | bytes 10000000 | tf_op jit(solution)/shard_map/join_wide/pallas_call | solution.py:702
  288.5 3.3 %join_pair.1 = (f32[2304,128]{1,0:T(8,128)}, f32[2304,128]{1,0:T(8,128)}, f32[1,1152]{1,0:T(1,128)}, f32[1,1152]{1,0:T(1,128)}) custom-call(s32[1]{0:T(128)} %bitcast.7.idx_ref, f32[1160,256]{1,0:T(8,128)} %copy-done.5, f32[1160,256]{1,0:T(8,128)} %collective-permute-done.5.other_ref), custom_call_target="tpu_custom_call" | custom-call | flops 10000000000 | bytes 10000000 | tf_op jit(solution)/shard_map/join_pair/pallas_call | solution.py:729
  291.8 1.3 reduce
  293.1 1.3 reduce.1
  294.4 6.2 %join_rows.1 = f32[1024,1152]{1,0:T(8,128)} custom-call(s32[1]{0:T(128)} %bitcast.7.idx_ref, f32[512,1152]{1,0:T(8,128)} %copy-done.3, f32[512,1152]{1,0:T(8,128)} %collective-permute-done.10.other_ref), custom_call_target="tpu_custom_call" | custom-call | flops 10000000000 | bytes 10000000 | tf_op jit(solution)/shard_map/join_rows/pallas_call | solution.py:751
  (29 shorter events, 0.1 us)
Async XLA Ops:
  0.6 196.6 %collective-permute-start.7 = (bf16[1024,1152]{1,0:T(8,128)(2,1)}, bf16[1024,1152]{1,0:T(8,128)(2,1)S(1)}, u32[]{:S(2)}, u32[]{:S(2)}) collective-permute-start(bf16[1024,1152]{1,0:T(8,128)(2,1)} %bitcast.28), channel_id=1, source_target_pairs={{2,0},{3,1},{6,4},{7,5},{10,8},{11,9},{14,12},{15,13}} | collective-permute-start | bytes 7077896 | tf_op jit(solution)/shard_map/ppermute | solution.py:768
  1.9 195.3 %collective-permute-start.8 = (bf16[1024,1152]{1,0:T(8,128)(2,1)}, bf16[1024,1152]{1,0:T(8,128)(2,1)}, u32[]{:S(2)}, u32[]{:S(2)}) collective-permute-start(bf16[1024,1152]{1,0:T(8,128)(2,1)} %bitcast.29), channel_id=1, source_target_pairs={{0,2},{1,3},{4,6},{5,7},{8,10},{9,11},{12,14},{13,15}} | collective-permute-start | bytes 7077896 | tf_op jit(solution)/shard_map/ppermute | solution.py:768
  9.9 3.6 %copy-start.7 = (s32[1,1024]{1,0:T(1,128)S(1)}, s32[1,1024]{1,0:T(1,128)}, u32[]{:S(2)}) copy-start(s32[1,1024]{1,0:T(1,128)} %param.10) | copy-start | bytes 12292
  16.7 83.2 %copy-start.6 = (f32[1152]{0:T(1024)S(1)}, f32[1152]{0:T(1024)}, u32[]{:S(2)}) copy-start(f32[1152]{0:T(1024)} %param.17) | copy-start | bytes 13828
  83.0 114.2 %collective-permute-start.6 = (bf16[1024,1024]{1,0:T(8,128)(2,1)}, bf16[1024,1024]{1,0:T(8,128)(2,1)}, u32[]{:S(2)}, u32[]{:S(2)}) collective-permute-start(bf16[1024,1024]{1,0:T(8,128)(2,1)} %get-tuple-element.36.o_ref), channel_id=1, source_target_pairs={{0,2},{2,0},{1,3},{3,1},{4,6},{6,4},{5,7},{7,5},{8,10},{10,8},{9,1... | collective-permute-start | bytes 6291464 | tf_op jit(solution)/shard_map/ppermute | solution.py:768
  122.9 92.8 %collective-permute-start = (f32[2,1024,256]{2,1,0:T(8,128)}, f32[2,1024,256]{2,1,0:T(8,128)}, u32[]{:S(2)}, u32[]{:S(2)}) collective-permute-start(f32[2,1024,256]{2,1,0:T(8,128)} %get-tuple-element.50), channel_id=1, source_target_pairs={{2,0},{3,1},{6,4},{7,5},{10,8},{11,9},{14,12},{15,13}} | collective-permute-start | bytes 6291464 | tf_op jit(solution)/shard_map/ppermute | solution.py:768
  168.6 80.4 %collective-permute-start.1 = (f32[1152,512]{1,0:T(8,128)}, f32[1152,512]{1,0:T(8,128)}, u32[]{:S(2)}, u32[]{:S(2)}) collective-permute-start(f32[1152,512]{1,0:T(8,128)} %get-tuple-element.54), channel_id=1, source_target_pairs={{0,2},{2,0},{1,3},{3,1},{4,6},{6,4},{5,7},{7,5},{8,10},{10,8},{9,1... | collective-permute-start | bytes 7077896 | tf_op jit(solution)/shard_map/ppermute | solution.py:768
  197.2 1.4 copy-start.8
  215.7 37.7 %collective-permute-start.9 = (f32[512,1152]{1,0:T(8,128)}, f32[512,1152]{1,0:T(8,128)}, u32[]{:S(2)}, u32[]{:S(2)}) collective-permute-start(f32[512,1152]{1,0:T(8,128)} %get-tuple-element.61), channel_id=1, source_target_pairs={{0,1},{1,0},{2,3},{3,2},{4,5},{5,4},{6,7},{7,6},{8,9},{9,8},{10,11... | collective-permute-start | bytes 7077896 | tf_op jit(solution)/shard_map/ppermute | solution.py:768
  215.7 33.4 %copy-start = (f32[1152,512]{1,0:T(8,128)S(1)}, f32[1152,512]{1,0:T(8,128)}, u32[]{:S(2)}) copy-start(f32[1152,512]{1,0:T(8,128)} %get-tuple-element.54) | copy-start | bytes 7077892
  228.8 22.6 %copy-start.4 = (f32[1160,256]{1,0:T(8,128)S(1)}, f32[1160,256]{1,0:T(8,128)}, u32[]{:S(2)}) copy-start(f32[1160,256]{1,0:T(8,128)} %get-tuple-element.55) | copy-start | bytes 3563524
  228.8 22.6 %collective-permute-start.3 = (f32[1160,256]{1,0:T(8,128)}, f32[1160,256]{1,0:T(8,128)S(1)}, u32[]{:S(2)}, u32[]{:S(2)}) collective-permute-start(f32[1160,256]{1,0:T(8,128)} %get-tuple-element.56), channel_id=1, source_target_pairs={{0,1},{1,0},{2,3},{3,2},{4,5},{5,4},{6,7},{7,6},{8,9},{9,8},{10,11... | collective-permute-start | bytes 3563528 | tf_op jit(solution)/shard_map/ppermute | solution.py:768
  251.3 4.5 %copy-start.2 = (f32[1152,512]{1,0:T(8,128)}, f32[1152,512]{1,0:T(8,128)S(1)}, u32[]{:S(2)}) copy-start(f32[1152,512]{1,0:T(8,128)S(1)} %add.12.mine_ref) | copy-start | bytes 7077892
  251.3 2.5 copy-start.1
  251.3 29.1 %collective-permute-start.2 = (f32[1152,512]{1,0:T(8,128)S(1)}, f32[1152,512]{1,0:T(8,128)}, u32[]{:S(2)}, u32[]{:S(2)}) collective-permute-start(f32[1152,512]{1,0:T(8,128)S(1)} %add.12.mine_ref), channel_id=1, source_target_pairs={{0,1},{1,0},{2,3},{3,2},{4,5},{5,4},{6,7},{7,6},{8,9},{9,8},{10,11... | collective-permute-start | bytes 7077896 | tf_op jit(solution)/shard_map/ppermute | solution.py:768
  251.6 28.6 %collective-permute-start.4 = (f32[1160,256]{1,0:T(8,128)S(1)}, f32[1160,256]{1,0:T(8,128)S(1)}, u32[]{:S(2)}, u32[]{:S(2)}) collective-permute-start(f32[1160,256]{1,0:T(8,128)S(1)} %add.13), channel_id=1, source_target_pairs={{0,2},{2,0},{1,3},{3,1},{4,6},{6,4},{5,7},{7,5},{8,10},{10,8},{9,1... | collective-permute-start | bytes 3563528 | tf_op jit(solution)/shard_map/ppermute | solution.py:768
  255.8 32.7 %copy-start.3 = (f32[512,1152]{1,0:T(8,128)}, f32[512,1152]{1,0:T(8,128)S(1)}, u32[]{:S(2)}) copy-start(f32[512,1152]{1,0:T(8,128)S(1)} %add.15.mine_ref) | copy-start | bytes 7077892
  255.8 38.6 %collective-permute-start.10 = (f32[512,1152]{1,0:T(8,128)S(1)}, f32[512,1152]{1,0:T(8,128)}, u32[]{:S(2)}, u32[]{:S(2)}) collective-permute-start(f32[512,1152]{1,0:T(8,128)S(1)} %add.15.mine_ref), channel_id=1, source_target_pairs={{0,1},{1,0},{2,3},{3,2},{4,5},{5,4},{6,7},{7,6},{8,9},{9,8},{10,11... | collective-permute-start | bytes 7077896 | tf_op jit(solution)/shard_map/ppermute | solution.py:768
  280.4 8.1 %copy-start.5 = (f32[1160,256]{1,0:T(8,128)}, f32[1160,256]{1,0:T(8,128)S(1)}, u32[]{:S(2)}) copy-start(f32[1160,256]{1,0:T(8,128)S(1)} %add.14.mine_ref) | copy-start | bytes 3563524
  280.4 8.1 %collective-permute-start.5 = (f32[1160,256]{1,0:T(8,128)S(1)}, f32[1160,256]{1,0:T(8,128)}, u32[]{:S(2)}, u32[]{:S(2)}) collective-permute-start(f32[1160,256]{1,0:T(8,128)S(1)} %add.14.mine_ref), channel_id=1, source_target_pairs={{0,1},{1,0},{2,3},{3,2},{4,5},{5,4},{6,7},{7,6},{8,9},{9,8},{10,11... | collective-permute-start | bytes 3563528 | tf_op jit(solution)/shard_map/ppermute | solution.py:768

commit v6 on v5

--- a/solution.py
+++ b/solution.py
@@ -47,13 +47,6 @@
 
 
 COST = pl.CostEstimate(flops=10**10, bytes_accessed=10**7, transcendentals=0)
-
-
-def meet_sibling(rank):
-    sibling = {"cp": rank + 1 - 2 * (rank % 2)}
-    barrier = pltpu.get_barrier_semaphore()
-    pl.semaphore_signal(barrier, inc=1, device_id=sibling, device_id_type=pl.DeviceIdType.MESH)
-    pl.semaphore_wait(barrier, 1)
 
 
 def to_sibling(rank, src, dst, send, recv):
@@ -130,7 +123,7 @@
         rows = rows_of(i)
         x = x_ref[...].astype(F32)
         rstd = lax.rsqrt(jnp.mean(x * x, axis=-1, keepdims=True) + NORM_EPS)
-        a = (x * rstd * (1.0 + gain_ref[...])).astype(BF16)
+        a = (x * rstd * (1.0 + gain_ref[...][None, :])).astype(BF16)
         a_s[rows, :] = a
         own_s[0, rows, :] = rope(dot(a, wk_ref[...]).astype(BF16).astype(F32), cos_ref[rows, :], sin_ref[rows, :]).astype(BF16)
         own_s[1, rows, :] = dot(a, wv_ref[...]).astype(BF16)
@@ -291,7 +284,7 @@
 
 def post_kernel(o_ref, out_ref, lse_ref, x_ref, dy_ref, wo_ref, gain_ref, y_ref, do_ref, dz_ref, stat_ref, dgain_ref):
     heads, bq, hd = out_ref.shape
-    gain = 1.0 + gain_ref[...]
+    gain = 1.0 + gain_ref[...][None, :]
     dy = dy_ref[...].astype(F32)
     unit, dz = post_norm(o_ref[...], wo_ref[...], gain, dy)
     y_ref[...] = (x_ref[...].astype(F32) + (unit * gain).astype(BF16).astype(F32)).astype(BF16)
@@ -321,7 +314,7 @@
     return pl.pallas_call(
         post_kernel,
         grid=(tokens // bq,),
-        in_specs=[rows2(heads * hd), rows3, rows2(128), rows2(dim), rows2(dim), whole(wo.shape), whole((1, dim))],
+        in_specs=[rows2(heads * hd), rows3, rows2(128), rows2(dim), rows2(dim), whole(wo.shape), whole((dim,))],
         out_specs=[rows2(dim), rows3, rows2(dim), pl.BlockSpec((8, bq), lambda i: (0, i)), whole((1, dim))],
         out_shape=[
             jax.ShapeDtypeStruct((tokens, dim), BF16),
@@ -343,7 +336,7 @@
     i = pl.program_id(0)
     rows = pl.ds(pl.multiple_of(i * bt, bt), bt)
     dy = jnp.where(idx_ref[0] >= 2, pdy_high_ref[...], pdy_low_ref[...]).astype(F32)
-    pdz_ref[rows, :] = post_norm(po_ref[rows, :], wo_ref[...], 1.0 + gain_ref[...], dy)[1]
+    pdz_ref[rows, :] = post_norm(po_ref[rows, :], wo_ref[...], 1.0 + gain_ref[...][None, :], dy)[1]
 
     @pl.when(i == pl.num_programs(0) - 1)
     def _():
@@ -371,7 +364,7 @@
             rows2,
             rows2,
             whole(wo.shape),
-            whole((1, dim)),
+            whole((dim,)),
         ],
         out_specs=[whole((width // 2, dim))] * 2,
         out_shape=[jax.ShapeDtypeStruct((width // 2, dim), F32)] * 2,
@@ -402,123 +395,95 @@
         dqt_ref[h, :, rows] += dot(kt, ds)
 
 
-def backward_far_kernel(q_ref, do_ref, stat_ref, mid_ref, far_ref, dfar_ref, dqt_ref, send_ref, recv_ref, send_sem, recv_sem):
-    tokens = q_ref.shape[1]
-    bq = 512
-    rank = lax.axis_index("cp")
-    i = pl.program_id(0)
-    per = send_ref.shape[0]
-
-    @pl.when(i == 0)
-    def _():
-        dqt_ref[...] = jnp.zeros_like(dqt_ref)
-        meet_sibling(rank)
-
-    def copy(slot):
-        return to_sibling(rank, send_ref.at[slot], recv_ref.at[slot], send_sem.at[slot], recv_sem.at[slot])
-
-    def block(kv_ref, dkv_ref):
-        k, v = kv_ref[0], kv_ref[1]
-        kt = k.T
-
-        def step(j, _):
-            backward_tile(q_ref, do_ref, stat_ref, dqt_ref, dkv_ref, k, v, kt, j * bq, bq, False)
-            return 0
-
-        lax.fori_loop(0, tokens // bq, step, 0)
-
-    @pl.when(jnp.logical_and(rank >= 2, i < per))
-    def _():
-        mine = send_ref.at[i]
-        mine[...] = jnp.zeros_like(mine)
-        block(mid_ref, mine)
-        copy(i).start()
-
-    @pl.when(jnp.logical_and(rank >= 2, i >= per))
-    def _():
-        copy(i - per).wait()
-        dfar_ref[...] = recv_ref[i - per]
-        block(far_ref, dfar_ref)
-
-
-def backward_far(q, d_out, stat, mid, far):
-    heads, tokens, hd = q.shape
-    bk = 256
-    per = tokens // bk
-    early = pl.BlockSpec((2, bk, hd), lambda i: (0, jnp.minimum(i, per - 1), 0))
-    late = pl.BlockSpec((2, bk, hd), lambda i: (0, jnp.maximum(i - per, 0), 0))
-    return pl.pallas_call(
-        backward_far_kernel,
-        grid=(2 * per,),
-        in_specs=[whole(q.shape), whole(d_out.shape), whole(stat.shape), early, late],
-        out_specs=[late, whole((heads, hd, tokens))],
-        out_shape=[
-            jax.ShapeDtypeStruct((2, tokens, hd), F32),
-            jax.ShapeDtypeStruct((heads, hd, tokens), F32),
-        ],
-        scratch_shapes=[
-            pltpu.VMEM((per, 2, bk, hd), F32),
-            pltpu.VMEM((per, 2, bk, hd), F32),
-            pltpu.SemaphoreType.DMA((per,)),
-            pltpu.SemaphoreType.DMA((per,)),
-        ],
-        compiler_params=pltpu.CompilerParams(vmem_limit_bytes=VMEM_LIMIT, collective_id=0, has_side_effects=True),
-        cost_estimate=COST,
-        name="backward_far",
-    )(q, d_out, stat, mid, far)
-
-
-def backward_local_kernel(q_ref, do_ref, stat_ref, own_ref, near_ref, dqt_in_ref, cos_ref, sin_ref, at_ref,
-                          down_ref, dq_ref, dwq_ref, dqt_ref, near_send, near_recv, dwq_send, dwq_recv,
-                          near_send_sem, near_recv_sem, dwq_send_sem, dwq_recv_sem):
+def backward_kernel(q_ref, do_ref, stat_ref, own_ref, near_ref, far_ref, mid_ref, cos_ref, sin_ref, at_ref,
+                    down_ref, dq_ref, dwq_ref,
+                    dqt_s, near_out, near_in, mid_out, mid_in, far_out, far_in, dwq_out, dwq_in,
+                    near_send, near_recv, mid_send, mid_recv, far_send, far_recv, dwq_send, dwq_recv):
     heads, tokens, hd = q_ref.shape
     half = hd // 2
     bk = own_ref.shape[1]
+    big = 2 * bk
+    tiles = tokens // bk
     rank = lax.axis_index("cp")
     core = rank % 2
     i = pl.program_id(0)
-    steps = pl.num_programs(0)
+    across = {"cp": (rank + 2) % 4}
+    mesh_id = pl.DeviceIdType.MESH
+
+    def near_copy(n):
+        return to_sibling(rank, near_out.at[n], near_in.at[n], near_send.at[n], near_recv.at[n])
+
+    def mid_copy(n):
+        return to_sibling(rank, mid_out.at[n], mid_in.at[n], mid_send.at[n], mid_recv.at[n])
+
+    def far_copy(n):
+        return pltpu.make_async_remote_copy(
+            src_ref=far_out.at[n], dst_ref=far_in.at[n], send_sem=far_send.at[n], recv_sem=far_recv.at[n],
+            device_id=across, device_id_type=mesh_id,
+        )
 
     @pl.when(i == 0)
     def _():
-        dqt_ref[...] = dqt_in_ref[...]
-        meet_sibling(rank)
-
-    def near_copy(slot):
-        return to_sibling(rank, near_send.at[slot], near_recv.at[slot], near_send_sem.at[slot], near_recv_sem.at[slot])
-
-    @pl.when(core == 1)
-    def _():
-        k, v = near_ref[0], near_ref[1]
+        dqt_s[...] = jnp.zeros_like(dqt_s)
+        barrier = pltpu.get_barrier_semaphore()
+        for other in (across, {"cp": rank + 1 - 2 * core}):
+            pl.semaphore_signal(barrier, inc=1, device_id=other, device_id_type=mesh_id)
+        pl.semaphore_wait(barrier, 2)
+
+    def all_rows(kv_ref, dkv_ref):
+        k, v = kv_ref[0], kv_ref[1]
         kt = k.T
-        mine = near_send.at[i]
+
+        def step(j, _):
+            backward_tile(q_ref, do_ref, stat_ref, dqt_s, dkv_ref, k, v, kt, j * big, big, False)
+            return 0
+
+        lax.fori_loop(0, tokens // big, step, 0)
+
+    @pl.when(jnp.logical_and(rank >= 2, i < tiles))
+    def _():
+        mine = mid_out.at[i]
         mine[...] = jnp.zeros_like(mine)
-
-        def step(j, _):
-            backward_tile(q_ref, do_ref, stat_ref, dqt_ref, mine, k, v, kt, j * 512, 512, False)
+        all_rows(mid_ref, mine)
+        mid_copy(i).start()
+
+    @pl.when(jnp.logical_and(rank >= 2, jnp.logical_and(i >= tiles, i < 2 * tiles)))
+    def _():
+        n = i - tiles
+        mid_copy(n).wait()
+        mine = far_out.at[n]
+        mine[...] = mid_in[n]
+        all_rows(far_ref, mine)
+        far_copy(n).start()
+
+    n = i - 2 * tiles
+
+    @pl.when(jnp.logical_and(core == 1, n >= 0))
+    def _():
+        mine = near_out.at[n]
+        mine[...] = jnp.zeros_like(mine)
+        all_rows(near_ref, mine)
+        near_copy(n).start()
+
+    @pl.when(n >= 0)
+    def _():
+        down = down_ref.at[:, pl.ds(pl.multiple_of(n * bk, bk), bk), :]
+        down[...] = jnp.zeros_like(down)
+        k, v = own_ref[0], own_ref[1]
+        kt = k.T
+        backward_tile(q_ref, do_ref, stat_ref, dqt_s, down, k, v, kt, n * bk, bk, True)
+
+        def own_step(j, _):
+            backward_tile(q_ref, do_ref, stat_ref, dqt_s, down, k, v, kt, j * bk, bk, False)
             return 0
 
-        lax.fori_loop(0, tokens // 512, step, 0)
-        near_copy(i).start()
-
-    own_rows = pl.ds(pl.multiple_of(i * bk, bk), bk)
-    down = down_ref.at[:, own_rows, :]
-    down[...] = jnp.zeros_like(down)
-    k, v = own_ref[0], own_ref[1]
-    kt = k.T
-    backward_tile(q_ref, do_ref, stat_ref, dqt_ref, down, k, v, kt, i * bk, bk, True)
-
-    def own_step(j, _):
-        backward_tile(q_ref, do_ref, stat_ref, dqt_ref, down, k, v, kt, j * bk, bk, False)
-        return 0
-
-    lax.fori_loop(i + 1, steps, own_step, 0)
-
-    @pl.when(i == steps - 1)
+        lax.fori_loop(n + 1, tiles, own_step, 0)
+
+    @pl.when(n == tiles - 1)
     def _():
         scale = QUERY_SCALE ** -0.5
         for h in range(heads):
-            dq = dqt_ref[h].T
+            dq = dqt_s[h].T
             first, second = dq[:, :half], dq[:, half:]
             cosine, sine = cos_ref[...], sin_ref[...]
             dq_ref[:, h * hd:h * hd + half] = ((first * cosine + second * sine) * scale).astype(BF16)
@@ -536,47 +501,57 @@
 
             lax.fori_loop(0, dim // bd, rows_step, 0)
 
-        product(dwq_send, 1)
-        copy = to_sibling(rank, dwq_send, dwq_recv, dwq_send_sem, dwq_recv_sem)
+        product(dwq_out, 1)
+        copy = to_sibling(rank, dwq_out, dwq_in, dwq_send, dwq_recv)
         copy.start()
         product(dwq_ref, 0)
 
-        @pl.when(core == 1)
-        def _():
-            for slot in range(near_send.shape[0]):
-                near_copy(slot).wait_send()
-
-        @pl.when(core == 0)
-        def _():
-            for slot in range(near_recv.shape[0]):
-                near_copy(slot).wait_recv()
-                down_ref[:, slot * bk:(slot + 1) * bk, :] += near_recv[slot]
-
+        def gather(copy_of, arrived):
+            for t in range(tiles):
+                copy_of(t).wait_recv()
+                down_ref[:, t * bk:(t + 1) * bk, :] += arrived[t]
+
+        def left(copy_of):
+            for t in range(tiles):
+                copy_of(t).wait_send()
+
+        pl.when(core == 1)(lambda: left(near_copy))
+        pl.when(core == 0)(lambda: gather(near_copy, near_in))
         copy.wait()
-        dwq_ref[...] += dwq_recv[...]
-
-
-def backward_local(q, d_out, stat, own, near, dqt, cosine, sine, at):
+        dwq_ref[...] += dwq_in[...]
+        pl.when(rank < 2)(lambda: gather(far_copy, far_in))
+        pl.when(rank >= 2)(lambda: left(far_copy))
+
+
+def backward(q, d_out, stat, own, near, far, mid, cosine, sine, at):
     heads, tokens, hd = q.shape
     dim = at.shape[0]
     bk = 256
-    per = tokens // bk
+    tiles = tokens // bk
     width = heads * hd // 2
-    kv_spec = stack_spec(2, bk, hd)
+
+    def phase(first):
+        return pl.BlockSpec((2, bk, hd), lambda i: (0, jnp.clip(i - first, 0, tiles - 1), 0))
+
+    def held(array):
+        zeros = (0,) * array.ndim
+        return pl.BlockSpec(array.shape, lambda i: zeros, pipeline_mode=pl.Buffered(1))
+
     dma = pltpu.SemaphoreType.DMA
     return pl.pallas_call(
-        backward_local_kernel,
-        grid=(per,),
+        backward_kernel,
+        grid=(3 * tiles,),
         in_specs=[
-            whole(q.shape),
-            whole(d_out.shape),
-            whole(stat.shape),
-            kv_spec,
-            kv_spec,
-            whole(dqt.shape),
-            whole(cosine.shape),
-            whole(sine.shape),
-            whole(at.shape),
+            held(q),
+            held(d_out),
+            held(stat),
+            phase(2 * tiles),
+            phase(2 * tiles),
+            phase(tiles),
+            phase(0),
+            held(cosine),
+            held(sine),
+            held(at),
         ],
         out_specs=[whole((2, tokens, hd)), whole((tokens, heads * hd)), whole((dim, width))],
         out_shape=[
@@ -584,33 +559,24 @@
             jax.ShapeDtypeStruct((tokens, heads * hd), BF16),
             jax.ShapeDtypeStruct((dim, width), F32),
         ],
-        scratch_shapes=[
-            pltpu.VMEM((heads, hd, tokens), F32),
-            pltpu.VMEM((per, 2, bk, hd), F32),
-            pltpu.VMEM((per, 2, bk, hd), F32),
-            pltpu.VMEM((dim, width), F32),
-            pltpu.VMEM((dim, width), F32),
-            dma((per,)),
-            dma((per,)),
-            dma,
-            dma,
-        ],
-        compiler_params=pltpu.CompilerParams(vmem_limit_bytes=VMEM_LIMIT, collective_id=1, has_side_effects=True),
+        scratch_shapes=[pltpu.VMEM((heads, hd, tokens), F32)] + [pltpu.VMEM((tiles, 2, bk, hd), F32)] * 6
+        + [pltpu.VMEM((dim, width), F32)] * 2 + [dma((tiles,))] * 6 + [dma] * 2,
+        compiler_params=pltpu.CompilerParams(vmem_limit_bytes=VMEM_LIMIT, collective_id=0, has_side_effects=True),
         cost_estimate=COST,
-        name="backward_local",
-    )(q, d_out, stat, own, near, dqt, cosine, sine, at)
-
-
-def tail_kernel(idx_ref, down_ref, dfar_ref, cos_ref, sin_ref, at_ref, dq_ref, wq_ref, wk_ref, wv_ref,
+        name="backward",
+    )(q, d_out, stat, own, near, far, mid, cosine, sine, at)
+
+
+def tail_kernel(idx_ref, down_ref, cos_ref, sin_ref, at_ref, dq_ref, wq_ref, wk_ref, wv_ref,
                 x_ref, dy_ref, gain_ref, dpost_ref, dx_ref, mine_ref, theirs_ref, dgain_ref):
     _, half = cos_ref.shape
     dim = x_ref.shape[1]
     i = pl.program_id(0)
-    dk = down_ref[0] + dfar_ref[0]
+    dk = down_ref[0]
     cosine, sine = cos_ref[...], sin_ref[...]
     first, second = dk[:, :half], dk[:, half:]
     dk = jnp.concatenate([first * cosine + second * sine, second * cosine - first * sine], axis=1).astype(BF16)
-    dv = (down_ref[1] + dfar_ref[1]).astype(BF16)
+    dv = down_ref[1].astype(BF16)
 
     @pl.when(i == 0)
     def _():
@@ -630,7 +596,7 @@
     rstd = lax.rsqrt(jnp.mean(x * x, axis=-1, keepdims=True) + NORM_EPS)
     unit = x * rstd
     dgain_ref[...] += jnp.sum(da * unit, axis=0, keepdims=True)
-    g = da * (1.0 + gain_ref[...])
+    g = da * (1.0 + gain_ref[...][None, :])
     dx = rstd * (g - unit * jnp.mean(g * unit, axis=-1, keepdims=True))
     dx_ref[...] = (dy_ref[...].astype(F32) + dx).astype(BF16)
 
@@ -642,7 +608,7 @@
                 ref[dim + c // 2:dim + c // 2 + 1, c % 2 * 128:(c % 2 + 1) * 128] = row[:, c * 128:(c + 1) * 128]
 
 
-def tail(idx, down, dfar, cosine, sine, at, dq, wq, wk, wv, x, dy, gain, dpost):
+def tail(idx, down, cosine, sine, at, dq, wq, wk, wv, x, dy, gain, dpost):
     tokens, dim = x.shape
     hd = wk.shape[1]
     width = wq.shape[1]
@@ -656,7 +622,6 @@
         in_specs=[
             pl.BlockSpec(memory_space=pltpu.SMEM),
             kv_spec,
-            kv_spec,
             rope_spec,
             rope_spec,
             pl.BlockSpec((dim, bt), lambda i: (0, i)),
@@ -666,7 +631,7 @@
             whole(wv.shape),
             rows2,
             rows2,
-            whole((1, dim)),
+            whole((dim,)),
             whole((1, dim)),
         ],
         out_specs=[rows2, whole((dim + 8, hd)), whole((dim + 8, hd))],
@@ -679,7 +644,7 @@
         compiler_params=params(),
         cost_estimate=COST,
         name="tail",
-    )(idx, down, dfar, cosine, sine, at, dq, wq, wk, wv, x, dy, gain, dpost)
+    )(idx, down, cosine, sine, at, dq, wq, wk, wv, x, dy, gain, dpost)
 
 
 def join_wide_kernel(idx_ref, mine_ref, other_ref, out_ref):
@@ -714,14 +679,14 @@
 
 def join_pair_kernel(idx_ref, mine_ref, other_ref, first_ref, second_ref, dpre_ref, dpost_ref):
     core0 = idx_ref[0] % 2 == 0
-    dim = dpre_ref.shape[1]
+    dim = dpre_ref.shape[0]
     mine, other = mine_ref[...], other_ref[...]
     first, second = jnp.where(core0, mine, other), jnp.where(core0, other, mine)
     for src, out_ref, gain_ref in ((first, first_ref, dpre_ref), (second, second_ref, dpost_ref)):
         for c in range(2):
             out_ref[pl.ds(c, dim, stride=2), :] = src[0:dim, c * 128:(c + 1) * 128]
         for c in range(dim // 128):
-            gain_ref[:, c * 128:(c + 1) * 128] = src[dim + c // 2:dim + c // 2 + 1, c % 2 * 128:(c % 2 + 1) * 128]
+            gain_ref[c * 128:(c + 1) * 128] = src[dim + c // 2, c % 2 * 128:(c % 2 + 1) * 128]
 
 
 def join_pair(idx, mine, other):
@@ -729,13 +694,13 @@
     outs = pl.pallas_call(
         join_pair_kernel,
         in_specs=[pl.BlockSpec(memory_space=pltpu.SMEM), whole(mine.shape), whole(mine.shape)],
-        out_specs=[whole((dim * 2, 128))] * 2 + [whole((1, dim))] * 2,
-        out_shape=[jax.ShapeDtypeStruct((dim * 2, 128), F32)] * 2 + [jax.ShapeDtypeStruct((1, dim), F32)] * 2,
+        out_specs=[whole((dim * 2, 128))] * 2 + [whole((dim,))] * 2,
+        out_shape=[jax.ShapeDtypeStruct((dim * 2, 128), F32)] * 2 + [jax.ShapeDtypeStruct((dim,), F32)] * 2,
         compiler_params=params(),
         cost_estimate=COST,
         name="join_pair",
     )(idx, mine, other)
-    return [o.reshape(dim, 1, width) for o in outs[:2]] + [o.reshape(dim) for o in outs[2:]]
+    return [o.reshape(dim, 1, width) for o in outs[:2]] + list(outs[2:])
 
 
 def join_rows_kernel(idx_ref, mine_ref, other_ref, out_ref):
@@ -784,8 +749,8 @@
         wo = w_out.reshape(heads * hd, dim)
         x = x_in.reshape(tokens, dim)
         dy = dy_out.reshape(tokens, dim)
-        gain_pre = w_pre.reshape(1, dim)
-        gain_post = w_post.reshape(1, dim)
+        gain_pre = w_pre
+        gain_post = w_post
         inv_freq = ROPE_BASE ** (jnp.arange(half, dtype=F32) * (-2.0 / hd))
         angles = positions.reshape(tokens, 1).astype(F32) * inv_freq
         cosine, sine = jnp.cos(angles), jnp.sin(angles)
@@ -796,15 +761,13 @@
         partner_o = permute(o, across)
         y, d_out, dz, stat, dgain_post = post(o, out, lse, x, dy, wo, gain_post)
 
-        dfar, dqt = backward_far(q, d_out, stat, mid, far)
-        dfar_in = permute(dfar, [(2, 0), (3, 1)])
-        down, dq, dwq_part = backward_local(q, d_out, stat, own, near, dqt, cosine, sine, act_t)
+        down, dq, dwq_part = backward(q, d_out, stat, own, near, far, mid, cosine, sine, act_t)
         dwq_mine = dwq_part + permute(dwq_part, across)
         dwq_other = permute(dwq_mine, beside)
         dwo = grad_wo(idx, o, dz, partner_o, dy_high, dy_low, wo, gain_post)
         dwo_mine = dwo[0] + permute(dwo[1], beside)
         dwo_other = permute(dwo_mine, beside)
-        dx, *dwkv = tail(idx, down, dfar_in, cosine, sine, act_t, dq, wq, wk, wv, x, dy, gain_pre, dgain_post)
+        dx, *dwkv = tail(idx, down, cosine, sine, act_t, dq, wq, wk, wv, x, dy, gain_pre, dgain_post)
         dwkv_mine, dwkv_other = sum_halves(dwkv)
 
         dwo_full = join_rows(idx, dwo_mine, dwo_other)

time: 301 us -> 293 us (0.973)
  starting transfers between devices: 57.1 us -> 28.8 us
  Pallas kernels: 181 us -> 208 us
  other arithmetic: 10.3 us -> 7.14 us
  local copies, waits for them, and re-layouts: 7.4 us -> 4.36 us
    ppermute x11 -> x10, starting transfers between devices: 57.1 us -> 28.8 us  [permute(): return lax.ppermute(value, 'cp', pairs)]
    pallas_call x2 -> x1, Pallas kernels: 52.8 us -> 78.9 us  [backward(): pl.pallas_call(backward_kernel, grid=(3 * tiles,), in_specs=[held(q), hel...]
    ppermute x11 -> x10, waiting for transfers between devices: 44.1 us -> 43.2 us  [permute(): return lax.ppermute(value, 'cp', pairs)]
  transfers between devices with their start and end apart: 11 -> 10, of which waited for: 2 -> 3; matrix products, arithmetic and copies ran while one was open for 5% -> 4% of each run, Pallas kernels for 58% -> 69%
where the time goes in v6:
time: 293 us; the launch traced here: 292 us
  Pallas kernels  208 us (71%)
  waiting for transfers between devices  43.2 us (15%)
  starting transfers between devices  28.8 us (10%)
  other arithmetic  7.14 us (2%)
  local copies, waits for them, and re-layouts  4.36 us (1%)
    pallas_call x1, Pallas kernels, backward(): pl.pallas_call(backward_kernel, grid=(3 * tiles,), in_specs=[held(q), hel...  78.9 us
    pallas_call x1, Pallas kernels, forward(): pl.pallas_call(forward_kernel, grid=(done + tiles,), in_specs=[pl.BlockSp...  67.6 us
    ppermute x10, waiting for transfers between devices, permute(): return lax.ppermute(value, 'cp', pairs)  43.2 us
    ppermute x10, starting transfers between devices, permute(): return lax.ppermute(value, 'cp', pairs)  28.8 us
    pallas_call x1, Pallas kernels, grad_wo(): pl.pallas_call(grad_wo_kernel, grid=(tokens // bt,), in_specs=[pl.BlockSp...  17.2 us
    pallas_call x1, Pallas kernels, post(): pl.pallas_call(post_kernel, grid=(tokens // bq,), in_specs=[rows2(heads *...  14.1 us
    pallas_call x1, Pallas kernels, tail(): pl.pallas_call(tail_kernel, grid=(tokens // bt,), in_specs=[pl.BlockSpec(...  12.7 us
    pallas_call x1, Pallas kernels, join_wide(): pl.pallas_call(join_wide_kernel, grid=(dim // bd,), in_specs=[pl.BlockSpe...  7.67 us
  transfers between devices with their start and end apart: 10, of which 3 were waited for; matrix products, arithmetic and copies ran while one was open for 4% of the time, Pallas kernels for 69%

profile of v6, /device:TPU:0, one launch (start us, length us, event | category | flops | bytes accessed | tf_op | source)
XLA Modules:
  0.0 291.9 jit_solution(9915096827838092547)
XLA Ops:
  0.6 1.3 collective-permute-start.6
  1.9 8.0 %collective-permute-start.7 = (bf16[1024,1152]{1,0:T(8,128)(2,1)}, bf16[1024,1152]{1,0:T(8,128)(2,1)}, u32[]{:S(2)}, u32[]{:S(2)}) collective-permute-start(bf16[1024,1152]{1,0:T(8,128)(2,1)} %bitcast.27), channel_id=1, source_target_pairs={{0,2},{1,3},{4,6},{5,7},{8,10},{9,11},{12,14},{13,15}} | collective-permute-start | bytes 7077896 | tf_op jit(solution)/shard_map/ppermute | solution.py:733
  9.9 3.6 %copy.20 = bf16[144,8,4,256]{3,1,2,0:T(8,128)(2,1)} copy(bf16[144,8,4,256]{3,2,1,0:T(4,128)(2,1)} %bitcast.19) | data formatting | bytes 4718592
  13.6 3.0 %multiply_sine_fusion = (f32[1024,128]{1,0:T(8,128)}, f32[1024,128]{1,0:T(8,128)}) fusion(f32[128]{0:T(128)S(1)} %multiply_power_fusion, f32[1024]{0:T(1024)S(1)} %bitcast.22), kind=kLoop, calls=%fused_computation | loop fusion | flops 131072 | bytes 1053184 | tf_op jit(solution)/shard_map/sin | solution.py:756
  16.6 67.6 %forward.1 = (bf16[1152,1024]{1,0:T(8,128)(2,1)}, bf16[4,1024,256]{2,1,0:T(8,128)(2,1)}, bf16[2,1024,256]{2,1,0:T(8,128)(2,1)}, bf16[2,1024,256]{2,1,0:T(8,128)(...) custom-call(bf16[1024,1152]{1,0:T(8,128)(2,1)} %bitcast.23, ...), custom_call_target="tpu_custom_call" | custom-call | flops 10000000000 | bytes 10000000 | tf_op jit(solution)/shard_map/forward/pallas_call | solution.py:226
  84.2 16.9 %collective-permute-start.5 = (bf16[1024,1024]{1,0:T(8,128)(2,1)}, bf16[1024,1024]{1,0:T(8,128)(2,1)}, u32[]{:S(2)}, u32[]{:S(2)}) collective-permute-start(bf16[1024,1024]{1,0:T(8,128)(2,1)} %get-tuple-element.34.o_ref), channel_id=1, source_target_pairs={{0,2},{2,0},{1,3},{3,1},{4,6},{6,4},{5,7},{7,5},{8,10},{10,8},{9,1... | collective-permute-start | bytes 6291464 | tf_op jit(solution)/shard_map/ppermute | solution.py:733
  101.1 14.1 %post.1 = (bf16[1024,1152]{1,0:T(8,128)(2,1)}, bf16[4,1024,256]{2,1,0:T(8,128)(2,1)}, bf16[1024,1152]{1,0:T(8,128)(2,1)}, f32[8,1024]{1,0:T(8,128)}, f32[1,1152]{1,0:T(1,128)}) custom-call(bf16[1024,1024]{1,0:T(8,128)(2,1)} %get-tuple-element.34.o_ref, f32[4,1024,256]{2,1,0:T(8,128)} %get-tuple-element.35.out_ref, f32[1024,128]{1,0:T(8,128)} %get-tuple-element.36.lse_ref, ...), custom_call_target="tpu_custom_call" | custom-call | flops 10000000000 | bytes 10000000 | tf_op jit(solution)/shard_map/post/pallas_call | solution.py:314
  115.2 78.9 %backward.1 = (f32[2,1024,256]{2,1,0:T(8,128)}, bf16[1024,1024]{1,0:T(8,128)(2,1)}, f32[1152,512]{1,0:T(8,128)}) custom-call(bf16[4,1024,256]{2,1,0:T(8,128)(2,1)} %get-tuple-element.38.q_ref, bf16[4,1024,256]{2,1,0:T(8,128)(2,1)} %get-tuple-element.39.do_ref, f32[8,1024]{1,0:T(8,128)} %get-tuple-element.40.stat_ref, ...), custom_call_target="tpu_custom_call" | custom-call | flops 10000000000 | bytes 10000000 | tf_op jit(solution)/shard_map/backward/pallas_call | solution.py:541
  194.2 0.0 collective-permute-start
  194.2 12.7 %tail.1 = (bf16[1024,1152]{1,0:T(8,128)(2,1)}, f32[1160,256]{1,0:T(8,128)}, f32[1160,256]{1,0:T(8,128)}) custom-call(s32[1]{0:T(128)} %bitcast.7.idx_ref, f32[2,1024,256]{2,1,0:T(8,128)} %get-tuple-element.46.down_ref, f32[1024,128]{1,0:T(8,128)} %get-tuple-element.69.cos_ref, f32[1024,128]{1,0:T(8,128)} %get-tuple-element.68.sin_ref, ...), custom_call_target="tpu_custom_call" | custom-call | flops 10000000000 | bytes 10000000 | tf_op jit(solution)/shard_map/tail/pallas_call | solution.py:619
  206.9 0.0 collective-permute-start.2
  207.0 0.0 collective-permute-done.6.pdy_low_ref
  207.0 0.0 collective-permute-done.7.pdy_high_ref
  207.0 17.2 %grad_wo.1 = (f32[512,1152]{1,0:T(8,128)}, f32[512,1152]{1,0:T(8,128)}) custom-call(s32[1]{0:T(128)} %bitcast.7.idx_ref, bf16[1024,1024]{1,0:T(8,128)(2,1)} %get-tuple-element.34.o_ref, bf16[1024,1152]{1,0:T(8,128)(2,1)} %get-tuple-element.55.dz_ref, bf16[1024,1024]{1,0:T(8,128)(2,1)} %collective-permute-done.5.po_ref, ...), custom_call_target="tpu_custom_call" | custom-call | flops 10000000000 | bytes 10000000 | tf_op jit(solution)/shard_map/grad_wo/pallas_call | solution.py:356
  224.2 0.5 collective-permute-start.8
  224.7 0.0 collective-permute-done.2
  224.7 1.7 add.13
  226.3 2.0 collective-permute-start.3
  228.4 20.1 %collective-permute-done = f32[1152,512]{1,0:T(8,128)S(1)} collective-permute-done((f32[1152,512]{1,0:T(8,128)}, f32[1152,512]{1,0:T(8,128)S(1)}, u32[]{:S(2)}, u32[]{:S(2)}) %collective-permute-start) | collective-permute-done | bytes 2359328 | tf_op jit(solution)/shard_map/ppermute | solution.py:733
  248.5 1.9 add.12.mine_ref
  250.5 0.0 collective-permute-start.1
  250.5 21.0 %collective-permute-done.3 = f32[1160,256]{1,0:T(8,128)S(1)} collective-permute-done((f32[1160,256]{1,0:T(8,128)S(1)}, f32[1160,256]{1,0:T(8,128)S(1)}, u32[]{:S(2)}, u32[]{:S(2)}) %collective-permute-start.3) | collective-permute-done | bytes 1187872 | tf_op jit(solution)/shard_map/ppermute | solution.py:733
  271.5 0.2 add.14.mine_ref
  271.7 0.0 collective-permute-start.4
  271.7 0.0 collective-permute-done.8
  271.8 0.2 add.15.mine_ref
  272.0 0.7 copy-done.4
  272.7 0.0 collective-permute-start.9
  272.7 2.0 collective-permute-done.4.other_ref
  274.7 3.3 %join_pair.1 = (f32[2304,128]{1,0:T(8,128)}, f32[2304,128]{1,0:T(8,128)}, f32[1152]{0:T(1024)}, f32[1152]{0:T(1024)}) custom-call(s32[1]{0:T(128)} %bitcast.7.idx_ref, f32[1160,256]{1,0:T(8,128)} %copy-done.4, f32[1160,256]{1,0:T(8,128)} %collective-permute-done.4.other_ref), custom_call_target="tpu_custom_call" | custom-call | flops 10000000000 | bytes 10000000 | tf_op jit(solution)/shard_map/join_pair/pallas_call | solution.py:694
  278.0 7.7 %join_wide.1 = f32[9216,128]{1,0:T(8,128)} custom-call(s32[1]{0:T(128)} %bitcast.7.idx_ref, f32[1152,512]{1,0:T(8,128)} %add.12.mine_ref, f32[1152,512]{1,0:T(8,128)} %collective-permute-done.1.other_ref), custom_call_target="tpu_custom_call" | custom-call | flops 10000000000 | bytes 10000000 | tf_op jit(solution)/shard_map/join_wide/pallas_call | solution.py:667
  285.7 6.2 %join_rows.1 = f32[1024,1152]{1,0:T(8,128)} custom-call(s32[1]{0:T(128)} %bitcast.7.idx_ref, f32[512,1152]{1,0:T(8,128)} %copy-done.2, f32[512,1152]{1,0:T(8,128)} %collective-permute-done.9.other_ref), custom_call_target="tpu_custom_call" | custom-call | flops 10000000000 | bytes 10000000 | tf_op jit(solution)/shard_map/join_rows/pallas_call | solution.py:716
  (16 shorter events, 0.0 us)
Async XLA Ops:
  0.6 206.4 %collective-permute-start.6 = (bf16[1024,1152]{1,0:T(8,128)(2,1)}, bf16[1024,1152]{1,0:T(8,128)(2,1)}, u32[]{:S(2)}, u32[]{:S(2)}) collective-permute-start(bf16[1024,1152]{1,0:T(8,128)(2,1)} %bitcast.26), channel_id=1, source_target_pairs={{2,0},{3,1},{6,4},{7,5},{10,8},{11,9},{14,12},{15,13}} | collective-permute-start | bytes 7077896 | tf_op jit(solution)/shard_map/ppermute | solution.py:733
  1.9 205.1 %collective-permute-start.7 = (bf16[1024,1152]{1,0:T(8,128)(2,1)}, bf16[1024,1152]{1,0:T(8,128)(2,1)}, u32[]{:S(2)}, u32[]{:S(2)}) collective-permute-start(bf16[1024,1152]{1,0:T(8,128)(2,1)} %bitcast.27), channel_id=1, source_target_pairs={{0,2},{1,3},{4,6},{5,7},{8,10},{9,11},{12,14},{13,15}} | collective-permute-start | bytes 7077896 | tf_op jit(solution)/shard_map/ppermute | solution.py:733
  9.9 3.7 %copy-start.5 = (s32[1,1024]{1,0:T(1,128)S(1)}, s32[1,1024]{1,0:T(1,128)}, u32[]{:S(2)}) copy-start(s32[1,1024]{1,0:T(1,128)} %param.10) | copy-start | bytes 12292
  84.2 122.7 %collective-permute-start.5 = (bf16[1024,1024]{1,0:T(8,128)(2,1)}, bf16[1024,1024]{1,0:T(8,128)(2,1)}, u32[]{:S(2)}, u32[]{:S(2)}) collective-permute-start(bf16[1024,1024]{1,0:T(8,128)(2,1)} %get-tuple-element.34.o_ref), channel_id=1, source_target_pairs={{0,2},{2,0},{1,3},{3,1},{4,6},{6,4},{5,7},{7,5},{8,10},{10,8},{9,1... | collective-permute-start | bytes 6291464 | tf_op jit(solution)/shard_map/ppermute | solution.py:733
  194.2 54.4 %collective-permute-start = (f32[1152,512]{1,0:T(8,128)}, f32[1152,512]{1,0:T(8,128)S(1)}, u32[]{:S(2)}, u32[]{:S(2)}) collective-permute-start(f32[1152,512]{1,0:T(8,128)} %get-tuple-element.50), channel_id=1, source_target_pairs={{0,2},{2,0},{1,3},{3,1},{4,6},{6,4},{5,7},{7,5},{8,10},{10,8},{9,1... | collective-permute-start | bytes 7077896 | tf_op jit(solution)/shard_map/ppermute | solution.py:733
  206.9 17.8 %collective-permute-start.2 = (f32[1160,256]{1,0:T(8,128)}, f32[1160,256]{1,0:T(8,128)}, u32[]{:S(2)}, u32[]{:S(2)}) collective-permute-start(f32[1160,256]{1,0:T(8,128)} %get-tuple-element.52), channel_id=1, source_target_pairs={{0,1},{1,0},{2,3},{3,2},{4,5},{5,4},{6,7},{7,6},{8,9},{9,8},{10,11... | collective-permute-start | bytes 3563528 | tf_op jit(solution)/shard_map/ppermute | solution.py:733
  207.0 17.7 %copy-start.3 = (f32[1160,256]{1,0:T(8,128)S(1)}, f32[1160,256]{1,0:T(8,128)}, u32[]{:S(2)}) copy-start(f32[1160,256]{1,0:T(8,128)} %get-tuple-element.51) | copy-start | bytes 3563524
  224.2 24.3 %copy-start = (f32[1152,512]{1,0:T(8,128)S(1)}, f32[1152,512]{1,0:T(8,128)}, u32[]{:S(2)}) copy-start(f32[1152,512]{1,0:T(8,128)} %get-tuple-element.50) | copy-start | bytes 7077892
  224.2 47.5 %collective-permute-start.8 = (f32[512,1152]{1,0:T(8,128)}, f32[512,1152]{1,0:T(8,128)S(1)}, u32[]{:S(2)}, u32[]{:S(2)}) collective-permute-start(f32[512,1152]{1,0:T(8,128)} %get-tuple-element.57), channel_id=1, source_target_pairs={{0,1},{1,0},{2,3},{3,2},{4,5},{5,4},{6,7},{7,6},{8,9},{9,8},{10,11... | collective-permute-start | bytes 7077896 | tf_op jit(solution)/shard_map/ppermute | solution.py:733
  226.3 45.1 %collective-permute-start.3 = (f32[1160,256]{1,0:T(8,128)S(1)}, f32[1160,256]{1,0:T(8,128)S(1)}, u32[]{:S(2)}, u32[]{:S(2)}) collective-permute-start(f32[1160,256]{1,0:T(8,128)S(1)} %add.13), channel_id=1, source_target_pairs={{0,2},{2,0},{1,3},{3,1},{4,6},{6,4},{5,7},{7,5},{8,10},{10,8},{9,1... | collective-permute-start | bytes 3563528 | tf_op jit(solution)/shard_map/ppermute | solution.py:733
  250.5 21.3 %copy-start.1 = (f32[512,1152]{1,0:T(8,128)S(1)}, f32[512,1152]{1,0:T(8,128)}, u32[]{:S(2)}) copy-start(f32[512,1152]{1,0:T(8,128)} %get-tuple-element.56) | copy-start | bytes 7077892
  250.5 27.6 %collective-permute-start.1 = (f32[1152,512]{1,0:T(8,128)}, f32[1152,512]{1,0:T(8,128)}, u32[]{:S(2)}, u32[]{:S(2)}) collective-permute-start(f32[1152,512]{1,0:T(8,128)} %add.12.mine_ref), channel_id=1, source_target_pairs={{0,1},{1,0},{2,3},{3,2},{4,5},{5,4},{6,7},{7,6},{8,9},{9,8},{10,11... | collective-permute-start | bytes 7077896 | tf_op jit(solution)/shard_map/ppermute | solution.py:733
  271.7 1.0 copy-start.4
  271.7 3.0 %collective-permute-start.4 = (f32[1160,256]{1,0:T(8,128)S(1)}, f32[1160,256]{1,0:T(8,128)}, u32[]{:S(2)}, u32[]{:S(2)}) collective-permute-start(f32[1160,256]{1,0:T(8,128)S(1)} %add.14.mine_ref), channel_id=1, source_target_pairs={{0,1},{1,0},{2,3},{3,2},{4,5},{5,4},{6,7},{7,6},{8,9},{9,8},{10,11... | collective-permute-start | bytes 3563528 | tf_op jit(solution)/shard_map/ppermute | solution.py:733
  272.7 5.3 %copy-start.2 = (f32[512,1152]{1,0:T(8,128)}, f32[512,1152]{1,0:T(8,128)S(1)}, u32[]{:S(2)}) copy-start(f32[512,1152]{1,0:T(8,128)S(1)} %add.15.mine_ref) | copy-start | bytes 7077892
  272.7 13.0 %collective-permute-start.9 = (f32[512,1152]{1,0:T(8,128)S(1)}, f32[512,1152]{1,0:T(8,128)}, u32[]{:S(2)}, u32[]{:S(2)}) collective-permute-start(f32[512,1152]{1,0:T(8,128)S(1)} %add.15.mine_ref), channel_id=1, source_target_pairs={{0,1},{1,0},{2,3},{3,2},{4,5},{5,4},{6,7},{7,6},{8,9},{9,8},{10,11... | collective-permute-start | bytes 7077896 | tf_op jit(solution)/shard_map/ppermute | solution.py:733

commit v7 on v6

--- a/solution.py
+++ b/solution.py
@@ -677,29 +677,40 @@
     return out.reshape(dim, 2, heads, 128).transpose(0, 2, 1, 3).reshape(dim, heads, 256)
 
 
-def join_pair_kernel(idx_ref, mine_ref, other_ref, first_ref, second_ref, dpre_ref, dpost_ref):
+def join_pair_kernel(idx_ref, a_ref, b_ref, c_ref, d_ref, ga_ref, gb_ref, gc_ref, gd_ref, first_ref, second_ref, dpre_ref, dpost_ref):
     core0 = idx_ref[0] % 2 == 0
     dim = dpre_ref.shape[0]
-    mine, other = mine_ref[...], other_ref[...]
-    first, second = jnp.where(core0, mine, other), jnp.where(core0, other, mine)
-    for src, out_ref, gain_ref in ((first, first_ref, dpre_ref), (second, second_ref, dpost_ref)):
+    rows = a_ref.shape[0]
+
+    def ordered(mine, other):
+        return jnp.where(core0, mine, other), jnp.where(core0, other, mine)
+
+    for src, out_ref in zip(ordered(a_ref[...] + b_ref[...], c_ref[...] + d_ref[...]), (first_ref, second_ref)):
         for c in range(2):
-            out_ref[pl.ds(c, dim, stride=2), :] = src[0:dim, c * 128:(c + 1) * 128]
-        for c in range(dim // 128):
-            gain_ref[c * 128:(c + 1) * 128] = src[dim + c // 2, c % 2 * 128:(c % 2 + 1) * 128]
-
-
-def join_pair(idx, mine, other):
-    dim, width = mine.shape[0] - 8, mine.shape[1]
+            out_ref[pl.ds(c, rows, stride=2), :] = src[:, c * 128:(c + 1) * 128]
+
+    @pl.when(pl.program_id(0) == 0)
+    def _():
+        for src, gain_ref in zip(ordered(ga_ref[...] + gb_ref[...], gc_ref[...] + gd_ref[...]), (dpre_ref, dpost_ref)):
+            for c in range(dim // 128):
+                gain_ref[c * 128:(c + 1) * 128] = src[c // 2, c % 2 * 128:(c % 2 + 1) * 128]
+
+
+def join_pair(idx, *parts):
+    dim, width = parts[0].shape[0] - 8, parts[0].shape[1]
+    bd = dim // 3
+    gain_rows = dim // 8
     outs = pl.pallas_call(
         join_pair_kernel,
-        in_specs=[pl.BlockSpec(memory_space=pltpu.SMEM), whole(mine.shape), whole(mine.shape)],
-        out_specs=[whole((dim * 2, 128))] * 2 + [whole((dim,))] * 2,
+        grid=(dim // bd,),
+        in_specs=[pl.BlockSpec(memory_space=pltpu.SMEM)] + [rows_spec(bd, width)] * 4
+        + [pl.BlockSpec((8, width), lambda i: (gain_rows, 0))] * 4,
+        out_specs=[rows_spec(bd * 2, 128)] * 2 + [whole((dim,))] * 2,
         out_shape=[jax.ShapeDtypeStruct((dim * 2, 128), F32)] * 2 + [jax.ShapeDtypeStruct((dim,), F32)] * 2,
         compiler_params=params(),
         cost_estimate=COST,
         name="join_pair",
-    )(idx, mine, other)
+    )(idx, *parts, *parts)
     return [o.reshape(dim, 1, width) for o in outs[:2]] + list(outs[2:])
 
 
@@ -731,12 +742,6 @@
 
     def permute(value, pairs):
         return lax.ppermute(value, "cp", pairs)
-
-    def sum_halves(parts):
-        theirs = permute(parts[1], beside)
-        mine = parts[0] + theirs
-        mine = mine + permute(mine, across)
-        return mine, permute(mine, beside)
 
     def local_step(x_in, positions, dy_out, w_query, w_key, w_value, w_out, w_pre, w_post):
         batch, tokens, dim = x_in.shape
@@ -768,11 +773,15 @@
         dwo_mine = dwo[0] + permute(dwo[1], beside)
         dwo_other = permute(dwo_mine, beside)
         dx, *dwkv = tail(idx, down, cosine, sine, act_t, dq, wq, wk, wv, x, dy, gain_pre, dgain_post)
-        dwkv_mine, dwkv_other = sum_halves(dwkv)
+        theirs_in, mine_in = permute(dwkv[1], beside), permute(dwkv[0], beside)
+        chip_mine = dwkv[0] + theirs_in
+        chip_other = dwkv[1] + mine_in
+        far_mine = permute(chip_mine, across)
+        far_other = permute(far_mine, beside)
 
         dwo_full = join_rows(idx, dwo_mine, dwo_other)
         dwq_full = join_wide(idx, dwq_mine, dwq_other, heads)
-        dwk_full, dwv_full, dpre_full, dpost_full = join_pair(idx, dwkv_mine, dwkv_other)
+        dwk_full, dwv_full, dpre_full, dpost_full = join_pair(idx, chip_mine, far_mine, chip_other, far_other)
         return (
             y.reshape(batch, tokens, dim),
             dx.reshape(batch, tokens, dim),

time: 293 us -> 293 us (level)
    ppermute x10 -> x11, waiting for transfers between devices: 43.2 us -> 40.8 us  [permute(): return lax.ppermute(value, 'cp', pairs)]
    ppermute x10 -> x11, starting transfers between devices: 28.8 us -> 29.1 us  [permute(): return lax.ppermute(value, 'cp', pairs)]
  transfers between devices with their start and end apart: 10 -> 11, of which waited for: 3 -> 3; matrix products, arithmetic and copies ran while one was open for 4% -> 4% of each run, Pallas kernels for 69% -> 69%
where the time goes in v7:
time: 293 us
  Pallas kernels  209 us (71%)
  waiting for transfers between devices  40.8 us (14%)
  starting transfers between devices  29.1 us (10%)
  other arithmetic  8.12 us (3%)
  local copies, waits for them, and re-layouts  5.11 us (2%)
    pallas_call x1, Pallas kernels, backward(): pl.pallas_call(backward_kernel, grid=(3 * tiles,), in_specs=[held(q), hel...  78.9 us
    pallas_call x1, Pallas kernels, forward(): pl.pallas_call(forward_kernel, grid=(done + tiles,), in_specs=[pl.BlockSp...  67.6 us
    ppermute x11, waiting for transfers between devices, permute(): return lax.ppermute(value, 'cp', pairs)  40.8 us
    ppermute x11, starting transfers between devices, permute(): return lax.ppermute(value, 'cp', pairs)  29.1 us
    pallas_call x1, Pallas kernels, grad_wo(): pl.pallas_call(grad_wo_kernel, grid=(tokens // bt,), in_specs=[pl.BlockSp...  17.1 us
    pallas_call x1, Pallas kernels, post(): pl.pallas_call(post_kernel, grid=(tokens // bq,), in_specs=[rows2(heads *...  14.1 us
    pallas_call x1, Pallas kernels, tail(): pl.pallas_call(tail_kernel, grid=(tokens // bt,), in_specs=[pl.BlockSpec(...  12.7 us
    pallas_call x1, Pallas kernels, join_wide(): pl.pallas_call(join_wide_kernel, grid=(dim // bd,), in_specs=[pl.BlockSpe...  7.67 us
  transfers between devices with their start and end apart: 11, of which 3 were waited for; matrix products, arithmetic and copies ran while one was open for 4% of the time, Pallas kernels for 69%

profile of v7, /device:TPU:0, one launch (start us, length us, event | category | flops | bytes accessed | tf_op | source)
XLA Modules:
  0.0 292.7 jit_solution(7987143268500459559)
XLA Ops:
  0.6 1.3 collective-permute-start.7
  1.9 8.0 %collective-permute-start.8 = (bf16[1024,1152]{1,0:T(8,128)(2,1)}, bf16[1024,1152]{1,0:T(8,128)(2,1)}, u32[]{:S(2)}, u32[]{:S(2)}) collective-permute-start(bf16[1024,1152]{1,0:T(8,128)(2,1)} %bitcast.27), channel_id=1, source_target_pairs={{0,2},{1,3},{4,6},{5,7},{8,10},{9,11},{12,14},{13,15}} | collective-permute-start | bytes 7077896 | tf_op jit(solution)/shard_map/ppermute | solution.py:744
  9.9 3.6 %copy.20 = bf16[144,8,4,256]{3,1,2,0:T(8,128)(2,1)} copy(bf16[144,8,4,256]{3,2,1,0:T(4,128)(2,1)} %bitcast.19) | data formatting | bytes 4718592
  13.6 3.0 %multiply_sine_fusion = (f32[1024,128]{1,0:T(8,128)}, f32[1024,128]{1,0:T(8,128)}) fusion(f32[128]{0:T(128)S(1)} %multiply_power_fusion, f32[1024]{0:T(1024)S(1)} %bitcast.22), kind=kLoop, calls=%fused_computation | loop fusion | flops 131072 | bytes 1053184 | tf_op jit(solution)/shard_map/sin | solution.py:761
  16.6 67.6 %forward.1 = (bf16[1152,1024]{1,0:T(8,128)(2,1)}, bf16[4,1024,256]{2,1,0:T(8,128)(2,1)}, bf16[2,1024,256]{2,1,0:T(8,128)(2,1)}, bf16[2,1024,256]{2,1,0:T(8,128)(...) custom-call(bf16[1024,1152]{1,0:T(8,128)(2,1)} %bitcast.23, ...), custom_call_target="tpu_custom_call" | custom-call | flops 10000000000 | bytes 10000000 | tf_op jit(solution)/shard_map/forward/pallas_call | solution.py:226
  84.2 16.8 %collective-permute-start.6 = (bf16[1024,1024]{1,0:T(8,128)(2,1)}, bf16[1024,1024]{1,0:T(8,128)(2,1)}, u32[]{:S(2)}, u32[]{:S(2)}) collective-permute-start(bf16[1024,1024]{1,0:T(8,128)(2,1)} %get-tuple-element.34.o_ref), channel_id=1, source_target_pairs={{0,2},{2,0},{1,3},{3,1},{4,6},{6,4},{5,7},{7,5},{8,10},{10,8},{9,1... | collective-permute-start | bytes 6291464 | tf_op jit(solution)/shard_map/ppermute | solution.py:744
  101.0 14.1 %post.1 = (bf16[1024,1152]{1,0:T(8,128)(2,1)}, bf16[4,1024,256]{2,1,0:T(8,128)(2,1)}, bf16[1024,1152]{1,0:T(8,128)(2,1)}, f32[8,1024]{1,0:T(8,128)}, f32[1,1152]{1,0:T(1,128)}) custom-call(bf16[1024,1024]{1,0:T(8,128)(2,1)} %get-tuple-element.34.o_ref, f32[4,1024,256]{2,1,0:T(8,128)} %get-tuple-element.35.out_ref, f32[1024,128]{1,0:T(8,128)} %get-tuple-element.36.lse_ref, ...), custom_call_target="tpu_custom_call" | custom-call | flops 10000000000 | bytes 10000000 | tf_op jit(solution)/shard_map/post/pallas_call | solution.py:314
  115.2 78.9 %backward.1 = (f32[2,1024,256]{2,1,0:T(8,128)}, bf16[1024,1024]{1,0:T(8,128)(2,1)}, f32[1152,512]{1,0:T(8,128)}) custom-call(bf16[4,1024,256]{2,1,0:T(8,128)(2,1)} %get-tuple-element.38.q_ref, bf16[4,1024,256]{2,1,0:T(8,128)(2,1)} %get-tuple-element.39.do_ref, f32[8,1024]{1,0:T(8,128)} %get-tuple-element.40.stat_ref, ...), custom_call_target="tpu_custom_call" | custom-call | flops 10000000000 | bytes 10000000 | tf_op jit(solution)/shard_map/backward/pallas_call | solution.py:541
  194.0 0.0 collective-permute-start
  194.1 12.7 %tail.1 = (bf16[1024,1152]{1,0:T(8,128)(2,1)}, f32[1160,256]{1,0:T(8,128)}, f32[1160,256]{1,0:T(8,128)}) custom-call(s32[1]{0:T(128)} %bitcast.7.idx_ref, f32[2,1024,256]{2,1,0:T(8,128)} %get-tuple-element.46.down_ref, f32[1024,128]{1,0:T(8,128)} %get-tuple-element.69.cos_ref, f32[1024,128]{1,0:T(8,128)} %get-tuple-element.68.sin_ref, ...), custom_call_target="tpu_custom_call" | custom-call | flops 10000000000 | bytes 10000000 | tf_op jit(solution)/shard_map/tail/pallas_call | solution.py:619
  206.8 0.0 collective-permute-start.2
  206.8 0.0 collective-permute-done.7.pdy_low_ref
  206.9 0.0 collective-permute-done.8.pdy_high_ref
  206.9 17.1 %grad_wo.1 = (f32[512,1152]{1,0:T(8,128)}, f32[512,1152]{1,0:T(8,128)}) custom-call(s32[1]{0:T(128)} %bitcast.7.idx_ref, bf16[1024,1024]{1,0:T(8,128)(2,1)} %get-tuple-element.34.o_ref, bf16[1024,1152]{1,0:T(8,128)(2,1)} %get-tuple-element.55.dz_ref, bf16[1024,1024]{1,0:T(8,128)(2,1)} %collective-permute-done.6.po_ref, ...), custom_call_target="tpu_custom_call" | custom-call | flops 10000000000 | bytes 10000000 | tf_op jit(solution)/shard_map/grad_wo/pallas_call | solution.py:356
  224.0 0.5 collective-permute-start.9
  224.5 1.7 add.13.a_ref.ga_ref
  226.2 0.0 copy-start.5
  226.2 2.0 collective-permute-start.3
  228.2 20.2 %collective-permute-done = f32[1152,512]{1,0:T(8,128)S(1)} collective-permute-done((f32[1152,512]{1,0:T(8,128)}, f32[1152,512]{1,0:T(8,128)S(1)}, u32[]{:S(2)}, u32[]{:S(2)}) %collective-permute-start) | collective-permute-done | bytes 2359328 | tf_op jit(solution)/shard_map/ppermute | solution.py:744
  248.4 2.0 add.12.mine_ref
  250.4 0.0 collective-permute-start.1
  250.4 0.5 collective-permute-start.4
  250.9 20.5 %collective-permute-done.3.b_ref.gb_ref = f32[1160,256]{1,0:T(8,128)S(1)} collective-permute-done((f32[1160,256]{1,0:T(8,128)S(1)}, f32[1160,256]{1,0:T(8,128)S(1)}, u32[]{:S(2)}, u32[]{:S(2)}) %collective-permute-start.3) | collective-permute-done | bytes 1187872 | tf_op jit(solution)/shard_map/ppermute | solution.py:744
  271.3 0.0 collective-permute-start.5
  271.4 0.2 add.15.mine_ref
  271.6 0.8 copy-done.7
  272.4 0.6 copy-done.3
  273.1 1.2 add.14.c_ref.gc_ref
  274.3 0.1 collective-permute-done.5.d_ref.gd_ref
  274.3 4.5 %join_pair.1 = (f32[2304,128]{1,0:T(8,128)}, f32[2304,128]{1,0:T(8,128)}, f32[1152]{0:T(1024)}, f32[1152]{0:T(1024)}) custom-call(s32[1]{0:T(128)} %bitcast.7.idx_ref, f32[1160,256]{1,0:T(8,128)} %copy-done.5, f32[1160,256]{1,0:T(8,128)} %copy-done.7, f32[1160,256]{1,0:T(8,128)} %add.14.c_ref.gc_ref, f32[1160,256]{1,0:T(8,128)} %collective-permute-done.5.d_ref.gd_ref, ...), custom_call_target="tpu_custom_call" | custom-call | flops 10000000000 | bytes 10000000 | tf_op jit(solution)/shard_map/join_pair/pallas_call | solution.py:703
  278.9 7.7 %join_wide.1 = f32[9216,128]{1,0:T(8,128)} custom-call(s32[1]{0:T(128)} %bitcast.7.idx_ref, f32[1152,512]{1,0:T(8,128)} %add.12.mine_ref, f32[1152,512]{1,0:T(8,128)} %collective-permute-done.1.other_ref), custom_call_target="tpu_custom_call" | custom-call | flops 10000000000 | bytes 10000000 | tf_op jit(solution)/shard_map/join_wide/pallas_call | solution.py:667
  286.5 6.2 %join_rows.1 = f32[1024,1152]{1,0:T(8,128)} custom-call(s32[1]{0:T(128)} %bitcast.7.idx_ref, f32[512,1152]{1,0:T(8,128)} %copy-done.2, f32[512,1152]{1,0:T(8,128)} %collective-permute-done.10.other_ref), custom_call_target="tpu_custom_call" | custom-call | flops 10000000000 | bytes 10000000 | tf_op jit(solution)/shard_map/join_rows/pallas_call | solution.py:727
  (22 shorter events, 0.1 us)
Async XLA Ops:
  0.6 206.2 %collective-permute-start.7 = (bf16[1024,1152]{1,0:T(8,128)(2,1)}, bf16[1024,1152]{1,0:T(8,128)(2,1)}, u32[]{:S(2)}, u32[]{:S(2)}) collective-permute-start(bf16[1024,1152]{1,0:T(8,128)(2,1)} %bitcast.26), channel_id=1, source_target_pairs={{2,0},{3,1},{6,4},{7,5},{10,8},{11,9},{14,12},{15,13}} | collective-permute-start | bytes 7077896 | tf_op jit(solution)/shard_map/ppermute | solution.py:744
  1.9 204.9 %collective-permute-start.8 = (bf16[1024,1152]{1,0:T(8,128)(2,1)}, bf16[1024,1152]{1,0:T(8,128)(2,1)}, u32[]{:S(2)}, u32[]{:S(2)}) collective-permute-start(bf16[1024,1152]{1,0:T(8,128)(2,1)} %bitcast.27), channel_id=1, source_target_pairs={{0,2},{1,3},{4,6},{5,7},{8,10},{9,11},{12,14},{13,15}} | collective-permute-start | bytes 7077896 | tf_op jit(solution)/shard_map/ppermute | solution.py:744
  9.9 3.7 %copy-start.6 = (s32[1,1024]{1,0:T(1,128)S(1)}, s32[1,1024]{1,0:T(1,128)}, u32[]{:S(2)}) copy-start(s32[1,1024]{1,0:T(1,128)} %param.10) | copy-start | bytes 12292
  84.2 122.6 %collective-permute-start.6 = (bf16[1024,1024]{1,0:T(8,128)(2,1)}, bf16[1024,1024]{1,0:T(8,128)(2,1)}, u32[]{:S(2)}, u32[]{:S(2)}) collective-permute-start(bf16[1024,1024]{1,0:T(8,128)(2,1)} %get-tuple-element.34.o_ref), channel_id=1, source_target_pairs={{0,2},{2,0},{1,3},{3,1},{4,6},{6,4},{5,7},{7,5},{8,10},{10,8},{9,1... | collective-permute-start | bytes 6291464 | tf_op jit(solution)/shard_map/ppermute | solution.py:744
  194.0 54.4 %collective-permute-start = (f32[1152,512]{1,0:T(8,128)}, f32[1152,512]{1,0:T(8,128)S(1)}, u32[]{:S(2)}, u32[]{:S(2)}) collective-permute-start(f32[1152,512]{1,0:T(8,128)} %get-tuple-element.50), channel_id=1, source_target_pairs={{0,2},{2,0},{1,3},{3,1},{4,6},{6,4},{5,7},{7,5},{8,10},{10,8},{9,1... | collective-permute-start | bytes 7077896 | tf_op jit(solution)/shard_map/ppermute | solution.py:744
  206.8 17.7 %collective-permute-start.2 = (f32[1160,256]{1,0:T(8,128)}, f32[1160,256]{1,0:T(8,128)}, u32[]{:S(2)}, u32[]{:S(2)}) collective-permute-start(f32[1160,256]{1,0:T(8,128)} %get-tuple-element.52), channel_id=1, source_target_pairs={{0,1},{1,0},{2,3},{3,2},{4,5},{5,4},{6,7},{7,6},{8,9},{9,8},{10,11... | collective-permute-start | bytes 3563528 | tf_op jit(solution)/shard_map/ppermute | solution.py:744
  206.9 17.6 %copy-start.4 = (f32[1160,256]{1,0:T(8,128)S(1)}, f32[1160,256]{1,0:T(8,128)}, u32[]{:S(2)}) copy-start(f32[1160,256]{1,0:T(8,128)} %get-tuple-element.51) | copy-start | bytes 3563524
  224.0 24.4 %copy-start = (f32[1152,512]{1,0:T(8,128)S(1)}, f32[1152,512]{1,0:T(8,128)}, u32[]{:S(2)}) copy-start(f32[1152,512]{1,0:T(8,128)} %get-tuple-element.50) | copy-start | bytes 7077892
  224.0 47.3 %collective-permute-start.9 = (f32[512,1152]{1,0:T(8,128)}, f32[512,1152]{1,0:T(8,128)S(1)}, u32[]{:S(2)}, u32[]{:S(2)}) collective-permute-start(f32[512,1152]{1,0:T(8,128)} %get-tuple-element.57), channel_id=1, source_target_pairs={{0,1},{1,0},{2,3},{3,2},{4,5},{5,4},{6,7},{7,6},{8,9},{9,8},{10,11... | collective-permute-start | bytes 7077896 | tf_op jit(solution)/shard_map/ppermute | solution.py:744
  226.2 24.2 %copy-start.5 = (f32[1160,256]{1,0:T(8,128)}, f32[1160,256]{1,0:T(8,128)S(1)}, u32[]{:S(2)}) copy-start(f32[1160,256]{1,0:T(8,128)S(1)} %add.13.a_ref.ga_ref) | copy-start | bytes 3563524
  226.2 45.2 %copy-start.1 = (f32[512,1152]{1,0:T(8,128)S(1)}, f32[512,1152]{1,0:T(8,128)}, u32[]{:S(2)}) copy-start(f32[512,1152]{1,0:T(8,128)} %get-tuple-element.56) | copy-start | bytes 7077892
  226.2 45.2 %collective-permute-start.3 = (f32[1160,256]{1,0:T(8,128)S(1)}, f32[1160,256]{1,0:T(8,128)S(1)}, u32[]{:S(2)}, u32[]{:S(2)}) collective-permute-start(f32[1160,256]{1,0:T(8,128)S(1)} %add.13.a_ref.ga_ref), channel_id=1, source_target_pairs={{0,2},{2,0},{1,3},{3,1},{4,6},{6,4},{5,7},{7,5},{8,10},{10,8},{9,1... | collective-permute-start | bytes 3563528 | tf_op jit(solution)/shard_map/ppermute | solution.py:744
  250.4 28.5 %collective-permute-start.1 = (f32[1152,512]{1,0:T(8,128)}, f32[1152,512]{1,0:T(8,128)}, u32[]{:S(2)}, u32[]{:S(2)}) collective-permute-start(f32[1152,512]{1,0:T(8,128)} %add.12.mine_ref), channel_id=1, source_target_pairs={{0,1},{1,0},{2,3},{3,2},{4,5},{5,4},{6,7},{7,6},{8,9},{9,8},{10,11... | collective-permute-start | bytes 7077896 | tf_op jit(solution)/shard_map/ppermute | solution.py:744
  250.4 22.1 %collective-permute-start.4 = (f32[1160,256]{1,0:T(8,128)S(1)}, f32[1160,256]{1,0:T(8,128)S(1)}, u32[]{:S(2)}, u32[]{:S(2)}) collective-permute-start(f32[1160,256]{1,0:T(8,128)S(1)} %copy-done.4), channel_id=1, source_target_pairs={{0,1},{1,0},{2,3},{3,2},{4,5},{5,4},{6,7},{7,6},{8,9},{9,8},{10,11... | collective-permute-start | bytes 3563528 | tf_op jit(solution)/shard_map/ppermute | solution.py:744
  271.3 1.1 copy-start.7
  271.3 3.0 %collective-permute-start.5 = (f32[1160,256]{1,0:T(8,128)S(1)}, f32[1160,256]{1,0:T(8,128)}, u32[]{:S(2)}, u32[]{:S(2)}) collective-permute-start(f32[1160,256]{1,0:T(8,128)S(1)} %collective-permute-done.3.b_ref.gb_ref), channel_id=1, source_target_pairs={{0,1},{1,0},{2,3},{3,2},{4,5},{5,4},{6,7},{7,6},{8,9},{9,8},{10,11... | collective-permute-start | bytes 3563528 | tf_op jit(solution)/shard_map/ppermute | solution.py:744
  271.4 1.7 copy-start.3
  272.4 6.4 %copy-start.2 = (f32[512,1152]{1,0:T(8,128)}, f32[512,1152]{1,0:T(8,128)S(1)}, u32[]{:S(2)}) copy-start(f32[512,1152]{1,0:T(8,128)S(1)} %add.15.mine_ref) | copy-start | bytes 7077892
  272.4 14.1 %collective-permute-start.10 = (f32[512,1152]{1,0:T(8,128)S(1)}, f32[512,1152]{1,0:T(8,128)}, u32[]{:S(2)}, u32[]{:S(2)}) collective-permute-start(f32[512,1152]{1,0:T(8,128)S(1)} %add.15.mine_ref), channel_id=1, source_target_pairs={{0,1},{1,0},{2,3},{3,2},{4,5},{5,4},{6,7},{7,6},{8,9},{9,8},{10,11... | collective-permute-start | bytes 7077896 | tf_op jit(solution)/shard_map/ppermute | solution.py:744

commit v8 on v6

--- a/solution.py
+++ b/solution.py
@@ -1,3 +1,4 @@
+import functools
 import math
 
 import jax
@@ -677,30 +678,43 @@
     return out.reshape(dim, 2, heads, 128).transpose(0, 2, 1, 3).reshape(dim, heads, 256)
 
 
-def join_pair_kernel(idx_ref, mine_ref, other_ref, first_ref, second_ref, dpre_ref, dpost_ref):
+def join_pair_kernel(idx_ref, a_ref, b_ref, c_ref, d_ref, *refs, last):
     core0 = idx_ref[0] % 2 == 0
-    dim = dpre_ref.shape[0]
-    mine, other = mine_ref[...], other_ref[...]
-    first, second = jnp.where(core0, mine, other), jnp.where(core0, other, mine)
-    for src, out_ref, gain_ref in ((first, first_ref, dpre_ref), (second, second_ref, dpost_ref)):
+
+    def ordered(mine, other):
+        return jnp.where(core0, mine, other), jnp.where(core0, other, mine)
+
+    rows = a_ref.shape[0] - (8 if last else 0)
+    outs = refs[2:] if last else refs
+    for n, src in enumerate(ordered(a_ref[...] + b_ref[...], c_ref[...] + d_ref[...])):
         for c in range(2):
-            out_ref[pl.ds(c, dim, stride=2), :] = src[0:dim, c * 128:(c + 1) * 128]
-        for c in range(dim // 128):
-            gain_ref[c * 128:(c + 1) * 128] = src[dim + c // 2, c % 2 * 128:(c % 2 + 1) * 128]
-
-
-def join_pair(idx, mine, other):
-    dim, width = mine.shape[0] - 8, mine.shape[1]
-    outs = pl.pallas_call(
-        join_pair_kernel,
-        in_specs=[pl.BlockSpec(memory_space=pltpu.SMEM), whole(mine.shape), whole(mine.shape)],
-        out_specs=[whole((dim * 2, 128))] * 2 + [whole((dim,))] * 2,
-        out_shape=[jax.ShapeDtypeStruct((dim * 2, 128), F32)] * 2 + [jax.ShapeDtypeStruct((dim,), F32)] * 2,
+            outs[n][pl.ds(c, rows, stride=2), :] = src[0:rows, c * 128:(c + 1) * 128]
+        if last:
+            gain_ref = outs[n + 2]
+            for c in range(gain_ref.shape[0] // 128):
+                gain_ref[c * 128:(c + 1) * 128] = src[rows + c // 2, c % 2 * 128:(c % 2 + 1) * 128]
+
+
+def join_pair(idx, parts, dim, begun=()):
+    rows, width = parts[0].shape
+    last = bool(begun)
+    bd = rows - 8 if last else dim // 3
+    steps = rows // bd
+    first = dim // bd - 1 if last else 0
+    out_spec = pl.BlockSpec((bd * 2, 128), lambda i: (i + first, 0))
+    part_spec = whole(parts[0].shape) if last else rows_spec(bd, width)
+    pair = [jax.ShapeDtypeStruct((dim * 2, 128), F32)] * 2
+    return pl.pallas_call(
+        functools.partial(join_pair_kernel, last=last),
+        grid=(steps,),
+        in_specs=[pl.BlockSpec(memory_space=pltpu.SMEM)] + [part_spec] * 4 + [pl.BlockSpec(memory_space=pl.ANY)] * len(begun),
+        out_specs=[out_spec] * 2 + [whole((dim,))] * len(begun),
+        out_shape=pair + [jax.ShapeDtypeStruct((dim,), F32)] * len(begun),
+        input_output_aliases={5: 0, 6: 1} if last else {},
         compiler_params=params(),
         cost_estimate=COST,
-        name="join_pair",
-    )(idx, mine, other)
-    return [o.reshape(dim, 1, width) for o in outs[:2]] + list(outs[2:])
+        name="join_last" if last else "join_first",
+    )(idx, *parts, *begun)
 
 
 def join_rows_kernel(idx_ref, mine_ref, other_ref, out_ref):
@@ -731,12 +745,6 @@
 
     def permute(value, pairs):
         return lax.ppermute(value, "cp", pairs)
-
-    def sum_halves(parts):
-        theirs = permute(parts[1], beside)
-        mine = parts[0] + theirs
-        mine = mine + permute(mine, across)
-        return mine, permute(mine, beside)
 
     def local_step(x_in, positions, dy_out, w_query, w_key, w_value, w_out, w_pre, w_post):
         batch, tokens, dim = x_in.shape
@@ -768,17 +776,25 @@
         dwo_mine = dwo[0] + permute(dwo[1], beside)
         dwo_other = permute(dwo_mine, beside)
         dx, *dwkv = tail(idx, down, cosine, sine, act_t, dq, wq, wk, wv, x, dy, gain_pre, dgain_post)
-        dwkv_mine, dwkv_other = sum_halves(dwkv)
+        theirs_in, mine_in = permute(dwkv[1], beside), permute(dwkv[0], beside)
+        split = dim // 3 * 2
+        pieces = []
+        for rows in (slice(0, split), slice(split, None)):
+            chip_mine = dwkv[0][rows] + theirs_in[rows]
+            chip_other = dwkv[1][rows] + mine_in[rows]
+            far_mine = permute(chip_mine, across)
+            pieces.append((chip_mine, far_mine, chip_other, permute(far_mine, beside)))
+        begun = join_pair(idx, pieces[0], dim)
+        dwk_full, dwv_full, dpre_full, dpost_full = join_pair(idx, pieces[1], dim, tuple(begun))
 
         dwo_full = join_rows(idx, dwo_mine, dwo_other)
         dwq_full = join_wide(idx, dwq_mine, dwq_other, heads)
-        dwk_full, dwv_full, dpre_full, dpost_full = join_pair(idx, dwkv_mine, dwkv_other)
         return (
             y.reshape(batch, tokens, dim),
             dx.reshape(batch, tokens, dim),
             dwq_full,
-            dwk_full,
-            dwv_full,
+            dwk_full.reshape(dim, 1, hd),
+            dwv_full.reshape(dim, 1, hd),
             dwo_full.reshape(heads, hd, dim),
             dpre_full,
             dpost_full,

time: 293 us -> 297 us (1.014)
    ppermute x10 -> x13, waiting for transfers between devices: 43.2 us -> 42.1 us  [permute(): return lax.ppermute(value, 'cp', pairs)]
    ppermute x10 -> x13, starting transfers between devices: 28.8 us -> 29.6 us  [permute(): return lax.ppermute(value, 'cp', pairs)]
  transfers between devices with their start and end apart: 10 -> 13, of which waited for: 3 -> 2; matrix products, arithmetic and copies ran while one was open for 4% -> 5% of each run, Pallas kernels for 69% -> 69%
where the time goes in v8:
time: 297 us
  Pallas kernels  210 us (71%)
  waiting for transfers between devices  42.1 us (14%)
  starting transfers between devices  29.6 us (10%)
  other arithmetic  9.91 us (3%)
  local copies, waits for them, and re-layouts  4.43 us (1%)
    pallas_call x1, Pallas kernels, backward(): pl.pallas_call(backward_kernel, grid=(3 * tiles,), in_specs=[held(q), hel...  78.9 us
    pallas_call x1, Pallas kernels, forward(): pl.pallas_call(forward_kernel, grid=(done + tiles,), in_specs=[pl.BlockSp...  67.6 us
    ppermute x13, waiting for transfers between devices, permute(): return lax.ppermute(value, 'cp', pairs)  42.1 us
    ppermute x13, starting transfers between devices, permute(): return lax.ppermute(value, 'cp', pairs)  29.6 us
    pallas_call x1, Pallas kernels, grad_wo(): pl.pallas_call(grad_wo_kernel, grid=(tokens // bt,), in_specs=[pl.BlockSp...  17.2 us
    pallas_call x1, Pallas kernels, post(): pl.pallas_call(post_kernel, grid=(tokens // bq,), in_specs=[rows2(heads *...  14.1 us
    pallas_call x1, Pallas kernels, tail(): pl.pallas_call(tail_kernel, grid=(tokens // bt,), in_specs=[pl.BlockSpec(...  12.7 us
    pallas_call x1, Pallas kernels, join_wide(): pl.pallas_call(join_wide_kernel, grid=(dim // bd,), in_specs=[pl.BlockSpe...  7.66 us
  transfers between devices with their start and end apart: 13, of which 2 were waited for; matrix products, arithmetic and copies ran while one was open for 5% of the time, Pallas kernels for 69%

profile of v8, /device:TPU:0, one launch (start us, length us, event | category | flops | bytes accessed | tf_op | source)
XLA Modules:
  0.0 296.6 jit_solution(10811037254046597685)
XLA Ops:
  0.6 1.3 collective-permute-start.9
  1.9 8.0 %collective-permute-start.10 = (bf16[1024,1152]{1,0:T(8,128)(2,1)}, bf16[1024,1152]{1,0:T(8,128)(2,1)}, u32[]{:S(2)}, u32[]{:S(2)}) collective-permute-start(bf16[1024,1152]{1,0:T(8,128)(2,1)} %bitcast.27), channel_id=1, source_target_pairs={{0,2},{1,3},{4,6},{5,7},{8,10},{9,11},{12,14},{13,15}} | collective-permute-start | bytes 7077896 | tf_op jit(solution)/shard_map/ppermute | solution.py:747
  9.9 3.6 %copy.22 = bf16[144,8,4,256]{3,1,2,0:T(8,128)(2,1)} copy(bf16[144,8,4,256]{3,2,1,0:T(4,128)(2,1)} %bitcast.19) | data formatting | bytes 4718592
  13.6 3.0 %multiply_sine_fusion = (f32[1024,128]{1,0:T(8,128)}, f32[1024,128]{1,0:T(8,128)}) fusion(f32[128]{0:T(128)S(1)} %multiply_power_fusion, f32[1024]{0:T(1024)S(1)} %bitcast.22), kind=kLoop, calls=%fused_computation.2 | loop fusion | flops 131072 | bytes 1053184 | tf_op jit(solution)/shard_map/sin | solution.py:764
  16.6 67.6 %forward.1 = (bf16[1152,1024]{1,0:T(8,128)(2,1)}, bf16[4,1024,256]{2,1,0:T(8,128)(2,1)}, bf16[2,1024,256]{2,1,0:T(8,128)(2,1)}, bf16[2,1024,256]{2,1,0:T(8,128)(...) custom-call(bf16[1024,1152]{1,0:T(8,128)(2,1)} %bitcast.23, ...), custom_call_target="tpu_custom_call" | custom-call | flops 10000000000 | bytes 10000000 | tf_op jit(solution)/shard_map/forward/pallas_call | solution.py:227
  84.2 16.8 %collective-permute-start.8 = (bf16[1024,1024]{1,0:T(8,128)(2,1)}, bf16[1024,1024]{1,0:T(8,128)(2,1)}, u32[]{:S(2)}, u32[]{:S(2)}) collective-permute-start(bf16[1024,1024]{1,0:T(8,128)(2,1)} %get-tuple-element.36.o_ref), channel_id=1, source_target_pairs={{0,2},{2,0},{1,3},{3,1},{4,6},{6,4},{5,7},{7,5},{8,10},{10,8},{9,1... | collective-permute-start | bytes 6291464 | tf_op jit(solution)/shard_map/ppermute | solution.py:747
  101.0 14.1 %post.1 = (bf16[1024,1152]{1,0:T(8,128)(2,1)}, bf16[4,1024,256]{2,1,0:T(8,128)(2,1)}, bf16[1024,1152]{1,0:T(8,128)(2,1)}, f32[8,1024]{1,0:T(8,128)}, f32[1,1152]{1,0:T(1,128)}) custom-call(bf16[1024,1024]{1,0:T(8,128)(2,1)} %get-tuple-element.36.o_ref, f32[4,1024,256]{2,1,0:T(8,128)} %get-tuple-element.37.out_ref, f32[1024,128]{1,0:T(8,128)} %get-tuple-element.38.lse_ref, ...), custom_call_target="tpu_custom_call" | custom-call | flops 10000000000 | bytes 10000000 | tf_op jit(solution)/shard_map/post/pallas_call | solution.py:315
  115.2 78.9 %backward.1 = (f32[2,1024,256]{2,1,0:T(8,128)}, bf16[1024,1024]{1,0:T(8,128)(2,1)}, f32[1152,512]{1,0:T(8,128)}) custom-call(bf16[4,1024,256]{2,1,0:T(8,128)(2,1)} %get-tuple-element.40.q_ref, bf16[4,1024,256]{2,1,0:T(8,128)(2,1)} %get-tuple-element.41.do_ref, f32[8,1024]{1,0:T(8,128)} %get-tuple-element.42.stat_ref, ...), custom_call_target="tpu_custom_call" | custom-call | flops 10000000000 | bytes 10000000 | tf_op jit(solution)/shard_map/backward/pallas_call | solution.py:542
  194.0 0.0 collective-permute-start
  194.1 12.7 %tail.1 = (bf16[1024,1152]{1,0:T(8,128)(2,1)}, f32[1160,256]{1,0:T(8,128)}, f32[1160,256]{1,0:T(8,128)}) custom-call(s32[1]{0:T(128)} %bitcast.7.idx_ref, f32[2,1024,256]{2,1,0:T(8,128)} %get-tuple-element.48.down_ref, f32[1024,128]{1,0:T(8,128)} %get-tuple-element.73.cos_ref, f32[1024,128]{1,0:T(8,128)} %get-tuple-element.72.sin_ref, ...), custom_call_target="tpu_custom_call" | custom-call | flops 10000000000 | bytes 10000000 | tf_op jit(solution)/shard_map/tail/pallas_call | solution.py:620
  206.8 0.0 collective-permute-start.2
  206.9 17.2 %grad_wo.1 = (f32[512,1152]{1,0:T(8,128)}, f32[512,1152]{1,0:T(8,128)}) custom-call(s32[1]{0:T(128)} %bitcast.7.idx_ref, bf16[1024,1024]{1,0:T(8,128)(2,1)} %get-tuple-element.36.o_ref, bf16[1024,1152]{1,0:T(8,128)(2,1)} %get-tuple-element.59.dz_ref, bf16[1024,1024]{1,0:T(8,128)(2,1)} %collective-permute-done.8.po_ref, ...), custom_call_target="tpu_custom_call" | custom-call | flops 10000000000 | bytes 10000000 | tf_op jit(solution)/shard_map/grad_wo/pallas_call | solution.py:357
  224.1 0.5 collective-permute-start.11
  224.6 0.1 collective-permute-start.4
  224.6 1.4 slice_add_fusion.1.a_ref
  226.0 0.0 copy-start.5
  226.0 2.0 collective-permute-start.6
  228.1 34.7 %collective-permute-done.6.b_ref = f32[768,256]{1,0:T(8,128)S(1)} collective-permute-done((f32[768,256]{1,0:T(8,128)S(1)}, f32[768,256]{1,0:T(8,128)S(1)}, u32[]{:S(2)}, u32[]{:S(2)}) %collective-permute-start.6) | collective-permute-done | bytes 786464 | tf_op jit(solution)/shard_map/ppermute | solution.py:747
  262.8 1.3 slice_add_fusion.3.a_ref
  264.1 0.3 collective-permute-start.3
  264.5 1.9 add.18.mine_ref
  266.4 0.8 slice_add_fusion.2.c_ref
  267.3 1.0 slice_add_fusion.c_ref
  268.3 7.4 %collective-permute-done.3.b_ref = f32[392,256]{1,0:T(8,128)} collective-permute-done((f32[392,256]{1,0:T(8,128)S(1)}, f32[392,256]{1,0:T(8,128)}, u32[]{:S(2)}, u32[]{:S(2)}) %collective-permute-start.3) | collective-permute-done | bytes 401440 | tf_op jit(solution)/shard_map/ppermute | solution.py:747
  275.7 0.3 add.23.mine_ref
  276.0 0.5 collective-permute-start.12
  276.6 3.1 %join_first.1 = (f32[2304,128]{1,0:T(8,128)}, f32[2304,128]{1,0:T(8,128)}) custom-call(s32[1]{0:T(128)} %bitcast.7.idx_ref, f32[768,256]{1,0:T(8,128)} %copy-done.5, f32[768,256]{1,0:T(8,128)} %copy-done.8, f32[768,256]{1,0:T(8,128)} %slice_add_fusion.c_ref, f32[768,256]{1,0:T(8,128)} %collective-permute-done.7.d_ref), custom_call_target="tpu_custom_call" | custom-call | flops 10000000000 | bytes 10000000 | tf_op jit(solution)/shard_map/join_first/pallas_call | solution.py:707
  279.6 0.0 copy-start.9
  279.6 0.7 copy-done.9
  280.4 2.3 join_last.1
  282.7 7.7 %join_wide.1 = f32[9216,128]{1,0:T(8,128)} custom-call(s32[1]{0:T(128)} %bitcast.7.idx_ref, f32[1152,512]{1,0:T(8,128)} %add.18.mine_ref, f32[1152,512]{1,0:T(8,128)} %collective-permute-done.1.other_ref), custom_call_target="tpu_custom_call" | custom-call | flops 10000000000 | bytes 10000000 | tf_op jit(solution)/shard_map/join_wide/pallas_call | solution.py:668
  290.4 6.2 %join_rows.1 = f32[1024,1152]{1,0:T(8,128)} custom-call(s32[1]{0:T(128)} %bitcast.7.idx_ref, f32[512,1152]{1,0:T(8,128)} %copy-done.2, f32[512,1152]{1,0:T(8,128)} %collective-permute-done.12.other_ref), custom_call_target="tpu_custom_call" | custom-call | flops 10000000000 | bytes 10000000 | tf_op jit(solution)/shard_map/join_rows/pallas_call | solution.py:730
  (33 shorter events, 0.1 us)
Async XLA Ops:
  0.6 206.3 %collective-permute-start.9 = (bf16[1024,1152]{1,0:T(8,128)(2,1)}, bf16[1024,1152]{1,0:T(8,128)(2,1)}, u32[]{:S(2)}, u32[]{:S(2)}) collective-permute-start(bf16[1024,1152]{1,0:T(8,128)(2,1)} %bitcast.26), channel_id=1, source_target_pairs={{2,0},{3,1},{6,4},{7,5},{10,8},{11,9},{14,12},{15,13}} | collective-permute-start | bytes 7077896 | tf_op jit(solution)/shard_map/ppermute | solution.py:747
  1.9 205.0 %collective-permute-start.10 = (bf16[1024,1152]{1,0:T(8,128)(2,1)}, bf16[1024,1152]{1,0:T(8,128)(2,1)}, u32[]{:S(2)}, u32[]{:S(2)}) collective-permute-start(bf16[1024,1152]{1,0:T(8,128)(2,1)} %bitcast.27), channel_id=1, source_target_pairs={{0,2},{1,3},{4,6},{5,7},{8,10},{9,11},{12,14},{13,15}} | collective-permute-start | bytes 7077896 | tf_op jit(solution)/shard_map/ppermute | solution.py:747
  9.9 3.7 %copy-start.7 = (s32[1,1024]{1,0:T(1,128)S(1)}, s32[1,1024]{1,0:T(1,128)}, u32[]{:S(2)}) copy-start(s32[1,1024]{1,0:T(1,128)} %param.10) | copy-start | bytes 12292
  84.2 122.7 %collective-permute-start.8 = (bf16[1024,1024]{1,0:T(8,128)(2,1)}, bf16[1024,1024]{1,0:T(8,128)(2,1)}, u32[]{:S(2)}, u32[]{:S(2)}) collective-permute-start(bf16[1024,1024]{1,0:T(8,128)(2,1)} %get-tuple-element.36.o_ref), channel_id=1, source_target_pairs={{0,2},{2,0},{1,3},{3,1},{4,6},{6,4},{5,7},{7,5},{8,10},{10,8},{9,1... | collective-permute-start | bytes 6291464 | tf_op jit(solution)/shard_map/ppermute | solution.py:747
  194.0 70.4 %collective-permute-start = (f32[1152,512]{1,0:T(8,128)}, f32[1152,512]{1,0:T(8,128)S(1)}, u32[]{:S(2)}, u32[]{:S(2)}) collective-permute-start(f32[1152,512]{1,0:T(8,128)} %get-tuple-element.52), channel_id=1, source_target_pairs={{0,2},{2,0},{1,3},{3,1},{4,6},{6,4},{5,7},{7,5},{8,10},{10,8},{9,1... | collective-permute-start | bytes 7077896 | tf_op jit(solution)/shard_map/ppermute | solution.py:747
  206.8 17.8 %collective-permute-start.2 = (f32[1160,256]{1,0:T(8,128)}, f32[1160,256]{1,0:T(8,128)}, u32[]{:S(2)}, u32[]{:S(2)}) collective-permute-start(f32[1160,256]{1,0:T(8,128)} %get-tuple-element.54), channel_id=1, source_target_pairs={{0,1},{1,0},{2,3},{3,2},{4,5},{5,4},{6,7},{7,6},{8,9},{9,8},{10,11... | collective-permute-start | bytes 3563528 | tf_op jit(solution)/shard_map/ppermute | solution.py:747
  206.9 17.6 %copy-start.4 = (f32[1160,256]{1,0:T(8,128)S(1)}, f32[1160,256]{1,0:T(8,128)}, u32[]{:S(2)}) copy-start(f32[1160,256]{1,0:T(8,128)} %get-tuple-element.53) | copy-start | bytes 3563524
  224.1 40.4 %copy-start = (f32[1152,512]{1,0:T(8,128)S(1)}, f32[1152,512]{1,0:T(8,128)}, u32[]{:S(2)}) copy-start(f32[1152,512]{1,0:T(8,128)} %get-tuple-element.52) | copy-start | bytes 7077892
  224.1 51.6 %collective-permute-start.11 = (f32[512,1152]{1,0:T(8,128)}, f32[512,1152]{1,0:T(8,128)S(1)}, u32[]{:S(2)}, u32[]{:S(2)}) collective-permute-start(f32[512,1152]{1,0:T(8,128)} %get-tuple-element.61), channel_id=1, source_target_pairs={{0,1},{1,0},{2,3},{3,2},{4,5},{5,4},{6,7},{7,6},{8,9},{9,8},{10,11... | collective-permute-start | bytes 7077896 | tf_op jit(solution)/shard_map/ppermute | solution.py:747
  224.6 41.9 %collective-permute-start.4 = (f32[1160,256]{1,0:T(8,128)S(1)}, f32[1160,256]{1,0:T(8,128)S(1)}, u32[]{:S(2)}, u32[]{:S(2)}) collective-permute-start(f32[1160,256]{1,0:T(8,128)S(1)} %copy-done.4), channel_id=1, source_target_pairs={{0,1},{1,0},{2,3},{3,2},{4,5},{5,4},{6,7},{7,6},{8,9},{9,8},{10,11... | collective-permute-start | bytes 3563528 | tf_op jit(solution)/shard_map/ppermute | solution.py:747
  226.0 36.7 %copy-start.5 = (f32[768,256]{1,0:T(8,128)}, f32[768,256]{1,0:T(8,128)S(1)}, u32[]{:S(2)}) copy-start(f32[768,256]{1,0:T(8,128)S(1)} %slice_add_fusion.1.a_ref) | copy-start | bytes 2359300
  226.0 36.7 %collective-permute-start.6 = (f32[768,256]{1,0:T(8,128)S(1)}, f32[768,256]{1,0:T(8,128)S(1)}, u32[]{:S(2)}, u32[]{:S(2)}) collective-permute-start(f32[768,256]{1,0:T(8,128)S(1)} %slice_add_fusion.1.a_ref), channel_id=1, source_target_pairs={{0,2},{2,0},{1,3},{3,1},{4,6},{6,4},{5,7},{7,5},{8,10},{10,8},{9,1... | collective-permute-start | bytes 2359304 | tf_op jit(solution)/shard_map/ppermute | solution.py:747
  262.8 3.6 %copy-start.8 = (f32[768,256]{1,0:T(8,128)}, f32[768,256]{1,0:T(8,128)S(1)}, u32[]{:S(2)}) copy-start(f32[768,256]{1,0:T(8,128)S(1)} %collective-permute-done.6.b_ref) | copy-start | bytes 2359300
  262.8 13.8 %collective-permute-start.7 = (f32[768,256]{1,0:T(8,128)S(1)}, f32[768,256]{1,0:T(8,128)}, u32[]{:S(2)}, u32[]{:S(2)}) collective-permute-start(f32[768,256]{1,0:T(8,128)S(1)} %collective-permute-done.6.b_ref), channel_id=1, source_target_pairs={{0,1},{1,0},{2,3},{3,2},{4,5},{5,4},{6,7},{7,6},{8,9},{9,8},{10,11... | collective-permute-start | bytes 2359304 | tf_op jit(solution)/shard_map/ppermute | solution.py:747
  264.1 2.3 copy-start.6
  264.1 2.3 copy-start.3
  264.1 11.6 %collective-permute-start.3 = (f32[392,256]{1,0:T(8,128)S(1)}, f32[392,256]{1,0:T(8,128)}, u32[]{:S(2)}, u32[]{:S(2)}) collective-permute-start(f32[392,256]{1,0:T(8,128)S(1)} %slice_add_fusion.3.a_ref), channel_id=1, source_target_pairs={{0,2},{2,0},{1,3},{3,1},{4,6},{6,4},{5,7},{7,5},{8,10},{10,8},{9,1... | collective-permute-start | bytes 1204232 | tf_op jit(solution)/shard_map/ppermute | solution.py:747
  266.4 9.3 %copy-start.1 = (f32[512,1152]{1,0:T(8,128)S(1)}, f32[512,1152]{1,0:T(8,128)}, u32[]{:S(2)}) copy-start(f32[512,1152]{1,0:T(8,128)} %get-tuple-element.60) | copy-start | bytes 7077892
  266.4 16.3 %collective-permute-start.1 = (f32[1152,512]{1,0:T(8,128)}, f32[1152,512]{1,0:T(8,128)}, u32[]{:S(2)}, u32[]{:S(2)}) collective-permute-start(f32[1152,512]{1,0:T(8,128)} %add.18.mine_ref), channel_id=1, source_target_pairs={{0,1},{1,0},{2,3},{3,2},{4,5},{5,4},{6,7},{7,6},{8,9},{9,8},{10,11... | collective-permute-start | bytes 7077896 | tf_op jit(solution)/shard_map/ppermute | solution.py:747
  275.7 4.0 %collective-permute-start.5 = (f32[392,256]{1,0:T(8,128)}, f32[392,256]{1,0:T(8,128)S(1)}, u32[]{:S(2)}, u32[]{:S(2)}) collective-permute-start(f32[392,256]{1,0:T(8,128)} %collective-permute-done.3.b_ref), channel_id=1, source_target_pairs={{0,1},{1,0},{2,3},{3,2},{4,5},{5,4},{6,7},{7,6},{8,9},{9,8},{10,11... | collective-permute-start | bytes 1204232 | tf_op jit(solution)/shard_map/ppermute | solution.py:747
  276.0 3.6 %copy-start.2 = (f32[512,1152]{1,0:T(8,128)}, f32[512,1152]{1,0:T(8,128)S(1)}, u32[]{:S(2)}) copy-start(f32[512,1152]{1,0:T(8,128)S(1)} %add.23.mine_ref) | copy-start | bytes 7077892
  276.0 14.4 %collective-permute-start.12 = (f32[512,1152]{1,0:T(8,128)S(1)}, f32[512,1152]{1,0:T(8,128)}, u32[]{:S(2)}, u32[]{:S(2)}) collective-permute-start(f32[512,1152]{1,0:T(8,128)S(1)} %add.23.mine_ref), channel_id=1, source_target_pairs={{0,1},{1,0},{2,3},{3,2},{4,5},{5,4},{6,7},{7,6},{8,9},{9,8},{10,11... | collective-permute-start | bytes 7077896 | tf_op jit(solution)/shard_map/ppermute | solution.py:747
  279.6 0.8 copy-start.9

commit v9 on v8

--- a/solution.py
+++ b/solution.py
@@ -397,8 +397,8 @@
 
 
 def backward_kernel(q_ref, do_ref, stat_ref, own_ref, near_ref, far_ref, mid_ref, cos_ref, sin_ref, at_ref,
-                    down_ref, dq_ref, dwq_ref,
-                    dqt_s, near_out, near_in, mid_out, mid_in, far_out, far_in, dwq_out, dwq_in,
+                    down_hbm, dq_hbm, dwq_hbm,
+                    down_ref, dq_ref, dwq_ref, out_sem, dqt_s, near_out, near_in, mid_out, mid_in, far_out, far_in, dwq_out, dwq_in,
                     near_send, near_recv, mid_send, mid_recv, far_send, far_recv, dwq_send, dwq_recv):
     heads, tokens, hd = q_ref.shape
     half = hd // 2
@@ -489,6 +489,9 @@
             cosine, sine = cos_ref[...], sin_ref[...]
             dq_ref[:, h * hd:h * hd + half] = ((first * cosine + second * sine) * scale).astype(BF16)
             dq_ref[:, h * hd + half:(h + 1) * hd] = ((second * cosine - first * sine) * scale).astype(BF16)
+        written = [pltpu.make_async_copy(src, dst, out_sem.at[slot]) for slot, (src, dst) in
+                   enumerate(((dq_ref, dq_hbm), (dwq_ref, dwq_hbm), (down_ref, down_hbm)))]
+        written[0].start()
         dim, width = dwq_ref.shape
         bd = dim // 3
 
@@ -520,8 +523,20 @@
         pl.when(core == 0)(lambda: gather(near_copy, near_in))
         copy.wait()
         dwq_ref[...] += dwq_in[...]
-        pl.when(rank < 2)(lambda: gather(far_copy, far_in))
-        pl.when(rank >= 2)(lambda: left(far_copy))
+        written[1].start()
+
+        @pl.when(rank < 2)
+        def _():
+            gather(far_copy, far_in)
+            written[2].start()
+
+        @pl.when(rank >= 2)
+        def _():
+            written[2].start()
+            left(far_copy)
+
+        for copy_out in written:
+            copy_out.wait()
 
 
 def backward(q, d_out, stat, own, near, far, mid, cosine, sine, at):
@@ -554,13 +569,19 @@
             held(sine),
             held(at),
         ],
-        out_specs=[whole((2, tokens, hd)), whole((tokens, heads * hd)), whole((dim, width))],
+        out_specs=[pl.BlockSpec(memory_space=pl.ANY)] * 3,
         out_shape=[
             jax.ShapeDtypeStruct((2, tokens, hd), F32),
             jax.ShapeDtypeStruct((tokens, heads * hd), BF16),
             jax.ShapeDtypeStruct((dim, width), F32),
         ],
-        scratch_shapes=[pltpu.VMEM((heads, hd, tokens), F32)] + [pltpu.VMEM((tiles, 2, bk, hd), F32)] * 6
+        scratch_shapes=[
+            pltpu.VMEM((2, tokens, hd), F32),
+            pltpu.VMEM((tokens, heads * hd), BF16),
+            pltpu.VMEM((dim, width), F32),
+            dma((3,)),
+            pltpu.VMEM((heads, hd, tokens), F32),
+        ] + [pltpu.VMEM((tiles, 2, bk, hd), F32)] * 6
         + [pltpu.VMEM((dim, width), F32)] * 2 + [dma((tiles,))] * 6 + [dma] * 2,
         compiler_params=pltpu.CompilerParams(vmem_limit_bytes=VMEM_LIMIT, collective_id=0, has_side_effects=True),
         cost_estimate=COST,
@@ -773,7 +794,8 @@
         dwq_mine = dwq_part + permute(dwq_part, across)
         dwq_other = permute(dwq_mine, beside)
         dwo = grad_wo(idx, o, dz, partner_o, dy_high, dy_low, wo, gain_post)
-        dwo_mine = dwo[0] + permute(dwo[1], beside)
+        dwo_in = permute(dwo[1], beside)
+        dwo_mine = dwo[0] + dwo_in
         dwo_other = permute(dwo_mine, beside)
         dx, *dwkv = tail(idx, down, cosine, sine, act_t, dq, wq, wk, wv, x, dy, gain_pre, dgain_post)
         theirs_in, mine_in = permute(dwkv[1], beside), permute(dwkv[0], beside)

time: 297 us -> 296 us (level)
  transfers between devices with their start and end apart: 13 -> 13, of which waited for: 2 -> 2; matrix products, arithmetic and copies ran while one was open for 5% -> 5% of each run, Pallas kernels for 69% -> 68%
where the time goes in v9:
time: 296 us; the launch traced here: 295 us
  Pallas kernels  208 us (70%)
  waiting for transfers between devices  42.1 us (14%)
  starting transfers between devices  29.6 us (10%)
  other arithmetic  9.91 us (3%)
  local copies, waits for them, and re-layouts  4.43 us (1%)
    pallas_call x1, Pallas kernels, backward(): pl.pallas_call(backward_kernel, grid=(3 * tiles,), in_specs=[held(q), hel...  77.5 us
    pallas_call x1, Pallas kernels, forward(): pl.pallas_call(forward_kernel, grid=(done + tiles,), in_specs=[pl.BlockSp...  67.6 us
    ppermute x13, waiting for transfers between devices, permute(): return lax.ppermute(value, 'cp', pairs)  42.1 us
    ppermute x13, starting transfers between devices, permute(): return lax.ppermute(value, 'cp', pairs)  29.6 us
    pallas_call x1, Pallas kernels, grad_wo(): pl.pallas_call(grad_wo_kernel, grid=(tokens // bt,), in_specs=[pl.BlockSp...  17.2 us
    pallas_call x1, Pallas kernels, post(): pl.pallas_call(post_kernel, grid=(tokens // bq,), in_specs=[rows2(heads *...  14.1 us
    pallas_call x1, Pallas kernels, tail(): pl.pallas_call(tail_kernel, grid=(tokens // bt,), in_specs=[pl.BlockSpec(...  12.7 us
    pallas_call x1, Pallas kernels, join_wide(): pl.pallas_call(join_wide_kernel, grid=(dim // bd,), in_specs=[pl.BlockSpe...  7.66 us
  transfers between devices with their start and end apart: 13, of which 2 were waited for; matrix products, arithmetic and copies ran while one was open for 5% of the time, Pallas kernels for 68%

profile of v9, /device:TPU:0, one launch (start us, length us, event | category | flops | bytes accessed | tf_op | source)
XLA Modules:
  0.0 295.2 jit_solution(11920798554033642260)
XLA Ops:
  0.6 1.3 collective-permute-start.9
  1.9 8.0 %collective-permute-start.10 = (bf16[1024,1152]{1,0:T(8,128)(2,1)}, bf16[1024,1152]{1,0:T(8,128)(2,1)}, u32[]{:S(2)}, u32[]{:S(2)}) collective-permute-start(bf16[1024,1152]{1,0:T(8,128)(2,1)} %bitcast.27), channel_id=1, source_target_pairs={{0,2},{1,3},{4,6},{5,7},{8,10},{9,11},{12,14},{13,15}} | collective-permute-start | bytes 7077896 | tf_op jit(solution)/shard_map/ppermute | solution.py:768
  9.9 3.6 %copy.22 = bf16[144,8,4,256]{3,1,2,0:T(8,128)(2,1)} copy(bf16[144,8,4,256]{3,2,1,0:T(4,128)(2,1)} %bitcast.19) | data formatting | bytes 4718592
  13.6 3.0 %multiply_sine_fusion = (f32[1024,128]{1,0:T(8,128)}, f32[1024,128]{1,0:T(8,128)}) fusion(f32[128]{0:T(128)S(1)} %multiply_power_fusion, f32[1024]{0:T(1024)S(1)} %bitcast.22), kind=kLoop, calls=%fused_computation.2 | loop fusion | flops 131072 | bytes 1053184 | tf_op jit(solution)/shard_map/sin | solution.py:785
  16.6 67.6 %forward.1 = (bf16[1152,1024]{1,0:T(8,128)(2,1)}, bf16[4,1024,256]{2,1,0:T(8,128)(2,1)}, bf16[2,1024,256]{2,1,0:T(8,128)(2,1)}, bf16[2,1024,256]{2,1,0:T(8,128)(...) custom-call(bf16[1024,1152]{1,0:T(8,128)(2,1)} %bitcast.23, ...), custom_call_target="tpu_custom_call" | custom-call | flops 10000000000 | bytes 10000000 | tf_op jit(solution)/shard_map/forward/pallas_call | solution.py:227
  84.2 16.8 %collective-permute-start.8 = (bf16[1024,1024]{1,0:T(8,128)(2,1)}, bf16[1024,1024]{1,0:T(8,128)(2,1)}, u32[]{:S(2)}, u32[]{:S(2)}) collective-permute-start(bf16[1024,1024]{1,0:T(8,128)(2,1)} %get-tuple-element.36.o_ref), channel_id=1, source_target_pairs={{0,2},{2,0},{1,3},{3,1},{4,6},{6,4},{5,7},{7,5},{8,10},{10,8},{9,1... | collective-permute-start | bytes 6291464 | tf_op jit(solution)/shard_map/ppermute | solution.py:768
  101.0 14.1 %post.1 = (bf16[1024,1152]{1,0:T(8,128)(2,1)}, bf16[4,1024,256]{2,1,0:T(8,128)(2,1)}, bf16[1024,1152]{1,0:T(8,128)(2,1)}, f32[8,1024]{1,0:T(8,128)}, f32[1,1152]{1,0:T(1,128)}) custom-call(bf16[1024,1024]{1,0:T(8,128)(2,1)} %get-tuple-element.36.o_ref, f32[4,1024,256]{2,1,0:T(8,128)} %get-tuple-element.37.out_ref, f32[1024,128]{1,0:T(8,128)} %get-tuple-element.38.lse_ref, ...), custom_call_target="tpu_custom_call" | custom-call | flops 10000000000 | bytes 10000000 | tf_op jit(solution)/shard_map/post/pallas_call | solution.py:315
  115.2 77.5 %backward.1 = (f32[2,1024,256]{2,1,0:T(8,128)}, bf16[1024,1024]{1,0:T(8,128)(2,1)}, f32[1152,512]{1,0:T(8,128)}) custom-call(bf16[4,1024,256]{2,1,0:T(8,128)(2,1)} %get-tuple-element.40.q_ref, bf16[4,1024,256]{2,1,0:T(8,128)(2,1)} %get-tuple-element.41.do_ref, f32[8,1024]{1,0:T(8,128)} %get-tuple-element.42.stat_ref, ...), custom_call_target="tpu_custom_call" | custom-call | flops 10000000000 | bytes 10000000 | tf_op jit(solution)/shard_map/backward/pallas_call | solution.py:557
  192.7 0.0 collective-permute-start
  192.7 12.7 %tail.1 = (bf16[1024,1152]{1,0:T(8,128)(2,1)}, f32[1160,256]{1,0:T(8,128)}, f32[1160,256]{1,0:T(8,128)}) custom-call(s32[1]{0:T(128)} %bitcast.7.idx_ref, f32[2,1024,256]{2,1,0:T(8,128)} %get-tuple-element.48.down_ref, f32[1024,128]{1,0:T(8,128)} %get-tuple-element.73.cos_ref, f32[1024,128]{1,0:T(8,128)} %get-tuple-element.72.sin_ref, ...), custom_call_target="tpu_custom_call" | custom-call | flops 10000000000 | bytes 10000000 | tf_op jit(solution)/shard_map/tail/pallas_call | solution.py:641
  205.4 0.0 collective-permute-start.2
  205.5 17.2 %grad_wo.1 = (f32[512,1152]{1,0:T(8,128)}, f32[512,1152]{1,0:T(8,128)}) custom-call(s32[1]{0:T(128)} %bitcast.7.idx_ref, bf16[1024,1024]{1,0:T(8,128)(2,1)} %get-tuple-element.36.o_ref, bf16[1024,1152]{1,0:T(8,128)(2,1)} %get-tuple-element.59.dz_ref, bf16[1024,1024]{1,0:T(8,128)(2,1)} %collective-permute-done.8.po_ref, ...), custom_call_target="tpu_custom_call" | custom-call | flops 10000000000 | bytes 10000000 | tf_op jit(solution)/shard_map/grad_wo/pallas_call | solution.py:357
  222.7 0.5 collective-permute-start.11
  223.2 0.1 collective-permute-start.4
  223.2 1.4 slice_add_fusion.1.a_ref
  224.6 0.0 copy-start.5
  224.6 2.0 collective-permute-start.6
  226.7 34.7 %collective-permute-done.6.b_ref = f32[768,256]{1,0:T(8,128)S(1)} collective-permute-done((f32[768,256]{1,0:T(8,128)S(1)}, f32[768,256]{1,0:T(8,128)S(1)}, u32[]{:S(2)}, u32[]{:S(2)}) %collective-permute-start.6) | collective-permute-done | bytes 786464 | tf_op jit(solution)/shard_map/ppermute | solution.py:768
  261.4 1.3 slice_add_fusion.3.a_ref
  262.7 0.3 collective-permute-start.3
  263.1 1.9 add.18.mine_ref
  265.0 0.8 slice_add_fusion.2.c_ref
  265.9 1.0 slice_add_fusion.c_ref
  266.9 7.4 %collective-permute-done.3.b_ref = f32[392,256]{1,0:T(8,128)} collective-permute-done((f32[392,256]{1,0:T(8,128)S(1)}, f32[392,256]{1,0:T(8,128)}, u32[]{:S(2)}, u32[]{:S(2)}) %collective-permute-start.3) | collective-permute-done | bytes 401440 | tf_op jit(solution)/shard_map/ppermute | solution.py:768
  274.3 0.3 add.23.mine_ref
  274.6 0.5 collective-permute-start.12
  275.2 3.1 %join_first.1 = (f32[2304,128]{1,0:T(8,128)}, f32[2304,128]{1,0:T(8,128)}) custom-call(s32[1]{0:T(128)} %bitcast.7.idx_ref, f32[768,256]{1,0:T(8,128)} %copy-done.5, f32[768,256]{1,0:T(8,128)} %copy-done.8, f32[768,256]{1,0:T(8,128)} %slice_add_fusion.c_ref, f32[768,256]{1,0:T(8,128)} %collective-permute-done.7.d_ref), custom_call_target="tpu_custom_call" | custom-call | flops 10000000000 | bytes 10000000 | tf_op jit(solution)/shard_map/join_first/pallas_call | solution.py:728
  278.2 0.0 copy-start.9
  278.3 0.7 copy-done.9
  279.0 2.3 join_last.1
  281.3 7.7 %join_wide.1 = f32[9216,128]{1,0:T(8,128)} custom-call(s32[1]{0:T(128)} %bitcast.7.idx_ref, f32[1152,512]{1,0:T(8,128)} %add.18.mine_ref, f32[1152,512]{1,0:T(8,128)} %collective-permute-done.1.other_ref), custom_call_target="tpu_custom_call" | custom-call | flops 10000000000 | bytes 10000000 | tf_op jit(solution)/shard_map/join_wide/pallas_call | solution.py:689
  289.0 6.2 %join_rows.1 = f32[1024,1152]{1,0:T(8,128)} custom-call(s32[1]{0:T(128)} %bitcast.7.idx_ref, f32[512,1152]{1,0:T(8,128)} %copy-done.2, f32[512,1152]{1,0:T(8,128)} %collective-permute-done.12.other_ref), custom_call_target="tpu_custom_call" | custom-call | flops 10000000000 | bytes 10000000 | tf_op jit(solution)/shard_map/join_rows/pallas_call | solution.py:751
  (33 shorter events, 0.1 us)
Async XLA Ops:
  0.6 204.9 %collective-permute-start.9 = (bf16[1024,1152]{1,0:T(8,128)(2,1)}, bf16[1024,1152]{1,0:T(8,128)(2,1)}, u32[]{:S(2)}, u32[]{:S(2)}) collective-permute-start(bf16[1024,1152]{1,0:T(8,128)(2,1)} %bitcast.26), channel_id=1, source_target_pairs={{2,0},{3,1},{6,4},{7,5},{10,8},{11,9},{14,12},{15,13}} | collective-permute-start | bytes 7077896 | tf_op jit(solution)/shard_map/ppermute | solution.py:768
  1.9 203.6 %collective-permute-start.10 = (bf16[1024,1152]{1,0:T(8,128)(2,1)}, bf16[1024,1152]{1,0:T(8,128)(2,1)}, u32[]{:S(2)}, u32[]{:S(2)}) collective-permute-start(bf16[1024,1152]{1,0:T(8,128)(2,1)} %bitcast.27), channel_id=1, source_target_pairs={{0,2},{1,3},{4,6},{5,7},{8,10},{9,11},{12,14},{13,15}} | collective-permute-start | bytes 7077896 | tf_op jit(solution)/shard_map/ppermute | solution.py:768
  9.9 3.7 %copy-start.7 = (s32[1,1024]{1,0:T(1,128)S(1)}, s32[1,1024]{1,0:T(1,128)}, u32[]{:S(2)}) copy-start(s32[1,1024]{1,0:T(1,128)} %param.10) | copy-start | bytes 12292
  84.2 121.3 %collective-permute-start.8 = (bf16[1024,1024]{1,0:T(8,128)(2,1)}, bf16[1024,1024]{1,0:T(8,128)(2,1)}, u32[]{:S(2)}, u32[]{:S(2)}) collective-permute-start(bf16[1024,1024]{1,0:T(8,128)(2,1)} %get-tuple-element.36.o_ref), channel_id=1, source_target_pairs={{0,2},{2,0},{1,3},{3,1},{4,6},{6,4},{5,7},{7,5},{8,10},{10,8},{9,1... | collective-permute-start | bytes 6291464 | tf_op jit(solution)/shard_map/ppermute | solution.py:768
  192.7 70.4 %collective-permute-start = (f32[1152,512]{1,0:T(8,128)}, f32[1152,512]{1,0:T(8,128)S(1)}, u32[]{:S(2)}, u32[]{:S(2)}) collective-permute-start(f32[1152,512]{1,0:T(8,128)} %get-tuple-element.52), channel_id=1, source_target_pairs={{0,2},{2,0},{1,3},{3,1},{4,6},{6,4},{5,7},{7,5},{8,10},{10,8},{9,1... | collective-permute-start | bytes 7077896 | tf_op jit(solution)/shard_map/ppermute | solution.py:768
  205.4 17.8 %collective-permute-start.2 = (f32[1160,256]{1,0:T(8,128)}, f32[1160,256]{1,0:T(8,128)}, u32[]{:S(2)}, u32[]{:S(2)}) collective-permute-start(f32[1160,256]{1,0:T(8,128)} %get-tuple-element.54), channel_id=1, source_target_pairs={{0,1},{1,0},{2,3},{3,2},{4,5},{5,4},{6,7},{7,6},{8,9},{9,8},{10,11... | collective-permute-start | bytes 3563528 | tf_op jit(solution)/shard_map/ppermute | solution.py:768
  205.5 17.6 %copy-start.4 = (f32[1160,256]{1,0:T(8,128)S(1)}, f32[1160,256]{1,0:T(8,128)}, u32[]{:S(2)}) copy-start(f32[1160,256]{1,0:T(8,128)} %get-tuple-element.53) | copy-start | bytes 3563524
  222.7 40.4 %copy-start = (f32[1152,512]{1,0:T(8,128)S(1)}, f32[1152,512]{1,0:T(8,128)}, u32[]{:S(2)}) copy-start(f32[1152,512]{1,0:T(8,128)} %get-tuple-element.52) | copy-start | bytes 7077892
  222.7 51.6 %collective-permute-start.11 = (f32[512,1152]{1,0:T(8,128)}, f32[512,1152]{1,0:T(8,128)S(1)}, u32[]{:S(2)}, u32[]{:S(2)}) collective-permute-start(f32[512,1152]{1,0:T(8,128)} %get-tuple-element.61), channel_id=1, source_target_pairs={{0,1},{1,0},{2,3},{3,2},{4,5},{5,4},{6,7},{7,6},{8,9},{9,8},{10,11... | collective-permute-start | bytes 7077896 | tf_op jit(solution)/shard_map/ppermute | solution.py:768
  223.2 41.9 %collective-permute-start.4 = (f32[1160,256]{1,0:T(8,128)S(1)}, f32[1160,256]{1,0:T(8,128)S(1)}, u32[]{:S(2)}, u32[]{:S(2)}) collective-permute-start(f32[1160,256]{1,0:T(8,128)S(1)} %copy-done.4), channel_id=1, source_target_pairs={{0,1},{1,0},{2,3},{3,2},{4,5},{5,4},{6,7},{7,6},{8,9},{9,8},{10,11... | collective-permute-start | bytes 3563528 | tf_op jit(solution)/shard_map/ppermute | solution.py:768
  224.6 36.7 %copy-start.5 = (f32[768,256]{1,0:T(8,128)}, f32[768,256]{1,0:T(8,128)S(1)}, u32[]{:S(2)}) copy-start(f32[768,256]{1,0:T(8,128)S(1)} %slice_add_fusion.1.a_ref) | copy-start | bytes 2359300
  224.6 36.7 %collective-permute-start.6 = (f32[768,256]{1,0:T(8,128)S(1)}, f32[768,256]{1,0:T(8,128)S(1)}, u32[]{:S(2)}, u32[]{:S(2)}) collective-permute-start(f32[768,256]{1,0:T(8,128)S(1)} %slice_add_fusion.1.a_ref), channel_id=1, source_target_pairs={{0,2},{2,0},{1,3},{3,1},{4,6},{6,4},{5,7},{7,5},{8,10},{10,8},{9,1... | collective-permute-start | bytes 2359304 | tf_op jit(solution)/shard_map/ppermute | solution.py:768
  261.4 3.6 %copy-start.8 = (f32[768,256]{1,0:T(8,128)}, f32[768,256]{1,0:T(8,128)S(1)}, u32[]{:S(2)}) copy-start(f32[768,256]{1,0:T(8,128)S(1)} %collective-permute-done.6.b_ref) | copy-start | bytes 2359300
  261.4 13.8 %collective-permute-start.7 = (f32[768,256]{1,0:T(8,128)S(1)}, f32[768,256]{1,0:T(8,128)}, u32[]{:S(2)}, u32[]{:S(2)}) collective-permute-start(f32[768,256]{1,0:T(8,128)S(1)} %collective-permute-done.6.b_ref), channel_id=1, source_target_pairs={{0,1},{1,0},{2,3},{3,2},{4,5},{5,4},{6,7},{7,6},{8,9},{9,8},{10,11... | collective-permute-start | bytes 2359304 | tf_op jit(solution)/shard_map/ppermute | solution.py:768
  262.7 2.3 copy-start.6
  262.7 2.3 copy-start.3
  262.7 11.6 %collective-permute-start.3 = (f32[392,256]{1,0:T(8,128)S(1)}, f32[392,256]{1,0:T(8,128)}, u32[]{:S(2)}, u32[]{:S(2)}) collective-permute-start(f32[392,256]{1,0:T(8,128)S(1)} %slice_add_fusion.3.a_ref), channel_id=1, source_target_pairs={{0,2},{2,0},{1,3},{3,1},{4,6},{6,4},{5,7},{7,5},{8,10},{10,8},{9,1... | collective-permute-start | bytes 1204232 | tf_op jit(solution)/shard_map/ppermute | solution.py:768
  265.0 9.3 %copy-start.1 = (f32[512,1152]{1,0:T(8,128)S(1)}, f32[512,1152]{1,0:T(8,128)}, u32[]{:S(2)}) copy-start(f32[512,1152]{1,0:T(8,128)} %get-tuple-element.60) | copy-start | bytes 7077892
  265.0 16.3 %collective-permute-start.1 = (f32[1152,512]{1,0:T(8,128)}, f32[1152,512]{1,0:T(8,128)}, u32[]{:S(2)}, u32[]{:S(2)}) collective-permute-start(f32[1152,512]{1,0:T(8,128)} %add.18.mine_ref), channel_id=1, source_target_pairs={{0,1},{1,0},{2,3},{3,2},{4,5},{5,4},{6,7},{7,6},{8,9},{9,8},{10,11... | collective-permute-start | bytes 7077896 | tf_op jit(solution)/shard_map/ppermute | solution.py:768
  274.3 4.0 %collective-permute-start.5 = (f32[392,256]{1,0:T(8,128)}, f32[392,256]{1,0:T(8,128)S(1)}, u32[]{:S(2)}, u32[]{:S(2)}) collective-permute-start(f32[392,256]{1,0:T(8,128)} %collective-permute-done.3.b_ref), channel_id=1, source_target_pairs={{0,1},{1,0},{2,3},{3,2},{4,5},{5,4},{6,7},{7,6},{8,9},{9,8},{10,11... | collective-permute-start | bytes 1204232 | tf_op jit(solution)/shard_map/ppermute | solution.py:768
  274.6 3.6 %copy-start.2 = (f32[512,1152]{1,0:T(8,128)}, f32[512,1152]{1,0:T(8,128)S(1)}, u32[]{:S(2)}) copy-start(f32[512,1152]{1,0:T(8,128)S(1)} %add.23.mine_ref) | copy-start | bytes 7077892
  274.6 14.4 %collective-permute-start.12 = (f32[512,1152]{1,0:T(8,128)S(1)}, f32[512,1152]{1,0:T(8,128)}, u32[]{:S(2)}, u32[]{:S(2)}) collective-permute-start(f32[512,1152]{1,0:T(8,128)S(1)} %add.23.mine_ref), channel_id=1, source_target_pairs={{0,1},{1,0},{2,3},{3,2},{4,5},{5,4},{6,7},{7,6},{8,9},{9,8},{10,11... | collective-permute-start | bytes 7077896 | tf_op jit(solution)/shard_map/ppermute | solution.py:768
  278.2 0.8 copy-start.9

commit v10 on v9

--- a/solution.py
+++ b/solution.py
@@ -16,6 +16,7 @@
 LOG2E = math.log2(math.e)
 CAP2 = SOFT_CAP * LOG2E
 INV_CAP = 1.0 / SOFT_CAP
+SHIFT2 = 20.0
 
 
 F32 = jnp.float32
@@ -70,7 +71,7 @@
         keep = lax.broadcasted_iota(jnp.int32, (bq, bk), 1) <= lax.broadcasted_iota(jnp.int32, (bq, bk), 0)
     for h in range(heads):
         s = dot(q_ref[h], k, NT)
-        p = jnp.exp2(jnp.tanh(s * INV_CAP) * CAP2)
+        p = jnp.exp2(jnp.tanh(s * INV_CAP) * CAP2 - SHIFT2)
         if masked:
             p = jnp.where(keep, p, 0.0)
         part = p[:, 0:128]
@@ -197,7 +198,7 @@
         lse = jnp.zeros((bt, 128), F32)
         for h in range(heads):
             total = jnp.sum(sum_s[h, rows, :], axis=-1, keepdims=True)
-            lse = jnp.where(lane == h, jnp.log2(total), lse)
+            lse = jnp.where(lane == h, jnp.log2(total) + SHIFT2, lse)
             out = acc_s[h, rows, :] / total
             out_ref[h] = out
             o_ref[:, h * hd:(h + 1) * hd] = out.astype(BF16)
@@ -699,14 +700,14 @@
     return out.reshape(dim, 2, heads, 128).transpose(0, 2, 1, 3).reshape(dim, heads, 256)
 
 
-def join_pair_kernel(idx_ref, a_ref, b_ref, c_ref, d_ref, *refs, last):
+def join_pair_kernel(idx_ref, a_ref, b_ref, c_ref, d_ref, *refs, last, held):
     core0 = idx_ref[0] % 2 == 0
 
     def ordered(mine, other):
         return jnp.where(core0, mine, other), jnp.where(core0, other, mine)
 
     rows = a_ref.shape[0] - (8 if last else 0)
-    outs = refs[2:] if last else refs
+    outs = refs[held:]
     for n, src in enumerate(ordered(a_ref[...] + b_ref[...], c_ref[...] + d_ref[...])):
         for c in range(2):
             outs[n][pl.ds(c, rows, stride=2), :] = src[0:rows, c * 128:(c + 1) * 128]
@@ -716,25 +717,23 @@
                 gain_ref[c * 128:(c + 1) * 128] = src[rows + c // 2, c % 2 * 128:(c % 2 + 1) * 128]
 
 
-def join_pair(idx, parts, dim, begun=()):
+def join_pair(idx, parts, dim, start, begun=()):
     rows, width = parts[0].shape
-    last = bool(begun)
-    bd = rows - 8 if last else dim // 3
-    steps = rows // bd
-    first = dim // bd - 1 if last else 0
+    last = start + rows > dim
+    bd = rows - 8 if last else 256
+    first = start // bd
     out_spec = pl.BlockSpec((bd * 2, 128), lambda i: (i + first, 0))
     part_spec = whole(parts[0].shape) if last else rows_spec(bd, width)
-    pair = [jax.ShapeDtypeStruct((dim * 2, 128), F32)] * 2
+    gains = 2 if last else 0
     return pl.pallas_call(
-        functools.partial(join_pair_kernel, last=last),
-        grid=(steps,),
+        functools.partial(join_pair_kernel, last=last, held=len(begun)),
+        grid=(rows // bd,),
         in_specs=[pl.BlockSpec(memory_space=pltpu.SMEM)] + [part_spec] * 4 + [pl.BlockSpec(memory_space=pl.ANY)] * len(begun),
-        out_specs=[out_spec] * 2 + [whole((dim,))] * len(begun),
-        out_shape=pair + [jax.ShapeDtypeStruct((dim,), F32)] * len(begun),
-        input_output_aliases={5: 0, 6: 1} if last else {},
+        out_specs=[out_spec] * 2 + [whole((dim,))] * gains,
+        out_shape=[jax.ShapeDtypeStruct((dim * 2, 128), F32)] * 2 + [jax.ShapeDtypeStruct((dim,), F32)] * gains,
+        input_output_aliases={5: 0, 6: 1} if begun else {},
         compiler_params=params(),
         cost_estimate=COST,
-        name="join_last" if last else "join_first",
     )(idx, *parts, *begun)
 
 
@@ -799,15 +798,18 @@
         dwo_other = permute(dwo_mine, beside)
         dx, *dwkv = tail(idx, down, cosine, sine, act_t, dq, wq, wk, wv, x, dy, gain_pre, dgain_post)
         theirs_in, mine_in = permute(dwkv[1], beside), permute(dwkv[0], beside)
-        split = dim // 3 * 2
+        bounds = (0, 512, dim - dim % 512, dim + 8)
         pieces = []
-        for rows in (slice(0, split), slice(split, None)):
+        for n in range(3):
+            rows = slice(bounds[n], bounds[n + 1])
             chip_mine = dwkv[0][rows] + theirs_in[rows]
             chip_other = dwkv[1][rows] + mine_in[rows]
             far_mine = permute(chip_mine, across)
             pieces.append((chip_mine, far_mine, chip_other, permute(far_mine, beside)))
-        begun = join_pair(idx, pieces[0], dim)
-        dwk_full, dwv_full, dpre_full, dpost_full = join_pair(idx, pieces[1], dim, tuple(begun))
+        joined = ()
+        for n in range(3):
+            joined = join_pair(idx, pieces[n], dim, bounds[n], tuple(joined))
+        dwk_full, dwv_full, dpre_full, dpost_full = joined
 
         dwo_full = join_rows(idx, dwo_mine, dwo_other)
         dwq_full = join_wide(idx, dwq_mine, dwq_other, heads)

time: 296 us -> 318 us (1.074)
  waiting for transfers between devices: 42.1 us -> 52.7 us
  other arithmetic: 9.91 us -> 16.4 us
    ppermute x13 -> x15, waiting for transfers between devices: 42.1 us -> 52.7 us  [permute(): return lax.ppermute(value, 'cp', pairs)]
    unnamed x21 -> x31, local copies, waits for them, and re-layouts: 4.43 us -> 7.35 us
    pallas_call x2 -> x3, Pallas kernels: 5.42 us -> 6.73 us  [join_pair(): pl.pallas_call(functools.partial(join_pair_kernel, last=last, held=len(be...]
    ppermute x13 -> x15, starting transfers between devices: 29.6 us -> 29.9 us  [permute(): return lax.ppermute(value, 'cp', pairs)]
  transfers between devices with their start and end apart: 13 -> 15, of which waited for: 2 -> 2; matrix products, arithmetic and copies ran while one was open for 5% -> 6% of each run, Pallas kernels for 68% -> 64%
where the time goes in v10:
time: 318 us; the launch traced here: 317 us
  Pallas kernels  210 us (66%)
  waiting for transfers between devices  52.7 us (17%)
  starting transfers between devices  29.9 us (9%)
  other arithmetic  16.4 us (5%)
  local copies, waits for them, and re-layouts  7.35 us (2%)
    pallas_call x1, Pallas kernels, backward(): pl.pallas_call(backward_kernel, grid=(3 * tiles,), in_specs=[held(q), hel...  77.5 us
    pallas_call x1, Pallas kernels, forward(): pl.pallas_call(forward_kernel, grid=(done + tiles,), in_specs=[pl.BlockSp...  67.6 us
    ppermute x15, waiting for transfers between devices, permute(): return lax.ppermute(value, 'cp', pairs)  52.7 us
    ppermute x15, starting transfers between devices, permute(): return lax.ppermute(value, 'cp', pairs)  29.9 us
    pallas_call x1, Pallas kernels, grad_wo(): pl.pallas_call(grad_wo_kernel, grid=(tokens // bt,), in_specs=[pl.BlockSp...  17.3 us
    pallas_call x1, Pallas kernels, post(): pl.pallas_call(post_kernel, grid=(tokens // bq,), in_specs=[rows2(heads *...  14.1 us
    pallas_call x1, Pallas kernels, tail(): pl.pallas_call(tail_kernel, grid=(tokens // bt,), in_specs=[pl.BlockSpec(...  12.8 us
    pallas_call x1, Pallas kernels, join_wide(): pl.pallas_call(join_wide_kernel, grid=(dim // bd,), in_specs=[pl.BlockSpe...  7.66 us
  transfers between devices with their start and end apart: 15, of which 2 were waited for; matrix products, arithmetic and copies ran while one was open for 6% of the time, Pallas kernels for 64%

profile of v10, /device:TPU:0, one launch (start us, length us, event | category | flops | bytes accessed | tf_op | source)
XLA Modules:
  0.0 317.1 jit_solution(7466722406028812176)
XLA Ops:
  0.6 1.3 collective-permute-start.11
  1.9 7.9 %collective-permute-start.12 = (bf16[1024,1152]{1,0:T(8,128)(2,1)}, bf16[1024,1152]{1,0:T(8,128)(2,1)}, u32[]{:S(2)}, u32[]{:S(2)}) collective-permute-start(bf16[1024,1152]{1,0:T(8,128)(2,1)} %bitcast.27), channel_id=1, source_target_pairs={{0,2},{1,3},{4,6},{5,7},{8,10},{9,11},{12,14},{13,15}} | collective-permute-start | bytes 7077896 | tf_op jit(solution)/shard_map/ppermute | solution.py:767
  9.9 3.6 %copy.24 = bf16[144,8,4,256]{3,1,2,0:T(8,128)(2,1)} copy(bf16[144,8,4,256]{3,2,1,0:T(4,128)(2,1)} %bitcast.19) | data formatting | bytes 4718592
  13.5 3.0 multiply_sine_fusion
  16.6 67.6 %forward.1 = (bf16[1152,1024]{1,0:T(8,128)(2,1)}, bf16[4,1024,256]{2,1,0:T(8,128)(2,1)}, bf16[2,1024,256]{2,1,0:T(8,128)(2,1)}, bf16[2,1024,256]{2,1,0:T(8,128)(...) custom-call(bf16[1024,1152]{1,0:T(8,128)(2,1)} %bitcast.23, ...), custom_call_target="tpu_custom_call" | custom-call | flops 10000000000 | bytes 10000000 | tf_op jit(solution)/shard_map/forward/pallas_call | solution.py:228
  84.3 16.9 %collective-permute-start.10 = (bf16[1024,1024]{1,0:T(8,128)(2,1)}, bf16[1024,1024]{1,0:T(8,128)(2,1)}, u32[]{:S(2)}, u32[]{:S(2)}) collective-permute-start(bf16[1024,1024]{1,0:T(8,128)(2,1)} %get-tuple-element.38.o_ref), channel_id=1, source_target_pairs={{0,2},{2,0},{1,3},{3,1},{4,6},{6,4},{5,7},{7,5},{8,10},{10,8},{9,1... | collective-permute-start | bytes 6291464 | tf_op jit(solution)/shard_map/ppermute | solution.py:767
  101.1 14.1 %post.1 = (bf16[1024,1152]{1,0:T(8,128)(2,1)}, bf16[4,1024,256]{2,1,0:T(8,128)(2,1)}, bf16[1024,1152]{1,0:T(8,128)(2,1)}, f32[8,1024]{1,0:T(8,128)}, f32[1,1152]{1,0:T(1,128)}) custom-call(bf16[1024,1024]{1,0:T(8,128)(2,1)} %get-tuple-element.38.o_ref, f32[4,1024,256]{2,1,0:T(8,128)} %get-tuple-element.39.out_ref, f32[1024,128]{1,0:T(8,128)} %get-tuple-element.40.lse_ref, ...), custom_call_target="tpu_custom_call" | custom-call | flops 10000000000 | bytes 10000000 | tf_op jit(solution)/shard_map/post/pallas_call | solution.py:316
  115.3 77.5 %backward.1 = (f32[2,1024,256]{2,1,0:T(8,128)}, bf16[1024,1024]{1,0:T(8,128)(2,1)}, f32[1152,512]{1,0:T(8,128)}) custom-call(bf16[4,1024,256]{2,1,0:T(8,128)(2,1)} %get-tuple-element.42.q_ref, bf16[4,1024,256]{2,1,0:T(8,128)(2,1)} %get-tuple-element.43.do_ref, f32[8,1024]{1,0:T(8,128)} %get-tuple-element.44.stat_ref, ...), custom_call_target="tpu_custom_call" | custom-call | flops 10000000000 | bytes 10000000 | tf_op jit(solution)/shard_map/backward/pallas_call | solution.py:558
  192.8 12.8 %tail.1 = (bf16[1024,1152]{1,0:T(8,128)(2,1)}, f32[1160,256]{1,0:T(8,128)}, f32[1160,256]{1,0:T(8,128)}) custom-call(s32[1]{0:T(128)} %bitcast.7.idx_ref, f32[2,1024,256]{2,1,0:T(8,128)} %get-tuple-element.50.down_ref, f32[1024,128]{1,0:T(8,128)} %get-tuple-element.81.cos_ref, f32[1024,128]{1,0:T(8,128)} %get-tuple-element.80.sin_ref, ...), custom_call_target="tpu_custom_call" | custom-call | flops 10000000000 | bytes 10000000 | tf_op jit(solution)/shard_map/tail/pallas_call | solution.py:642
  205.7 0.5 collective-permute-start.4
  206.2 17.3 %grad_wo.1 = (f32[512,1152]{1,0:T(8,128)}, f32[512,1152]{1,0:T(8,128)}) custom-call(s32[1]{0:T(128)} %bitcast.7.idx_ref, bf16[1024,1024]{1,0:T(8,128)(2,1)} %get-tuple-element.38.o_ref, bf16[1024,1152]{1,0:T(8,128)(2,1)} %get-tuple-element.63.dz_ref, bf16[1024,1024]{1,0:T(8,128)(2,1)} %collective-permute-done.10.po_ref, ...), custom_call_target="tpu_custom_call" | custom-call | flops 10000000000 | bytes 10000000 | tf_op jit(solution)/shard_map/grad_wo/pallas_call | solution.py:358
  223.6 1.4 slice_add_fusion.1
  225.0 2.0 collective-permute-start.8
  227.1 44.0 %collective-permute-done.8.b_ref = f32[512,256]{1,0:T(8,128)S(1)} collective-permute-done((f32[512,256]{1,0:T(8,128)S(1)}, f32[512,256]{1,0:T(8,128)S(1)}, u32[]{:S(2)}, u32[]{:S(2)}) %collective-permute-start.8) | collective-permute-done | bytes 524320 | tf_op jit(solution)/shard_map/ppermute | solution.py:767
  271.1 1.1 slice_add_fusion.5.a_ref
  272.2 2.3 slice_add_fusion
  274.5 1.6 slice_add_fusion.4.c_ref
  276.1 8.7 %collective-permute-done.3.b_ref = f32[136,256]{1,0:T(8,128)S(1)} collective-permute-done((f32[136,256]{1,0:T(8,128)S(1)}, f32[136,256]{1,0:T(8,128)S(1)}, u32[]{:S(2)}, u32[]{:S(2)}) %collective-permute-start.3) | collective-permute-done | bytes 139296 | tf_op jit(solution)/shard_map/ppermute | solution.py:767
  284.8 0.5 collective-permute-start.7
  285.3 3.6 %add.24.mine_ref = f32[1152,512]{1,0:T(8,128)} add(f32[1152,512]{1,0:T(8,128)S(1)} %copy-done, f32[1152,512]{1,0:T(8,128)} %collective-permute-done) | non-fusion elementwise | flops 589824 | bytes 7077888 | tf_op jit(solution)/shard_map/add | solution.py:793
  289.0 0.2 collective-permute-start.1
  289.2 0.8 copy-done.11
  290.0 2.5 shard_map.152
  292.5 3.4 %add.31.mine_ref = f32[512,1152]{1,0:T(8,128)} add(f32[512,1152]{1,0:T(8,128)S(1)} %copy-done.1, f32[512,1152]{1,0:T(8,128)} %collective-permute-done.13) | non-fusion elementwise | flops 589824 | bytes 7077888 | tf_op jit(solution)/shard_map/add | solution.py:797
  295.9 0.3 collective-permute-start.14
  296.2 0.8 copy-done.12
  297.0 2.4 shard_map.153
  299.4 0.7 copy-done.14
  300.1 1.8 shard_map.154
  301.9 7.7 %join_wide.1 = f32[9216,128]{1,0:T(8,128)} custom-call(s32[1]{0:T(128)} %bitcast.7.idx_ref, f32[1152,512]{1,0:T(8,128)} %add.24.mine_ref, f32[1152,512]{1,0:T(8,128)} %collective-permute-done.1.other_ref), custom_call_target="tpu_custom_call" | custom-call | flops 10000000000 | bytes 10000000 | tf_op jit(solution)/shard_map/join_wide/pallas_call | solution.py:690
  309.6 1.4 copy-done.8
  311.0 6.2 %join_rows.1 = f32[1024,1152]{1,0:T(8,128)} custom-call(s32[1]{0:T(128)} %bitcast.7.idx_ref, f32[512,1152]{1,0:T(8,128)} %add.31.mine_ref, f32[512,1152]{1,0:T(8,128)} %copy-done.8), custom_call_target="tpu_custom_call" | custom-call | flops 10000000000 | bytes 10000000 | tf_op jit(solution)/shard_map/join_rows/pallas_call | solution.py:750
  (48 shorter events, 0.4 us)
Async XLA Ops:
  0.6 205.6 %collective-permute-start.11 = (bf16[1024,1152]{1,0:T(8,128)(2,1)}, bf16[1024,1152]{1,0:T(8,128)(2,1)}, u32[]{:S(2)}, u32[]{:S(2)}) collective-permute-start(bf16[1024,1152]{1,0:T(8,128)(2,1)} %bitcast.26), channel_id=1, source_target_pairs={{2,0},{3,1},{6,4},{7,5},{10,8},{11,9},{14,12},{15,13}} | collective-permute-start | bytes 7077896 | tf_op jit(solution)/shard_map/ppermute | solution.py:767
  1.9 204.3 %collective-permute-start.12 = (bf16[1024,1152]{1,0:T(8,128)(2,1)}, bf16[1024,1152]{1,0:T(8,128)(2,1)}, u32[]{:S(2)}, u32[]{:S(2)}) collective-permute-start(bf16[1024,1152]{1,0:T(8,128)(2,1)} %bitcast.27), channel_id=1, source_target_pairs={{0,2},{1,3},{4,6},{5,7},{8,10},{9,11},{12,14},{13,15}} | collective-permute-start | bytes 7077896 | tf_op jit(solution)/shard_map/ppermute | solution.py:767
  9.9 3.7 %copy-start.7 = (s32[1,1024]{1,0:T(1,128)S(1)}, s32[1,1024]{1,0:T(1,128)}, u32[]{:S(2)}) copy-start(s32[1,1024]{1,0:T(1,128)} %param.10) | copy-start | bytes 12292
  84.3 121.5 %collective-permute-start.10 = (bf16[1024,1024]{1,0:T(8,128)(2,1)}, bf16[1024,1024]{1,0:T(8,128)(2,1)}, u32[]{:S(2)}, u32[]{:S(2)}) collective-permute-start(bf16[1024,1024]{1,0:T(8,128)(2,1)} %get-tuple-element.38.o_ref), channel_id=1, source_target_pairs={{0,2},{2,0},{1,3},{3,1},{4,6},{6,4},{5,7},{7,5},{8,10},{10,8},{9,1... | collective-permute-start | bytes 6291464 | tf_op jit(solution)/shard_map/ppermute | solution.py:767
  192.8 12.9 %copy-start = (f32[1152,512]{1,0:T(8,128)S(1)}, f32[1152,512]{1,0:T(8,128)}, u32[]{:S(2)}) copy-start(f32[1152,512]{1,0:T(8,128)} %get-tuple-element.54) | copy-start | bytes 7077892
  205.6 18.0 %collective-permute-start.2 = (f32[1160,256]{1,0:T(8,128)}, f32[1160,256]{1,0:T(8,128)}, u32[]{:S(2)}, u32[]{:S(2)}) collective-permute-start(f32[1160,256]{1,0:T(8,128)} %get-tuple-element.56), channel_id=1, source_target_pairs={{0,1},{1,0},{2,3},{3,2},{4,5},{5,4},{6,7},{7,6},{8,9},{9,8},{10,11... | collective-permute-start | bytes 3563528 | tf_op jit(solution)/shard_map/ppermute | solution.py:767
  205.7 79.7 %collective-permute-start = (f32[1152,512]{1,0:T(8,128)S(1)}, f32[1152,512]{1,0:T(8,128)}, u32[]{:S(2)}, u32[]{:S(2)}) collective-permute-start(f32[1152,512]{1,0:T(8,128)S(1)} %copy-done), channel_id=1, source_target_pairs={{0,2},{2,0},{1,3},{3,1},{4,6},{6,4},{5,7},{7,5},{8,10},{10,8},{9,1... | collective-permute-start | bytes 7077896 | tf_op jit(solution)/shard_map/ppermute | solution.py:767
  205.7 66.4 %collective-permute-start.4 = (f32[1160,256]{1,0:T(8,128)}, f32[1160,256]{1,0:T(8,128)}, u32[]{:S(2)}, u32[]{:S(2)}) collective-permute-start(f32[1160,256]{1,0:T(8,128)} %get-tuple-element.55), channel_id=1, source_target_pairs={{0,1},{1,0},{2,3},{3,2},{4,5},{5,4},{6,7},{7,6},{8,9},{9,8},{10,11... | collective-permute-start | bytes 3563528 | tf_op jit(solution)/shard_map/ppermute | solution.py:767
  206.2 17.4 %copy-start.3 = (f32[1160,256]{1,0:T(8,128)S(1)}, f32[1160,256]{1,0:T(8,128)}, u32[]{:S(2)}) copy-start(f32[1160,256]{1,0:T(8,128)} %get-tuple-element.55) | copy-start | bytes 3563524
  223.5 48.7 %copy-start.2 = (f32[1160,256]{1,0:T(8,128)S(1)}, f32[1160,256]{1,0:T(8,128)}, u32[]{:S(2)}) copy-start(f32[1160,256]{1,0:T(8,128)} %get-tuple-element.56) | copy-start | bytes 3563524
  223.5 69.0 %collective-permute-start.13 = (f32[512,1152]{1,0:T(8,128)}, f32[512,1152]{1,0:T(8,128)}, u32[]{:S(2)}, u32[]{:S(2)}) collective-permute-start(f32[512,1152]{1,0:T(8,128)} %get-tuple-element.65), channel_id=1, source_target_pairs={{0,1},{1,0},{2,3},{3,2},{4,5},{5,4},{6,7},{7,6},{8,9},{9,8},{10,11... | collective-permute-start | bytes 7077896 | tf_op jit(solution)/shard_map/ppermute | solution.py:767
  225.0 59.8 %copy-start.5 = (f32[512,256]{1,0:T(8,128)}, f32[512,256]{1,0:T(8,128)S(1)}, u32[]{:S(2)}) copy-start(f32[512,256]{1,0:T(8,128)S(1)} %get-tuple-element.78.a_ref) | copy-start | bytes 1572868
  225.0 63.9 %copy-start.4 = (f32[512,256]{1,0:T(8,128)}, f32[512,256]{1,0:T(8,128)S(1)}, u32[]{:S(2)}) copy-start(f32[512,256]{1,0:T(8,128)S(1)} %get-tuple-element.79.a_ref) | copy-start | bytes 1572868
  225.0 46.0 %collective-permute-start.8 = (f32[512,256]{1,0:T(8,128)S(1)}, f32[512,256]{1,0:T(8,128)S(1)}, u32[]{:S(2)}, u32[]{:S(2)}) collective-permute-start(f32[512,256]{1,0:T(8,128)S(1)} %get-tuple-element.78.a_ref), channel_id=1, source_target_pairs={{0,2},{2,0},{1,3},{3,1},{4,6},{6,4},{5,7},{7,5},{8,10},{10,8},{9,1... | collective-permute-start | bytes 1572872 | tf_op jit(solution)/shard_map/ppermute | solution.py:767
  227.0 57.8 %collective-permute-start.6 = (f32[512,256]{1,0:T(8,128)S(1)}, f32[512,256]{1,0:T(8,128)S(1)}, u32[]{:S(2)}, u32[]{:S(2)}) collective-permute-start(f32[512,256]{1,0:T(8,128)S(1)} %get-tuple-element.79.a_ref), channel_id=1, source_target_pairs={{0,2},{2,0},{1,3},{3,1},{4,6},{6,4},{5,7},{7,5},{8,10},{10,8},{9,1... | collective-permute-start | bytes 1572872 | tf_op jit(solution)/shard_map/ppermute | solution.py:767
  271.1 17.9 %copy-start.10 = (f32[512,256]{1,0:T(8,128)}, f32[512,256]{1,0:T(8,128)S(1)}, u32[]{:S(2)}) copy-start(f32[512,256]{1,0:T(8,128)S(1)} %collective-permute-done.8.b_ref) | copy-start | bytes 1572868
  271.1 18.1 %collective-permute-start.9 = (f32[512,256]{1,0:T(8,128)S(1)}, f32[512,256]{1,0:T(8,128)S(1)}, u32[]{:S(2)}, u32[]{:S(2)}) collective-permute-start(f32[512,256]{1,0:T(8,128)S(1)} %collective-permute-done.8.b_ref), channel_id=1, source_target_pairs={{0,1},{1,0},{2,3},{3,2},{4,5},{5,4},{6,7},{7,6},{8,9},{9,8},{10,11... | collective-permute-start | bytes 1572872 | tf_op jit(solution)/shard_map/ppermute | solution.py:767
  272.1 13.2 %copy-start.6 = (f32[136,256]{1,0:T(8,128)}, f32[136,256]{1,0:T(8,128)S(1)}, u32[]{:S(2)}) copy-start(f32[136,256]{1,0:T(8,128)S(1)} %slice_add_fusion.5.a_ref) | copy-start | bytes 417796
  272.2 12.6 %collective-permute-start.3 = (f32[136,256]{1,0:T(8,128)S(1)}, f32[136,256]{1,0:T(8,128)S(1)}, u32[]{:S(2)}, u32[]{:S(2)}) collective-permute-start(f32[136,256]{1,0:T(8,128)S(1)} %slice_add_fusion.5.a_ref), channel_id=1, source_target_pairs={{0,2},{2,0},{1,3},{3,1},{4,6},{6,4},{5,7},{7,5},{8,10},{10,8},{9,1... | collective-permute-start | bytes 417800 | tf_op jit(solution)/shard_map/ppermute | solution.py:767
  284.8 4.2 %copy-start.13 = (f32[136,256]{1,0:T(8,128)}, f32[136,256]{1,0:T(8,128)S(1)}, u32[]{:S(2)}) copy-start(f32[136,256]{1,0:T(8,128)S(1)} %collective-permute-done.3.b_ref) | copy-start | bytes 417796
  284.8 14.6 %collective-permute-start.5 = (f32[136,256]{1,0:T(8,128)S(1)}, f32[136,256]{1,0:T(8,128)S(1)}, u32[]{:S(2)}, u32[]{:S(2)}) collective-permute-start(f32[136,256]{1,0:T(8,128)S(1)} %collective-permute-done.3.b_ref), channel_id=1, source_target_pairs={{0,1},{1,0},{2,3},{3,2},{4,5},{5,4},{6,7},{7,6},{8,9},{9,8},{10,11... | collective-permute-start | bytes 417800 | tf_op jit(solution)/shard_map/ppermute | solution.py:767
  284.8 4.2 %copy-start.9 = (f32[512,256]{1,0:T(8,128)}, f32[512,256]{1,0:T(8,128)S(1)}, u32[]{:S(2)}) copy-start(f32[512,256]{1,0:T(8,128)S(1)} %collective-permute-done.6.b_ref) | copy-start | bytes 1572868
  284.8 11.4 %collective-permute-start.7 = (f32[512,256]{1,0:T(8,128)S(1)}, f32[512,256]{1,0:T(8,128)S(1)}, u32[]{:S(2)}, u32[]{:S(2)}) collective-permute-start(f32[512,256]{1,0:T(8,128)S(1)} %collective-permute-done.6.b_ref), channel_id=1, source_target_pairs={{0,1},{1,0},{2,3},{3,2},{4,5},{5,4},{6,7},{7,6},{8,9},{9,8},{10,11... | collective-permute-start | bytes 1572872 | tf_op jit(solution)/shard_map/ppermute | solution.py:767
  289.0 12.9 %collective-permute-start.1 = (f32[1152,512]{1,0:T(8,128)}, f32[1152,512]{1,0:T(8,128)}, u32[]{:S(2)}, u32[]{:S(2)}) collective-permute-start(f32[1152,512]{1,0:T(8,128)} %add.24.mine_ref), channel_id=1, source_target_pairs={{0,1},{1,0},{2,3},{3,2},{4,5},{5,4},{6,7},{7,6},{8,9},{9,8},{10,11... | collective-permute-start | bytes 7077896 | tf_op jit(solution)/shard_map/ppermute | solution.py:767
  289.2 0.8 copy-start.11
  290.0 2.5 copy-start.1
  295.9 13.7 %collective-permute-start.14 = (f32[512,1152]{1,0:T(8,128)}, f32[512,1152]{1,0:T(8,128)S(1)}, u32[]{:S(2)}, u32[]{:S(2)}) collective-permute-start(f32[512,1152]{1,0:T(8,128)} %add.31.mine_ref), channel_id=1, source_target_pairs={{0,1},{1,0},{2,3},{3,2},{4,5},{5,4},{6,7},{7,6},{8,9},{9,8},{10,11... | collective-permute-start | bytes 7077896 | tf_op jit(solution)/shard_map/ppermute | solution.py:767
  296.2 0.8 copy-start.12
  299.4 0.7 copy-start.14
  309.6 1.4 copy-start.8

commit v11 on v9

--- a/solution.py
+++ b/solution.py
@@ -16,6 +16,7 @@
 LOG2E = math.log2(math.e)
 CAP2 = SOFT_CAP * LOG2E
 INV_CAP = 1.0 / SOFT_CAP
+SHIFT2 = 20.0
 
 
 F32 = jnp.float32
@@ -70,7 +71,7 @@
         keep = lax.broadcasted_iota(jnp.int32, (bq, bk), 1) <= lax.broadcasted_iota(jnp.int32, (bq, bk), 0)
     for h in range(heads):
         s = dot(q_ref[h], k, NT)
-        p = jnp.exp2(jnp.tanh(s * INV_CAP) * CAP2)
+        p = jnp.exp2(jnp.tanh(s * INV_CAP) * CAP2 - SHIFT2)
         if masked:
             p = jnp.where(keep, p, 0.0)
         part = p[:, 0:128]
@@ -80,9 +81,9 @@
         acc_ref[h] += dot(p.astype(BF16), v)
 
 
-def forward_kernel(x_ref, gain_ref, wk_ref, wv_ref, wq_ref, cos_ref, sin_ref,
+def forward_kernel(x_ref, gain_ref, wk_ref, wv_ref, wq_hbm, cos_ref, sin_ref,
                    at_ref, q_ref, own_ref, near_ref, far_ref, mid_ref, o_ref, out_ref, lse_ref,
-                   a_s, own_s, near_s, far_s, mid_s, acc_s, sum_s,
+                   wq_s, wq_sem, a_s, own_s, near_s, far_s, mid_s, acc_s, sum_s,
                    far_send, far_recv, near_send, near_recv, mid_send, mid_recv):
     heads, tokens, hd = q_ref.shape
     bt = x_ref.shape[0]
@@ -112,8 +113,11 @@
         rows = rows_of(c, big)
         return to_sibling(rank, far_s.at[:, rows, :], mid_s.at[:, rows, :], mid_send.at[c], mid_recv.at[c])
 
+    load_wq = pltpu.make_async_copy(wq_hbm, wq_s, wq_sem)
+
     @pl.when(i == 0)
     def _():
+        load_wq.start()
         barrier = pltpu.get_barrier_semaphore()
         for other in (across, {"cp": rank + 1 - 2 * core}):
             pl.semaphore_signal(barrier, inc=1, device_id=other, device_id_type=mesh_id)
@@ -130,7 +134,6 @@
         own_s[1, rows, :] = dot(a, wv_ref[...]).astype(BF16)
         pl.when(rank < 2)(lambda: far_copy(i).start())
         pl.when(core == 0)(lambda: near_copy(i).start())
-        at_ref[...] = a.T
 
     def attend(t, kv_ref, start, size, masked):
         rows, keys = rows_of(t), pl.ds(pl.multiple_of(start, bt), size)
@@ -142,9 +145,12 @@
         t = i - tiles
         rows = rows_of(t)
         a = a_s[rows, :]
+        at_ref[...] = a.T
+        own_ref[...] = own_s[:, rows, :]
+        pl.when(t == 0)(lambda: load_wq.wait())
         scale = QUERY_SCALE ** -0.5
         for h in range(heads):
-            q = dot(a, wq_ref[:, h * hd:(h + 1) * hd]).astype(BF16).astype(F32)
+            q = dot(a, wq_s[:, h * hd:(h + 1) * hd]).astype(BF16).astype(F32)
             q_ref[h, rows, :] = (rope(q, cos_ref[rows, :], sin_ref[rows, :]) * scale).astype(BF16)
         acc_s[:, rows, :] = jnp.zeros((heads, bt, hd), F32)
         sum_s[:, rows, :] = jnp.zeros((heads, bt, 128), F32)
@@ -197,12 +203,12 @@
         lse = jnp.zeros((bt, 128), F32)
         for h in range(heads):
             total = jnp.sum(sum_s[h, rows, :], axis=-1, keepdims=True)
-            lse = jnp.where(lane == h, jnp.log2(total), lse)
+            lse = jnp.where(lane == h, jnp.log2(total) + SHIFT2, lse)
             out = acc_s[h, rows, :] / total
             out_ref[h] = out
             o_ref[:, h * hd:(h + 1) * hd] = out.astype(BF16)
         lse_ref[...] = lse
-        for dst, src in ((own_ref, own_s), (near_ref, near_s), (far_ref, far_s), (mid_ref, mid_s)):
+        for dst, src in ((near_ref, near_s), (far_ref, far_s), (mid_ref, mid_s)):
             dst[...] = src[:, rows, :]
 
     @pl.when(last == tiles - 1)
@@ -221,6 +227,7 @@
     done = 2 * tiles + 2 * chunks
     dma = pltpu.SemaphoreType.DMA
     early = lambda i: jnp.minimum(i, tiles - 1)
+    second = lambda i: jnp.clip(i - tiles, 0, tiles - 1)
     late = lambda i: jnp.maximum(i - done, 0)
     kv_shape = jax.ShapeDtypeStruct((2, tokens, hd), BF16)
     kv_out = pl.BlockSpec((2, bt, hd), lambda i: (0, late(i), 0))
@@ -232,14 +239,14 @@
             whole(gain.shape),
             whole(wk.shape),
             whole(wv.shape),
-            whole(wq.shape),
+            pl.BlockSpec(memory_space=pl.ANY),
             whole(cosine.shape),
             whole(sine.shape),
         ],
         out_specs=[
-            pl.BlockSpec((dim, bt), lambda i: (0, early(i))),
+            pl.BlockSpec((dim, bt), lambda i: (0, second(i))),
             whole((heads, tokens, hd)),
-            kv_out,
+            pl.BlockSpec((2, bt, hd), lambda i: (0, second(i), 0)),
             kv_out,
             kv_out,
             kv_out,
@@ -258,7 +265,7 @@
             jax.ShapeDtypeStruct((heads, tokens, hd), F32),
             jax.ShapeDtypeStruct((tokens, 128), F32),
         ],
-        scratch_shapes=[pltpu.VMEM((tokens, dim), BF16)] + [pltpu.VMEM((2, tokens, hd), BF16)] * 4 + [
+        scratch_shapes=[pltpu.VMEM(wq.shape, BF16), dma, pltpu.VMEM((tokens, dim), BF16)] + [pltpu.VMEM((2, tokens, hd), BF16)] * 4 + [
             pltpu.VMEM((heads, tokens, hd), F32),
             pltpu.VMEM((heads, tokens, 128), F32),
             dma((tiles,)),

time: 296 us -> 296 us (level)
  transfers between devices with their start and end apart: 13 -> 13, of which waited for: 2 -> 2; matrix products, arithmetic and copies ran while one was open for 5% -> 5% of each run, Pallas kernels for 68% -> 69%
where the time goes in v11:
time: 296 us; the launch traced here: 295 us
  Pallas kernels  208 us (70%)
  waiting for transfers between devices  42.1 us (14%)
  starting transfers between devices  29.5 us (10%)
  other arithmetic  9.91 us (3%)
  local copies, waits for them, and re-layouts  4.43 us (1%)
    pallas_call x1, Pallas kernels, backward(): pl.pallas_call(backward_kernel, grid=(3 * tiles,), in_specs=[held(q), hel...  77.5 us
    pallas_call x1, Pallas kernels, forward(): pl.pallas_call(forward_kernel, grid=(done + tiles,), in_specs=[pl.BlockSp...  67.6 us
    ppermute x13, waiting for transfers between devices, permute(): return lax.ppermute(value, 'cp', pairs)  42.1 us
    ppermute x13, starting transfers between devices, permute(): return lax.ppermute(value, 'cp', pairs)  29.5 us
    pallas_call x1, Pallas kernels, grad_wo(): pl.pallas_call(grad_wo_kernel, grid=(tokens // bt,), in_specs=[pl.BlockSp...  17.2 us
    pallas_call x1, Pallas kernels, post(): pl.pallas_call(post_kernel, grid=(tokens // bq,), in_specs=[rows2(heads *...  14.1 us
    pallas_call x1, Pallas kernels, tail(): pl.pallas_call(tail_kernel, grid=(tokens // bt,), in_specs=[pl.BlockSpec(...  12.7 us
    pallas_call x1, Pallas kernels, join_wide(): pl.pallas_call(join_wide_kernel, grid=(dim // bd,), in_specs=[pl.BlockSpe...  7.66 us
  transfers between devices with their start and end apart: 13, of which 2 were waited for; matrix products, arithmetic and copies ran while one was open for 5% of the time, Pallas kernels for 69%

profile of v11, /device:TPU:0, one launch (start us, length us, event | category | flops | bytes accessed | tf_op | source)
XLA Modules:
  0.0 295.1 jit_solution(3963715536761246087)
XLA Ops:
  0.6 1.3 collective-permute-start.9
  1.9 8.0 %collective-permute-start.10 = (bf16[1024,1152]{1,0:T(8,128)(2,1)}, bf16[1024,1152]{1,0:T(8,128)(2,1)}, u32[]{:S(2)}, u32[]{:S(2)}) collective-permute-start(bf16[1024,1152]{1,0:T(8,128)(2,1)} %bitcast.27), channel_id=1, source_target_pairs={{0,2},{1,3},{4,6},{5,7},{8,10},{9,11},{12,14},{13,15}} | collective-permute-start | bytes 7077896 | tf_op jit(solution)/shard_map/ppermute | solution.py:775
  9.9 3.6 %copy.22 = bf16[144,8,4,256]{3,1,2,0:T(8,128)(2,1)} copy(bf16[144,8,4,256]{3,2,1,0:T(4,128)(2,1)} %bitcast.19) | data formatting | bytes 4718592
  13.6 3.0 %multiply_sine_fusion = (f32[1024,128]{1,0:T(8,128)}, f32[1024,128]{1,0:T(8,128)}) fusion(f32[128]{0:T(128)S(1)} %multiply_power_fusion, f32[1024]{0:T(1024)S(1)} %bitcast.22), kind=kLoop, calls=%fused_computation.2 | loop fusion | flops 131072 | bytes 1053184 | tf_op jit(solution)/shard_map/sin | solution.py:792
  16.6 67.6 %forward.1 = (bf16[1152,1024]{1,0:T(8,128)(2,1)}, bf16[4,1024,256]{2,1,0:T(8,128)(2,1)}, bf16[2,1024,256]{2,1,0:T(8,128)(2,1)}, bf16[2,1024,256]{2,1,0:T(8,128)(...) custom-call(bf16[1024,1152]{1,0:T(8,128)(2,1)} %bitcast.23, ...), custom_call_target="tpu_custom_call" | custom-call | flops 10000000000 | bytes 10000000 | tf_op jit(solution)/shard_map/forward/pallas_call | solution.py:234
  84.2 16.7 %collective-permute-start.8 = (bf16[1024,1024]{1,0:T(8,128)(2,1)}, bf16[1024,1024]{1,0:T(8,128)(2,1)}, u32[]{:S(2)}, u32[]{:S(2)}) collective-permute-start(bf16[1024,1024]{1,0:T(8,128)(2,1)} %get-tuple-element.36.o_ref), channel_id=1, source_target_pairs={{0,2},{2,0},{1,3},{3,1},{4,6},{6,4},{5,7},{7,5},{8,10},{10,8},{9,1... | collective-permute-start | bytes 6291464 | tf_op jit(solution)/shard_map/ppermute | solution.py:775
  101.0 14.1 %post.1 = (bf16[1024,1152]{1,0:T(8,128)(2,1)}, bf16[4,1024,256]{2,1,0:T(8,128)(2,1)}, bf16[1024,1152]{1,0:T(8,128)(2,1)}, f32[8,1024]{1,0:T(8,128)}, f32[1,1152]{1,0:T(1,128)}) custom-call(bf16[1024,1024]{1,0:T(8,128)(2,1)} %get-tuple-element.36.o_ref, f32[4,1024,256]{2,1,0:T(8,128)} %get-tuple-element.37.out_ref, f32[1024,128]{1,0:T(8,128)} %get-tuple-element.38.lse_ref, ...), custom_call_target="tpu_custom_call" | custom-call | flops 10000000000 | bytes 10000000 | tf_op jit(solution)/shard_map/post/pallas_call | solution.py:322
  115.1 77.5 %backward.1 = (f32[2,1024,256]{2,1,0:T(8,128)}, bf16[1024,1024]{1,0:T(8,128)(2,1)}, f32[1152,512]{1,0:T(8,128)}) custom-call(bf16[4,1024,256]{2,1,0:T(8,128)(2,1)} %get-tuple-element.40.q_ref, bf16[4,1024,256]{2,1,0:T(8,128)(2,1)} %get-tuple-element.41.do_ref, f32[8,1024]{1,0:T(8,128)} %get-tuple-element.42.stat_ref, ...), custom_call_target="tpu_custom_call" | custom-call | flops 10000000000 | bytes 10000000 | tf_op jit(solution)/shard_map/backward/pallas_call | solution.py:564
  192.6 0.0 collective-permute-start
  192.6 12.7 %tail.1 = (bf16[1024,1152]{1,0:T(8,128)(2,1)}, f32[1160,256]{1,0:T(8,128)}, f32[1160,256]{1,0:T(8,128)}) custom-call(s32[1]{0:T(128)} %bitcast.7.idx_ref, f32[2,1024,256]{2,1,0:T(8,128)} %get-tuple-element.48.down_ref, f32[1024,128]{1,0:T(8,128)} %get-tuple-element.73.cos_ref, f32[1024,128]{1,0:T(8,128)} %get-tuple-element.72.sin_ref, ...), custom_call_target="tpu_custom_call" | custom-call | flops 10000000000 | bytes 10000000 | tf_op jit(solution)/shard_map/tail/pallas_call | solution.py:648
  205.4 0.0 collective-permute-start.2
  205.5 17.2 %grad_wo.1 = (f32[512,1152]{1,0:T(8,128)}, f32[512,1152]{1,0:T(8,128)}) custom-call(s32[1]{0:T(128)} %bitcast.7.idx_ref, bf16[1024,1024]{1,0:T(8,128)(2,1)} %get-tuple-element.36.o_ref, bf16[1024,1152]{1,0:T(8,128)(2,1)} %get-tuple-element.59.dz_ref, bf16[1024,1024]{1,0:T(8,128)(2,1)} %collective-permute-done.8.po_ref, ...), custom_call_target="tpu_custom_call" | custom-call | flops 10000000000 | bytes 10000000 | tf_op jit(solution)/shard_map/grad_wo/pallas_call | solution.py:364
  222.6 0.5 collective-permute-start.11
  223.1 0.1 collective-permute-start.4
  223.1 1.4 slice_add_fusion.1.a_ref
  224.6 0.0 copy-start.5
  224.6 2.0 collective-permute-start.6
  226.6 34.7 %collective-permute-done.6.b_ref = f32[768,256]{1,0:T(8,128)S(1)} collective-permute-done((f32[768,256]{1,0:T(8,128)S(1)}, f32[768,256]{1,0:T(8,128)S(1)}, u32[]{:S(2)}, u32[]{:S(2)}) %collective-permute-start.6) | collective-permute-done | bytes 786464 | tf_op jit(solution)/shard_map/ppermute | solution.py:775
  261.3 1.3 slice_add_fusion.3.a_ref
  262.7 0.3 collective-permute-start.3
  263.0 1.9 add.18.mine_ref
  265.0 0.8 slice_add_fusion.2.c_ref
  265.8 1.0 slice_add_fusion.c_ref
  266.8 7.4 %collective-permute-done.3.b_ref = f32[392,256]{1,0:T(8,128)} collective-permute-done((f32[392,256]{1,0:T(8,128)S(1)}, f32[392,256]{1,0:T(8,128)}, u32[]{:S(2)}, u32[]{:S(2)}) %collective-permute-start.3) | collective-permute-done | bytes 401440 | tf_op jit(solution)/shard_map/ppermute | solution.py:775
  274.2 0.3 add.23.mine_ref
  274.5 0.5 collective-permute-start.12
  275.1 3.1 %join_first.1 = (f32[2304,128]{1,0:T(8,128)}, f32[2304,128]{1,0:T(8,128)}) custom-call(s32[1]{0:T(128)} %bitcast.7.idx_ref, f32[768,256]{1,0:T(8,128)} %copy-done.5, f32[768,256]{1,0:T(8,128)} %copy-done.8, f32[768,256]{1,0:T(8,128)} %slice_add_fusion.c_ref, f32[768,256]{1,0:T(8,128)} %collective-permute-done.7.d_ref), custom_call_target="tpu_custom_call" | custom-call | flops 10000000000 | bytes 10000000 | tf_op jit(solution)/shard_map/join_first/pallas_call | solution.py:735
  278.2 0.0 copy-start.9
  278.2 0.7 copy-done.9
  278.9 2.3 join_last.1
  281.3 7.7 %join_wide.1 = f32[9216,128]{1,0:T(8,128)} custom-call(s32[1]{0:T(128)} %bitcast.7.idx_ref, f32[1152,512]{1,0:T(8,128)} %add.18.mine_ref, f32[1152,512]{1,0:T(8,128)} %collective-permute-done.1.other_ref), custom_call_target="tpu_custom_call" | custom-call | flops 10000000000 | bytes 10000000 | tf_op jit(solution)/shard_map/join_wide/pallas_call | solution.py:696
  288.9 6.2 %join_rows.1 = f32[1024,1152]{1,0:T(8,128)} custom-call(s32[1]{0:T(128)} %bitcast.7.idx_ref, f32[512,1152]{1,0:T(8,128)} %copy-done.2, f32[512,1152]{1,0:T(8,128)} %collective-permute-done.12.other_ref), custom_call_target="tpu_custom_call" | custom-call | flops 10000000000 | bytes 10000000 | tf_op jit(solution)/shard_map/join_rows/pallas_call | solution.py:758
  (33 shorter events, 0.1 us)
Async XLA Ops:
  0.6 204.8 %collective-permute-start.9 = (bf16[1024,1152]{1,0:T(8,128)(2,1)}, bf16[1024,1152]{1,0:T(8,128)(2,1)}, u32[]{:S(2)}, u32[]{:S(2)}) collective-permute-start(bf16[1024,1152]{1,0:T(8,128)(2,1)} %bitcast.26), channel_id=1, source_target_pairs={{2,0},{3,1},{6,4},{7,5},{10,8},{11,9},{14,12},{15,13}} | collective-permute-start | bytes 7077896 | tf_op jit(solution)/shard_map/ppermute | solution.py:775
  1.9 203.5 %collective-permute-start.10 = (bf16[1024,1152]{1,0:T(8,128)(2,1)}, bf16[1024,1152]{1,0:T(8,128)(2,1)}, u32[]{:S(2)}, u32[]{:S(2)}) collective-permute-start(bf16[1024,1152]{1,0:T(8,128)(2,1)} %bitcast.27), channel_id=1, source_target_pairs={{0,2},{1,3},{4,6},{5,7},{8,10},{9,11},{12,14},{13,15}} | collective-permute-start | bytes 7077896 | tf_op jit(solution)/shard_map/ppermute | solution.py:775
  9.9 3.7 %copy-start.7 = (s32[1,1024]{1,0:T(1,128)S(1)}, s32[1,1024]{1,0:T(1,128)}, u32[]{:S(2)}) copy-start(s32[1,1024]{1,0:T(1,128)} %param.10) | copy-start | bytes 12292
  84.2 121.2 %collective-permute-start.8 = (bf16[1024,1024]{1,0:T(8,128)(2,1)}, bf16[1024,1024]{1,0:T(8,128)(2,1)}, u32[]{:S(2)}, u32[]{:S(2)}) collective-permute-start(bf16[1024,1024]{1,0:T(8,128)(2,1)} %get-tuple-element.36.o_ref), channel_id=1, source_target_pairs={{0,2},{2,0},{1,3},{3,1},{4,6},{6,4},{5,7},{7,5},{8,10},{10,8},{9,1... | collective-permute-start | bytes 6291464 | tf_op jit(solution)/shard_map/ppermute | solution.py:775
  192.6 70.4 %collective-permute-start = (f32[1152,512]{1,0:T(8,128)}, f32[1152,512]{1,0:T(8,128)S(1)}, u32[]{:S(2)}, u32[]{:S(2)}) collective-permute-start(f32[1152,512]{1,0:T(8,128)} %get-tuple-element.52), channel_id=1, source_target_pairs={{0,2},{2,0},{1,3},{3,1},{4,6},{6,4},{5,7},{7,5},{8,10},{10,8},{9,1... | collective-permute-start | bytes 7077896 | tf_op jit(solution)/shard_map/ppermute | solution.py:775
  205.4 17.8 %collective-permute-start.2 = (f32[1160,256]{1,0:T(8,128)}, f32[1160,256]{1,0:T(8,128)}, u32[]{:S(2)}, u32[]{:S(2)}) collective-permute-start(f32[1160,256]{1,0:T(8,128)} %get-tuple-element.54), channel_id=1, source_target_pairs={{0,1},{1,0},{2,3},{3,2},{4,5},{5,4},{6,7},{7,6},{8,9},{9,8},{10,11... | collective-permute-start | bytes 3563528 | tf_op jit(solution)/shard_map/ppermute | solution.py:775
  205.4 17.6 %copy-start.4 = (f32[1160,256]{1,0:T(8,128)S(1)}, f32[1160,256]{1,0:T(8,128)}, u32[]{:S(2)}) copy-start(f32[1160,256]{1,0:T(8,128)} %get-tuple-element.53) | copy-start | bytes 3563524
  222.6 40.4 %copy-start = (f32[1152,512]{1,0:T(8,128)S(1)}, f32[1152,512]{1,0:T(8,128)}, u32[]{:S(2)}) copy-start(f32[1152,512]{1,0:T(8,128)} %get-tuple-element.52) | copy-start | bytes 7077892
  222.6 51.6 %collective-permute-start.11 = (f32[512,1152]{1,0:T(8,128)}, f32[512,1152]{1,0:T(8,128)S(1)}, u32[]{:S(2)}, u32[]{:S(2)}) collective-permute-start(f32[512,1152]{1,0:T(8,128)} %get-tuple-element.61), channel_id=1, source_target_pairs={{0,1},{1,0},{2,3},{3,2},{4,5},{5,4},{6,7},{7,6},{8,9},{9,8},{10,11... | collective-permute-start | bytes 7077896 | tf_op jit(solution)/shard_map/ppermute | solution.py:775
  223.1 41.9 %collective-permute-start.4 = (f32[1160,256]{1,0:T(8,128)S(1)}, f32[1160,256]{1,0:T(8,128)S(1)}, u32[]{:S(2)}, u32[]{:S(2)}) collective-permute-start(f32[1160,256]{1,0:T(8,128)S(1)} %copy-done.4), channel_id=1, source_target_pairs={{0,1},{1,0},{2,3},{3,2},{4,5},{5,4},{6,7},{7,6},{8,9},{9,8},{10,11... | collective-permute-start | bytes 3563528 | tf_op jit(solution)/shard_map/ppermute | solution.py:775
  224.6 36.7 %copy-start.5 = (f32[768,256]{1,0:T(8,128)}, f32[768,256]{1,0:T(8,128)S(1)}, u32[]{:S(2)}) copy-start(f32[768,256]{1,0:T(8,128)S(1)} %slice_add_fusion.1.a_ref) | copy-start | bytes 2359300
  224.6 36.7 %collective-permute-start.6 = (f32[768,256]{1,0:T(8,128)S(1)}, f32[768,256]{1,0:T(8,128)S(1)}, u32[]{:S(2)}, u32[]{:S(2)}) collective-permute-start(f32[768,256]{1,0:T(8,128)S(1)} %slice_add_fusion.1.a_ref), channel_id=1, source_target_pairs={{0,2},{2,0},{1,3},{3,1},{4,6},{6,4},{5,7},{7,5},{8,10},{10,8},{9,1... | collective-permute-start | bytes 2359304 | tf_op jit(solution)/shard_map/ppermute | solution.py:775
  261.3 3.6 %copy-start.8 = (f32[768,256]{1,0:T(8,128)}, f32[768,256]{1,0:T(8,128)S(1)}, u32[]{:S(2)}) copy-start(f32[768,256]{1,0:T(8,128)S(1)} %collective-permute-done.6.b_ref) | copy-start | bytes 2359300
  261.3 13.8 %collective-permute-start.7 = (f32[768,256]{1,0:T(8,128)S(1)}, f32[768,256]{1,0:T(8,128)}, u32[]{:S(2)}, u32[]{:S(2)}) collective-permute-start(f32[768,256]{1,0:T(8,128)S(1)} %collective-permute-done.6.b_ref), channel_id=1, source_target_pairs={{0,1},{1,0},{2,3},{3,2},{4,5},{5,4},{6,7},{7,6},{8,9},{9,8},{10,11... | collective-permute-start | bytes 2359304 | tf_op jit(solution)/shard_map/ppermute | solution.py:775
  262.6 2.3 copy-start.6
  262.6 2.3 copy-start.3
  262.7 11.6 %collective-permute-start.3 = (f32[392,256]{1,0:T(8,128)S(1)}, f32[392,256]{1,0:T(8,128)}, u32[]{:S(2)}, u32[]{:S(2)}) collective-permute-start(f32[392,256]{1,0:T(8,128)S(1)} %slice_add_fusion.3.a_ref), channel_id=1, source_target_pairs={{0,2},{2,0},{1,3},{3,1},{4,6},{6,4},{5,7},{7,5},{8,10},{10,8},{9,1... | collective-permute-start | bytes 1204232 | tf_op jit(solution)/shard_map/ppermute | solution.py:775
  264.9 9.3 %copy-start.1 = (f32[512,1152]{1,0:T(8,128)S(1)}, f32[512,1152]{1,0:T(8,128)}, u32[]{:S(2)}) copy-start(f32[512,1152]{1,0:T(8,128)} %get-tuple-element.60) | copy-start | bytes 7077892
  264.9 16.3 %collective-permute-start.1 = (f32[1152,512]{1,0:T(8,128)}, f32[1152,512]{1,0:T(8,128)}, u32[]{:S(2)}, u32[]{:S(2)}) collective-permute-start(f32[1152,512]{1,0:T(8,128)} %add.18.mine_ref), channel_id=1, source_target_pairs={{0,1},{1,0},{2,3},{3,2},{4,5},{5,4},{6,7},{7,6},{8,9},{9,8},{10,11... | collective-permute-start | bytes 7077896 | tf_op jit(solution)/shard_map/ppermute | solution.py:775
  274.2 4.0 %collective-permute-start.5 = (f32[392,256]{1,0:T(8,128)}, f32[392,256]{1,0:T(8,128)S(1)}, u32[]{:S(2)}, u32[]{:S(2)}) collective-permute-start(f32[392,256]{1,0:T(8,128)} %collective-permute-done.3.b_ref), channel_id=1, source_target_pairs={{0,1},{1,0},{2,3},{3,2},{4,5},{5,4},{6,7},{7,6},{8,9},{9,8},{10,11... | collective-permute-start | bytes 1204232 | tf_op jit(solution)/shard_map/ppermute | solution.py:775
  274.5 3.6 %copy-start.2 = (f32[512,1152]{1,0:T(8,128)}, f32[512,1152]{1,0:T(8,128)S(1)}, u32[]{:S(2)}) copy-start(f32[512,1152]{1,0:T(8,128)S(1)} %add.23.mine_ref) | copy-start | bytes 7077892
  274.5 14.4 %collective-permute-start.12 = (f32[512,1152]{1,0:T(8,128)S(1)}, f32[512,1152]{1,0:T(8,128)}, u32[]{:S(2)}, u32[]{:S(2)}) collective-permute-start(f32[512,1152]{1,0:T(8,128)S(1)} %add.23.mine_ref), channel_id=1, source_target_pairs={{0,1},{1,0},{2,3},{3,2},{4,5},{5,4},{6,7},{7,6},{8,9},{9,8},{10,11... | collective-permute-start | bytes 7077896 | tf_op jit(solution)/shard_map/ppermute | solution.py:775
  278.2 0.8 copy-start.9

commit v12 on v11

--- a/solution.py
+++ b/solution.py
@@ -81,9 +81,9 @@
         acc_ref[h] += dot(p.astype(BF16), v)
 
 
-def forward_kernel(x_ref, gain_ref, wk_ref, wv_ref, wq_hbm, cos_ref, sin_ref,
-                   at_ref, q_ref, own_ref, near_ref, far_ref, mid_ref, o_ref, out_ref, lse_ref,
-                   wq_s, wq_sem, a_s, own_s, near_s, far_s, mid_s, acc_s, sum_s,
+def forward_kernel(x_ref, gain_ref, wk_ref, wv_ref, wq_hbm, cos_ref, sin_ref, dy_hbm,
+                   at_ref, q_ref, own_ref, near_ref, far_ref, mid_ref, o_ref, out_ref, lse_ref, dy_far,
+                   dy_send, dy_recv, wq_s, wq_sem, a_s, own_s, near_s, far_s, mid_s, acc_s, sum_s,
                    far_send, far_recv, near_send, near_recv, mid_send, mid_recv):
     heads, tokens, hd = q_ref.shape
     bt = x_ref.shape[0]
@@ -114,6 +114,10 @@
         return to_sibling(rank, far_s.at[:, rows, :], mid_s.at[:, rows, :], mid_send.at[c], mid_recv.at[c])
 
     load_wq = pltpu.make_async_copy(wq_hbm, wq_s, wq_sem)
+    dy_copy = pltpu.make_async_remote_copy(
+        src_ref=dy_hbm.at[0:bt, :], dst_ref=dy_far, send_sem=dy_send, recv_sem=dy_recv,
+        device_id=across, device_id_type=mesh_id,
+    )
 
     @pl.when(i == 0)
     def _():
@@ -147,6 +151,7 @@
         a = a_s[rows, :]
         at_ref[...] = a.T
         own_ref[...] = own_s[:, rows, :]
+        pl.when(jnp.logical_and(t == 0, rank < 2))(lambda: dy_copy.start())
         pl.when(t == 0)(lambda: load_wq.wait())
         scale = QUERY_SCALE ** -0.5
         for h in range(heads):
@@ -213,12 +218,13 @@
 
     @pl.when(last == tiles - 1)
     def _():
-        pl.when(rank < 2)(lambda: [far_copy(n).wait_send() for n in range(tiles)] and None)
+        pl.when(rank < 2)(lambda: [far_copy(n).wait_send() for n in range(tiles)] and dy_copy.wait_send())
+        pl.when(rank >= 2)(lambda: dy_copy.wait_recv())
         pl.when(core == 0)(lambda: [near_copy(n).wait_send() for n in range(tiles)] and None)
         pl.when(rank >= 2)(lambda: [mid_copy(n).wait_send() for n in range(chunks)] and None)
 
 
-def forward(x, gain, wk, wv, wq, cosine, sine, heads):
+def forward(x, gain, wk, wv, wq, cosine, sine, dy, heads):
     tokens, dim = x.shape
     hd = wk.shape[1]
     bt = 256
@@ -242,6 +248,7 @@
             pl.BlockSpec(memory_space=pl.ANY),
             whole(cosine.shape),
             whole(sine.shape),
+            pl.BlockSpec(memory_space=pl.ANY),
         ],
         out_specs=[
             pl.BlockSpec((dim, bt), lambda i: (0, second(i))),
@@ -253,6 +260,7 @@
             pl.BlockSpec((bt, heads * hd), lambda i: (late(i), 0)),
             pl.BlockSpec((heads, bt, hd), lambda i: (0, late(i), 0)),
             pl.BlockSpec((bt, 128), lambda i: (late(i), 0)),
+            pl.BlockSpec(memory_space=pl.ANY),
         ],
         out_shape=[
             jax.ShapeDtypeStruct((dim, tokens), BF16),
@@ -264,8 +272,9 @@
             jax.ShapeDtypeStruct((tokens, heads * hd), BF16),
             jax.ShapeDtypeStruct((heads, tokens, hd), F32),
             jax.ShapeDtypeStruct((tokens, 128), F32),
-        ],
-        scratch_shapes=[pltpu.VMEM(wq.shape, BF16), dma, pltpu.VMEM((tokens, dim), BF16)] + [pltpu.VMEM((2, tokens, hd), BF16)] * 4 + [
+            jax.ShapeDtypeStruct((bt, dim), BF16),
+        ],
+        scratch_shapes=[dma, dma, pltpu.VMEM(wq.shape, BF16), dma, pltpu.VMEM((tokens, dim), BF16)] + [pltpu.VMEM((2, tokens, hd), BF16)] * 4 + [
             pltpu.VMEM((heads, tokens, hd), F32),
             pltpu.VMEM((heads, tokens, 128), F32),
             dma((tiles,)),
@@ -278,7 +287,7 @@
         compiler_params=pltpu.CompilerParams(vmem_limit_bytes=VMEM_LIMIT, collective_id=2, has_side_effects=True),
         cost_estimate=COST,
         name="forward",
-    )(x, gain, wk, wv, wq, cosine, sine)
+    )(x, gain, wk, wv, wq, cosine, sine, dy)
 
 
 def post_norm(o, wo, gain, dy):
@@ -337,13 +346,14 @@
     )(o, out, lse, x, dy, wo, gain)
 
 
-def grad_wo_kernel(idx_ref, o_ref, dz_ref, po_ref, pdy_low_ref, pdy_high_ref, wo_ref, gain_ref, mine_ref, theirs_ref, pdz_ref):
+def grad_wo_kernel(idx_ref, o_ref, dz_ref, po_ref, pdy_low_ref, pdy_head_ref, pdy_high_ref, wo_ref, gain_ref, mine_ref, theirs_ref, pdz_ref):
     _, width = o_ref.shape
     bt = pdy_low_ref.shape[0]
     hd = 256
     i = pl.program_id(0)
     rows = pl.ds(pl.multiple_of(i * bt, bt), bt)
-    dy = jnp.where(idx_ref[0] >= 2, pdy_high_ref[...], pdy_low_ref[...]).astype(F32)
+    high = jnp.where(i == 0, pdy_head_ref[...], pdy_high_ref[...])
+    dy = jnp.where(idx_ref[0] >= 2, high, pdy_low_ref[...]).astype(F32)
     pdz_ref[rows, :] = post_norm(po_ref[rows, :], wo_ref[...], 1.0 + gain_ref[...][None, :], dy)[1]
 
     @pl.when(i == pl.num_programs(0) - 1)
@@ -356,7 +366,7 @@
                 ref[hh * hd:(hh + 1) * hd, :] = dot(o_ref[:, cols].T, dz_ref[...]) + dot(po_ref[:, cols].T, pdz_ref[...])
 
 
-def grad_wo(idx, o, dz, po, pdy_low, pdy_high, wo, gain):
+def grad_wo(idx, o, dz, po, pdy_low, pdy_head, pdy_high, wo, gain):
     tokens, width = o.shape
     dim = dz.shape[1]
     bt = 256
@@ -370,7 +380,8 @@
             whole(dz.shape),
             whole(o.shape),
             rows2,
-            rows2,
+            whole(pdy_head.shape),
+            pl.BlockSpec((bt, dim), lambda i: (jnp.maximum(i - 1, 0), 0)),
             whole(wo.shape),
             whole((dim,)),
         ],
@@ -380,7 +391,7 @@
         compiler_params=params(),
         cost_estimate=COST,
         name="grad_wo",
-    )(idx, o, dz, po, pdy_low, pdy_high, wo, gain)
+    )(idx, o, dz, po, pdy_low, pdy_head, pdy_high, wo, gain)
 
 
 def backward_tile(q_ref, do_ref, stat_ref, dqt_ref, dkv_ref, k, v, kt, start, bq, masked):
@@ -691,7 +702,7 @@
 
 def join_wide(idx, mine, other, heads):
     dim, width = mine.shape
-    bd = 128
+    bd = dim // 3
     spec = rows_spec(bd, width)
     out = pl.pallas_call(
         join_wide_kernel,
@@ -792,15 +803,15 @@
         cosine, sine = jnp.cos(angles), jnp.sin(angles)
 
         dy_high = permute(dy, [(2, 0), (3, 1)])
-        act_t, q, own, near, far, mid, o, out, lse = forward(x, gain_pre, wk, wv, wq, cosine, sine, heads)
-        dy_low = permute(dy, [(0, 2), (1, 3)])
+        act_t, q, own, near, far, mid, o, out, lse, dy_head = forward(x, gain_pre, wk, wv, wq, cosine, sine, dy, heads)
+        dy_low = permute(dy[dy_head.shape[0]:], [(0, 2), (1, 3)])
         partner_o = permute(o, across)
         y, d_out, dz, stat, dgain_post = post(o, out, lse, x, dy, wo, gain_post)
 
         down, dq, dwq_part = backward(q, d_out, stat, own, near, far, mid, cosine, sine, act_t)
         dwq_mine = dwq_part + permute(dwq_part, across)
         dwq_other = permute(dwq_mine, beside)
-        dwo = grad_wo(idx, o, dz, partner_o, dy_high, dy_low, wo, gain_post)
+        dwo = grad_wo(idx, o, dz, partner_o, dy_high, dy_head, dy_low, wo, gain_post)
         dwo_in = permute(dwo[1], beside)
         dwo_mine = dwo[0] + dwo_in
         dwo_other = permute(dwo_mine, beside)

time: 296 us -> 254 us (0.86)
  Pallas kernels: 208 us -> 181 us
  starting transfers between devices: 29.5 us -> 14.5 us
    pallas_call x1, Pallas kernels: 67.6 us -> 45 us  [forward(): pl.pallas_call(forward_kernel, grid=(done + tiles,), in_specs=[pl.BlockSp...]
    ppermute x13, starting transfers between devices: 29.5 us -> 14.5 us  [permute(): return lax.ppermute(value, 'cp', pairs)]
    pallas_call x1, Pallas kernels: 77.5 us -> 73.9 us  [backward(): pl.pallas_call(backward_kernel, grid=(3 * tiles,), in_specs=[held(q), hel...]
  transfers between devices with their start and end apart: 13 -> 13, of which waited for: 2 -> 2; matrix products, arithmetic and copies ran while one was open for 5% -> 6% of each run, Pallas kernels for 69% -> 69%
where the time goes in v12:
time: 254 us; the launch traced here: 253 us
  Pallas kernels  181 us (71%)
  waiting for transfers between devices  41.5 us (16%)
  starting transfers between devices  14.5 us (6%)
  other arithmetic  9.9 us (4%)
  local copies, waits for them, and re-layouts  5.77 us (2%)
    pallas_call x1, Pallas kernels, backward(): pl.pallas_call(backward_kernel, grid=(3 * tiles,), in_specs=[held(q), hel...  73.9 us
    pallas_call x1, Pallas kernels, forward(): pl.pallas_call(forward_kernel, grid=(done + tiles,), in_specs=[pl.BlockSp...  45 us
    ppermute x13, waiting for transfers between devices, permute(): return lax.ppermute(value, 'cp', pairs)  41.5 us
    pallas_call x1, Pallas kernels, grad_wo(): pl.pallas_call(grad_wo_kernel, grid=(tokens // bt,), in_specs=[pl.BlockSp...  17.7 us
    ppermute x13, starting transfers between devices, permute(): return lax.ppermute(value, 'cp', pairs)  14.5 us
    pallas_call x1, Pallas kernels, post(): pl.pallas_call(post_kernel, grid=(tokens // bq,), in_specs=[rows2(heads *...  14.1 us
    pallas_call x1, Pallas kernels, tail(): pl.pallas_call(tail_kernel, grid=(tokens // bt,), in_specs=[pl.BlockSpec(...  12.7 us
    pallas_call x1, Pallas kernels, join_rows(): pl.pallas_call(join_rows_kernel, grid=(2, steps), in_specs=[pl.BlockSpec(...  6.17 us
  transfers between devices with their start and end apart: 13, of which 2 were waited for; matrix products, arithmetic and copies ran while one was open for 6% of the time, Pallas kernels for 69%

profile of v12, /device:TPU:0, one launch (start us, length us, event | category | flops | bytes accessed | tf_op | source)
XLA Modules:
  0.0 253.1 jit_solution(8382264689809585060)
XLA Ops:
  0.6 1.3 collective-permute-start.9
  1.9 0.0 copy-start.8
  2.0 3.6 %copy.22 = bf16[144,8,4,256]{3,1,2,0:T(8,128)(2,1)} copy(bf16[144,8,4,256]{3,2,1,0:T(4,128)(2,1)} %bitcast.21) | data formatting | bytes 4718592
  5.6 3.0 %multiply_sine_fusion = (f32[1024,128]{1,0:T(8,128)}, f32[1024,128]{1,0:T(8,128)}) fusion(f32[128]{0:T(128)S(1)} %multiply_power_fusion, f32[1024]{0:T(1024)S(1)} %bitcast.28), kind=kLoop, calls=%fused_computation.3 | loop fusion | flops 131072 | bytes 1053184 | tf_op jit(solution)/shard_map/sin | solution.py:803
  8.7 45.0 %forward.1 = (bf16[1152,1024]{1,0:T(8,128)(2,1)}, bf16[4,1024,256]{2,1,0:T(8,128)(2,1)}, bf16[2,1024,256]{2,1,0:T(8,128)(2,1)}, bf16[2,1024,256]{2,1,0:T(8,128)(...) custom-call(bf16[1024,1152]{1,0:T(8,128)(2,1)} %bitcast.29, ...), custom_call_target="tpu_custom_call" | custom-call | flops 10000000000 | bytes 10000000 | tf_op jit(solution)/shard_map/forward/pallas_call | solution.py:240
  53.7 5.1 %collective-permute-start.8 = (bf16[1024,1024]{1,0:T(8,128)(2,1)}, bf16[1024,1024]{1,0:T(8,128)(2,1)}, u32[]{:S(2)}, u32[]{:S(2)}) collective-permute-start(bf16[1024,1024]{1,0:T(8,128)(2,1)} %get-tuple-element.37.o_ref), channel_id=1, source_target_pairs={{0,2},{2,0},{1,3},{3,1},{4,6},{6,4},{5,7},{7,5},{8,10},{10,8},{9,1... | collective-permute-start | bytes 6291464 | tf_op jit(solution)/shard_map/ppermute | solution.py:786
  58.8 1.3 slice_bitcast_fusion
  60.1 3.1 %collective-permute-start.10 = (bf16[768,1152]{1,0:T(8,128)(2,1)}, bf16[768,1152]{1,0:T(8,128)(2,1)}, u32[]{:S(2)}, u32[]{:S(2)}) collective-permute-start(bf16[768,1152]{1,0:T(8,128)(2,1)} %slice_bitcast_fusion), channel_id=1, source_target_pairs={{0,2},{1,3},{4,6},{5,7},{8,10},{9,11},{12,14},{13,15}} | collective-permute-start | bytes 5308424 | tf_op jit(solution)/shard_map/ppermute | solution.py:786
  63.3 14.1 %post.1 = (bf16[1024,1152]{1,0:T(8,128)(2,1)}, bf16[4,1024,256]{2,1,0:T(8,128)(2,1)}, bf16[1024,1152]{1,0:T(8,128)(2,1)}, f32[8,1024]{1,0:T(8,128)}, f32[1,1152]{1,0:T(1,128)}) custom-call(bf16[1024,1024]{1,0:T(8,128)(2,1)} %get-tuple-element.37.o_ref, f32[4,1024,256]{2,1,0:T(8,128)} %get-tuple-element.38.out_ref, f32[1024,128]{1,0:T(8,128)} %get-tuple-element.39.lse_ref, ...), custom_call_target="tpu_custom_call" | custom-call | flops 10000000000 | bytes 10000000 | tf_op jit(solution)/shard_map/post/pallas_call | solution.py:331
  77.4 73.9 %backward.1 = (f32[2,1024,256]{2,1,0:T(8,128)}, bf16[1024,1024]{1,0:T(8,128)(2,1)}, f32[1152,512]{1,0:T(8,128)}) custom-call(bf16[4,1024,256]{2,1,0:T(8,128)(2,1)} %get-tuple-element.41.q_ref, bf16[4,1024,256]{2,1,0:T(8,128)(2,1)} %get-tuple-element.42.do_ref, f32[8,1024]{1,0:T(8,128)} %get-tuple-element.43.stat_ref, ...), custom_call_target="tpu_custom_call" | custom-call | flops 10000000000 | bytes 10000000 | tf_op jit(solution)/shard_map/backward/pallas_call | solution.py:575
  151.3 1.3 collective-permute-start
  152.6 12.7 %tail.1 = (bf16[1024,1152]{1,0:T(8,128)(2,1)}, f32[1160,256]{1,0:T(8,128)}, f32[1160,256]{1,0:T(8,128)}) custom-call(s32[1]{0:T(128)} %bitcast.7.idx_ref, f32[2,1024,256]{2,1,0:T(8,128)} %get-tuple-element.49.down_ref, f32[1024,128]{1,0:T(8,128)} %get-tuple-element.75.cos_ref, f32[1024,128]{1,0:T(8,128)} %get-tuple-element.74.sin_ref, ...), custom_call_target="tpu_custom_call" | custom-call | flops 10000000000 | bytes 10000000 | tf_op jit(solution)/shard_map/tail/pallas_call | solution.py:659
  165.3 0.0 collective-permute-start.2
  165.4 17.7 %grad_wo.1 = (f32[512,1152]{1,0:T(8,128)}, f32[512,1152]{1,0:T(8,128)}) custom-call(s32[1]{0:T(128)} %bitcast.7.idx_ref, bf16[1024,1024]{1,0:T(8,128)(2,1)} %get-tuple-element.37.o_ref, bf16[1024,1152]{1,0:T(8,128)(2,1)} %get-tuple-element.60.dz_ref, bf16[1024,1024]{1,0:T(8,128)(2,1)} %collective-permute-done.8.po_ref, ...), custom_call_target="tpu_custom_call" | custom-call | flops 10000000000 | bytes 10000000 | tf_op jit(solution)/shard_map/grad_wo/pallas_call | solution.py:374
  183.0 0.5 collective-permute-start.11
  183.5 0.1 collective-permute-start.4
  183.5 1.4 slice_add_fusion.1.a_ref
  185.0 0.8 collective-permute-start.6
  185.7 35.5 %collective-permute-done.6.b_ref = f32[768,256]{1,0:T(8,128)S(1)} collective-permute-done((f32[768,256]{1,0:T(8,128)S(1)}, f32[768,256]{1,0:T(8,128)S(1)}, u32[]{:S(2)}, u32[]{:S(2)}) %collective-permute-start.6) | collective-permute-done | bytes 786464 | tf_op jit(solution)/shard_map/ppermute | solution.py:786
  221.2 1.3 slice_add_fusion.3.a_ref
  222.6 1.8 collective-permute-start.3
  224.4 1.9 add.18.mine_ref
  226.4 0.8 slice_add_fusion.2.c_ref
  227.2 1.0 slice_add_fusion.c_ref
  228.2 6.0 %collective-permute-done.3.b_ref = f32[392,256]{1,0:T(8,128)} collective-permute-done((f32[392,256]{1,0:T(8,128)S(1)}, f32[392,256]{1,0:T(8,128)}, u32[]{:S(2)}, u32[]{:S(2)}) %collective-permute-start.3) | collective-permute-done | bytes 401440 | tf_op jit(solution)/shard_map/ppermute | solution.py:786
  234.2 0.3 add.23.mine_ref
  234.5 0.5 collective-permute-start.12
  235.0 3.1 %join_first.1 = (f32[2304,128]{1,0:T(8,128)}, f32[2304,128]{1,0:T(8,128)}) custom-call(s32[1]{0:T(128)} %bitcast.7.idx_ref, f32[768,256]{1,0:T(8,128)} %copy-done.6, f32[768,256]{1,0:T(8,128)} %copy-done.9, f32[768,256]{1,0:T(8,128)} %slice_add_fusion.c_ref, f32[768,256]{1,0:T(8,128)} %collective-permute-done.7.d_ref), custom_call_target="tpu_custom_call" | custom-call | flops 10000000000 | bytes 10000000 | tf_op jit(solution)/shard_map/join_first/pallas_call | solution.py:746
  238.1 0.7 copy-done.10
  238.9 2.3 join_last.1
  241.2 5.8 %join_wide.1 = f32[9216,128]{1,0:T(8,128)} custom-call(s32[1]{0:T(128)} %bitcast.7.idx_ref, f32[1152,512]{1,0:T(8,128)} %add.18.mine_ref, f32[1152,512]{1,0:T(8,128)} %collective-permute-done.1.other_ref), custom_call_target="tpu_custom_call" | custom-call | flops 10000000000 | bytes 10000000 | tf_op jit(solution)/shard_map/join_wide/pallas_call | solution.py:707
  247.0 6.2 %join_rows.1 = f32[1024,1152]{1,0:T(8,128)} custom-call(s32[1]{0:T(128)} %bitcast.7.idx_ref, f32[512,1152]{1,0:T(8,128)} %copy-done.2, f32[512,1152]{1,0:T(8,128)} %collective-permute-done.12.other_ref), custom_call_target="tpu_custom_call" | custom-call | flops 10000000000 | bytes 10000000 | tf_op jit(solution)/shard_map/join_rows/pallas_call | solution.py:769
  (36 shorter events, 0.1 us)
Async XLA Ops:
  0.6 164.7 %collective-permute-start.9 = (bf16[1024,1152]{1,0:T(8,128)(2,1)}, bf16[1024,1152]{1,0:T(8,128)(2,1)}, u32[]{:S(2)}, u32[]{:S(2)}) collective-permute-start(bf16[1024,1152]{1,0:T(8,128)(2,1)} %bitcast.24), channel_id=1, source_target_pairs={{2,0},{3,1},{6,4},{7,5},{10,8},{11,9},{14,12},{15,13}} | collective-permute-start | bytes 7077896 | tf_op jit(solution)/shard_map/ppermute | solution.py:786
  1.9 3.7 %copy-start.8 = (s32[1,1024]{1,0:T(1,128)S(1)}, s32[1,1024]{1,0:T(1,128)}, u32[]{:S(2)}) copy-start(s32[1,1024]{1,0:T(1,128)} %param.10) | copy-start | bytes 12292
  8.7 50.1 %copy-start.3 = (bf16[1,1024,1152]{2,1,0:T(8,128)(2,1)S(1)}, bf16[1,1024,1152]{2,1,0:T(8,128)(2,1)}, u32[]{:S(2)}) copy-start(bf16[1,1024,1152]{2,1,0:T(8,128)(2,1)} %param.11) | copy-start | bytes 7077892
  53.7 111.7 %collective-permute-start.8 = (bf16[1024,1024]{1,0:T(8,128)(2,1)}, bf16[1024,1024]{1,0:T(8,128)(2,1)}, u32[]{:S(2)}, u32[]{:S(2)}) collective-permute-start(bf16[1024,1024]{1,0:T(8,128)(2,1)} %get-tuple-element.37.o_ref), channel_id=1, source_target_pairs={{0,2},{2,0},{1,3},{3,1},{4,6},{6,4},{5,7},{7,5},{8,10},{10,8},{9,1... | collective-permute-start | bytes 6291464 | tf_op jit(solution)/shard_map/ppermute | solution.py:786
  60.1 105.2 %collective-permute-start.10 = (bf16[768,1152]{1,0:T(8,128)(2,1)}, bf16[768,1152]{1,0:T(8,128)(2,1)}, u32[]{:S(2)}, u32[]{:S(2)}) collective-permute-start(bf16[768,1152]{1,0:T(8,128)(2,1)} %slice_bitcast_fusion), channel_id=1, source_target_pairs={{0,2},{1,3},{4,6},{5,7},{8,10},{9,11},{12,14},{13,15}} | collective-permute-start | bytes 5308424 | tf_op jit(solution)/shard_map/ppermute | solution.py:786
  151.3 73.1 %collective-permute-start = (f32[1152,512]{1,0:T(8,128)}, f32[1152,512]{1,0:T(8,128)S(1)}, u32[]{:S(2)}, u32[]{:S(2)}) collective-permute-start(f32[1152,512]{1,0:T(8,128)} %get-tuple-element.53), channel_id=1, source_target_pairs={{0,2},{2,0},{1,3},{3,1},{4,6},{6,4},{5,7},{7,5},{8,10},{10,8},{9,1... | collective-permute-start | bytes 7077896 | tf_op jit(solution)/shard_map/ppermute | solution.py:786
  165.3 18.3 %collective-permute-start.2 = (f32[1160,256]{1,0:T(8,128)}, f32[1160,256]{1,0:T(8,128)}, u32[]{:S(2)}, u32[]{:S(2)}) collective-permute-start(f32[1160,256]{1,0:T(8,128)} %get-tuple-element.55), channel_id=1, source_target_pairs={{0,1},{1,0},{2,3},{3,2},{4,5},{5,4},{6,7},{7,6},{8,9},{9,8},{10,11... | collective-permute-start | bytes 3563528 | tf_op jit(solution)/shard_map/ppermute | solution.py:786
  165.3 18.1 %copy-start.5 = (f32[1160,256]{1,0:T(8,128)S(1)}, f32[1160,256]{1,0:T(8,128)}, u32[]{:S(2)}) copy-start(f32[1160,256]{1,0:T(8,128)} %get-tuple-element.54) | copy-start | bytes 3563524
  183.0 41.4 %copy-start = (f32[1152,512]{1,0:T(8,128)S(1)}, f32[1152,512]{1,0:T(8,128)}, u32[]{:S(2)}) copy-start(f32[1152,512]{1,0:T(8,128)} %get-tuple-element.53) | copy-start | bytes 7077892
  183.0 51.1 %collective-permute-start.11 = (f32[512,1152]{1,0:T(8,128)}, f32[512,1152]{1,0:T(8,128)S(1)}, u32[]{:S(2)}, u32[]{:S(2)}) collective-permute-start(f32[512,1152]{1,0:T(8,128)} %get-tuple-element.63), channel_id=1, source_target_pairs={{0,1},{1,0},{2,3},{3,2},{4,5},{5,4},{6,7},{7,6},{8,9},{9,8},{10,11... | collective-permute-start | bytes 7077896 | tf_op jit(solution)/shard_map/ppermute | solution.py:786
  183.5 42.9 %collective-permute-start.4 = (f32[1160,256]{1,0:T(8,128)S(1)}, f32[1160,256]{1,0:T(8,128)S(1)}, u32[]{:S(2)}, u32[]{:S(2)}) collective-permute-start(f32[1160,256]{1,0:T(8,128)S(1)} %copy-done.5), channel_id=1, source_target_pairs={{0,1},{1,0},{2,3},{3,2},{4,5},{5,4},{6,7},{7,6},{8,9},{9,8},{10,11... | collective-permute-start | bytes 3563528 | tf_op jit(solution)/shard_map/ppermute | solution.py:786
  185.0 36.3 %copy-start.6 = (f32[768,256]{1,0:T(8,128)}, f32[768,256]{1,0:T(8,128)S(1)}, u32[]{:S(2)}) copy-start(f32[768,256]{1,0:T(8,128)S(1)} %slice_add_fusion.1.a_ref) | copy-start | bytes 2359300
  185.0 36.2 %collective-permute-start.6 = (f32[768,256]{1,0:T(8,128)S(1)}, f32[768,256]{1,0:T(8,128)S(1)}, u32[]{:S(2)}, u32[]{:S(2)}) collective-permute-start(f32[768,256]{1,0:T(8,128)S(1)} %slice_add_fusion.1.a_ref), channel_id=1, source_target_pairs={{0,2},{2,0},{1,3},{3,1},{4,6},{6,4},{5,7},{7,5},{8,10},{10,8},{9,1... | collective-permute-start | bytes 2359304 | tf_op jit(solution)/shard_map/ppermute | solution.py:786
  221.2 5.1 %copy-start.9 = (f32[768,256]{1,0:T(8,128)}, f32[768,256]{1,0:T(8,128)S(1)}, u32[]{:S(2)}) copy-start(f32[768,256]{1,0:T(8,128)S(1)} %collective-permute-done.6.b_ref) | copy-start | bytes 2359300
  221.2 13.8 %collective-permute-start.7 = (f32[768,256]{1,0:T(8,128)S(1)}, f32[768,256]{1,0:T(8,128)}, u32[]{:S(2)}, u32[]{:S(2)}) collective-permute-start(f32[768,256]{1,0:T(8,128)S(1)} %collective-permute-done.6.b_ref), channel_id=1, source_target_pairs={{0,1},{1,0},{2,3},{3,2},{4,5},{5,4},{6,7},{7,6},{8,9},{9,8},{10,11... | collective-permute-start | bytes 2359304 | tf_op jit(solution)/shard_map/ppermute | solution.py:786
  222.6 3.8 %copy-start.7 = (f32[392,256]{1,0:T(8,128)}, f32[392,256]{1,0:T(8,128)S(1)}, u32[]{:S(2)}) copy-start(f32[392,256]{1,0:T(8,128)S(1)} %slice_add_fusion.3.a_ref) | copy-start | bytes 1204228
  222.6 3.8 %copy-start.4 = (f32[1160,256]{1,0:T(8,128)S(1)}, f32[1160,256]{1,0:T(8,128)}, u32[]{:S(2)}) copy-start(f32[1160,256]{1,0:T(8,128)} %get-tuple-element.55) | copy-start | bytes 3563524
  222.6 11.6 %collective-permute-start.3 = (f32[392,256]{1,0:T(8,128)S(1)}, f32[392,256]{1,0:T(8,128)}, u32[]{:S(2)}, u32[]{:S(2)}) collective-permute-start(f32[392,256]{1,0:T(8,128)S(1)} %slice_add_fusion.3.a_ref), channel_id=1, source_target_pairs={{0,2},{2,0},{1,3},{3,1},{4,6},{6,4},{5,7},{7,5},{8,10},{10,8},{9,1... | collective-permute-start | bytes 1204232 | tf_op jit(solution)/shard_map/ppermute | solution.py:786
  226.3 7.8 %copy-start.1 = (f32[512,1152]{1,0:T(8,128)S(1)}, f32[512,1152]{1,0:T(8,128)}, u32[]{:S(2)}) copy-start(f32[512,1152]{1,0:T(8,128)} %get-tuple-element.62) | copy-start | bytes 7077892
  226.3 14.9 %collective-permute-start.1 = (f32[1152,512]{1,0:T(8,128)}, f32[1152,512]{1,0:T(8,128)}, u32[]{:S(2)}, u32[]{:S(2)}) collective-permute-start(f32[1152,512]{1,0:T(8,128)} %add.18.mine_ref), channel_id=1, source_target_pairs={{0,1},{1,0},{2,3},{3,2},{4,5},{5,4},{6,7},{7,6},{8,9},{9,8},{10,11... | collective-permute-start | bytes 7077896 | tf_op jit(solution)/shard_map/ppermute | solution.py:786
  234.1 4.0 %collective-permute-start.5 = (f32[392,256]{1,0:T(8,128)}, f32[392,256]{1,0:T(8,128)S(1)}, u32[]{:S(2)}, u32[]{:S(2)}) collective-permute-start(f32[392,256]{1,0:T(8,128)} %collective-permute-done.3.b_ref), channel_id=1, source_target_pairs={{0,1},{1,0},{2,3},{3,2},{4,5},{5,4},{6,7},{7,6},{8,9},{9,8},{10,11... | collective-permute-start | bytes 1204232 | tf_op jit(solution)/shard_map/ppermute | solution.py:786
  234.5 3.6 %copy-start.2 = (f32[512,1152]{1,0:T(8,128)}, f32[512,1152]{1,0:T(8,128)S(1)}, u32[]{:S(2)}) copy-start(f32[512,1152]{1,0:T(8,128)S(1)} %add.23.mine_ref) | copy-start | bytes 7077892
  234.5 12.5 %collective-permute-start.12 = (f32[512,1152]{1,0:T(8,128)S(1)}, f32[512,1152]{1,0:T(8,128)}, u32[]{:S(2)}, u32[]{:S(2)}) collective-permute-start(f32[512,1152]{1,0:T(8,128)S(1)} %add.23.mine_ref), channel_id=1, source_target_pairs={{0,1},{1,0},{2,3},{3,2},{4,5},{5,4},{6,7},{7,6},{8,9},{9,8},{10,11... | collective-permute-start | bytes 7077896 | tf_op jit(solution)/shard_map/ppermute | solution.py:786
  238.1 0.8 copy-start.10

commit v13 on v12

--- a/solution.py
+++ b/solution.py
@@ -741,8 +741,9 @@
     steps = rows // bd
     first = dim // bd - 1 if last else 0
     out_spec = pl.BlockSpec((bd * 2, 128), lambda i: (i + first, 0))
-    part_spec = whole(parts[0].shape) if last else rows_spec(bd, width)
+    part_spec = pl.BlockSpec(memory_space=pltpu.VMEM) if last else rows_spec(bd, width)
     pair = [jax.ShapeDtypeStruct((dim * 2, 128), F32)] * 2
+    held = [pltpu.with_memory_space_constraint(p, pltpu.VMEM) if last and n % 2 else p for n, p in enumerate(parts)]
     return pl.pallas_call(
         functools.partial(join_pair_kernel, last=last),
         grid=(steps,),
@@ -753,7 +754,7 @@
         compiler_params=params(),
         cost_estimate=COST,
         name="join_last" if last else "join_first",
-    )(idx, *parts, *begun)
+    )(idx, *held, *begun)
 
 
 def join_rows_kernel(idx_ref, mine_ref, other_ref, out_ref):

time: 254 us -> 253 us (level)
  no operation moved by 1% of the time
where the time goes in v13:
time: 253 us; the launch traced here: 252 us
  Pallas kernels  180 us (71%)
  waiting for transfers between devices  41.7 us (16%)
  starting transfers between devices  14.5 us (6%)
  other arithmetic  9.89 us (4%)
  local copies, waits for them, and re-layouts  5.01 us (2%)
    pallas_call x1, Pallas kernels, backward(): pl.pallas_call(backward_kernel, grid=(3 * tiles,), in_specs=[held(q), hel...  73.8 us
    pallas_call x1, Pallas kernels, forward(): pl.pallas_call(forward_kernel, grid=(done + tiles,), in_specs=[pl.BlockSp...  45 us
    ppermute x13, waiting for transfers between devices, permute(): return lax.ppermute(value, 'cp', pairs)  41.7 us
    pallas_call x1, Pallas kernels, grad_wo(): pl.pallas_call(grad_wo_kernel, grid=(tokens // bt,), in_specs=[pl.BlockSp...  17.4 us
    ppermute x13, starting transfers between devices, permute(): return lax.ppermute(value, 'cp', pairs)  14.5 us
    pallas_call x1, Pallas kernels, post(): pl.pallas_call(post_kernel, grid=(tokens // bq,), in_specs=[rows2(heads *...  14.1 us
    pallas_call x1, Pallas kernels, tail(): pl.pallas_call(tail_kernel, grid=(tokens // bt,), in_specs=[pl.BlockSpec(...  12.7 us
    pallas_call x1, Pallas kernels, join_rows(): pl.pallas_call(join_rows_kernel, grid=(2, steps), in_specs=[pl.BlockSpec(...  6.17 us
  transfers between devices with their start and end apart: 13, of which 2 were waited for; matrix products, arithmetic and copies ran while one was open for 6% of the time, Pallas kernels for 69%

profile of v13, /device:TPU:0, one launch (start us, length us, event | category | flops | bytes accessed | tf_op | source)
XLA Modules:
  0.0 252.1 jit_solution(4250385005070547170)
XLA Ops:
  0.6 1.3 collective-permute-start.9
  1.9 0.0 copy-start.7
  2.0 3.6 %copy.22 = bf16[144,8,4,256]{3,1,2,0:T(8,128)(2,1)} copy(bf16[144,8,4,256]{3,2,1,0:T(4,128)(2,1)} %bitcast.21) | data formatting | bytes 4718592
  5.6 3.0 %multiply_sine_fusion = (f32[1024,128]{1,0:T(8,128)}, f32[1024,128]{1,0:T(8,128)}) fusion(f32[128]{0:T(128)S(1)} %multiply_power_fusion, f32[1024]{0:T(1024)S(1)} %bitcast.28), kind=kLoop, calls=%fused_computation.3 | loop fusion | flops 131072 | bytes 1053184 | tf_op jit(solution)/shard_map/sin | solution.py:804
  8.7 45.0 %forward.1 = (bf16[1152,1024]{1,0:T(8,128)(2,1)}, bf16[4,1024,256]{2,1,0:T(8,128)(2,1)}, bf16[2,1024,256]{2,1,0:T(8,128)(2,1)}, bf16[2,1024,256]{2,1,0:T(8,128)(...) custom-call(bf16[1024,1152]{1,0:T(8,128)(2,1)} %bitcast.29, ...), custom_call_target="tpu_custom_call" | custom-call | flops 10000000000 | bytes 10000000 | tf_op jit(solution)/shard_map/forward/pallas_call | solution.py:240
  53.7 5.1 %collective-permute-start.8 = (bf16[1024,1024]{1,0:T(8,128)(2,1)}, bf16[1024,1024]{1,0:T(8,128)(2,1)}, u32[]{:S(2)}, u32[]{:S(2)}) collective-permute-start(bf16[1024,1024]{1,0:T(8,128)(2,1)} %get-tuple-element.37.o_ref), channel_id=1, source_target_pairs={{0,2},{2,0},{1,3},{3,1},{4,6},{6,4},{5,7},{7,5},{8,10},{10,8},{9,1... | collective-permute-start | bytes 6291464 | tf_op jit(solution)/shard_map/ppermute | solution.py:787
  58.7 1.3 slice_bitcast_fusion
  60.1 3.2 %collective-permute-start.10 = (bf16[768,1152]{1,0:T(8,128)(2,1)}, bf16[768,1152]{1,0:T(8,128)(2,1)}, u32[]{:S(2)}, u32[]{:S(2)}) collective-permute-start(bf16[768,1152]{1,0:T(8,128)(2,1)} %slice_bitcast_fusion), channel_id=1, source_target_pairs={{0,2},{1,3},{4,6},{5,7},{8,10},{9,11},{12,14},{13,15}} | collective-permute-start | bytes 5308424 | tf_op jit(solution)/shard_map/ppermute | solution.py:787
  63.3 14.1 %post.1 = (bf16[1024,1152]{1,0:T(8,128)(2,1)}, bf16[4,1024,256]{2,1,0:T(8,128)(2,1)}, bf16[1024,1152]{1,0:T(8,128)(2,1)}, f32[8,1024]{1,0:T(8,128)}, f32[1,1152]{1,0:T(1,128)}) custom-call(bf16[1024,1024]{1,0:T(8,128)(2,1)} %get-tuple-element.37.o_ref, f32[4,1024,256]{2,1,0:T(8,128)} %get-tuple-element.38.out_ref, f32[1024,128]{1,0:T(8,128)} %get-tuple-element.39.lse_ref, ...), custom_call_target="tpu_custom_call" | custom-call | flops 10000000000 | bytes 10000000 | tf_op jit(solution)/shard_map/post/pallas_call | solution.py:331
  77.4 73.8 %backward.1 = (f32[2,1024,256]{2,1,0:T(8,128)}, bf16[1024,1024]{1,0:T(8,128)(2,1)}, f32[1152,512]{1,0:T(8,128)}) custom-call(bf16[4,1024,256]{2,1,0:T(8,128)(2,1)} %get-tuple-element.41.q_ref, bf16[4,1024,256]{2,1,0:T(8,128)(2,1)} %get-tuple-element.42.do_ref, f32[8,1024]{1,0:T(8,128)} %get-tuple-element.43.stat_ref, ...), custom_call_target="tpu_custom_call" | custom-call | flops 10000000000 | bytes 10000000 | tf_op jit(solution)/shard_map/backward/pallas_call | solution.py:575
  151.2 1.4 collective-permute-start
  152.6 12.7 %tail.1 = (bf16[1024,1152]{1,0:T(8,128)(2,1)}, f32[1160,256]{1,0:T(8,128)}, f32[1160,256]{1,0:T(8,128)}) custom-call(s32[1]{0:T(128)} %bitcast.7.idx_ref, f32[2,1024,256]{2,1,0:T(8,128)} %get-tuple-element.49.down_ref, f32[1024,128]{1,0:T(8,128)} %get-tuple-element.75.cos_ref, f32[1024,128]{1,0:T(8,128)} %get-tuple-element.74.sin_ref, ...), custom_call_target="tpu_custom_call" | custom-call | flops 10000000000 | bytes 10000000 | tf_op jit(solution)/shard_map/tail/pallas_call | solution.py:659
  165.3 0.0 collective-permute-start.2
  165.4 17.4 %grad_wo.1 = (f32[512,1152]{1,0:T(8,128)}, f32[512,1152]{1,0:T(8,128)}) custom-call(s32[1]{0:T(128)} %bitcast.7.idx_ref, bf16[1024,1024]{1,0:T(8,128)(2,1)} %get-tuple-element.37.o_ref, bf16[1024,1152]{1,0:T(8,128)(2,1)} %get-tuple-element.60.dz_ref, bf16[1024,1024]{1,0:T(8,128)(2,1)} %collective-permute-done.8.po_ref, ...), custom_call_target="tpu_custom_call" | custom-call | flops 10000000000 | bytes 10000000 | tf_op jit(solution)/shard_map/grad_wo/pallas_call | solution.py:374
  182.8 0.5 collective-permute-start.11
  183.3 0.0 collective-permute-start.4
  183.3 1.4 slice_add_fusion.1.a_ref
  184.7 0.0 copy-start.5
  184.7 0.7 collective-permute-start.6
  185.4 35.8 %collective-permute-done.6.b_ref = f32[768,256]{1,0:T(8,128)S(1)} collective-permute-done((f32[768,256]{1,0:T(8,128)S(1)}, f32[768,256]{1,0:T(8,128)S(1)}, u32[]{:S(2)}, u32[]{:S(2)}) %collective-permute-start.6) | collective-permute-done | bytes 786464 | tf_op jit(solution)/shard_map/ppermute | solution.py:787
  221.2 1.3 slice_add_fusion.3.a_ref
  222.6 1.8 collective-permute-start.3
  224.4 1.9 add.18.mine_ref
  226.4 0.8 slice_add_fusion.2.c_ref
  227.2 1.0 slice_add_fusion.c_ref
  228.2 5.9 %collective-permute-done.3.b_ref = f32[392,256]{1,0:T(8,128)S(1)} collective-permute-done((f32[392,256]{1,0:T(8,128)S(1)}, f32[392,256]{1,0:T(8,128)S(1)}, u32[]{:S(2)}, u32[]{:S(2)}) %collective-permute-start.3) | collective-permute-done | bytes 401440 | tf_op jit(solution)/shard_map/ppermute | solution.py:787
  234.1 0.3 add.23.mine_ref
  234.4 0.5 collective-permute-start.12
  234.9 3.1 %join_first.1 = (f32[2304,128]{1,0:T(8,128)}, f32[2304,128]{1,0:T(8,128)}) custom-call(s32[1]{0:T(128)} %bitcast.7.idx_ref, f32[768,256]{1,0:T(8,128)} %copy-done.5, f32[768,256]{1,0:T(8,128)} %copy-done.8, f32[768,256]{1,0:T(8,128)} %slice_add_fusion.c_ref, f32[768,256]{1,0:T(8,128)} %collective-permute-done.7.d_ref), custom_call_target="tpu_custom_call" | custom-call | flops 10000000000 | bytes 10000000 | tf_op jit(solution)/shard_map/join_first/pallas_call | solution.py:747
  238.0 2.2 join_last.1
  240.2 5.7 %join_wide.1 = f32[9216,128]{1,0:T(8,128)} custom-call(s32[1]{0:T(128)} %bitcast.7.idx_ref, f32[1152,512]{1,0:T(8,128)} %add.18.mine_ref, f32[1152,512]{1,0:T(8,128)} %collective-permute-done.1.other_ref), custom_call_target="tpu_custom_call" | custom-call | flops 10000000000 | bytes 10000000 | tf_op jit(solution)/shard_map/join_wide/pallas_call | solution.py:707
  245.9 6.2 %join_rows.1 = f32[1024,1152]{1,0:T(8,128)} custom-call(s32[1]{0:T(128)} %bitcast.7.idx_ref, f32[512,1152]{1,0:T(8,128)} %copy-done.2, f32[512,1152]{1,0:T(8,128)} %collective-permute-done.12.other_ref), custom_call_target="tpu_custom_call" | custom-call | flops 10000000000 | bytes 10000000 | tf_op jit(solution)/shard_map/join_rows/pallas_call | solution.py:770
  (32 shorter events, 0.1 us)
Async XLA Ops:
  0.6 164.7 %collective-permute-start.9 = (bf16[1024,1152]{1,0:T(8,128)(2,1)}, bf16[1024,1152]{1,0:T(8,128)(2,1)}, u32[]{:S(2)}, u32[]{:S(2)}) collective-permute-start(bf16[1024,1152]{1,0:T(8,128)(2,1)} %bitcast.24), channel_id=1, source_target_pairs={{2,0},{3,1},{6,4},{7,5},{10,8},{11,9},{14,12},{15,13}} | collective-permute-start | bytes 7077896 | tf_op jit(solution)/shard_map/ppermute | solution.py:787
  1.9 3.7 %copy-start.7 = (s32[1,1024]{1,0:T(1,128)S(1)}, s32[1,1024]{1,0:T(1,128)}, u32[]{:S(2)}) copy-start(s32[1,1024]{1,0:T(1,128)} %param.10) | copy-start | bytes 12292
  8.7 50.1 %copy-start.3 = (bf16[1,1024,1152]{2,1,0:T(8,128)(2,1)S(1)}, bf16[1,1024,1152]{2,1,0:T(8,128)(2,1)}, u32[]{:S(2)}) copy-start(bf16[1,1024,1152]{2,1,0:T(8,128)(2,1)} %param.11) | copy-start | bytes 7077892
  53.7 111.7 %collective-permute-start.8 = (bf16[1024,1024]{1,0:T(8,128)(2,1)}, bf16[1024,1024]{1,0:T(8,128)(2,1)}, u32[]{:S(2)}, u32[]{:S(2)}) collective-permute-start(bf16[1024,1024]{1,0:T(8,128)(2,1)} %get-tuple-element.37.o_ref), channel_id=1, source_target_pairs={{0,2},{2,0},{1,3},{3,1},{4,6},{6,4},{5,7},{7,5},{8,10},{10,8},{9,1... | collective-permute-start | bytes 6291464 | tf_op jit(solution)/shard_map/ppermute | solution.py:787
  60.1 105.3 %collective-permute-start.10 = (bf16[768,1152]{1,0:T(8,128)(2,1)}, bf16[768,1152]{1,0:T(8,128)(2,1)}, u32[]{:S(2)}, u32[]{:S(2)}) collective-permute-start(bf16[768,1152]{1,0:T(8,128)(2,1)} %slice_bitcast_fusion), channel_id=1, source_target_pairs={{0,2},{1,3},{4,6},{5,7},{8,10},{9,11},{12,14},{13,15}} | collective-permute-start | bytes 5308424 | tf_op jit(solution)/shard_map/ppermute | solution.py:787
  151.2 73.2 %collective-permute-start = (f32[1152,512]{1,0:T(8,128)}, f32[1152,512]{1,0:T(8,128)S(1)}, u32[]{:S(2)}, u32[]{:S(2)}) collective-permute-start(f32[1152,512]{1,0:T(8,128)} %get-tuple-element.53), channel_id=1, source_target_pairs={{0,2},{2,0},{1,3},{3,1},{4,6},{6,4},{5,7},{7,5},{8,10},{10,8},{9,1... | collective-permute-start | bytes 7077896 | tf_op jit(solution)/shard_map/ppermute | solution.py:787
  165.3 18.0 %collective-permute-start.2 = (f32[1160,256]{1,0:T(8,128)}, f32[1160,256]{1,0:T(8,128)S(1)}, u32[]{:S(2)}, u32[]{:S(2)}) collective-permute-start(f32[1160,256]{1,0:T(8,128)} %get-tuple-element.55), channel_id=1, source_target_pairs={{0,1},{1,0},{2,3},{3,2},{4,5},{5,4},{6,7},{7,6},{8,9},{9,8},{10,11... | collective-permute-start | bytes 3563528 | tf_op jit(solution)/shard_map/ppermute | solution.py:787
  182.8 41.6 %copy-start = (f32[1152,512]{1,0:T(8,128)S(1)}, f32[1152,512]{1,0:T(8,128)}, u32[]{:S(2)}) copy-start(f32[1152,512]{1,0:T(8,128)} %get-tuple-element.53) | copy-start | bytes 7077892
  182.8 51.3 %collective-permute-start.11 = (f32[512,1152]{1,0:T(8,128)}, f32[512,1152]{1,0:T(8,128)S(1)}, u32[]{:S(2)}, u32[]{:S(2)}) collective-permute-start(f32[512,1152]{1,0:T(8,128)} %get-tuple-element.63), channel_id=1, source_target_pairs={{0,1},{1,0},{2,3},{3,2},{4,5},{5,4},{6,7},{7,6},{8,9},{9,8},{10,11... | collective-permute-start | bytes 7077896 | tf_op jit(solution)/shard_map/ppermute | solution.py:787
  183.3 43.1 %collective-permute-start.4 = (f32[1160,256]{1,0:T(8,128)}, f32[1160,256]{1,0:T(8,128)S(1)}, u32[]{:S(2)}, u32[]{:S(2)}) collective-permute-start(f32[1160,256]{1,0:T(8,128)} %get-tuple-element.54), channel_id=1, source_target_pairs={{0,1},{1,0},{2,3},{3,2},{4,5},{5,4},{6,7},{7,6},{8,9},{9,8},{10,11... | collective-permute-start | bytes 3563528 | tf_op jit(solution)/shard_map/ppermute | solution.py:787
  184.7 36.5 %copy-start.5 = (f32[768,256]{1,0:T(8,128)}, f32[768,256]{1,0:T(8,128)S(1)}, u32[]{:S(2)}) copy-start(f32[768,256]{1,0:T(8,128)S(1)} %slice_add_fusion.1.a_ref) | copy-start | bytes 2359300
  184.7 36.5 %collective-permute-start.6 = (f32[768,256]{1,0:T(8,128)S(1)}, f32[768,256]{1,0:T(8,128)S(1)}, u32[]{:S(2)}, u32[]{:S(2)}) collective-permute-start(f32[768,256]{1,0:T(8,128)S(1)} %slice_add_fusion.1.a_ref), channel_id=1, source_target_pairs={{0,2},{2,0},{1,3},{3,1},{4,6},{6,4},{5,7},{7,5},{8,10},{10,8},{9,1... | collective-permute-start | bytes 2359304 | tf_op jit(solution)/shard_map/ppermute | solution.py:787
  221.2 5.1 %copy-start.8 = (f32[768,256]{1,0:T(8,128)}, f32[768,256]{1,0:T(8,128)S(1)}, u32[]{:S(2)}) copy-start(f32[768,256]{1,0:T(8,128)S(1)} %collective-permute-done.6.b_ref) | copy-start | bytes 2359300
  221.2 13.7 %collective-permute-start.7 = (f32[768,256]{1,0:T(8,128)S(1)}, f32[768,256]{1,0:T(8,128)}, u32[]{:S(2)}, u32[]{:S(2)}) collective-permute-start(f32[768,256]{1,0:T(8,128)S(1)} %collective-permute-done.6.b_ref), channel_id=1, source_target_pairs={{0,1},{1,0},{2,3},{3,2},{4,5},{5,4},{6,7},{7,6},{8,9},{9,8},{10,11... | collective-permute-start | bytes 2359304 | tf_op jit(solution)/shard_map/ppermute | solution.py:787
  222.6 3.8 %copy-start.6 = (f32[392,256]{1,0:T(8,128)}, f32[392,256]{1,0:T(8,128)S(1)}, u32[]{:S(2)}) copy-start(f32[392,256]{1,0:T(8,128)S(1)} %slice_add_fusion.3.a_ref) | copy-start | bytes 1204228
  222.6 3.8 %copy-start.4 = (f32[1160,256]{1,0:T(8,128)S(1)}, f32[1160,256]{1,0:T(8,128)}, u32[]{:S(2)}) copy-start(f32[1160,256]{1,0:T(8,128)} %get-tuple-element.55) | copy-start | bytes 3563524
  222.6 11.5 %collective-permute-start.3 = (f32[392,256]{1,0:T(8,128)S(1)}, f32[392,256]{1,0:T(8,128)S(1)}, u32[]{:S(2)}, u32[]{:S(2)}) collective-permute-start(f32[392,256]{1,0:T(8,128)S(1)} %slice_add_fusion.3.a_ref), channel_id=1, source_target_pairs={{0,2},{2,0},{1,3},{3,1},{4,6},{6,4},{5,7},{7,5},{8,10},{10,8},{9,1... | collective-permute-start | bytes 1204232 | tf_op jit(solution)/shard_map/ppermute | solution.py:787
  226.3 7.7 %copy-start.1 = (f32[512,1152]{1,0:T(8,128)S(1)}, f32[512,1152]{1,0:T(8,128)}, u32[]{:S(2)}) copy-start(f32[512,1152]{1,0:T(8,128)} %get-tuple-element.62) | copy-start | bytes 7077892
  226.3 13.8 %collective-permute-start.1 = (f32[1152,512]{1,0:T(8,128)}, f32[1152,512]{1,0:T(8,128)}, u32[]{:S(2)}, u32[]{:S(2)}) collective-permute-start(f32[1152,512]{1,0:T(8,128)} %add.18.mine_ref), channel_id=1, source_target_pairs={{0,1},{1,0},{2,3},{3,2},{4,5},{5,4},{6,7},{7,6},{8,9},{9,8},{10,11... | collective-permute-start | bytes 7077896 | tf_op jit(solution)/shard_map/ppermute | solution.py:787
  234.0 4.0 %collective-permute-start.5 = (f32[392,256]{1,0:T(8,128)S(1)}, f32[392,256]{1,0:T(8,128)S(1)}, u32[]{:S(2)}, u32[]{:S(2)}) collective-permute-start(f32[392,256]{1,0:T(8,128)S(1)} %collective-permute-done.3.b_ref), channel_id=1, source_target_pairs={{0,1},{1,0},{2,3},{3,2},{4,5},{5,4},{6,7},{7,6},{8,9},{9,8},{10,11... | collective-permute-start | bytes 1204232 | tf_op jit(solution)/shard_map/ppermute | solution.py:787
  234.4 3.6 %copy-start.2 = (f32[512,1152]{1,0:T(8,128)}, f32[512,1152]{1,0:T(8,128)S(1)}, u32[]{:S(2)}) copy-start(f32[512,1152]{1,0:T(8,128)S(1)} %add.23.mine_ref) | copy-start | bytes 7077892
  234.4 11.5 %collective-permute-start.12 = (f32[512,1152]{1,0:T(8,128)S(1)}, f32[512,1152]{1,0:T(8,128)}, u32[]{:S(2)}, u32[]{:S(2)}) collective-permute-start(f32[512,1152]{1,0:T(8,128)S(1)} %add.23.mine_ref), channel_id=1, source_target_pairs={{0,1},{1,0},{2,3},{3,2},{4,5},{5,4},{6,7},{7,6},{8,9},{9,8},{10,11... | collective-permute-start | bytes 7077896 | tf_op jit(solution)/shard_map/ppermute | solution.py:787
